TPU v7x, 32 devices: a whole 2x2x4 slice. The times are simulated.
32 devices in a mesh: dp: 8 (over z, x), seq: 4 (over y, core).
Axes of the slice: x: 2, y: 2, z: 4, core: 2. Of those that a mesh axis runs over, the one named last changes fastest.
Arguments:
- hidden_in: bfloat16 [16, 2048, 768], P('dp', 'seq'), may hold values from -6 to 6
- w_query: bfloat16 [768, 768], P('seq', 'dp'), may hold values from -0.21875 to 0.21875
- w_key: bfloat16 [768, 768], P('seq', 'dp'), may hold values from -0.21875 to 0.21875
- w_value: bfloat16 [768, 768], P('seq', 'dp'), may hold values from -0.21875 to 0.21875
- w_output: bfloat16 [768, 768], P('seq', 'dp'), may hold values from -2.5 to 2.5
- w_inner: bfloat16 [768, 3072], P('seq', 'dp'), may hold values from -0.21875 to 0.21875
- w_outer: bfloat16 [3072, 768], P('dp', 'seq'), may hold values from -0.109375 to 0.109375
- pool_weight: float32 [2, 4, 768], P(None, None, ('dp', 'seq')), may hold values from -3 to 3
- ln_gain: float32 [2, 768], P(None, ('dp', 'seq')), may hold values from 0.25 to 1.75
- ln_bias: float32 [2, 768], P(None, ('dp', 'seq')), may hold values from -1.75 to 1.75
- branch_blocks: int32 [16, 8], P('dp'), may hold values from 64 to 256
- grad_out: bfloat16 [16, 2048, 768], P('dp', 'seq'), may hold values from -8 to 8
Outputs:
- hidden_out: bfloat16 [16, 2048, 768], P('dp', 'seq')
- grad_in: bfloat16 [16, 2048, 768], P('dp', 'seq')
- grad_query: float32 [768, 768], P('seq', 'dp')
- grad_key: float32 [768, 768], P('seq', 'dp')
- grad_value: float32 [768, 768], P('seq', 'dp')
- grad_output: float32 [768, 768], P('seq', 'dp')
- grad_inner: float32 [768, 3072], P('seq', 'dp')
- grad_outer: float32 [3072, 768], P('dp', 'seq')
- grad_pool: float32 [2, 4, 768], P(None, None, ('dp', 'seq'))
- grad_gain: float32 [2, 768], P(None, ('dp', 'seq'))
- grad_bias: float32 [2, 768], P(None, ('dp', 'seq'))
Inputs may be any that keep to these rules, and one draw needn't show every extreme that they name: Continuation c of group g follows the first 4 * branch_blocks[g, c] tokens of the group's prompt.
All inputs are finite; a program needn't handle non-finite values.
Results may differ from a plain program's by a relative error of at most 0.017.
Values may be sent and summed in bfloat16 or wider, within the bound.
A program may use at most 256 MiB of HBM per device.

v0:
```python
from functools import partial

import jax
import jax.numpy as jnp
from jax import lax
from jax.sharding import PartitionSpec as P

HEADS = 12
HEAD_DIM = 64
PROMPT = 1024
CONT = 8
CLEN = 128
WINDOW = 128
POOL_SPAN = 512
STRIDE = 4


eps_norm = 1e-05


def token_layout(positions_in, offsets):
    in_prompt = positions_in < PROMPT
    segment = jnp.where(in_prompt, -1, (positions_in - PROMPT) // CLEN)
    within = positions_in - PROMPT - segment * CLEN
    choose = (segment[:, None] == jnp.arange(CONT, dtype=jnp.int32)[None, :]).astype(jnp.int32)
    cont_start = jnp.sum(choose * offsets[None, :], axis=1)
    position = jnp.where(in_prompt, positions_in, cont_start + within)
    prompt_limit = jnp.where(in_prompt, PROMPT, cont_start)
    return (segment, position, prompt_limit)


def visible_keys(query_rows, key_index, offsets, reach):
    query_seg, query_pos, query_limit = token_layout(query_rows, offsets)
    key_seg, key_pos, key_limit = token_layout(key_index, offsets)
    prompt_key = (key_seg[None, :] < 0) & (key_pos[None, :] < query_limit[:, None])
    own_key = (key_seg[None, :] == query_seg[:, None]) & (query_seg[:, None] >= 0)
    distance = key_pos[None, :] - query_pos[:, None]
    return (prompt_key | own_key) & (distance >= -(reach // 2)) & (distance < reach // 2)


def key_mask(query_rows, offsets):
    group_len = PROMPT + CONT * CLEN
    full_keys = jnp.arange(group_len, dtype=jnp.int32)
    pooled_keys = jnp.arange(group_len // STRIDE, dtype=jnp.int32) * STRIDE
    return jnp.concatenate(
        [
            visible_keys(query_rows, full_keys, offsets, WINDOW),
            visible_keys(query_rows, pooled_keys, offsets, POOL_SPAN),
        ],
        axis=1,
    )


def pool_rows(source, weight):
    return jnp.sum(
        source.reshape(source.shape[0] // STRIDE, STRIDE, source.shape[1]) * weight[None, :, :],
        axis=1,
    )


def unpool(pooled_grad, weight):
    return (pooled_grad[:, None, :] * weight[None, :, :]).reshape(-1, pooled_grad.shape[1])


def pool_grad(pooled_grad, source):
    blocks_view = source.astype(jnp.float32).reshape(-1, STRIDE, source.shape[1])
    return jnp.sum(pooled_grad[:, None, :] * blocks_view, axis=0)


def layer_norm(source, gain, bias):
    centre = jnp.mean(source, axis=-1, keepdims=True)
    centred = source - centre
    spread = jnp.mean(centred * centred, axis=-1, keepdims=True)
    return centred * lax.rsqrt(spread + eps_norm) * gain + bias


def product(left, right):
    return jnp.dot(left, right, preferred_element_type=jnp.float32)


def product_left(left, right):
    return lax.dot_general(
        left, right, (((0,), (0,)), ((), ())), preferred_element_type=jnp.float32
    )


def product_right(left, right):
    return lax.dot_general(
        left, right, (((1,), (1,)), ((), ())), preferred_element_type=jnp.float32
    )


def add_pair(left_term, right_term):
    return left_term + right_term


def gather_weights(w_query, w_key, w_value, w_output, w_inner, w_outer):
    partial_rows = (
        lax.all_gather(w_query, "seq", axis=0, tiled=True),
        lax.all_gather(w_key, "seq", axis=0, tiled=True),
        lax.all_gather(w_value, "seq", axis=0, tiled=True),
        lax.all_gather(w_output, "seq", axis=0, tiled=True),
        lax.all_gather(w_inner, "seq", axis=0, tiled=True),
        lax.all_gather(w_outer, "seq", axis=1, tiled=True),
    )
    return (
        lax.all_gather(partial_rows[0], "dp", axis=1, tiled=True),
        lax.all_gather(partial_rows[1], "dp", axis=1, tiled=True),
        lax.all_gather(partial_rows[2], "dp", axis=1, tiled=True),
        lax.all_gather(partial_rows[3], "dp", axis=1, tiled=True),
        lax.all_gather(partial_rows[4], "dp", axis=1, tiled=True),
        lax.all_gather(partial_rows[5], "dp", axis=0, tiled=True),
    )


def reduce_grads(weight_grads):
    partial_sums = (
        lax.psum_scatter(weight_grads[0], "dp", scatter_dimension=1, tiled=True),
        lax.psum_scatter(weight_grads[1], "dp", scatter_dimension=1, tiled=True),
        lax.psum_scatter(weight_grads[2], "dp", scatter_dimension=1, tiled=True),
        lax.psum_scatter(weight_grads[3], "dp", scatter_dimension=1, tiled=True),
        lax.psum_scatter(weight_grads[4], "dp", scatter_dimension=1, tiled=True),
        lax.psum_scatter(weight_grads[5], "dp", scatter_dimension=0, tiled=True),
    )
    return (
        lax.psum_scatter(
            partial_sums[0].astype(jnp.bfloat16), "seq", scatter_dimension=0, tiled=True
        ).astype(jnp.float32),
        lax.psum_scatter(
            partial_sums[1].astype(jnp.bfloat16), "seq", scatter_dimension=0, tiled=True
        ).astype(jnp.float32),
        lax.psum_scatter(
            partial_sums[2].astype(jnp.bfloat16), "seq", scatter_dimension=0, tiled=True
        ).astype(jnp.float32),
        lax.psum_scatter(
            partial_sums[3].astype(jnp.bfloat16), "seq", scatter_dimension=0, tiled=True
        ).astype(jnp.float32),
        lax.psum_scatter(
            partial_sums[4].astype(jnp.bfloat16), "seq", scatter_dimension=0, tiled=True
        ).astype(jnp.float32),
        lax.psum_scatter(
            partial_sums[5].astype(jnp.bfloat16), "seq", scatter_dimension=1, tiled=True
        ).astype(jnp.float32),
    )


def forward(tokens_in, weights, pool_full, gain_full, bias_full, visible_mask):
    w_query, w_key, w_value, w_output, w_inner, w_outer = weights
    score_scale = 1.0 / HEAD_DIM**0.5
    queries = product(tokens_in, w_query).astype(jnp.bfloat16)
    key_rows = product(tokens_in, w_key).astype(jnp.bfloat16)
    value_rows = product(tokens_in, w_value).astype(jnp.bfloat16)
    pooled_keys = pool_rows(key_rows.astype(jnp.float32), pool_full[0]).astype(jnp.bfloat16)
    pooled_values = pool_rows(value_rows.astype(jnp.float32), pool_full[1]).astype(jnp.bfloat16)
    shared = (
        lax.all_gather(key_rows, "seq", axis=0, tiled=True),
        lax.all_gather(value_rows, "seq", axis=0, tiled=True),
        lax.all_gather(pooled_keys, "seq", axis=0, tiled=True),
        lax.all_gather(pooled_values, "seq", axis=0, tiled=True),
    )
    keys_all = jnp.concatenate([shared[0], shared[2]], axis=0)
    values_all = jnp.concatenate([shared[1], shared[3]], axis=0)

    def one_head(head_index):
        head_query = lax.dynamic_slice_in_dim(queries, head_index * HEAD_DIM, HEAD_DIM, 1)
        head_keys = lax.dynamic_slice_in_dim(keys_all, head_index * HEAD_DIM, HEAD_DIM, 1)
        head_values = lax.dynamic_slice_in_dim(values_all, head_index * HEAD_DIM, HEAD_DIM, 1)
        scores = jnp.where(
            visible_mask, product_right(head_query, head_keys) * score_scale, -1000000000.0
        )
        row_top = jnp.max(scores, axis=1, keepdims=True)
        exponent = jnp.exp(scores - row_top)
        row_total = jnp.sum(exponent, axis=1, keepdims=True)
        attend_weights = (exponent / row_total).astype(jnp.bfloat16)
        return (product(attend_weights, head_values), (row_top + jnp.log(row_total))[:, 0])

    head_outputs, log_total = lax.map(one_head, jnp.arange(HEADS, dtype=jnp.int32))
    attended = (
        jnp.transpose(head_outputs, (1, 0, 2)).reshape(tokens_in.shape[0], -1).astype(jnp.bfloat16)
    )
    mixed_rows = tokens_in.astype(jnp.float32) + product(attended, w_output)
    normed_first = layer_norm(mixed_rows, gain_full[0], bias_full[0])
    first_low = normed_first.astype(jnp.bfloat16)
    inner_act = product(first_low, w_inner)
    active = jax.nn.gelu(inner_act, approximate=False).astype(jnp.bfloat16)
    second = normed_first + product(active, w_outer)
    output = layer_norm(second, gain_full[1], bias_full[1]).astype(jnp.bfloat16)
    saved = (
        queries,
        key_rows,
        value_rows,
        keys_all,
        values_all,
        log_total,
        attended,
        mixed_rows,
        first_low,
        inner_act,
        active,
        second,
    )
    return (output, saved)


def backward(tokens_in, cotangent, weights, pool_full, gain_full, bias_full, visible_mask, saved):
    w_query, w_key, w_value, w_output, w_inner, w_outer = weights
    (
        queries,
        key_rows,
        value_rows,
        keys_all,
        values_all,
        log_total,
        attended,
        mixed_rows,
        first_low,
        inner_act,
        active,
        second,
    ) = saved
    score_scale = 1.0 / HEAD_DIM**0.5
    group_len = PROMPT + CONT * CLEN
    norm_value, second_back = jax.vjp(layer_norm, second, gain_full[1], bias_full[1])
    grad_second, gain_second, bias_second = second_back(cotangent.astype(jnp.float32))
    grad_ffn_out = grad_second.astype(jnp.bfloat16)
    grad_outer = product_left(active, grad_ffn_out)
    grad_active = product_right(grad_ffn_out, w_outer)
    gelu_value, gelu_back = jax.vjp(partial(jax.nn.gelu, approximate=False), inner_act)
    grad_inner_act = gelu_back(grad_active)[0].astype(jnp.bfloat16)
    grad_inner = product_left(first_low, grad_inner_act)
    grad_first = grad_second + product_right(grad_inner_act, w_inner)
    first_value, first_back = jax.vjp(layer_norm, mixed_rows, gain_full[0], bias_full[0])
    grad_mixed, gain_first, bias_first = first_back(grad_first)
    grad_branch = grad_mixed.astype(jnp.bfloat16)
    grad_output = product_left(attended, grad_branch)
    grad_attended = product_right(grad_branch, w_output).astype(jnp.bfloat16)

    def head_back(head_index):
        head_query = lax.dynamic_slice_in_dim(queries, head_index * HEAD_DIM, HEAD_DIM, 1)
        head_keys = lax.dynamic_slice_in_dim(keys_all, head_index * HEAD_DIM, HEAD_DIM, 1)
        head_values = lax.dynamic_slice_in_dim(values_all, head_index * HEAD_DIM, HEAD_DIM, 1)
        head_grad = lax.dynamic_slice_in_dim(grad_attended, head_index * HEAD_DIM, HEAD_DIM, 1)
        scores = jnp.where(
            visible_mask, product_right(head_query, head_keys) * score_scale, -1000000000.0
        )
        attend_weights = jnp.exp(scores - log_total[head_index][:, None])
        grad_weights = product_right(head_grad, head_values)
        centre = jnp.sum(attend_weights * grad_weights, axis=1, keepdims=True)
        grad_scores = (attend_weights * (grad_weights - centre)).astype(jnp.bfloat16)
        grad_head_query = product(grad_scores, head_keys) * score_scale
        grad_head_keys = product_left(grad_scores, head_query) * score_scale
        grad_head_values = product_left(attend_weights.astype(jnp.bfloat16), head_grad)
        return (grad_head_query, grad_head_keys, grad_head_values)

    per_query, per_keys, per_values = lax.map(head_back, jnp.arange(HEADS, dtype=jnp.int32))
    grad_queries = (
        jnp.transpose(per_query, (1, 0, 2)).reshape(tokens_in.shape[0], -1).astype(jnp.bfloat16)
    )
    grad_keys_all = jnp.transpose(per_keys, (1, 0, 2)).reshape(keys_all.shape[0], -1)
    grad_values_all = jnp.transpose(per_values, (1, 0, 2)).reshape(values_all.shape[0], -1)
    key_sums = (
        lax.psum_scatter(grad_keys_all[:group_len], "seq", scatter_dimension=0, tiled=True),
        lax.psum_scatter(grad_values_all[:group_len], "seq", scatter_dimension=0, tiled=True),
        lax.psum_scatter(grad_keys_all[group_len:], "seq", scatter_dimension=0, tiled=True),
        lax.psum_scatter(grad_values_all[group_len:], "seq", scatter_dimension=0, tiled=True),
    )
    grad_keys = (key_sums[0] + unpool(key_sums[2], pool_full[0])).astype(jnp.bfloat16)
    grad_values = (key_sums[1] + unpool(key_sums[3], pool_full[1])).astype(jnp.bfloat16)
    grad_pooling = jnp.stack([pool_grad(key_sums[2], key_rows), pool_grad(key_sums[3], value_rows)])
    grad_query_w = product_left(tokens_in, grad_queries)
    grad_key_w = product_left(tokens_in, grad_keys)
    grad_value_w = product_left(tokens_in, grad_values)
    grad_tokens = (
        grad_mixed
        + product_right(grad_queries, w_query)
        + product_right(grad_keys, w_key)
        + product_right(grad_values, w_value)
    )
    weight_grads = (grad_query_w, grad_key_w, grad_value_w, grad_output, grad_inner, grad_outer)
    small_terms = (
        grad_pooling,
        jnp.stack([gain_first, gain_second]),
        jnp.stack([bias_first, bias_second]),
    )
    return (weight_grads, small_terms, grad_tokens.astype(jnp.bfloat16))


def local(
    hidden_in,
    w_query,
    w_key,
    w_value,
    w_output,
    w_inner,
    w_outer,
    pool_weight,
    ln_gain,
    ln_bias,
    branch_blocks,
    grad_out,
):
    small_full = (
        lax.all_gather(pool_weight, ("dp", "seq"), axis=2, tiled=True),
        lax.all_gather(ln_gain, ("dp", "seq"), axis=1, tiled=True),
        lax.all_gather(ln_bias, ("dp", "seq"), axis=1, tiled=True),
    )
    pool_full, gain_full, bias_full = small_full
    micro_count = hidden_in.shape[0]
    shard_rows = hidden_in.shape[1]
    query_rows = lax.axis_index("seq") * shard_rows + jnp.arange(shard_rows, dtype=jnp.int32)
    outputs = []
    grads_in = []
    accum = None
    small_accum = None
    for micro_step in range(micro_count):
        weights = gather_weights(w_query, w_key, w_value, w_output, w_inner, w_outer)
        visible_mask = key_mask(query_rows, STRIDE * branch_blocks[micro_step])
        output, saved = forward(
            hidden_in[micro_step], weights, pool_full, gain_full, bias_full, visible_mask
        )
        weights = gather_weights(w_query, w_key, w_value, w_output, w_inner, w_outer)
        weight_grads, small_terms, grad_tokens = backward(
            hidden_in[micro_step],
            grad_out[micro_step],
            weights,
            pool_full,
            gain_full,
            bias_full,
            visible_mask,
            saved,
        )
        accum = weight_grads if micro_step == 0 else jax.tree.map(add_pair, accum, weight_grads)
        small_accum = (
            small_terms if micro_step == 0 else jax.tree.map(add_pair, small_accum, small_terms)
        )
        outputs.append(output)
        grads_in.append(grad_tokens)
    accum = reduce_grads(accum)
    small_sums = (
        lax.psum_scatter(small_accum[0], ("dp", "seq"), scatter_dimension=2, tiled=True),
        lax.psum_scatter(small_accum[1], ("dp", "seq"), scatter_dimension=1, tiled=True),
        lax.psum_scatter(small_accum[2], ("dp", "seq"), scatter_dimension=1, tiled=True),
    )
    return (
        jnp.stack(outputs),
        jnp.stack(grads_in),
        accum[0],
        accum[1],
        accum[2],
        accum[3],
        accum[4],
        accum[5],
        small_sums[0],
        small_sums[1],
        small_sums[2],
    )


def solution(mesh):
    in_specs = (
        P("dp", "seq", None),
        P("seq", "dp"),
        P("seq", "dp"),
        P("seq", "dp"),
        P("seq", "dp"),
        P("seq", "dp"),
        P("dp", "seq"),
        P(None, None, ("dp", "seq")),
        P(None, ("dp", "seq")),
        P(None, ("dp", "seq")),
        P("dp", None),
        P("dp", "seq", None),
    )
    out_specs = (
        P("dp", "seq", None),
        P("dp", "seq", None),
        P("seq", "dp"),
        P("seq", "dp"),
        P("seq", "dp"),
        P("seq", "dp"),
        P("seq", "dp"),
        P("dp", "seq"),
        P(None, None, ("dp", "seq")),
        P(None, ("dp", "seq")),
        P(None, ("dp", "seq")),
    )
    return jax.shard_map(local, mesh=mesh, in_specs=in_specs, out_specs=out_specs, check_vma=False)
```

profile of v0, /device:TPU:0, one launch (start us, length us, event | category | flops | bytes accessed | tf_op | source)
XLA Modules:
  0.0 2309.1 jit_solution(14259968953383337648)
XLA Ops:
  28.7 29.1 %all-gather.15.cloned.1.call-done = bf16[768,768]{0,1:T(8,128)(2,1)} async-done(((bf16[768,96]{0,1:T(8,128)(2,1)}), bf16[768,768]{0,1:T(8,128)(2,1)}) %all-gather.15.cloned.1.call-update) | async-done | bytes 1179664 | tf_op jit(solution)/shard_map/all_gather | solution.py:108
  61.1 39.3 %all-gather.19.cloned.1.call-done = bf16[768,768]{0,1:T(8,128)(2,1)} async-done(((bf16[768,96]{0,1:T(8,128)(2,1)}), bf16[768,768]{0,1:T(8,128)(2,1)}) %all-gather.19.cloned.1.call-update) | async-done | bytes 1179664 | tf_op jit(solution)/shard_map/all_gather | solution.py:109
  131.9 42.1 %all_gather.51 = f32[2,4,768]{1,0,2:T(2,128)S(1)} all-gather(f32[2,4,24]{1,0,2:T(2,128)S(1)} %copy.97), channel_id=1, replica_groups=mesh['dp'=8,'seq'=4] {'dp','seq'}, dimensions={2}, use_global_device_ids=true | all-gather | bytes 25344 | tf_op jit(solution)/shard_map/all_gather | solution.py:303
  174.9 36.7 %all-gather = f32[32,24,2]{1,2,0:T(2,128)S(1)} all-gather(f32[1,24,2]{1,2,0:T(2,128)S(1)} %bitcast.304), channel_id=1, replica_groups=mesh['dp'=8,'seq'=4] {'dp','seq'}, dimensions={0}, use_global_device_ids=true | all-gather | bytes 6336 | tf_op jit(solution)/shard_map/all_gather | solution.py:304
  212.4 38.3 %all-gather.1 = f32[32,24,2]{1,2,0:T(2,128)S(1)} all-gather(f32[1,24,2]{1,2,0:T(2,128)S(1)} %bitcast.305), channel_id=1, replica_groups=mesh['dp'=8,'seq'=4] {'dp','seq'}, dimensions={0}, use_global_device_ids=true | all-gather | bytes 6336 | tf_op jit(solution)/shard_map/all_gather | solution.py:305
  271.5 9.1 all_gather.125
  282.8 9.2 all_gather.127
  292.0 9.1 all_gather.52
  301.1 9.7 all_gather.56
  324.2 128.9 %while.53 = (s32[]{:T(128)}, bf16[12,512,64]{1,2,0:T(8,128)(2,1)}, f32[12,512]{1,0:T(8,128)S(1)}, s32[12]{0:T(128)S(1)}, bf16[512,768]{1,0:T(8,128)(2,1)S(1)}, /...) while((s32[]{:T(128)}, bf16[12,512,64]{1,2,0:T(8,128)(2,1)}, ...), condition=%wide.region_21.22_spmd, body=%wide.region_18.21_spmd.sunk | while | flops 346029568 | bytes 39605968 | solution.py:177
  462.7 122.1 %while.52 = (s32[]{:T(128)}, bf16[12,512,64]{1,2,0:T(8,128)(2,1)S(1)}, f32[12,512]{1,0:T(8,128)S(1)}, s32[12]{0:T(128)S(1)}, bf16[512,768]{1,0:T(8,128)(2,1)}, /...) while((s32[]{:T(128)}, ...), condition=%wide.region_8.9_spmd, body=%wide.region_5.8_spmd.sunk | while | flops 346029568 | bytes 39605968 | solution.py:177
  591.0 21.1 multiply_convert_fusion.2
  618.7 18.2 multiply_convert_fusion.3
  683.1 257.7 %while.54 = (s32[]{:T(128)}, bf16[12,512,64]{1,2,0:T(8,128)(2,1)}, f32[12,2560,64]{1,2,0:T(8,128)}, f32[12,2560,64]{1,2,0:T(8,128)}, s32[12]{0:T(128)S(1)}, /*in...) while((s32[]{:T(128)}, bf16[12,512,64]{1,2,0:T(8,128)(2,1)}, ...), condition=%wide.region_32.33_spmd, body=%wide.region_30.32_spmd.sunk | while | flops 850853376 | bytes 60307248 | solution.py:255
  954.6 258.2 %while.55 = (s32[]{:T(128)}, bf16[12,512,64]{1,2,0:T(8,128)(2,1)}, f32[12,2560,64]{1,2,0:T(8,128)}, f32[12,2560,64]{1,2,0:T(8,128)}, s32[12]{0:T(128)S(1)}, /*in...) while((s32[]{:T(128)}, bf16[12,512,64]{1,2,0:T(8,128)(2,1)}, ...), condition=%wide.region_43.44_spmd, body=%wide.region_41.43_spmd.sunk | while | flops 850853376 | bytes 60307248 | solution.py:255
  1272.4 28.0 %reduce-scatter.38.cloned.1.call-done = f32[512,768]{0,1:T(8,128)} async-done(((f32[2048,768]{0,1:T(8,128)}), f32[512,768]{0,1:T(8,128)}) %reduce-scatter.38.cloned.1.call-update) | async-done | bytes 1572880 | tf_op jit(solution)/shard_map/reduce_scatter | solution.py:263
  1305.7 55.1 %reduce-scatter.46.cloned.1.call-done = f32[512,768]{0,1:T(8,128)} async-done(((f32[2048,768]{0,1:T(8,128)}), f32[512,768]{0,1:T(8,128)}) %reduce-scatter.46.cloned.1.call-update) | async-done | bytes 1572880 | tf_op jit(solution)/shard_map/reduce_scatter | solution.py:263
  1365.7 25.5 %reduce-scatter.36.cloned.1.call-done = f32[128,768]{0,1:T(8,128)} async-done(((f32[512,768]{0,1:T(8,128)}), f32[128,768]{0,1:T(8,128)}) %reduce-scatter.36.cloned.1.call-update) | async-done | bytes 393232 | tf_op jit(solution)/shard_map/reduce_scatter | solution.py:264
  1392.4 29.3 %reduce-scatter.44.cloned.1.call-done = f32[128,768]{0,1:T(8,128)} async-done(((f32[512,768]{0,1:T(8,128)}), f32[128,768]{0,1:T(8,128)}) %reduce-scatter.44.cloned.1.call-update) | async-done | bytes 393232 | tf_op jit(solution)/shard_map/reduce_scatter | solution.py:264
  1432.5 49.6 %reduce-scatter.34.cloned.1.call-done = f32[512,768]{0,1:T(8,128)} async-done(((f32[2048,768]{0,1:T(8,128)}), f32[512,768]{0,1:T(8,128)}) %reduce-scatter.34.cloned.1.call-update) | async-done | bytes 1572880 | tf_op jit(solution)/shard_map/reduce_scatter | solution.py:262
  1487.2 55.1 %reduce-scatter.42.cloned.1.call-done = f32[512,768]{0,1:T(8,128)} async-done(((f32[2048,768]{0,1:T(8,128)}), f32[512,768]{0,1:T(8,128)}) %reduce-scatter.42.cloned.1.call-update) | async-done | bytes 1572880 | tf_op jit(solution)/shard_map/reduce_scatter | solution.py:262
  1558.3 57.2 %reduce-scatter.56.cloned.1.call-done = f32[768,96]{0,1:T(8,128)} async-done(((f32[768,768]{0,1:T(8,128)}), f32[768,96]{0,1:T(8,128)}) %reduce-scatter.56.cloned.1.call-update) | async-done | bytes 294928 | tf_op jit(solution)/shard_map/reduce_scatter | solution.py:121
  1624.7 63.0 %reduce-scatter.50.cloned.1.call-done = f32[768,96]{0,1:T(8,128)} async-done(((f32[768,768]{0,1:T(8,128)}), f32[768,96]{0,1:T(8,128)}) %reduce-scatter.50.cloned.1.call-update) | async-done | bytes 294928 | tf_op jit(solution)/shard_map/reduce_scatter | solution.py:118
  1698.4 61.7 %reduce-scatter.54.cloned.1.call-done = f32[768,96]{0,1:T(8,128)} async-done(((f32[768,768]{0,1:T(8,128)}), f32[768,96]{0,1:T(8,128)}) %reduce-scatter.54.cloned.1.call-update) | async-done | bytes 294928 | tf_op jit(solution)/shard_map/reduce_scatter | solution.py:120
  1763.7 68.8 %reduce-scatter.52.cloned.1.call-done = f32[768,96]{0,1:T(8,128)} async-done(((f32[768,768]{0,1:T(8,128)}), f32[768,96]{0,1:T(8,128)}) %reduce-scatter.52.cloned.1.call-update) | async-done | bytes 294928 | tf_op jit(solution)/shard_map/reduce_scatter | solution.py:119
  1836.3 161.1 %reduce-scatter.62.cloned.1.call-done = f32[384,768]{1,0:T(8,128)} async-done(((f32[3072,768]{1,0:T(8,128)}), f32[384,768]{1,0:T(8,128)}) %reduce-scatter.62.cloned.1.call-update) | async-done | bytes 1179664 | tf_op jit(solution)/shard_map/reduce_scatter | solution.py:123
  2003.6 40.0 %all-reduce.3 = (f32[2,4,768]{2,1,0:T(4,128)S(1)}, f32[2,768]{1,0:T(2,128)S(1)}, f32[2,768]{1,0:T(2,128)S(1)}) all-reduce(f32[2,4,768]{2,1,0:T(4,128)S(1)} %maximum_add_fusion, f32[2,768]{1,0:T(2,128)S(1)} %get-tuple-element.454, f32[2,768]{1,0:T(2,128)S(1)} %get-tuple-element.455), channel_id=22, replica_groups=mesh['dp'=8,'seq'=4] {'dp','seq'}, use_global_device_ids=true, to_apply=%region_64.65.clone | all-reduce | flops 9216 | bytes 73728
  2052.2 155.1 %reduce-scatter.58.cloned.1.call-done = f32[768,384]{1,0:T(8,128)} async-done(((f32[768,3072]{1,0:T(8,128)}), f32[768,384]{1,0:T(8,128)}) %reduce-scatter.58.cloned.1.call-update) | async-done | bytes 1179664 | tf_op jit(solution)/shard_map/reduce_scatter | solution.py:122
  2216.7 11.8 reduce-scatter.68.cloned.1.call-done
  2230.1 21.2 reduce-scatter.66.cloned.1.call-done
  2253.0 23.0 reduce-scatter.72.cloned.1.call-done
  2277.8 22.6 reduce-scatter.60.cloned.1.call-done
  (1003 shorter events, 1023.0 us)
Async XLA Ops:
  7.2 50.7 %all-gather.15.cloned.1.call-start = ((), (), s32[]{:S(2)}) async-start(), calls=%async_computation.21 | async-start | bytes 1327104 | tf_op jit(solution)/shard_map/all_gather | solution.py:108
  15.2 85.3 %all-gather.19.cloned.1.call-start = ((), (), s32[]{:S(2)}) async-start(), calls=%async_computation.23 | async-start | bytes 1327104 | tf_op jit(solution)/shard_map/all_gather | solution.py:109
  21.9 288.9 %all-gather.13.cloned.1.call-start = ((), (), s32[]{:S(2)}) async-start(), calls=%async_computation.20 | async-start | bytes 1327104 | tf_op jit(solution)/shard_map/all_gather | solution.py:107
  28.7 286.3 %all-gather.29.cloned.1.call-start = ((), (), s32[]{:S(2)}) async-start(), calls=%async_computation.28 | async-start | bytes 3932160 | tf_op jit(solution)/shard_map/all_gather | solution.py:156
  61.1 258.7 %all-gather.31.cloned.1.call-start = ((), (), s32[]{:S(2)}) async-start(), calls=%async_computation.29 | async-start | bytes 3932160 | tf_op jit(solution)/shard_map/all_gather | solution.py:157
  103.5 349.6 %all-gather.17.cloned.1.call-start = ((), (), s32[]{:S(2)}) async-start(), calls=%async_computation.22 | async-start | bytes 3932160 | tf_op jit(solution)/shard_map/all_gather | solution.py:156
  106.7 351.9 %all-gather.21.cloned.1.call-start = ((), (), s32[]{:S(2)}) async-start(), calls=%async_computation.24 | async-start | bytes 3932160 | tf_op jit(solution)/shard_map/all_gather | solution.py:157
  108.5 476.4 %all-gather.23.cloned.1.call-start = ((), (), s32[]{:S(2)}) async-start(), calls=%async_computation.25 | async-start | bytes 1327104 | tf_op jit(solution)/shard_map/all_gather | solution.py:110
  114.9 476.1 %all-gather.25.cloned.1.call-start = ((), (), s32[]{:S(2)}) async-start(), calls=%async_computation.26 | async-start | bytes 5308416 | tf_op jit(solution)/shard_map/all_gather | solution.py:111
  123.1 489.1 %all-gather.27.cloned.1.call-start = ((), (), s32[]{:S(2)}) async-start(), calls=%async_computation.27 | async-start | bytes 5308416 | tf_op jit(solution)/shard_map/all_gather | solution.py:112
  131.3 1128.9 %reduce-scatter.40.cloned.1.call-start = ((), (), s32[]{:S(2)}) async-start(), calls=%async_computation.33 | async-start | bytes 1966080 | tf_op jit(solution)/shard_map/reduce_scatter | solution.py:265
  212.4 456.0 %copy-start.66 = (f32[768]{0:T(1024)}, f32[768]{0:T(1024)S(1)}, u32[]{:S(2)}) copy-start(f32[768]{0:T(1024)S(1)} %get-tuple-element.301) | copy-start | bytes 9220
  670.9 579.8 %copy-start.26 = (f32[512,768]{1,0:T(8,128)}, f32[512,768]{1,0:T(8,128)S(1)}, u32[]{:S(2)}) copy-start(f32[512,768]{1,0:T(8,128)S(1)} %get-tuple-element.429) | copy-start | bytes 4718596
  943.6 318.0 %reduce-scatter.48.cloned.1.call-start = ((), (), s32[]{:S(2)}) async-start(), calls=%async_computation.37 | async-start | bytes 1966080 | tf_op jit(solution)/shard_map/reduce_scatter | solution.py:265
  1215.7 84.8 %reduce-scatter.38.cloned.1.call-start = ((), (), s32[]{:S(2)}) async-start(), calls=%async_computation.32 | async-start | bytes 7864320 | tf_op jit(solution)/shard_map/reduce_scatter | solution.py:263
  1222.2 138.5 %reduce-scatter.46.cloned.1.call-start = ((), (), s32[]{:S(2)}) async-start(), calls=%async_computation.36 | async-start | bytes 7864320 | tf_op jit(solution)/shard_map/reduce_scatter | solution.py:263
  1228.5 162.8 %reduce-scatter.36.cloned.1.call-start = ((), (), s32[]{:S(2)}) async-start(), calls=%async_computation.31 | async-start | bytes 1966080 | tf_op jit(solution)/shard_map/reduce_scatter | solution.py:264
  1231.3 190.4 %reduce-scatter.44.cloned.1.call-start = ((), (), s32[]{:S(2)}) async-start(), calls=%async_computation.35 | async-start | bytes 1966080 | tf_op jit(solution)/shard_map/reduce_scatter | solution.py:264
  1234.1 248.0 %reduce-scatter.34.cloned.1.call-start = ((), (), s32[]{:S(2)}) async-start(), calls=%async_computation.30 | async-start | bytes 7864320 | tf_op jit(solution)/shard_map/reduce_scatter | solution.py:262
  1240.5 301.9 %reduce-scatter.42.cloned.1.call-start = ((), (), s32[]{:S(2)}) async-start(), calls=%async_computation.34 | async-start | bytes 7864320 | tf_op jit(solution)/shard_map/reduce_scatter | solution.py:262
  1246.8 368.6 %reduce-scatter.56.cloned.1.call-start = ((), (), s32[]{:S(2)}) async-start(), calls=%async_computation.41 | async-start | bytes 2654208 | tf_op jit(solution)/shard_map/reduce_scatter | solution.py:121
  1253.2 434.5 %reduce-scatter.50.cloned.1.call-start = ((), (), s32[]{:S(2)}) async-start(), calls=%async_computation.38 | async-start | bytes 2654208 | tf_op jit(solution)/shard_map/reduce_scatter | solution.py:118
  1260.1 499.9 %reduce-scatter.54.cloned.1.call-start = ((), (), s32[]{:S(2)}) async-start(), calls=%async_computation.40 | async-start | bytes 2654208 | tf_op jit(solution)/shard_map/reduce_scatter | solution.py:120
  1365.7 466.8 %reduce-scatter.52.cloned.1.call-start = ((), (), s32[]{:S(2)}) async-start(), calls=%async_computation.39 | async-start | bytes 2654208 | tf_op jit(solution)/shard_map/reduce_scatter | solution.py:119
  1547.4 450.1 %reduce-scatter.62.cloned.1.call-start = ((), (), s32[]{:S(2)}) async-start(), calls=%async_computation.44 | async-start | bytes 10616832 | tf_op jit(solution)/shard_map/reduce_scatter | solution.py:123
  1558.2 487.3 %reduce-scatter.70.cloned.1.call-start = ((), (), s32[]{:S(2)}) async-start(), calls=%async_computation.48 | async-start | bytes 245760
  1617.3 429.9 %reduce-scatter.64.cloned.1.call-start = ((), (), s32[]{:S(2)}) async-start(), calls=%async_computation.45 | async-start | bytes 245760
  1689.5 517.8 %reduce-scatter.58.cloned.1.call-start = ((), (), s32[]{:S(2)}) async-start(), calls=%async_computation.42 | async-start | bytes 10616832 | tf_op jit(solution)/shard_map/reduce_scatter | solution.py:122
  1698.3 530.2 %reduce-scatter.68.cloned.1.call-start = ((), (), s32[]{:S(2)}) async-start(), calls=%async_computation.47 | async-start | bytes 245760
  1761.9 489.4 %reduce-scatter.66.cloned.1.call-start = ((), (), s32[]{:S(2)}) async-start(), calls=%async_computation.46 | async-start | bytes 245760
  1834.3 441.6 %reduce-scatter.72.cloned.1.call-start = ((), (), s32[]{:S(2)}) async-start(), calls=%async_computation.49 | async-start | bytes 737280
  1999.9 300.5 %reduce-scatter.60.cloned.1.call-start = ((), (), s32[]{:S(2)}) async-start(), calls=%async_computation.43 | async-start | bytes 737280 | tf_op jit(solution)/shard_map/reduce_scatter | solution.py:138
  (189 other events, 3949.1 us)
Sparse Core Ops, SparseCore 0:
  15.3 42.5 all-gather.14
  60.6 39.7 all-gather.18
  103.2 40.0 all-gather.12
  144.7 30.7 all-gather.28
  176.9 28.4 all-gather.30
  206.8 28.6 all-gather.16
  237.0 28.5 all-gather.20
  268.3 41.0 all-gather.22
  311.5 79.2 all-gather.24
  392.8 78.7 all-gather.26
  943.7 24.3 reduce-scatter.39
  1215.8 24.1 reduce-scatter.47
  1242.5 57.8 reduce-scatter.37
  1302.8 57.8 reduce-scatter.45
  1363.1 28.0 reduce-scatter.35
  1393.6 28.0 reduce-scatter.43
  1424.1 57.8 reduce-scatter.33
  1484.4 57.8 reduce-scatter.41
  1545.8 69.5 reduce-scatter.55
  1618.8 68.8 reduce-scatter.49
  1691.2 68.8 reduce-scatter.53
  1763.6 68.8 reduce-scatter.51
  1836.1 161.3 reduce-scatter.61
  1999.7 18.9 reduce-scatter.69
  2021.8 19.7 reduce-scatter.63
  2045.0 162.2 reduce-scatter.57
  2209.6 18.8 reduce-scatter.67
  2231.5 19.7 reduce-scatter.65
  2253.8 22.0 reduce-scatter.71
  2278.3 22.0 reduce-scatter.59
where the time goes:
time: 2320 us; the launch traced here: 2310 us
  waiting for transfers between devices  957 us (41%)
  matrix products  725 us (31%)
  blocking collectives  235 us (10%)
  local copies, waits for them, and re-layouts  212 us (9%)
  other arithmetic  82.3 us (4%)
  loops' own time  79.5 us (3%)
    dot_general x84, matrix products, product_right(): lax.dot_general(left, right, (((1,), (1,)), ((), ())), preferred_element_...  321 us
    dot_general x60, matrix products, product(): return jnp.dot(left, right, preferred_element_type=jnp.float32)  242 us
    dot_general x60, matrix products, product_left(): lax.dot_general(left, right, (((0,), (0,)), ((), ())), preferred_element_...  162 us
    reduce_scatter x1, waiting for transfers between devices, reduce_grads(): lax.psum_scatter(weight_grads[5], 'dp', scatter_dimension=0, tiled=True)  161 us
    reduce_scatter x1, waiting for transfers between devices, reduce_grads(): lax.psum_scatter(weight_grads[4], 'dp', scatter_dimension=1, tiled=True)  155 us
    reduce_scatter x2, waiting for transfers between devices, backward(): lax.psum_scatter(grad_keys_all[:group_len], 'seq', scatter_dimension=0, t...  105 us
    reduce_scatter x2, waiting for transfers between devices, backward(): lax.psum_scatter(grad_values_all[:group_len], 'seq', scatter_dimension=0,...  83.1 us
    reduce_scatter x1, waiting for transfers between devices, reduce_grads(): lax.psum_scatter(weight_grads[1], 'dp', scatter_dimension=1, tiled=True)  68.8 us
  transfers between devices with their start and end apart: 30, of which 18 were waited for; matrix products, arithmetic and copies ran while one was open for 29% of the time, Pallas kernels for 0%

commit v1 on v0

v1 whole, which is shorter than its diff:
```python
from functools import partial

import jax
import jax.numpy as jnp
from jax import lax
from jax.sharding import PartitionSpec as P

HEADS = 12
HEAD_DIM = 64
PROMPT = 1024
CONT = 8
CLEN = 128
WINDOW = 128
POOL_SPAN = 512
STRIDE = 4


eps_norm = 1e-05


def token_layout(positions_in, offsets):
    in_prompt = positions_in < PROMPT
    segment = jnp.where(in_prompt, -1, (positions_in - PROMPT) // CLEN)
    within = positions_in - PROMPT - segment * CLEN
    choose = (segment[:, None] == jnp.arange(CONT, dtype=jnp.int32)[None, :]).astype(jnp.int32)
    cont_start = jnp.sum(choose * offsets[None, :], axis=1)
    position = jnp.where(in_prompt, positions_in, cont_start + within)
    prompt_limit = jnp.where(in_prompt, PROMPT, cont_start)
    return (segment, position, prompt_limit)


def visible_keys(query_rows, key_index, offsets, reach):
    query_seg, query_pos, query_limit = token_layout(query_rows, offsets)
    key_seg, key_pos, key_limit = token_layout(key_index, offsets)
    prompt_key = (key_seg[None, :] < 0) & (key_pos[None, :] < query_limit[:, None])
    own_key = (key_seg[None, :] == query_seg[:, None]) & (query_seg[:, None] >= 0)
    distance = key_pos[None, :] - query_pos[:, None]
    return (prompt_key | own_key) & (distance >= -(reach // 2)) & (distance < reach // 2)


def key_mask(query_rows, offsets):
    group_len = PROMPT + CONT * CLEN
    full_keys = jnp.arange(group_len, dtype=jnp.int32)
    pooled_keys = jnp.arange(group_len // STRIDE, dtype=jnp.int32) * STRIDE
    return jnp.concatenate(
        [
            visible_keys(query_rows, full_keys, offsets, WINDOW),
            visible_keys(query_rows, pooled_keys, offsets, POOL_SPAN),
        ],
        axis=1,
    )


def pool_rows(source, weight):
    return jnp.sum(
        source.reshape(source.shape[0] // STRIDE, STRIDE, source.shape[1]) * weight[None, :, :],
        axis=1,
    )


def unpool(pooled_grad, weight):
    return (pooled_grad[:, None, :] * weight[None, :, :]).reshape(-1, pooled_grad.shape[1])


def pool_grad(pooled_grad, source):
    blocks_view = source.astype(jnp.float32).reshape(-1, STRIDE, source.shape[1])
    return jnp.sum(pooled_grad[:, None, :] * blocks_view, axis=0)


def layer_norm(source, gain, bias):
    centre = jnp.mean(source, axis=-1, keepdims=True)
    centred = source - centre
    spread = jnp.mean(centred * centred, axis=-1, keepdims=True)
    return centred * lax.rsqrt(spread + eps_norm) * gain + bias


def product(left, right):
    return jnp.dot(left, right, preferred_element_type=jnp.float32)


def product_left(left, right):
    return lax.dot_general(
        left, right, (((0,), (0,)), ((), ())), preferred_element_type=jnp.float32
    )


def product_right(left, right):
    return lax.dot_general(
        left, right, (((1,), (1,)), ((), ())), preferred_element_type=jnp.float32
    )


def add_pair(left_term, right_term):
    return left_term + right_term


def gather_weights(w_query, w_key, w_value, w_output, w_inner, w_outer):
    partial_rows = (
        lax.all_gather(w_query, "seq", axis=0, tiled=True),
        lax.all_gather(w_key, "seq", axis=0, tiled=True),
        lax.all_gather(w_value, "seq", axis=0, tiled=True),
        lax.all_gather(w_output, "seq", axis=0, tiled=True),
        lax.all_gather(w_inner, "seq", axis=0, tiled=True),
        lax.all_gather(w_outer, "seq", axis=1, tiled=True),
    )
    return (
        lax.all_gather(partial_rows[0], "dp", axis=1, tiled=True),
        lax.all_gather(partial_rows[1], "dp", axis=1, tiled=True),
        lax.all_gather(partial_rows[2], "dp", axis=1, tiled=True),
        lax.all_gather(partial_rows[3], "dp", axis=1, tiled=True),
        lax.all_gather(partial_rows[4], "dp", axis=1, tiled=True),
        lax.all_gather(partial_rows[5], "dp", axis=0, tiled=True),
    )


def reduce_grads(weight_grads):
    partial_sums = (
        lax.psum_scatter(weight_grads[0], "dp", scatter_dimension=1, tiled=True),
        lax.psum_scatter(weight_grads[1], "dp", scatter_dimension=1, tiled=True),
        lax.psum_scatter(weight_grads[2], "dp", scatter_dimension=1, tiled=True),
        lax.psum_scatter(weight_grads[3], "dp", scatter_dimension=1, tiled=True),
        lax.psum_scatter(weight_grads[4], "dp", scatter_dimension=1, tiled=True),
        lax.psum_scatter(weight_grads[5], "dp", scatter_dimension=0, tiled=True),
    )
    return (
        lax.psum_scatter(
            partial_sums[0].astype(jnp.bfloat16), "seq", scatter_dimension=0, tiled=True
        ).astype(jnp.float32),
        lax.psum_scatter(
            partial_sums[1].astype(jnp.bfloat16), "seq", scatter_dimension=0, tiled=True
        ).astype(jnp.float32),
        lax.psum_scatter(
            partial_sums[2].astype(jnp.bfloat16), "seq", scatter_dimension=0, tiled=True
        ).astype(jnp.float32),
        lax.psum_scatter(
            partial_sums[3].astype(jnp.bfloat16), "seq", scatter_dimension=0, tiled=True
        ).astype(jnp.float32),
        lax.psum_scatter(
            partial_sums[4].astype(jnp.bfloat16), "seq", scatter_dimension=0, tiled=True
        ).astype(jnp.float32),
        lax.psum_scatter(
            partial_sums[5].astype(jnp.bfloat16), "seq", scatter_dimension=1, tiled=True
        ).astype(jnp.float32),
    )


HALF_FULL = WINDOW // 2
HALF_POOL = POOL_SPAN // 2 // STRIDE
BLOCK_POOL = CLEN // STRIDE


def layout_of(index, offsets):
    in_prompt = index < PROMPT
    segment = jnp.where(in_prompt, -1, (index - PROMPT) // CLEN)
    within = index - PROMPT - segment * CLEN
    chosen = jnp.clip(segment, 0, CONT - 1)
    flat = chosen.reshape(chosen.shape[0], -1)
    cont_start = jnp.take_along_axis(offsets, flat, axis=1).reshape(index.shape)
    position = jnp.where(in_prompt, index, cont_start + within)
    limit = jnp.where(in_prompt, PROMPT, cont_start)
    return segment, position, limit


def window_rows(source, starts, length):
    groups, blocks = starts.shape
    return jnp.stack(
        [
            jnp.stack(
                [lax.dynamic_slice_in_dim(source[g], starts[g, b], length, 0) for b in range(blocks)]
            )
            for g in range(groups)
        ]
    )


def window_add(target, updates, starts):
    groups, blocks = starts.shape
    length = updates.shape[2]
    rows = []
    for g in range(groups):
        row = target[g]
        for b in range(blocks):
            start = starts[g, b]
            current = lax.dynamic_slice_in_dim(row, start, length, 0)
            row = lax.dynamic_update_slice_in_dim(row, current + updates[g, b], start, 0)
        rows.append(row)
    return jnp.stack(rows)


def block_geometry(seq_index, groups, shard_rows, offsets):
    group_len = PROMPT + CONT * CLEN
    pooled_len = group_len // STRIDE
    blocks = shard_rows // CLEN
    block_start = (seq_index * blocks + jnp.arange(blocks, dtype=jnp.int32)) * CLEN
    prompt_block = block_start < PROMPT
    cont_index = jnp.clip((block_start - PROMPT) // CLEN, 0, CONT - 1)
    anchor = jnp.where(prompt_block[None, :], block_start[None, :], offsets[:, cont_index])
    pooled_start = block_start // STRIDE
    intended = (
        anchor - HALF_FULL,
        jnp.broadcast_to(block_start + CLEN, anchor.shape),
        anchor // STRIDE - HALF_POOL,
        jnp.broadcast_to(pooled_start + BLOCK_POOL, anchor.shape),
    )
    limits = (group_len, group_len, pooled_len, pooled_len)
    lengths = (HALF_FULL, HALF_FULL, HALF_POOL, HALF_POOL)
    clamped = tuple(
        jnp.clip(start, 0, limit - length) for start, limit, length in zip(intended, limits, lengths)
    )
    ramp = lambda n: jnp.arange(n, dtype=jnp.int32)

    def span(window):
        actual = clamped[window][:, :, None] + ramp(lengths[window])
        offset = actual - intended[window][:, :, None]
        return actual, (offset >= 0) & (offset < lengths[window])

    before_full, before_full_ok = span(0)
    after_full, after_full_ok = span(1)
    before_pool, before_pool_ok = span(2)
    after_pool, after_pool_ok = span(3)
    after_ok = prompt_block[None, :, None]
    own_full = jnp.broadcast_to(block_start[None, :, None] + ramp(CLEN), anchor.shape + (CLEN,))
    own_pool = jnp.broadcast_to(
        pooled_start[None, :, None] + ramp(BLOCK_POOL), anchor.shape + (BLOCK_POOL,)
    )
    full_index = jnp.concatenate([before_full, own_full, after_full], axis=2)
    pooled_index = jnp.concatenate([before_pool, own_pool, after_pool], axis=2)
    full_valid = jnp.concatenate(
        [before_full_ok, jnp.ones(own_full.shape, bool), after_ok & after_full_ok], axis=2
    )
    pooled_valid = jnp.concatenate(
        [before_pool_ok, jnp.ones(own_pool.shape, bool), after_ok & after_pool_ok], axis=2
    )
    query_index = block_start[None, :, None] + ramp(CLEN)
    query_index = jnp.broadcast_to(query_index, anchor.shape + (CLEN,))
    q_seg, q_pos, q_lim = layout_of(query_index, offsets)

    def visible(key_token, valid, reach):
        k_seg, k_pos, _ = layout_of(key_token, offsets)
        k_seg, k_pos, valid = k_seg[:, :, None, :], k_pos[:, :, None, :], valid[:, :, None, :]
        prompt_key = (k_seg < 0) & (k_pos < q_lim[..., None])
        own_key = (k_seg == q_seg[..., None]) & (q_seg[..., None] >= 0)
        distance = k_pos - q_pos[..., None]
        return valid & (prompt_key | own_key) & (distance >= -(reach // 2)) & (distance < reach // 2)

    mask = jnp.concatenate(
        [
            visible(full_index, full_valid, WINDOW),
            visible(pooled_index * STRIDE, pooled_valid, POOL_SPAN),
        ],
        axis=3,
    )
    return clamped, mask


def attention_fwd(queries, kv_local, pkv_local, kv_all, pkv_all, starts, mask):
    groups, shard_rows, width = queries.shape
    blocks = shard_rows // CLEN
    score_scale = 1.0 / HEAD_DIM**0.5
    keys_cat = jnp.concatenate(
        [
            window_rows(kv_all, starts[0], HALF_FULL),
            kv_local.reshape(groups, blocks, CLEN, 2 * width),
            window_rows(kv_all, starts[1], HALF_FULL),
            window_rows(pkv_all, starts[2], HALF_POOL),
            pkv_local.reshape(groups, blocks, BLOCK_POOL, 2 * width),
            window_rows(pkv_all, starts[3], HALF_POOL),
        ],
        axis=2,
    )
    span = keys_cat.shape[2]
    head_keys = keys_cat[..., :width].reshape(groups, blocks, span, HEADS, HEAD_DIM)
    head_values = keys_cat[..., width:].reshape(groups, blocks, span, HEADS, HEAD_DIM)
    head_query = queries.reshape(groups, blocks, CLEN, HEADS, HEAD_DIM)
    scores = jnp.einsum(
        "gbqhd,gbkhd->gbhqk", head_query, head_keys, preferred_element_type=jnp.float32
    )
    scores = jnp.where(mask[:, :, None], scores * score_scale, -1000000000.0)
    row_top = jnp.max(scores, axis=-1, keepdims=True)
    exponent = jnp.exp(scores - row_top)
    row_total = jnp.sum(exponent, axis=-1, keepdims=True)
    probs = exponent / row_total
    attended = jnp.einsum(
        "gbhqk,gbkhd->gbqhd",
        probs.astype(jnp.bfloat16),
        head_values,
        preferred_element_type=jnp.float32,
    )
    attended = attended.reshape(groups * shard_rows, width).astype(jnp.bfloat16)
    return attended, (head_query, head_keys, head_values, probs)


def attention_bwd(grad_attended, saved, starts, seq_index):
    head_query, head_keys, head_values, probs = saved
    groups, blocks = head_query.shape[:2]
    width = HEADS * HEAD_DIM
    score_scale = 1.0 / HEAD_DIM**0.5
    head_grad = grad_attended.reshape(groups, blocks, CLEN, HEADS, HEAD_DIM)
    grad_probs = jnp.einsum(
        "gbqhd,gbkhd->gbhqk", head_grad, head_values, preferred_element_type=jnp.float32
    )
    centre = jnp.sum(probs * grad_probs, axis=-1, keepdims=True)
    grad_scores = (probs * (grad_probs - centre)).astype(jnp.bfloat16)
    grad_queries = jnp.einsum(
        "gbhqk,gbkhd->gbqhd", grad_scores, head_keys, preferred_element_type=jnp.float32
    ) * score_scale
    grad_keys = jnp.einsum(
        "gbhqk,gbqhd->gbkhd", grad_scores, head_query, preferred_element_type=jnp.float32
    ) * score_scale
    grad_values = jnp.einsum(
        "gbhqk,gbqhd->gbkhd",
        probs.astype(jnp.bfloat16),
        head_grad,
        preferred_element_type=jnp.float32,
    )
    span = grad_keys.shape[2]
    grad_kv = jnp.concatenate(
        [grad_keys.reshape(groups, blocks, span, width), grad_values.reshape(groups, blocks, span, width)],
        axis=3,
    )
    shard_rows = blocks * CLEN
    group_len = PROMPT + CONT * CLEN
    cut = (0, HALF_FULL, HALF_FULL + CLEN, 2 * HALF_FULL + CLEN)
    pcut = tuple(cut[-1] + c for c in (0, HALF_POOL, HALF_POOL + BLOCK_POOL, 2 * HALF_POOL + BLOCK_POOL))
    own_full = grad_kv[:, :, cut[1] : cut[2]].reshape(groups, shard_rows, 2 * width)
    own_pooled = grad_kv[:, :, pcut[1] : pcut[2]].reshape(groups, shard_rows // STRIDE, 2 * width)
    full = jnp.zeros((groups, group_len, 2 * width), jnp.float32)
    full = lax.dynamic_update_slice_in_dim(full, own_full, seq_index * shard_rows, 1)
    full = window_add(full, grad_kv[:, :, cut[0] : cut[1]], starts[0])
    full = window_add(full, grad_kv[:, :, cut[2] : cut[3]], starts[1])
    pooled = jnp.zeros((groups, group_len // STRIDE, 2 * width), jnp.float32)
    pooled = lax.dynamic_update_slice_in_dim(pooled, own_pooled, seq_index * shard_rows // STRIDE, 1)
    pooled = window_add(pooled, grad_kv[:, :, pcut[0] : pcut[1]], starts[2])
    pooled = window_add(pooled, grad_kv[:, :, pcut[2] : pcut[3]], starts[3])
    full = lax.psum_scatter(full, "seq", scatter_dimension=1, tiled=True)
    pooled = lax.psum_scatter(pooled, "seq", scatter_dimension=1, tiled=True)
    grad_queries = grad_queries.reshape(groups * shard_rows, width).astype(jnp.bfloat16)
    return grad_queries, full, pooled


def pool_grouped(source, weight):
    groups, rows, width = source.shape
    return jnp.sum(
        source.reshape(groups, rows // STRIDE, STRIDE, width) * weight[None, None], axis=2
    )


def unpool_grouped(pooled_grad, weight):
    groups, rows, width = pooled_grad.shape
    return (pooled_grad[:, :, None, :] * weight[None, None]).reshape(groups, rows * STRIDE, width)


def pool_grad_grouped(pooled_grad, source):
    groups, rows, width = source.shape
    blocks_view = source.astype(jnp.float32).reshape(groups, rows // STRIDE, STRIDE, width)
    return jnp.sum(pooled_grad[:, :, None, :] * blocks_view, axis=(0, 1))


def local(
    hidden_in,
    w_query,
    w_key,
    w_value,
    w_output,
    w_inner,
    w_outer,
    pool_weight,
    ln_gain,
    ln_bias,
    branch_blocks,
    grad_out,
):
    pool_full = lax.all_gather(pool_weight, ("dp", "seq"), axis=2, tiled=True)
    gain_full = lax.all_gather(ln_gain, ("dp", "seq"), axis=1, tiled=True)
    bias_full = lax.all_gather(ln_bias, ("dp", "seq"), axis=1, tiled=True)
    weights = gather_weights(w_query, w_key, w_value, w_output, w_inner, w_outer)
    wq, wk, wv, wo, wi, wu = weights
    groups, shard_rows, width = hidden_in.shape
    seq_index = lax.axis_index("seq")
    offsets = STRIDE * branch_blocks
    starts, mask = block_geometry(seq_index, groups, shard_rows, offsets)

    tokens = hidden_in.reshape(groups * shard_rows, width)
    queries = product(tokens, wq).astype(jnp.bfloat16)
    key_rows = product(tokens, wk).astype(jnp.bfloat16)
    value_rows = product(tokens, wv).astype(jnp.bfloat16)
    key_g = key_rows.reshape(groups, shard_rows, width)
    value_g = value_rows.reshape(groups, shard_rows, width)
    pooled_keys = pool_grouped(key_g.astype(jnp.float32), pool_full[0]).astype(jnp.bfloat16)
    pooled_values = pool_grouped(value_g.astype(jnp.float32), pool_full[1]).astype(jnp.bfloat16)
    kv_local = jnp.concatenate([key_g, value_g], axis=2)
    pkv_local = jnp.concatenate([pooled_keys, pooled_values], axis=2)
    kv_all = lax.all_gather(kv_local, "seq", axis=1, tiled=True)
    pkv_all = lax.all_gather(pkv_local, "seq", axis=1, tiled=True)
    attended, att_saved = attention_fwd(
        queries.reshape(groups, shard_rows, width), kv_local, pkv_local, kv_all, pkv_all, starts, mask
    )
    mixed_rows = tokens.astype(jnp.float32) + product(attended, wo)
    normed_first = layer_norm(mixed_rows, gain_full[0], bias_full[0])
    first_low = normed_first.astype(jnp.bfloat16)
    inner_act = product(first_low, wi)
    active = jax.nn.gelu(inner_act, approximate=False).astype(jnp.bfloat16)
    second = normed_first + product(active, wu)
    norm_value, second_back = jax.vjp(layer_norm, second, gain_full[1], bias_full[1])
    output = norm_value.astype(jnp.bfloat16)

    cotangent = grad_out.reshape(groups * shard_rows, width).astype(jnp.float32)
    grad_second, gain_second, bias_second = second_back(cotangent)
    grad_ffn_out = grad_second.astype(jnp.bfloat16)
    grad_outer = product_left(active, grad_ffn_out)
    grad_active = product_right(grad_ffn_out, wu)
    gelu_value, gelu_back = jax.vjp(partial(jax.nn.gelu, approximate=False), inner_act)
    grad_inner_act = gelu_back(grad_active)[0].astype(jnp.bfloat16)
    grad_inner = product_left(first_low, grad_inner_act)
    grad_first = grad_second + product_right(grad_inner_act, wi)
    first_value, first_back = jax.vjp(layer_norm, mixed_rows, gain_full[0], bias_full[0])
    grad_mixed, gain_first, bias_first = first_back(grad_first)
    grad_branch = grad_mixed.astype(jnp.bfloat16)
    grad_output = product_left(attended, grad_branch)
    grad_attended = product_right(grad_branch, wo).astype(jnp.bfloat16)

    grad_queries, grad_full, grad_pooled = attention_bwd(grad_attended, att_saved, starts, seq_index)
    grad_keys = (
        grad_full[..., :width] + unpool_grouped(grad_pooled[..., :width], pool_full[0])
    ).astype(jnp.bfloat16).reshape(groups * shard_rows, width)
    grad_values = (
        grad_full[..., width:] + unpool_grouped(grad_pooled[..., width:], pool_full[1])
    ).astype(jnp.bfloat16).reshape(groups * shard_rows, width)
    grad_pooling = jnp.stack(
        [
            pool_grad_grouped(grad_pooled[..., :width], key_g),
            pool_grad_grouped(grad_pooled[..., width:], value_g),
        ]
    )
    grad_query_w = product_left(tokens, grad_queries)
    grad_key_w = product_left(tokens, grad_keys)
    grad_value_w = product_left(tokens, grad_values)
    grad_tokens = (
        grad_mixed
        + product_right(grad_queries, wq)
        + product_right(grad_keys, wk)
        + product_right(grad_values, wv)
    )
    accum = reduce_grads((grad_query_w, grad_key_w, grad_value_w, grad_output, grad_inner, grad_outer))
    small_sums = (
        lax.psum_scatter(grad_pooling, ("dp", "seq"), scatter_dimension=2, tiled=True),
        lax.psum_scatter(
            jnp.stack([gain_first, gain_second]), ("dp", "seq"), scatter_dimension=1, tiled=True
        ),
        lax.psum_scatter(
            jnp.stack([bias_first, bias_second]), ("dp", "seq"), scatter_dimension=1, tiled=True
        ),
    )
    return (
        output.reshape(groups, shard_rows, width),
        grad_tokens.astype(jnp.bfloat16).reshape(groups, shard_rows, width),
        accum[0],
        accum[1],
        accum[2],
        accum[3],
        accum[4],
        accum[5],
        small_sums[0],
        small_sums[1],
        small_sums[2],
    )


def solution(mesh):
    in_specs = (
        P("dp", "seq", None),
        P("seq", "dp"),
        P("seq", "dp"),
        P("seq", "dp"),
        P("seq", "dp"),
        P("seq", "dp"),
        P("dp", "seq"),
        P(None, None, ("dp", "seq")),
        P(None, ("dp", "seq")),
        P(None, ("dp", "seq")),
        P("dp", None),
        P("dp", "seq", None),
    )
    out_specs = (
        P("dp", "seq", None),
        P("dp", "seq", None),
        P("seq", "dp"),
        P("seq", "dp"),
        P("seq", "dp"),
        P("seq", "dp"),
        P("seq", "dp"),
        P("dp", "seq"),
        P(None, None, ("dp", "seq")),
        P(None, ("dp", "seq")),
        P(None, ("dp", "seq")),
    )
    return jax.shard_map(local, mesh=mesh, in_specs=in_specs, out_specs=out_specs, check_vma=False)
```

time: 2320 us -> 1540 us (0.66)
  matrix products: 725 us -> 226 us
  waiting for transfers between devices: 957 us -> 654 us
  loops' own time: 79.5 us -> 0 us
  other arithmetic: 82.3 us -> 139 us
  between operations: 16.5 us -> 61.4 us
  local copies, waits for them, and re-layouts: 212 us -> 246 us
  blocking collectives: 235 us -> 202 us
    dot_general x84 -> x6, matrix products: 321 us -> 49 us  [product_right(): lax.dot_general(left, right, (((1,), (1,)), ((), ())), preferred_element_...]
    dot_general x60 -> x6, matrix products: 242 us -> 59.3 us  [product(): return jnp.dot(left, right, preferred_element_type=jnp.float32)]
    reduce_scatter x1, waiting for transfers between devices: 161 us -> 0.02 us  [reduce_grads(): lax.psum_scatter(weight_grads[5], 'dp', scatter_dimension=0, tiled=True)]
    dot_general x60 -> x6, matrix products: 162 us -> 36.6 us  [product_left(): lax.dot_general(left, right, (((0,), (0,)), ((), ())), preferred_element_...]
    another operation x4 -> x0, loops' own time: 79.5 us -> none  [the longest x2 63.2 us: backward(): lax.map(head_back, jnp.arange(HEADS, dtype=jnp.int32))]
    dot_general x0 -> x5, matrix products: none -> 67.3 us  [the longest x1 18.1 us: attention_bwd(): jnp.einsum('gbqhd,gbkhd->gbhqk', head_grad, head_values, preferred_elemen...]
    reduce_scatter x1, waiting for transfers between devices: 63 us -> 0.02 us  [reduce_grads(): lax.psum_scatter(weight_grads[0], 'dp', scatter_dimension=1, tiled=True)]
    reduce_scatter x1, waiting for transfers between devices: 57.2 us -> 0.02 us  [reduce_grads(): lax.psum_scatter(weight_grads[3], 'dp', scatter_dimension=1, tiled=True)]
  transfers between devices with their start and end apart: 30 -> 22, of which waited for: 18 -> 12; matrix products, arithmetic and copies ran while one was open for 29% -> 35% of each run, Pallas kernels for 0% -> 0%
where the time goes in v1:
time: 1540 us; the launch traced here: 1530 us
  waiting for transfers between devices  654 us (42%)
  local copies, waits for them, and re-layouts  246 us (16%)
  matrix products  226 us (15%)
  blocking collectives  202 us (13%)
  other arithmetic  139 us (9%)
  between operations  61.4 us (4%)
    reduce_scatter x1, waiting for transfers between devices, attention_bwd(): full = lax.psum_scatter(full, 'seq', scatter_dimension=1, tiled=True)  182 us
    reduce_scatter x1, waiting for transfers between devices, reduce_grads(): lax.psum_scatter(weight_grads[4], 'dp', scatter_dimension=1, tiled=True)  158 us
    reduce_scatter x1, waiting for transfers between devices, reduce_grads(): lax.psum_scatter(weight_grads[2], 'dp', scatter_dimension=1, tiled=True)  65.8 us
    reduce_scatter x1, waiting for transfers between devices, reduce_grads(): lax.psum_scatter(weight_grads[1], 'dp', scatter_dimension=1, tiled=True)  65.3 us
    dot_general x6, matrix products, product(): return jnp.dot(left, right, preferred_element_type=jnp.float32)  59.3 us
    reduce_scatter x1, waiting for transfers between devices, attention_bwd(): pooled = lax.psum_scatter(pooled, 'seq', scatter_dimension=1, tiled=True)  58.3 us
    unnamed x27, waiting for transfers between devices  58.2 us
    dot_general x6, matrix products, product_right(): lax.dot_general(left, right, (((1,), (1,)), ((), ())), preferred_element_...  49 us
  transfers between devices with their start and end apart: 22, of which 12 were waited for; matrix products, arithmetic and copies ran while one was open for 35% of the time, Pallas kernels for 0%

profile of v1, /device:TPU:0, one launch (start us, length us, event | category | flops | bytes accessed | tf_op | source)
XLA Modules:
  0.0 1529.1 jit_solution(4473963479327782481)
XLA Ops:
  29.5 44.7 %all_gather.56 = f32[2,4,768]{1,0,2:T(2,128)S(1)} all-gather(f32[2,4,24]{1,0,2:T(2,128)S(1)} %copy.123), channel_id=1, replica_groups=mesh['dp'=8,'seq'=4] {'dp','seq'}, dimensions={2}, use_global_device_ids=true | all-gather | bytes 25344 | tf_op jit(solution)/shard_map/all_gather | solution.py:373
  82.5 18.9 %all-gather.13.cloned.1.call-done = bf16[768,768]{0,1:T(8,128)(2,1)} async-done(((bf16[768,96]{0,1:T(8,128)(2,1)}), bf16[768,768]{0,1:T(8,128)(2,1)}) %all-gather.13.cloned.1.call-update) | async-done | bytes 1179664 | tf_op jit(solution)/shard_map/all_gather | solution.py:109
  184.3 9.0 gather_fusion.1
  199.0 39.3 %all-gather = f32[32,24,2]{1,2,0:T(2,128)S(1)} all-gather(f32[1,24,2]{1,2,0:T(2,128)S(1)} %bitcast.352), channel_id=1, replica_groups=mesh['dp'=8,'seq'=4] {'dp','seq'}, dimensions={0}, use_global_device_ids=true | all-gather | bytes 6336 | tf_op jit(solution)/shard_map/all_gather | solution.py:374
  238.3 36.7 %all-gather.1 = f32[32,24,2]{1,2,0:T(2,128)S(1)} all-gather(f32[1,24,2]{1,2,0:T(2,128)S(1)} %bitcast.353), channel_id=1, replica_groups=mesh['dp'=8,'seq'=4] {'dp','seq'}, dimensions={0}, use_global_device_ids=true | all-gather | bytes 6336 | tf_op jit(solution)/shard_map/all_gather | solution.py:375
  346.2 13.4 fusion.147
  359.6 10.7 fusion.32
  381.3 35.4 %multiply_convert_fusion.1 = (bf16[1024,3072]{1,0:T(8,128)(2,1)}, f32[1024,3072]{1,0:T(8,128)}, f32[1024,3072]{1,0:T(8,128)}) fusion(bf16[768,3072]{1,0:T(8,128)(2,1)} %all-gather.23.cloned.1.call-done, f32[1024,768]{1,0:T(8,128)S(1)} %get-tuple-element.189, f32[768]{0:T(1024)S(1)} %get-tuple-element.63, f32[768]{0:T(1024)S(1)} %get-tuple-element.211, ...), kind=kOutput, calls=%fused_computation.80 | convolution fusion | flops 5040242688 | bytes 39335936 | tf_op jit(solution)/shard_map/dot_general | solution.py:78
  416.6 45.5 %all-gather.25.cloned.1.call-done = bf16[3072,768]{0,1:T(8,128)(2,1)} async-done(((bf16[384,768]{0,1:T(8,128)(2,1)}), bf16[3072,768]{0,1:T(8,128)(2,1)}) %all-gather.25.cloned.1.call-update) | async-done | bytes 4718608 | tf_op jit(solution)/shard_map/all_gather | solution.py:112
  462.2 9.3 fusion.153
  476.5 18.0 %add_convert_fusion = bf16[1024,3072]{1,0:T(8,128)(2,1)} fusion(f32[1024,3072]{1,0:T(8,128)} %get-tuple-element.72, f32[1024,3072]{1,0:T(8,128)} %get-tuple-element.190, bf16[3072,768]{0,1:T(8,128)(2,1)} %all-gather.25.cloned.1.call-done, f32[1024,768]{1,0:T(8,128)S(1)} %get-tuple-element.70, f32[1024]{0:T(1024)S(1)} %negate_multiply_fusion.2), kind=kOutput, calls=%fused_computation.79 | convolution fusion | flops 4877451264 | bytes 39325696 | tf_op jit(solution)/shard_map/dot_general | solution.py:88
  494.4 10.1 multiply_reduce_fusion.1
  522.1 18.1 %multiply_reduce_fusion = (f32[2,4,12,128]{3,2,1,0:T(8,128)S(1)}, f32[2,4,12,128,416]{3,4,2,1,0:T(8,128)}) fusion(f32[2,4,12,128,416]{3,4,2,1,0:T(8,128)} %get-tuple-element.187, f32[2,4,12,128]{3,2,1,0:T(8,128)S(1)} %copy-done.37, bf16[2,4,416,12,64]{2,4,3,1,0:T(8,128)(2,1)} %bitcast.334, bf16[2,4,128,12,64]{2,1,0,4,3:T(4,128)(2,1)} %reshape.1168), kind=kOutput, calls=%fused_computation.73 | convolution fusion | flops 669634560 | bytes 47677440 | tf_op jit(solution)/shard_map/gbqhd,gbkhd->gbhqk/dot_general | solution.py:299
  540.2 14.1 multiply_convert_fusion
  573.9 10.9 fusion.124
  584.9 10.7 fusion.126
  597.0 16.4 %fusion.12 = f32[2,4,12,64,416]{4,3,2,1,0:T(8,128)} fusion(bf16[2,4,128,12,64]{2,1,0,4,3:T(4,128)(2,1)S(1)} %copy-done.27, f32[2,4,12,128,416]{3,4,2,1,0:T(8,128)} %get-tuple-element.187, f32[2,4,12,128]{3,2,1,0:T(8,128)S(1)} %copy-done.37), kind=kOutput, calls=%fused_computation.101 | convolution fusion | flops 664535040 | bytes 32292864 | tf_op jit(solution)/shard_map/gbhqk,gbqhd->gbkhd/dot_general | solution.py:310
  613.3 12.4 copy.145
  625.7 13.3 broadcast_multiply_fusion
  639.1 11.8 copy.144
  689.5 11.8 broadcast_in_dim.194
  704.3 24.2 %fusion.136 = (f32[1,2048,1536]{2,1,0:T(8,128)}, f32[2048,1536]{1,0:T(8,128)}, f32[2048,1536]{1,0:T(8,128)}, f32[1,2048,1536]{2,1,0:T(8,128)}) fusion(f32[2,2048,1536]{2,1,0:T(8,128)} %constant_dynamic-update-slice_fusion), kind=kLoop, calls=%fused_computation.438 | loop fusion | bytes 75497472 | tf_op jit(solution)/shard_map/slice | solution.py:181
  807.4 17.7 %pad_maximum_fusion = f32[2,2048,1536]{2,1,0:T(8,128)} fusion(f32[1,2048,1536]{2,1,0:T(8,128)} %dynamic_update_slice.122, f32[1,2048,1536]{2,1,0:T(8,128)} %dynamic_update_slice.114), kind=kLoop, calls=%fused_computation.71 | loop fusion | flops 6291456 | bytes 50331648 | tf_op jit(solution)/shard_map/stack | solution.py:187
  834.2 157.6 %reduce-scatter.40.cloned.1.call-done = f32[768,384]{1,0:T(8,128)} async-done(((f32[768,3072]{1,0:T(8,128)}), f32[768,384]{1,0:T(8,128)}) %reduce-scatter.40.cloned.1.call-update) | async-done | bytes 1179664 | tf_op jit(solution)/shard_map/reduce_scatter | solution.py:122
  994.0 58.3 %reduce-scatter.30.cloned.1.call-done = f32[2,128,1536]{2,1,0:T(8,128)} async-done(((f32[2,512,1536]{2,1,0:T(8,128)}), f32[2,128,1536]{2,1,0:T(8,128)}) %reduce-scatter.30.cloned.1.call-update) | async-done | bytes 1572880 | tf_op jit(solution)/shard_map/reduce_scatter | solution.py:336
  1055.1 181.7 %reduce-scatter.28.cloned.1.call-done = f32[2,512,1536]{2,1,0:T(8,128)} async-done(((f32[2,2048,1536]{2,1,0:T(8,128)}), f32[2,512,1536]{2,1,0:T(8,128)}) %reduce-scatter.28.cloned.1.call-update) | async-done | bytes 6291472 | tf_op jit(solution)/shard_map/reduce_scatter | solution.py:335
  1261.0 21.1 %reduce-scatter.46.cloned.1.call-done = bf16[192,96]{1,0:T(8,128)(2,1)} async-done(((bf16[768,96]{1,0:T(8,128)(2,1)}), bf16[192,96]{1,0:T(8,128)(2,1)}) %reduce-scatter.46.cloned.1.call-update) | async-done | bytes 36880
  1292.9 40.2 %all-reduce.3 = (f32[2,4,768]{2,1,0:T(4,128)S(1)}, f32[2,768]{1,0:T(2,128)S(1)}, f32[2,768]{1,0:T(2,128)S(1)}) all-reduce(f32[2,4,768]{2,1,0:T(4,128)S(1)} %pad_maximum_fusion.5, f32[2,768]{1,0:T(2,128)S(1)} %pad_maximum_fusion.6, f32[2,768]{1,0:T(2,128)S(1)} %pad_maximum_fusion.7), channel_id=16, replica_groups=mesh['dp'=8,'seq'=4] {'dp','seq'}, use_global_device_ids=true, to_apply=%region_29.30.clone | all-reduce | flops 9216 | bytes 73728
  1338.6 65.8 %reduce-scatter.36.cloned.1.call-done = f32[768,96]{0,1:T(8,128)} async-done(((f32[768,768]{0,1:T(8,128)}), f32[768,96]{0,1:T(8,128)}) %reduce-scatter.36.cloned.1.call-update) | async-done | bytes 294928 | tf_op jit(solution)/shard_map/reduce_scatter | solution.py:120
  1411.2 65.3 %reduce-scatter.34.cloned.1.call-done = f32[768,96]{0,1:T(8,128)} async-done(((f32[768,768]{0,1:T(8,128)}), f32[768,96]{0,1:T(8,128)}) %reduce-scatter.34.cloned.1.call-update) | async-done | bytes 294928 | tf_op jit(solution)/shard_map/reduce_scatter | solution.py:119
  1484.5 13.4 reduce-scatter.50.cloned.1.call-done
  1499.6 20.6 %reduce-scatter.48.cloned.1.call-done = bf16[192,96]{1,0:T(8,128)(2,1)} async-done(((bf16[768,96]{1,0:T(8,128)(2,1)}), bf16[192,96]{1,0:T(8,128)(2,1)}) %reduce-scatter.48.cloned.1.call-update) | async-done | bytes 36880
  (421 shorter events, 391.6 us)
Async XLA Ops:
  7.2 68.6 %copy-start.49 = (bf16[2,512,768]{2,1,0:T(8,128)(2,1)S(1)}, bf16[2,512,768]{2,1,0:T(8,128)(2,1)}, u32[]{:S(2)}) copy-start(bf16[2,512,768]{2,1,0:T(8,128)(2,1)} %param.12) | copy-start | bytes 4718596
  7.2 68.6 %all-gather.11.cloned.1.call-start = ((), (), s32[]{:S(2)}) async-start(), calls=%async_computation.14 | async-start | bytes 1327104 | tf_op jit(solution)/shard_map/all_gather | solution.py:108
  15.3 86.1 %all-gather.13.cloned.1.call-start = ((), (), s32[]{:S(2)}) async-start(), calls=%async_computation.15 | async-start | bytes 1327104 | tf_op jit(solution)/shard_map/all_gather | solution.py:109
  22.0 272.7 %all-gather.19.cloned.1.call-start = ((), (), s32[]{:S(2)}) async-start(), calls=%async_computation.18 | async-start | bytes 1327104 | tf_op jit(solution)/shard_map/all_gather | solution.py:107
  28.7 270.6 %all-gather.17.cloned.1.call-start = ((), (), s32[]{:S(2)}) async-start(), calls=%async_computation.17 | async-start | bytes 3932160 | tf_op jit(solution)/shard_map/all_gather | solution.py:394
  75.0 34.9 %copy-start.33 = (f32[4,768]{1,0:T(4,128)}, f32[4,768]{1,0:T(4,128)S(1)}, u32[]{:S(2)}) copy-start(f32[4,768]{1,0:T(4,128)S(1)} %copy.124) | copy-start | bytes 36868
  117.7 188.1 %all-gather.15.cloned.1.call-start = ((), (), s32[]{:S(2)}) async-start(), calls=%async_computation.16 | async-start | bytes 15728640 | tf_op jit(solution)/shard_map/all_gather | solution.py:393
  121.7 252.2 %all-gather.21.cloned.1.call-start = ((), (), s32[]{:S(2)}) async-start(), calls=%async_computation.19 | async-start | bytes 1327104 | tf_op jit(solution)/shard_map/all_gather | solution.py:110
  128.2 253.1 %all-gather.23.cloned.1.call-start = ((), (), s32[]{:S(2)}) async-start(), calls=%async_computation.20 | async-start | bytes 5308416 | tf_op jit(solution)/shard_map/all_gather | solution.py:111
  136.7 325.5 %all-gather.25.cloned.1.call-start = ((), (), s32[]{:S(2)}) async-start(), calls=%async_computation.21 | async-start | bytes 5308416 | tf_op jit(solution)/shard_map/all_gather | solution.py:112
  144.8 680.4 %reduce-scatter.38.cloned.1.call-start = ((), (), s32[]{:S(2)}) async-start(), calls=%async_computation.27 | async-start | bytes 2654208 | tf_op jit(solution)/shard_map/reduce_scatter | solution.py:121
  193.3 45.0 %copy-start.48 = (f32[2,24]{1,0:T(2,128)S(1)}, f32[2,24]{1,0:T(2,128)}, u32[]{:S(2)}) copy-start(f32[2,24]{1,0:T(2,128)} %param.21) | copy-start | bytes 580
  193.3 101.3 %copy-start.50 = (bf16[2,512,768]{2,1,0:T(8,128)(2,1)S(1)}, bf16[2,512,768]{2,1,0:T(8,128)(2,1)}, u32[]{:S(2)}) copy-start(bf16[2,512,768]{2,1,0:T(8,128)(2,1)} %param.12) | copy-start | bytes 4718596
  299.3 47.0 %copy-start.16 = (bf16[2,4,128,12,64]{2,1,0,4,3:T(4,128)(2,1)}, bf16[2,4,128,12,64]{2,1,0,4,3:T(4,128)(2,1)S(1)}, u32[]{:S(2)}) copy-start(bf16[2,4,128,12,64]{2,1,0,4,3:T(4,128)(2,1)S(1)} %reshape_reshape.3) | copy-start | bytes 4718596
  522.0 305.2 %reduce-scatter.32.cloned.1.call-start = ((), (), s32[]{:S(2)}) async-start(), calls=%async_computation.24 | async-start | bytes 2654208 | tf_op jit(solution)/shard_map/reduce_scatter | solution.py:118
  573.9 255.2 %reduce-scatter.44.cloned.1.call-start = ((), (), s32[]{:S(2)}) async-start(), calls=%async_computation.30 | async-start | bytes 10616832 | tf_op jit(solution)/shard_map/reduce_scatter | solution.py:123
  584.8 407.0 %reduce-scatter.40.cloned.1.call-start = ((), (), s32[]{:S(2)}) async-start(), calls=%async_computation.28 | async-start | bytes 10616832 | tf_op jit(solution)/shard_map/reduce_scatter | solution.py:122
  595.6 456.7 %reduce-scatter.30.cloned.1.call-start = ((), (), s32[]{:S(2)}) async-start(), calls=%async_computation.23 | async-start | bytes 7864320 | tf_op jit(solution)/shard_map/reduce_scatter | solution.py:336
  766.5 470.2 %reduce-scatter.28.cloned.1.call-start = ((), (), s32[]{:S(2)}) async-start(), calls=%async_computation.22 | async-start | bytes 31457280 | tf_op jit(solution)/shard_map/reduce_scatter | solution.py:335
  825.2 434.2 %reduce-scatter.52.cloned.1.call-start = ((), (), s32[]{:S(2)}) async-start(), calls=%async_computation.34 | async-start | bytes 245760
  827.1 454.9 %reduce-scatter.46.cloned.1.call-start = ((), (), s32[]{:S(2)}) async-start(), calls=%async_computation.31 | async-start | bytes 245760
  829.0 506.0 %reduce-scatter.54.cloned.1.call-start = ((), (), s32[]{:S(2)}) async-start(), calls=%async_computation.35 | async-start | bytes 737280
  831.5 505.4 %reduce-scatter.42.cloned.1.call-start = ((), (), s32[]{:S(2)}) async-start(), calls=%async_computation.29 | async-start | bytes 737280 | tf_op jit(solution)/shard_map/reduce_scatter | solution.py:138
  994.0 410.3 %reduce-scatter.36.cloned.1.call-start = ((), (), s32[]{:S(2)}) async-start(), calls=%async_computation.26 | async-start | bytes 2654208 | tf_op jit(solution)/shard_map/reduce_scatter | solution.py:120
  1054.4 183.9 %copy-start.13 = (f32[2,128,768]{2,0,1:T(2,128)}, f32[2,128,768]{2,0,1:T(2,128)S(1)}, u32[]{:S(2)}) copy-start(f32[2,128,768]{2,0,1:T(2,128)S(1)} %copy.149) | copy-start | bytes 2359300
  1055.0 187.4 %copy-start.14 = (f32[2,128,768]{2,0,1:T(2,128)}, f32[2,128,768]{2,0,1:T(2,128)S(1)}, u32[]{:S(2)}) copy-start(f32[2,128,768]{2,0,1:T(2,128)S(1)} %copy.146) | copy-start | bytes 2359300
  1246.5 229.9 %reduce-scatter.34.cloned.1.call-start = ((), (), s32[]{:S(2)}) async-start(), calls=%async_computation.25 | async-start | bytes 2654208 | tf_op jit(solution)/shard_map/reduce_scatter | solution.py:119
  1251.1 246.8 %reduce-scatter.50.cloned.1.call-start = ((), (), s32[]{:S(2)}) async-start(), calls=%async_computation.33 | async-start | bytes 245760
  1251.6 37.2 %copy-start.2 = (f32[2,128,4,768]{3,2,1,0:T(4,128)S(1)}, f32[2,128,4,768]{3,2,1,0:T(4,128)}, u32[]{:S(2)}) copy-start(f32[2,128,4,768]{3,2,1,0:T(4,128)} %copy-done.1) | copy-start | bytes 9437188
  1406.1 114.0 %reduce-scatter.48.cloned.1.call-start = ((), (), s32[]{:S(2)}) async-start(), calls=%async_computation.32 | async-start | bytes 245760
  1406.2 72.1 %copy-start.12 = (f32[1024,768]{1,0:T(8,128)S(1)}, f32[1024,768]{1,0:T(8,128)}, u32[]{:S(2)}) copy-start(f32[1024,768]{1,0:T(8,128)} %copy-done.11) | copy-start | bytes 9437188
  1406.2 72.1 %copy-start.41 = (f32[1024]{0:T(1024)S(1)}, f32[1024]{0:T(1024)}, u32[]{:S(2)}) copy-start(f32[1024]{0:T(1024)} %copy-done.40) | copy-start | bytes 12292
  (45 other events, 311.0 us)
Sparse Core Ops, SparseCore 0:
  15.4 43.4 all-gather.10
  61.7 39.6 all-gather.12
  103.6 39.8 all-gather.18
  144.8 27.1 all-gather.16
  173.5 82.5 all-gather.14
  258.7 41.1 all-gather.20
  302.0 79.2 all-gather.22
  383.3 78.7 all-gather.24
  522.1 67.7 reduce-scatter.37
  593.3 68.8 reduce-scatter.31
  665.8 161.3 reduce-scatter.43
  830.5 161.2 reduce-scatter.39
  994.3 57.9 reduce-scatter.29
  1054.8 181.9 reduce-scatter.27
  1239.6 19.7 reduce-scatter.51
  1262.2 19.7 reduce-scatter.45
  1284.4 22.1 reduce-scatter.53
  1308.9 22.1 reduce-scatter.41
  1334.6 69.6 reduce-scatter.35
  1407.7 68.7 reduce-scatter.33
  1478.9 18.9 reduce-scatter.49
  1500.4 19.7 reduce-scatter.47

commit v2 on v1

--- a/solution.py
+++ b/solution.py
@@ -94,54 +94,41 @@
     return left_term + right_term
 
 
+def gather_grouped(shards):
+    local_block = jnp.concatenate(shards, axis=1)
+    across = lax.all_gather(local_block, "dp", axis=1, tiled=False)
+    return lax.all_gather(across, "seq", axis=0, tiled=True)
+
+
+def split_grouped(gathered, widths):
+    pieces, at = [], 0
+    for width in widths:
+        piece = gathered[:, :, at : at + width]
+        pieces.append(piece.reshape(piece.shape[0], -1))
+        at += width
+    return pieces
+
+
 def gather_weights(w_query, w_key, w_value, w_output, w_inner, w_outer):
-    partial_rows = (
-        lax.all_gather(w_query, "seq", axis=0, tiled=True),
-        lax.all_gather(w_key, "seq", axis=0, tiled=True),
-        lax.all_gather(w_value, "seq", axis=0, tiled=True),
-        lax.all_gather(w_output, "seq", axis=0, tiled=True),
-        lax.all_gather(w_inner, "seq", axis=0, tiled=True),
-        lax.all_gather(w_outer, "seq", axis=1, tiled=True),
-    )
-    return (
-        lax.all_gather(partial_rows[0], "dp", axis=1, tiled=True),
-        lax.all_gather(partial_rows[1], "dp", axis=1, tiled=True),
-        lax.all_gather(partial_rows[2], "dp", axis=1, tiled=True),
-        lax.all_gather(partial_rows[3], "dp", axis=1, tiled=True),
-        lax.all_gather(partial_rows[4], "dp", axis=1, tiled=True),
-        lax.all_gather(partial_rows[5], "dp", axis=0, tiled=True),
-    )
-
-
-def reduce_grads(weight_grads):
-    partial_sums = (
-        lax.psum_scatter(weight_grads[0], "dp", scatter_dimension=1, tiled=True),
-        lax.psum_scatter(weight_grads[1], "dp", scatter_dimension=1, tiled=True),
-        lax.psum_scatter(weight_grads[2], "dp", scatter_dimension=1, tiled=True),
-        lax.psum_scatter(weight_grads[3], "dp", scatter_dimension=1, tiled=True),
-        lax.psum_scatter(weight_grads[4], "dp", scatter_dimension=1, tiled=True),
-        lax.psum_scatter(weight_grads[5], "dp", scatter_dimension=0, tiled=True),
-    )
-    return (
-        lax.psum_scatter(
-            partial_sums[0].astype(jnp.bfloat16), "seq", scatter_dimension=0, tiled=True
-        ).astype(jnp.float32),
-        lax.psum_scatter(
-            partial_sums[1].astype(jnp.bfloat16), "seq", scatter_dimension=0, tiled=True
-        ).astype(jnp.float32),
-        lax.psum_scatter(
-            partial_sums[2].astype(jnp.bfloat16), "seq", scatter_dimension=0, tiled=True
-        ).astype(jnp.float32),
-        lax.psum_scatter(
-            partial_sums[3].astype(jnp.bfloat16), "seq", scatter_dimension=0, tiled=True
-        ).astype(jnp.float32),
-        lax.psum_scatter(
-            partial_sums[4].astype(jnp.bfloat16), "seq", scatter_dimension=0, tiled=True
-        ).astype(jnp.float32),
-        lax.psum_scatter(
-            partial_sums[5].astype(jnp.bfloat16), "seq", scatter_dimension=1, tiled=True
-        ).astype(jnp.float32),
-    )
+    first = gather_grouped((w_query, w_key, w_value))
+    second = gather_grouped((w_output, w_inner, w_outer.T))
+    wq, wk, wv = split_grouped(first, (w_query.shape[1], w_key.shape[1], w_value.shape[1]))
+    wo, wi, wu_t = split_grouped(second, (w_output.shape[1], w_inner.shape[1], w_outer.shape[0]))
+    return (wq, wk, wv, wo, wi, wu_t.T)
+
+
+def reduce_grouped(grads):
+    dp_size = lax.psum(1, "dp")
+    chunks = [grad.reshape(grad.shape[0], dp_size, grad.shape[1] // dp_size) for grad in grads]
+    stacked = jnp.concatenate(chunks, axis=2)
+    over_seq = lax.psum_scatter(stacked, "seq", scatter_dimension=0, tiled=True)
+    over_dp = lax.psum_scatter(over_seq.astype(jnp.bfloat16), "dp", scatter_dimension=1, tiled=True)
+    over_dp = over_dp[:, 0].astype(jnp.float32)
+    pieces, at = [], 0
+    for chunk in chunks:
+        pieces.append(over_dp[:, at : at + chunk.shape[2]])
+        at += chunk.shape[2]
+    return pieces
 
 
 HALF_FULL = WINDOW // 2
@@ -418,6 +405,7 @@
     grad_branch = grad_mixed.astype(jnp.bfloat16)
     grad_output = product_left(attended, grad_branch)
     grad_attended = product_right(grad_branch, wo).astype(jnp.bfloat16)
+    early = reduce_grouped((grad_output, grad_inner, grad_outer.T))
 
     grad_queries, grad_full, grad_pooled = attention_bwd(grad_attended, att_saved, starts, seq_index)
     grad_keys = (
@@ -441,7 +429,8 @@
         + product_right(grad_keys, wk)
         + product_right(grad_values, wv)
     )
-    accum = reduce_grads((grad_query_w, grad_key_w, grad_value_w, grad_output, grad_inner, grad_outer))
+    late = reduce_grouped((grad_query_w, grad_key_w, grad_value_w))
+    accum = (late[0], late[1], late[2], early[0], early[1], early[2].T)
     small_sums = (
         lax.psum_scatter(grad_pooling, ("dp", "seq"), scatter_dimension=2, tiled=True),
         lax.psum_scatter(

time: 1540 us -> 1560 us (1.013)
  waiting for transfers between devices: 654 us -> 381 us
  local copies, waits for them, and re-layouts: 246 us -> 481 us
  other arithmetic: 139 us -> 216 us
  matrix products: 226 us -> 209 us
    reduce_scatter x1, waiting for transfers between devices: 182 us -> 90.4 us  [attention_bwd(): full = lax.psum_scatter(full, 'seq', scatter_dimension=1, tiled=True)]
    reduce_scatter x1, waiting for transfers between devices: 58.3 us -> 0.01 us  [attention_bwd(): pooled = lax.psum_scatter(pooled, 'seq', scatter_dimension=1, tiled=True)]
    unnamed x27 -> x11, waiting for transfers between devices: 58.2 us -> 0.18 us
    all_gather x6 -> x3, waiting for transfers between devices: 67.4 us -> 15.1 us  [the longest x1 15.1 us: gather_grouped(): across = lax.all_gather(local_block, 'dp', axis=1, tiled=False)]
    concatenate x0 -> x4, local copies, waits for them, and re-layouts: none -> 52.3 us  [the longest x1 44 us: attention_fwd(): jnp.concatenate([window_rows(kv_all, starts[0], HALF_FULL), kv_local.resh...]
    reshape x0 -> x7, local copies, waits for them, and re-layouts: none -> 29.5 us  [the longest x5 24.7 us: reduce_grouped(): grad.reshape(grad.shape[0], dp_size, grad.shape[1] // dp_size)]
    dynamic_slice x4 -> x3, local copies, waits for them, and re-layouts: 1.63 us -> 28.6 us  [window_rows(): lax.dynamic_slice_in_dim(source[g], starts[g, b], length, 0)]
    another operation x8 -> x12, other arithmetic: 3.49 us -> 30 us  [window_rows(): jnp.stack([jnp.stack([lax.dynamic_slice_in_dim(source[g], starts[g, b], l...]
  transfers between devices with their start and end apart: 22 -> 11, of which waited for: 12 -> 6; matrix products, arithmetic and copies ran while one was open for 35% -> 28% of each run, Pallas kernels for 0% -> 0%
where the time goes in v2:
time: 1560 us; the launch traced here: 1540 us
  local copies, waits for them, and re-layouts  481 us (31%)
  waiting for transfers between devices  381 us (24%)
  other arithmetic  216 us (14%)
  matrix products  209 us (13%)
  blocking collectives  196 us (13%)
  between operations  60.9 us (4%)
    reduce_scatter x2, waiting for transfers between devices, reduce_grouped(): over_seq = lax.psum_scatter(stacked, 'seq', scatter_dimension=0, tiled=True)  145 us
    reduce_scatter x2, waiting for transfers between devices, reduce_grouped(): lax.psum_scatter(over_seq.astype(jnp.bfloat16), 'dp', scatter_dimension=1...  129 us
    reduce_scatter x1, waiting for transfers between devices, attention_bwd(): full = lax.psum_scatter(full, 'seq', scatter_dimension=1, tiled=True)  90.4 us
    dot_general x6, matrix products, product(): return jnp.dot(left, right, preferred_element_type=jnp.float32)  56 us
    unnamed x197, local copies, waits for them, and re-layouts  48.5 us
    dynamic_update_slice x32, local copies, waits for them, and re-layouts, window_add(): lax.dynamic_update_slice_in_dim(row, current + updates[g, b], start, 0)  46.8 us
    concatenate x1, local copies, waits for them, and re-layouts, attention_fwd(): jnp.concatenate([window_rows(kv_all, starts[0], HALF_FULL), kv_local.resh...  44 us
    all_gather x1, blocking collectives, local(): pool_full = lax.all_gather(pool_weight, ('dp', 'seq'), axis=2, tiled=True)  43.7 us
  transfers between devices with their start and end apart: 11, of which 6 were waited for; matrix products, arithmetic and copies ran while one was open for 28% of the time, Pallas kernels for 0%

profile of v2, /device:TPU:0, one launch (start us, length us, event | category | flops | bytes accessed | tf_op | source)
XLA Modules:
  0.0 1544.2 jit_solution(5474983064292512882)
XLA Ops:
  10.1 35.4 %all-gather = bf16[192,2304]{0,1:T(8,128)(2,1)S(1)} all-gather(bf16[192,288]{0,1:T(8,128)(2,1)S(1)} %pad_maximum_fusion.13), channel_id=2, replica_groups=mesh['dp'=8,'seq'=4] {'dp'}, dimensions={1}, use_global_device_ids=true | all-gather | bytes 995328 | tf_op jit(solution)/shard_map/all_gather | solution.py:99
  48.5 43.7 %all_gather.37 = f32[2,4,768]{1,0,2:T(2,128)S(1)} all-gather(f32[2,4,24]{1,0,2:T(2,128)S(1)} %copy.147), channel_id=1, replica_groups=mesh['dp'=8,'seq'=4] {'dp','seq'}, dimensions={2}, use_global_device_ids=true | all-gather | bytes 25344 | tf_op jit(solution)/shard_map/all_gather | solution.py:360
  134.2 15.1 all-gather.19.cloned.1.call-done
  168.5 10.5 pad_maximum_fusion.4
  240.6 18.1 %gather_fusion.1 = s32[2048]{0:T(1024)} fusion(s32[2,8]{0,1:T(8,128)S(1)} %broadcast_multiply_fusion.3, s32[2048]{0:T(1024)S(1)} %bitcast.363), kind=kCustom, calls=%fused_computation.1 | custom fusion | bytes 32768 | tf_op jit(solution)/shard_map/jit(take_along_axis)/gather | solution.py:145
  272.6 39.2 %all-gather.3 = f32[32,24,2]{1,2,0:T(2,128)S(1)} all-gather(f32[1,24,2]{1,2,0:T(2,128)S(1)} %bitcast.425), channel_id=1, replica_groups=mesh['dp'=8,'seq'=4] {'dp','seq'}, dimensions={0}, use_global_device_ids=true | all-gather | bytes 6336 | tf_op jit(solution)/shard_map/all_gather | solution.py:361
  313.9 37.4 %all-gather.4 = f32[32,24,2]{1,2,0:T(2,128)S(1)} all-gather(f32[1,24,2]{1,2,0:T(2,128)} %bitcast.426), channel_id=1, replica_groups=mesh['dp'=8,'seq'=4] {'dp','seq'}, dimensions={0}, use_global_device_ids=true | all-gather | bytes 6336 | tf_op jit(solution)/shard_map/all_gather | solution.py:362
  429.6 14.1 fusion.142
  452.9 25.1 %fusion.141 = (bf16[1,2048,1536]{1,0,2:T(2,128)(2,1)S(1)}, bf16[1,2048,1536]{1,0,2:T(2,128)(2,1)}) fusion(bf16[2,2048,1536]{1,0,2:T(2,128)(2,1)} %all-gather.13.cloned.1.call-done), kind=kLoop, calls=%fused_computation.449 | loop fusion | bytes 25165824 | tf_op jit(solution)/shard_map/slice | solution.py:156
  477.9 26.2 %constant_dynamic-slice_fusion.19 = (bf16[1,64,1536]{1,0,2:T(2,128)(2,1)S(1)}, bf16[1,64,1536]{1,0,2:T(2,128)(2,1)S(1)}, bf16[1,64,1536]{1,0,2:T(2,128)(2,1)S(1)...) fusion(bf16[1,2048,1536]{1,0,2:T(2,128)(2,1)} %get-tuple-elemen, ...), kind=kLoop, calls=%fused_computation.287 | loop fusion | bytes 6291504 | tf_op jit(solution)/shard_map/dynamic_slice | solution.py:156
  531.7 44.0 %concatenate.86 = bf16[2,4,416,1536]{2,1,0,3:T(4,128)(2,1)} concatenate(bf16[2,4,64,1536]{2,1,0,3:T(4,128)(2,1)} %copy.151, bf16[2,4,128,1536]{2,1,0,3:T(4,128)(2,1)S(1)} %pad_maximum_fusion.6, bf16[2,4,64,1536]{2,1,0,3:T(4,128)(2,1)} %pad_maximum_fusion.7, bf16[2,4,64,1536]{2,1,0,3:T(4,128)(2,1)} %copy.152, bf16[2,4,32,1536]{2,1,0,3:T(4,128)(2,1)} %copy.153, ...), dimensions={2} | concatenate | bytes 20447232 | tf_op jit(solution)/shard_map/concatenate | solution.py:247
  593.4 13.4 fusion.153
  606.8 10.7 fusion.32
  625.7 34.6 %multiply_convert_fusion.1 = (bf16[1024,3072]{1,0:T(8,128)(2,1)S(1)}, f32[1024,3072]{1,0:T(8,128)}, f32[1024,3072]{1,0:T(8,128)}) fusion(bf16[768,3072]{1,0:T(8,128)(2,1)S(1)} %bitcast.393, f32[1024,768]{1,0:T(8,128)S(1)} %get-tuple-element.155, f32[768]{0:T(1024)S(1)} %copy-done.50, f32[768]{0:T(1024)S(1)} %get-tuple-element.177, f32[1024]{0:T(1024)S(1)} %fusion.108, ...), kind=kOutput, calls=%fused_computation.81 | convolution fusion | flops 5040242688 | bytes 39335936 | tf_op jit(solution)/shard_map/dot_general | solution.py:78
  672.1 18.8 %add_convert_fusion = bf16[1024,3072]{1,0:T(8,128)(2,1)} fusion(f32[1024,3072]{1,0:T(8,128)} %get-tuple-element.28, f32[1024,3072]{1,0:T(8,128)} %get-tuple-element.156, bf16[768,3072]{1,0:T(8,128)(2,1)} %bitcast.395, f32[1024,768]{1,0:T(8,128)} %get-tuple-element.26, f32[1024]{0:T(1024)S(1)} %negate_multiply_fusion.2), kind=kOutput, calls=%fused_computation.80 | convolution fusion | flops 4877451264 | bytes 39325696 | tf_op jit(solution)/shard_map/dot_general | solution.py:88
  706.9 16.2 %fusion.12 = f32[2,4,12,64,416]{4,3,2,1,0:T(8,128)} fusion(bf16[2,4,128,12,64]{2,1,0,4,3:T(4,128)(2,1)S(1)} %reshape.1214, f32[2,4,12,128,416]{3,4,2,1,0:T(8,128)} %get-tuple-element.153, f32[2,4,12,128]{3,2,1,0:T(8,128)S(1)} %copy-done.49), kind=kOutput, calls=%fused_computation.105 | convolution fusion | flops 664535040 | bytes 32292864 | tf_op jit(solution)/shard_map/gbhqk,gbqhd->gbkhd/dot_general | solution.py:297
  723.1 16.2 %multiply_reduce_fusion = (f32[2,4,12,128]{3,2,1,0:T(8,128)S(1)}, f32[2,4,12,128,416]{3,4,2,1,0:T(8,128)}) fusion(f32[2,4,12,128,416]{3,4,2,1,0:T(8,128)} %get-tuple-element.153, f32[2,4,12,128]{3,2,1,0:T(8,128)S(1)} %copy-done.49, bf16[2,4,416,12,64]{2,4,3,1,0:T(8,128)(2,1)} %bitcast.387, bf16[2,4,128,12,64]{2,1,0,4,3:T(4,128)(2,1)S(1)} %reshape.1214), kind=kOutput, calls=%fused_computation.74 | convolution fusion | flops 669634560 | bytes 47677440 | tf_op jit(solution)/shard_map/gbqhd,gbkhd->gbhqk/dot_general | solution.py:286
  739.3 11.9 copy.174
  751.2 17.8 %multiply_convert_fusion = bf16[2,4,12,128,416]{3,4,2,1,0:T(8,128)(2,1)} fusion(f32[2,4,12,128,416]{3,4,2,1,0:T(8,128)} %get-tuple-element.161, f32[2,4,12,128]{3,2,1,0:T(8,128)S(1)} %get-tuple-element.160, f32[2,4,12,128,416]{3,4,2,1,0:T(8,128)} %get-tuple-element.153, f32[2,4,12,128]{3,2,1,0:T(8,128)S(1)} %copy-done.49), kind=kLoop, calls=%fused_computation.73 | loop fusion | flops 20447232 | bytes 51216384 | tf_op jit(solution)/shard_map/convert_element_type | solution.py:290
  769.0 13.3 broadcast_multiply_fusion
  782.3 11.7 copy.173
  832.7 11.6 broadcast_in_dim.194
  850.2 23.3 %fusion.139 = (f32[1,2048,1536]{2,1,0:T(8,128)}, f32[2048,1536]{1,0:T(8,128)}, f32[2048,1536]{1,0:T(8,128)}, f32[1,2048,1536]{2,1,0:T(8,128)}) fusion(f32[2,2048,1536]{2,1,0:T(8,128)} %constant_dynamic-update-slice_fusion), kind=kLoop, calls=%fused_computation.447 | loop fusion | bytes 75497472 | tf_op jit(solution)/shard_map/slice | solution.py:168
  952.7 17.6 %pad_maximum_fusion = f32[2,2048,1536]{2,1,0:T(8,128)} fusion(f32[1,2048,1536]{2,1,0:T(8,128)} %dynamic_update_slice.122, f32[1,2048,1536]{2,1,0:T(8,128)} %dynamic_update_slice.114), kind=kLoop, calls=%fused_computation.71 | loop fusion | flops 6291456 | bytes 50331648 | tf_op jit(solution)/shard_map/stack | solution.py:174
  1009.9 14.9 pad_maximum_fusion.1
  1061.8 90.4 %reduce-scatter.10.cloned.1.call-done = f32[2,512,1536]{2,1,0:T(8,128)} async-done(((f32[2,2048,1536]{2,1,0:T(8,128)}), f32[2,512,1536]{2,1,0:T(8,128)}) %reduce-scatter.10.cloned.1.call-update) | async-done | bytes 6291472 | tf_op jit(solution)/shard_map/reduce_scatter | solution.py:322
  1177.5 12.5 pad_maximum_fusion.2
  1190.1 121.5 %reduce-scatter.18.cloned.1.call-done = f32[192,8,864]{2,0,1:T(8,128)} async-done(((f32[768,8,864]{2,0,1:T(8,128)}), f32[192,8,864]{2,0,1:T(8,128)}) %reduce-scatter.18.cloned.1.call-update) | async-done | bytes 5308432 | tf_op jit(solution)/shard_map/reduce_scatter | solution.py:124
  1328.1 40.4 %all-reduce.3 = (f32[2,4,768]{2,1,0:T(4,128)S(1)}, f32[2,768]{1,0:T(2,128)S(1)}, f32[2,768]{1,0:T(2,128)S(1)}) all-reduce(f32[2,4,768]{2,1,0:T(4,128)S(1)} %pad_maximum_fusion.14, f32[2,768]{1,0:T(2,128)S(1)} %pad_maximum_fusion.15, f32[2,768]{1,0:T(2,128)S(1)} %pad_maximum_fusion.16), channel_id=10, replica_groups=mesh['dp'=8,'seq'=4] {'dp','seq'}, use_global_device_ids=true, to_apply=%region_21.22.clone | all-reduce | flops 9216 | bytes 73728
  1369.2 23.8 %reduce-scatter.14.cloned.1.call-done = f32[192,8,288]{2,0,1:T(8,128)} async-done(((f32[768,8,288]{2,0,1:T(8,128)}), f32[192,8,288]{2,0,1:T(8,128)}) %reduce-scatter.14.cloned.1.call-update) | async-done | bytes 1769488 | tf_op jit(solution)/shard_map/reduce_scatter | solution.py:124
  1397.2 71.0 %reduce-scatter.20.cloned.1.call-done = bf16[192,1,864]{2,0,1:T(8,128)(2,1)} async-done(((bf16[192,8,864]{2,0,1:T(8,128)(2,1)}), bf16[192,1,864]{2,0,1:T(8,128)(2,1)}) %reduce-scatter.20.cloned.1.call-update) | async-done | bytes 331792 | tf_op jit(solution)/shard_map/reduce_scatter | solution.py:125
  1477.0 58.5 %reduce-scatter.16.cloned.1.call-done = bf16[192,1,288]{2,0,1:T(8,128)(2,1)} async-done(((bf16[192,8,288]{2,0,1:T(8,128)(2,1)}), bf16[192,1,288]{2,0,1:T(8,128)(2,1)}) %reduce-scatter.16.cloned.1.call-update) | async-done | bytes 110608 | tf_op jit(solution)/shard_map/reduce_scatter | solution.py:125
  (470 shorter events, 524.4 us)
Async XLA Ops:
  7.2 40.2 %copy-start.41 = (bf16[384,192]{0,1:T(8,128)(2,1)S(1)}, bf16[384,192]{0,1:T(8,128)(2,1)}, u32[]{:S(2)}) copy-start(bf16[384,192]{0,1:T(8,128)(2,1)} %param.18) | copy-start | bytes 442372
  7.2 40.2 %copy-start.42 = (bf16[192,384]{1,0:T(8,128)(2,1)S(1)}, bf16[192,384]{1,0:T(8,128)(2,1)}, u32[]{:S(2)}) copy-start(bf16[192,384]{1,0:T(8,128)(2,1)} %param.17) | copy-start | bytes 442372
  7.2 40.2 %copy-start.58 = (bf16[192,96]{1,0:T(8,128)(2,1)S(1)}, bf16[192,96]{1,0:T(8,128)(2,1)}, u32[]{:S(2)}) copy-start(bf16[192,96]{1,0:T(8,128)(2,1)} %param.16) | copy-start | bytes 110596
  7.2 86.5 %all-gather.11.cloned.1.call-start = ((), (), s32[]{:S(2)}) async-start(), calls=%async_computation.6 | async-start | bytes 5898240 | tf_op jit(solution)/shard_map/all_gather | solution.py:100
  9.1 39.3 %copy-start.69 = (f32[2,4,24]{2,1,0:T(4,128)S(1)}, f32[2,4,24]{2,1,0:T(4,128)}, u32[]{:S(2)}) copy-start(f32[2,4,24]{2,1,0:T(4,128)} %param.19) | copy-start | bytes 2308
  47.3 102.0 %all-gather.19.cloned.1.call-start = ((), (), s32[]{:S(2)}) async-start(), calls=%async_computation.16 | async-start | bytes 3096576 | tf_op jit(solution)/shard_map/all_gather | solution.py:99
  48.3 354.8 %all-gather.15.cloned.1.call-start = ((), (), s32[]{:S(2)}) async-start(), calls=%async_computation.8 | async-start | bytes 3932160 | tf_op jit(solution)/shard_map/all_gather | solution.py:381
  93.7 32.5 %copy-start.43 = (f32[4,768]{1,0:T(4,128)}, f32[4,768]{1,0:T(4,128)S(1)}, u32[]{:S(2)}) copy-start(f32[4,768]{1,0:T(4,128)S(1)} %copy.150) | copy-start | bytes 36868
  112.5 13.7 copy-start.4
  134.0 290.0 %all-gather.17.cloned.1.call-start = ((), (), s32[]{:S(2)}) async-start(), calls=%async_computation.9 | async-start | bytes 13762560 | tf_op jit(solution)/shard_map/all_gather | solution.py:100
  163.7 289.2 %all-gather.13.cloned.1.call-start = ((), (), s32[]{:S(2)}) async-start(), calls=%async_computation.7 | async-start | bytes 15728640 | tf_op jit(solution)/shard_map/all_gather | solution.py:380
  179.0 12.1 copy-start.75
  179.0 877.4 %reduce-scatter.12.cloned.1.call-start = ((), (), s32[]{:S(2)}) async-start(), calls=%async_computation.11 | async-start | bytes 7864320 | tf_op jit(solution)/shard_map/reduce_scatter | solution.py:323
  179.1 53.2 %copy-start.63 = (s32[4]{0:T(128)}, s32[4]{0:T(128)S(1)}, u32[]{:S(2)}) copy-start(s32[4]{0:T(128)S(1)} %broadcast_clamp_fusion.3) | copy-start | bytes 52
  232.3 26.3 %copy-start.54 = (s32[2,4,128]{2,1,0:T(4,128)}, s32[2,4,128]{2,1,0:T(4,128)S(1)}, u32[]{:S(2)}) copy-start(s32[2,4,128]{2,1,0:T(4,128)S(1)} %broadcast_in_dim.167) | copy-start | bytes 12292
  259.9 12.6 copy-start.76
  369.8 330.4 %copy-start.46 = (f32[768]{0:T(1024)}, f32[768]{0:T(1024)S(1)}, u32[]{:S(2)}) copy-start(f32[768]{0:T(1024)S(1)} %get-tuple-element.177) | copy-start | bytes 9220
  606.8 10.7 copy-start.48
  621.0 39.3 %slice-start.7 = ((s8[4718592]{0:T(1024)(128)(4,1)}), s8[4194304]{0:T(1024)(128)(4,1)S(1)}, s32[]{:S(2)}) async-start(s8[4718592]{0:T(1024)(128)(4,1)} %bitcast.396), calls=%async_computation.24 | async-start | bytes 8388608
  625.0 75.1 %copy-start.2 = (f32[1024,768]{1,0:T(8,128)}, f32[1024,768]{1,0:T(8,128)S(1)}, u32[]{:S(2)}) copy-start(f32[1024,768]{1,0:T(8,128)S(1)} %get-tuple-element.155) | copy-start | bytes 9437188
  625.1 75.1 %copy-start.37 = (f32[1024]{0:T(1024)}, f32[1024]{0:T(1024)S(1)}, u32[]{:S(2)}) copy-start(f32[1024]{0:T(1024)S(1)} %broadcast_multiply_fusion.2) | copy-start | bytes 12292
  625.6 74.6 %copy-start.39 = (f32[1024]{0:T(1024)}, f32[1024]{0:T(1024)S(1)}, u32[]{:S(2)}) copy-start(f32[1024]{0:T(1024)S(1)} %fusion.108) | copy-start | bytes 12292
  625.7 34.6 %slice-start.8 = ((s8[4718592]{0:T(1024)(128)(4,1)}), s8[524288]{0:T(1024)(128)(4,1)S(1)}, s32[]{:S(2)}) async-start(s8[4718592]{0:T(1024)(128)(4,1)} %bitcast.396), calls=%async_computation.25 | async-start | bytes 1048576
  672.1 18.8 %copy-start.72 = (f32[1024]{0:T(1024)}, f32[1024]{0:T(1024)S(1)}, u32[]{:S(2)}) copy-start(f32[1024]{0:T(1024)S(1)} %negate_multiply_fusion.2) | copy-start | bytes 12292
  751.2 17.8 %copy-start.24 = (bf16[2,4,128,12,64]{2,1,0,4,3:T(4,128)(2,1)S(1)}, bf16[2,4,128,12,64]{2,1,0,4,3:T(4,128)(2,1)}, u32[]{:S(2)}) copy-start(bf16[2,4,128,12,64]{2,1,0,4,3:T(4,128)(2,1)} %reshape_reshape.3) | copy-start | bytes 4718596
  807.1 12.6 slice-start
  832.7 11.6 copy-start.11
  911.2 241.0 %reduce-scatter.10.cloned.1.call-start = ((), (), s32[]{:S(2)}) async-start(), calls=%async_computation.10 | async-start | bytes 31457280 | tf_op jit(solution)/shard_map/reduce_scatter | solution.py:322
  970.3 341.4 %reduce-scatter.18.cloned.1.call-start = ((), (), s32[]{:S(2)}) async-start(), calls=%async_computation.14 | async-start | bytes 27525120 | tf_op jit(solution)/shard_map/reduce_scatter | solution.py:124
  1024.9 368.1 %reduce-scatter.14.cloned.1.call-start = ((), (), s32[]{:S(2)}) async-start(), calls=%async_computation.12 | async-start | bytes 11796480 | tf_op jit(solution)/shard_map/reduce_scatter | solution.py:124
  1190.1 278.1 %reduce-scatter.20.cloned.1.call-start = ((), (), s32[]{:S(2)}) async-start(), calls=%async_computation.15 | async-start | bytes 3096576 | tf_op jit(solution)/shard_map/reduce_scatter | solution.py:125
  1316.2 219.3 %reduce-scatter.16.cloned.1.call-start = ((), (), s32[]{:S(2)}) async-start(), calls=%async_computation.13 | async-start | bytes 1327104 | tf_op jit(solution)/shard_map/reduce_scatter | solution.py:125
  (67 other events, 236.6 us)
Sparse Core Ops, SparseCore 0:
  47.5 43.9 all-gather.10
  93.6 55.7 all-gather.18
  150.9 27.1 all-gather.14
  179.5 73.1 all-gather.16
  254.1 84.2 all-gather.12
  911.3 56.3 reduce-scatter.11
  970.4 181.7 reduce-scatter.9
  1154.8 156.8 reduce-scatter.17
  1314.3 78.7 reduce-scatter.13
  1396.4 71.6 reduce-scatter.19
  1471.5 63.9 reduce-scatter.15

commit v3 on v2

--- a/solution.py
+++ b/solution.py
@@ -117,17 +117,21 @@
     return (wq, wk, wv, wo, wi, wu_t.T)
 
 
-def reduce_grouped(grads):
+def reduce_seq_stage(grads):
     dp_size = lax.psum(1, "dp")
     chunks = [grad.reshape(grad.shape[0], dp_size, grad.shape[1] // dp_size) for grad in grads]
-    stacked = jnp.concatenate(chunks, axis=2)
-    over_seq = lax.psum_scatter(stacked, "seq", scatter_dimension=0, tiled=True)
-    over_dp = lax.psum_scatter(over_seq.astype(jnp.bfloat16), "dp", scatter_dimension=1, tiled=True)
-    over_dp = over_dp[:, 0].astype(jnp.float32)
+    stacked = jnp.concatenate(chunks, axis=2).astype(jnp.bfloat16)
+    return lax.psum_scatter(stacked, "seq", scatter_dimension=0, tiled=True), [c.shape[2] for c in chunks]
+
+
+def reduce_dp_stage(stages):
+    joined = jnp.concatenate([stage for stage, _ in stages], axis=2)
+    over_dp = lax.psum_scatter(joined, "dp", scatter_dimension=1, tiled=True)[:, 0].astype(jnp.float32)
     pieces, at = [], 0
-    for chunk in chunks:
-        pieces.append(over_dp[:, at : at + chunk.shape[2]])
-        at += chunk.shape[2]
+    for _, widths in stages:
+        for width in widths:
+            pieces.append(over_dp[:, at : at + width])
+            at += width
     return pieces
 
 
@@ -319,8 +323,10 @@
     pooled = lax.dynamic_update_slice_in_dim(pooled, own_pooled, seq_index * shard_rows // STRIDE, 1)
     pooled = window_add(pooled, grad_kv[:, :, pcut[0] : pcut[1]], starts[2])
     pooled = window_add(pooled, grad_kv[:, :, pcut[2] : pcut[3]], starts[3])
-    full = lax.psum_scatter(full, "seq", scatter_dimension=1, tiled=True)
-    pooled = lax.psum_scatter(pooled, "seq", scatter_dimension=1, tiled=True)
+    full = lax.psum_scatter(full.astype(jnp.bfloat16), "seq", scatter_dimension=1, tiled=True)
+    pooled = lax.psum_scatter(pooled.astype(jnp.bfloat16), "seq", scatter_dimension=1, tiled=True)
+    full = full.astype(jnp.float32)
+    pooled = pooled.astype(jnp.float32)
     grad_queries = grad_queries.reshape(groups * shard_rows, width).astype(jnp.bfloat16)
     return grad_queries, full, pooled
 
@@ -357,9 +363,14 @@
     branch_blocks,
     grad_out,
 ):
-    pool_full = lax.all_gather(pool_weight, ("dp", "seq"), axis=2, tiled=True)
-    gain_full = lax.all_gather(ln_gain, ("dp", "seq"), axis=1, tiled=True)
-    bias_full = lax.all_gather(ln_bias, ("dp", "seq"), axis=1, tiled=True)
+    pool_rows_count = pool_weight.shape[0] * pool_weight.shape[1]
+    small_local = jnp.concatenate(
+        [pool_weight.reshape(pool_rows_count, -1), ln_gain, ln_bias], axis=0
+    )
+    small_full = lax.all_gather(small_local, ("dp", "seq"), axis=1, tiled=True)
+    pool_full = small_full[:pool_rows_count].reshape(pool_weight.shape[0], pool_weight.shape[1], -1)
+    gain_full = small_full[pool_rows_count : pool_rows_count + ln_gain.shape[0]]
+    bias_full = small_full[pool_rows_count + ln_gain.shape[0] :]
     weights = gather_weights(w_query, w_key, w_value, w_output, w_inner, w_outer)
     wq, wk, wv, wo, wi, wu = weights
     groups, shard_rows, width = hidden_in.shape
@@ -405,7 +416,7 @@
     grad_branch = grad_mixed.astype(jnp.bfloat16)
     grad_output = product_left(attended, grad_branch)
     grad_attended = product_right(grad_branch, wo).astype(jnp.bfloat16)
-    early = reduce_grouped((grad_output, grad_inner, grad_outer.T))
+    early = reduce_seq_stage((grad_output, grad_inner, grad_outer.T))
 
     grad_queries, grad_full, grad_pooled = attention_bwd(grad_attended, att_saved, starts, seq_index)
     grad_keys = (
@@ -429,8 +440,9 @@
         + product_right(grad_keys, wk)
         + product_right(grad_values, wv)
     )
-    late = reduce_grouped((grad_query_w, grad_key_w, grad_value_w))
-    accum = (late[0], late[1], late[2], early[0], early[1], early[2].T)
+    late = reduce_seq_stage((grad_query_w, grad_key_w, grad_value_w))
+    pieces = reduce_dp_stage((early, late))
+    accum = (pieces[3], pieces[4], pieces[5], pieces[0], pieces[1], pieces[2].T)
     small_sums = (
         lax.psum_scatter(grad_pooling, ("dp", "seq"), scatter_dimension=2, tiled=True),
         lax.psum_scatter(

time: 1560 us -> 1250 us (0.80)
  waiting for transfers between devices: 381 us -> 162 us
  blocking collectives: 196 us -> 120 us
    reduce_scatter x6 -> x5, waiting for transfers between devices: 365 us -> 148 us  [the longest x2 113 us: reduce_seq_stage(): lax.psum_scatter(stacked, 'seq', scatter_dimension=0, tiled=True)]
    all_gather x3 -> x1, blocking collectives: 120 us -> 42.3 us  [local(): small_full = lax.all_gather(small_local, ('dp', 'seq'), axis=1, tiled=True)]
    another operation x0 -> x4, other arithmetic: none -> 16.8 us
    unnamed x197 -> x199, local copies, waits for them, and re-layouts: 48.5 us -> 47.1 us
  transfers between devices with their start and end apart: 11 -> 10, of which waited for: 6 -> 5; matrix products, arithmetic and copies ran while one was open for 28% -> 33% of each run, Pallas kernels for 0% -> 0%
where the time goes in v3:
time: 1250 us; the launch traced here: 1230 us
  local copies, waits for them, and re-layouts  467 us (37%)
  other arithmetic  209 us (17%)
  matrix products  209 us (17%)
  waiting for transfers between devices  162 us (13%)
  blocking collectives  120 us (10%)
  between operations  61.6 us (5%)
    reduce_scatter x2, waiting for transfers between devices, reduce_seq_stage(): lax.psum_scatter(stacked, 'seq', scatter_dimension=0, tiled=True)  113 us
    dot_general x6, matrix products, product(): return jnp.dot(left, right, preferred_element_type=jnp.float32)  56.1 us
    unnamed x199, local copies, waits for them, and re-layouts  47.1 us
    dynamic_update_slice x32, local copies, waits for them, and re-layouts, window_add(): lax.dynamic_update_slice_in_dim(row, current + updates[g, b], start, 0)  46.8 us
    concatenate x1, local copies, waits for them, and re-layouts, attention_fwd(): jnp.concatenate([window_rows(kv_all, starts[0], HALF_FULL), kv_local.resh...  44 us
    all_gather x1, blocking collectives, local(): small_full = lax.all_gather(small_local, ('dp', 'seq'), axis=1, tiled=True)  42.3 us
    unnamed x1, blocking collectives  41.9 us
    dot_general x6, matrix products, product_right(): lax.dot_general(left, right, (((1,), (1,)), ((), ())), preferred_element_...  40.5 us
  transfers between devices with their start and end apart: 10, of which 5 were waited for; matrix products, arithmetic and copies ran while one was open for 33% of the time, Pallas kernels for 0%

profile of v3, /device:TPU:0, one launch (start us, length us, event | category | flops | bytes accessed | tf_op | source)
XLA Modules:
  0.0 1228.7 jit_solution(6361456177470935023)
XLA Ops:
  10.1 35.4 %all-gather = bf16[192,2304]{0,1:T(8,128)(2,1)S(1)} all-gather(bf16[192,288]{0,1:T(8,128)(2,1)S(1)} %pad_maximum_fusion.14), channel_id=2, replica_groups=mesh['dp'=8,'seq'=4] {'dp'}, dimensions={1}, use_global_device_ids=true | all-gather | bytes 995328 | tf_op jit(solution)/shard_map/all_gather | solution.py:99
  48.5 42.3 %all-gather.2 = f32[32,24,12]{1,2,0:T(8,128)S(1)} all-gather(f32[1,24,12]{1,2,0:T(8,128)S(1)} %maximum_bitcast_fusion.9), channel_id=1, replica_groups=mesh['dp'=8,'seq'=4] {'dp','seq'}, dimensions={0}, use_global_device_ids=true | all-gather | bytes 38016 | tf_op jit(solution)/shard_map/all_gather | solution.py:370
  131.8 13.7 %all-gather.18.cloned.1.call-done = bf16[8,864,192]{1,2,0:T(8,128)(2,1)} async-done(((bf16[1,864,192]{1,2,0:T(8,128)(2,1)}), bf16[8,864,192]{1,2,0:T(8,128)(2,1)}) %all-gather.18.cloned.1.call-update) | async-done | bytes 2654224 | tf_op jit(solution)/shard_map/all_gather | solution.py:99
  164.6 10.5 pad_maximum_fusion.4
  216.2 9.3 gather_fusion.2
  237.7 18.1 %gather_fusion.1 = s32[2048]{0:T(1024)} fusion(s32[2,8]{0,1:T(8,128)S(1)} %broadcast_multiply_fusion.3, s32[2048]{0:T(1024)S(1)} %bitcast.356), kind=kCustom, calls=%fused_computation.1 | custom fusion | bytes 32768 | tf_op jit(solution)/shard_map/jit(take_along_axis)/gather | solution.py:149
  346.4 14.1 %fusion.143 = (bf16[768,8,384]{2,1,0:T(8,128)(2,1)}, bf16[768,8,384]{2,1,0:T(8,128)(2,1)}) fusion(bf16[768,8,864]{2,1,0:T(8,128)(2,1)} %all-gather.16.cloned.1.call-done), kind=kLoop, calls=%fused_computation.455 | loop fusion | bytes 18874368 | tf_op jit(solution)/shard_map/slice | solution.py:106
  369.6 25.2 %fusion.142 = (bf16[1,2048,1536]{1,0,2:T(2,128)(2,1)S(1)}, bf16[1,2048,1536]{1,0,2:T(2,128)(2,1)}) fusion(bf16[2,2048,1536]{1,0,2:T(2,128)(2,1)} %all-gather.12.cloned.1.call-done), kind=kLoop, calls=%fused_computation.454 | loop fusion | bytes 25165824 | tf_op jit(solution)/shard_map/slice | solution.py:160
  394.8 26.2 %constant_dynamic-slice_fusion.19 = (bf16[1,64,1536]{1,0,2:T(2,128)(2,1)S(1)}, bf16[1,64,1536]{1,0,2:T(2,128)(2,1)S(1)}, bf16[1,64,1536]{1,0,2:T(2,128)(2,1)S(1)...) fusion(bf16[1,2048,1536]{1,0,2:T(2,128)(2,1)} %get-tuple-elemen, ...), kind=kLoop, calls=%fused_computation.293 | loop fusion | bytes 6291504 | tf_op jit(solution)/shard_map/dynamic_slice | solution.py:160
  448.6 44.0 %concatenate.95 = bf16[2,4,416,1536]{2,1,0,3:T(4,128)(2,1)} concatenate(bf16[2,4,64,1536]{2,1,0,3:T(4,128)(2,1)} %copy.141, bf16[2,4,128,1536]{2,1,0,3:T(4,128)(2,1)S(1)} %pad_maximum_fusion.6, bf16[2,4,64,1536]{2,1,0,3:T(4,128)(2,1)} %pad_maximum_fusion.7, bf16[2,4,64,1536]{2,1,0,3:T(4,128)(2,1)} %copy.142, bf16[2,4,32,1536]{2,1,0,3:T(4,128)(2,1)} %copy.143, ...), dimensions={2} | concatenate | bytes 20447232 | tf_op jit(solution)/shard_map/concatenate | solution.py:251
  510.3 13.4 %fusion.154 = (f32[2,4,12,128]{3,2,1,0:T(8,128)S(1)}, f32[2,4,12,128,416]{3,4,2,1,0:T(8,128)}) fusion(pred[2,4,128,416]{2,3,1,0:T(8,128)(4,1)S(1)} %copy-done.37, bf16[2,4,416,12,64]{2,4,3,1,0:T(8,128)(2,1)} %bitcast.361, bf16[2,4,128,12,64]{2,1,0,4,3:T(4,128)(2,1)S(1)} %copy-done.22), kind=kOutput, calls=%fused_computation.466 | convolution fusion | flops 674759040 | bytes 27607040 | tf_op jit(solution)/shard_map/sub | solution.py:271
  523.7 10.7 fusion.35
  542.6 34.7 %multiply_convert_fusion.1 = (bf16[1024,3072]{1,0:T(8,128)(2,1)S(1)}, f32[1024,3072]{1,0:T(8,128)}, f32[1024,3072]{1,0:T(8,128)}) fusion(bf16[768,3072]{1,0:T(8,128)(2,1)S(1)} %bitcast.384, f32[1024,768]{1,0:T(8,128)S(1)} %get-tuple-element.156, f32[768]{0:T(1024)S(1)} %copy-done.69, f32[768]{0:T(1024)S(1)} %copy-done.61, f32[1024]{0:T(1024)S(1)} %fusion.111, ...), kind=kOutput, calls=%fused_computation.80 | convolution fusion | flops 5040242688 | bytes 39335936 | tf_op jit(solution)/shard_map/dot_general | solution.py:78
  589.1 18.9 %add_convert_fusion = bf16[1024,3072]{1,0:T(8,128)(2,1)} fusion(f32[1024,3072]{1,0:T(8,128)} %get-tuple-element.28, f32[1024,3072]{1,0:T(8,128)} %get-tuple-element.157, bf16[768,3072]{1,0:T(8,128)(2,1)} %bitcast.386, f32[1024,768]{1,0:T(8,128)} %get-tuple-element.26, f32[1024]{0:T(1024)S(1)} %negate_multiply_fusion.2), kind=kOutput, calls=%fused_computation.79 | convolution fusion | flops 4877451264 | bytes 39325696 | tf_op jit(solution)/shard_map/dot_general | solution.py:88
  608.0 9.2 multiply_reduce_fusion.1
  624.0 16.2 %fusion.12 = f32[2,4,12,64,416]{4,3,2,1,0:T(8,128)} fusion(bf16[2,4,128,12,64]{2,1,0,4,3:T(4,128)(2,1)S(1)} %reshape.1226, f32[2,4,12,128,416]{3,4,2,1,0:T(8,128)} %get-tuple-element.154, f32[2,4,12,128]{3,2,1,0:T(8,128)S(1)} %copy-done.45), kind=kOutput, calls=%fused_computation.101 | convolution fusion | flops 664535040 | bytes 32292864 | tf_op jit(solution)/shard_map/gbhqk,gbqhd->gbkhd/dot_general | solution.py:301
  640.2 16.2 %multiply_reduce_fusion = (f32[2,4,12,128]{3,2,1,0:T(8,128)S(1)}, f32[2,4,12,128,416]{3,4,2,1,0:T(8,128)}) fusion(f32[2,4,12,128,416]{3,4,2,1,0:T(8,128)} %get-tuple-element.154, f32[2,4,12,128]{3,2,1,0:T(8,128)S(1)} %copy-done.45, bf16[2,4,416,12,64]{2,4,3,1,0:T(8,128)(2,1)} %bitcast.378, bf16[2,4,128,12,64]{2,1,0,4,3:T(4,128)(2,1)S(1)} %reshape.1226), kind=kOutput, calls=%fused_computation.72 | convolution fusion | flops 669634560 | bytes 47677440 | tf_op jit(solution)/shard_map/gbqhd,gbkhd->gbhqk/dot_general | solution.py:290
  656.4 11.9 copy.162
  668.3 17.8 %multiply_convert_fusion = bf16[2,4,12,128,416]{3,4,2,1,0:T(8,128)(2,1)} fusion(f32[2,4,12,128,416]{3,4,2,1,0:T(8,128)} %get-tuple-element.162, f32[2,4,12,128]{3,2,1,0:T(8,128)S(1)} %get-tuple-element.161, f32[2,4,12,128,416]{3,4,2,1,0:T(8,128)} %get-tuple-element.154, f32[2,4,12,128]{3,2,1,0:T(8,128)S(1)} %copy-done.45), kind=kLoop, calls=%fused_computation.71 | loop fusion | flops 20447232 | bytes 51216384 | tf_op jit(solution)/shard_map/convert_element_type | solution.py:294
  686.1 13.3 %broadcast_multiply_fusion = f32[2,4,12,64,416]{4,3,2,1,0:T(8,128)} fusion(bf16[2,4,12,128,416]{3,4,2,1,0:T(8,128)(2,1)} %multiply_convert_fusion, bf16[2,4,128,12,64]{2,1,0,4,3:T(4,128)(2,1)S(1)} %copy-done.23), kind=kOutput, calls=%fused_computation.100 | convolution fusion | flops 656867328 | bytes 22020096 | tf_op jit(solution)/shard_map/gbhqk,gbqhd->gbkhd/dot_general | solution.py:298
  699.4 11.7 copy.161
  749.9 11.6 broadcast_in_dim.194
  767.3 23.4 %fusion.140 = (f32[1,2048,1536]{2,1,0:T(8,128)}, f32[2048,1536]{1,0:T(8,128)}, f32[2048,1536]{1,0:T(8,128)}, f32[1,2048,1536]{2,1,0:T(8,128)}) fusion(f32[2,2048,1536]{2,1,0:T(8,128)} %constant_dynamic-update-slice_fusion), kind=kLoop, calls=%fused_computation.452 | loop fusion | bytes 75497472 | tf_op jit(solution)/shard_map/slice | solution.py:172
  884.6 8.4 pad_maximum_fusion
  894.9 8.5 convolution_convert_fusion.1
  907.7 9.2 convolution_convert_fusion
  930.9 11.8 pad_maximum_fusion.1
  978.0 14.0 %reduce-scatter.9.cloned.1.call-done = bf16[2,512,1536]{2,1,0:T(8,128)(2,1)} async-done(((bf16[2,2048,1536]{2,1,0:T(8,128)(2,1)}), bf16[2,512,1536]{2,1,0:T(8,128)(2,1)}) %reduce-scatter.9.cloned.1.call-update) | async-done | bytes 3145744 | tf_op jit(solution)/shard_map/reduce_scatter | solution.py:326
  1019.5 62.7 %reduce-scatter.13.cloned.1.call-done = bf16[192,8,864]{2,0,1:T(8,128)(2,1)} async-done(((bf16[768,8,864]{2,0,1:T(8,128)(2,1)}), bf16[192,8,864]{2,0,1:T(8,128)(2,1)}) %reduce-scatter.13.cloned.1.call-update) | async-done | bytes 2654224 | tf_op jit(solution)/shard_map/reduce_scatter | solution.py:124
  1082.2 50.5 %reduce-scatter.15.cloned.1.call-done = bf16[192,8,288]{2,0,1:T(8,128)(2,1)} async-done(((bf16[768,8,288]{2,0,1:T(8,128)(2,1)}), bf16[192,8,288]{2,0,1:T(8,128)(2,1)}) %reduce-scatter.15.cloned.1.call-update) | async-done | bytes 884752 | tf_op jit(solution)/shard_map/reduce_scatter | solution.py:124
  1147.6 41.9 %all-reduce.3 = (f32[2,4,768]{2,1,0:T(4,128)S(1)}, f32[2,768]{1,0:T(2,128)S(1)}, f32[2,768]{1,0:T(2,128)S(1)}) all-reduce(f32[2,4,768]{2,1,0:T(4,128)S(1)} %pad_maximum_fusion.15, f32[2,768]{1,0:T(2,128)S(1)} %pad_maximum_fusion.16, f32[2,768]{1,0:T(2,128)S(1)} %pad_maximum_fusion.17), channel_id=9, replica_groups=mesh['dp'=8,'seq'=4] {'dp','seq'}, use_global_device_ids=true, to_apply=%region_20.21.clone | all-reduce | flops 9216 | bytes 73728
  1197.6 20.9 %reduce-scatter.17.cloned.1.call-done = bf16[192,1,1152]{2,0,1:T(8,128)(2,1)} async-done(((bf16[192,8,1152]{2,0,1:T(8,128)(2,1)}), bf16[192,1,1152]{2,0,1:T(8,128)(2,1)}) %reduce-scatter.17.cloned.1.call-update) | async-done | bytes 442384 | tf_op jit(solution)/shard_map/reduce_scatter | solution.py:129
  (468 shorter events, 491.6 us)
Async XLA Ops:
  7.2 40.2 %copy-start.39 = (bf16[384,192]{0,1:T(8,128)(2,1)S(1)}, bf16[384,192]{0,1:T(8,128)(2,1)}, u32[]{:S(2)}) copy-start(bf16[384,192]{0,1:T(8,128)(2,1)} %param.18) | copy-start | bytes 442372
  7.2 40.2 %copy-start.40 = (bf16[192,384]{1,0:T(8,128)(2,1)S(1)}, bf16[192,384]{1,0:T(8,128)(2,1)}, u32[]{:S(2)}) copy-start(bf16[192,384]{1,0:T(8,128)(2,1)} %param.17) | copy-start | bytes 442372
  7.2 40.2 %copy-start.51 = (bf16[192,96]{1,0:T(8,128)(2,1)S(1)}, bf16[192,96]{1,0:T(8,128)(2,1)}, u32[]{:S(2)}) copy-start(bf16[192,96]{1,0:T(8,128)(2,1)} %param.16) | copy-start | bytes 110596
  7.2 84.4 %all-gather.10.cloned.1.call-start = ((), (), s32[]{:S(2)}) async-start(), calls=%async_computation.5 | async-start | bytes 5898240 | tf_op jit(solution)/shard_map/all_gather | solution.py:100
  9.1 39.3 %copy-start.68 = (f32[2,4,24]{2,1,0:T(4,128)S(1)}, f32[2,4,24]{2,1,0:T(4,128)}, u32[]{:S(2)}) copy-start(f32[2,4,24]{2,1,0:T(4,128)} %param.19) | copy-start | bytes 2308
  9.1 39.3 %copy-start.76 = (f32[2,24]{1,0:T(2,128)S(1)}, f32[2,24]{1,0:T(2,128)}, u32[]{:S(2)}) copy-start(f32[2,24]{1,0:T(2,128)} %param.21) | copy-start | bytes 580
  9.2 39.3 %copy-start.77 = (f32[2,24]{1,0:T(2,128)S(1)}, f32[2,24]{1,0:T(2,128)}, u32[]{:S(2)}) copy-start(f32[2,24]{1,0:T(2,128)} %param.20) | copy-start | bytes 580
  47.4 98.2 %all-gather.18.cloned.1.call-start = ((), (), s32[]{:S(2)}) async-start(), calls=%async_computation.14 | async-start | bytes 3096576 | tf_op jit(solution)/shard_map/all_gather | solution.py:99
  48.4 271.3 %all-gather.14.cloned.1.call-start = ((), (), s32[]{:S(2)}) async-start(), calls=%async_computation.7 | async-start | bytes 3932160 | tf_op jit(solution)/shard_map/all_gather | solution.py:392
  91.6 32.1 %copy-start.41 = (f32[4,768]{1,0:T(4,128)}, f32[4,768]{1,0:T(4,128)S(1)}, u32[]{:S(2)}) copy-start(f32[4,768]{1,0:T(4,128)S(1)} %get-tuple-element.109) | copy-start | bytes 36868
  110.3 13.4 %copy-start.1 = (f32[2,128,4,768]{3,2,1,0:T(4,128)}, f32[2,128,4,768]{3,2,1,0:T(4,128)S(1)}, u32[]{:S(2)}) copy-start(f32[2,128,4,768]{3,2,1,0:T(4,128)S(1)} %reshape.1244) | copy-start | bytes 9437188
  131.5 209.2 %all-gather.16.cloned.1.call-start = ((), (), s32[]{:S(2)}) async-start(), calls=%async_computation.8 | async-start | bytes 13762560 | tf_op jit(solution)/shard_map/all_gather | solution.py:100
  159.9 209.8 %all-gather.12.cloned.1.call-start = ((), (), s32[]{:S(2)}) async-start(), calls=%async_computation.6 | async-start | bytes 15728640 | tf_op jit(solution)/shard_map/all_gather | solution.py:391
  175.1 13.1 %copy-start.78 = (s32[2,8]{1,0:T(2,128)S(1)}, s32[2,8]{1,0:T(2,128)}, u32[]{:S(2)}) copy-start(s32[2,8]{1,0:T(2,128)} %param.22) | copy-start | bytes 196
  175.2 797.7 %reduce-scatter.11.cloned.1.call-start = ((), (), s32[]{:S(2)}) async-start(), calls=%async_computation.10 | async-start | bytes 3932160 | tf_op jit(solution)/shard_map/reduce_scatter | solution.py:327
  192.7 36.1 %copy-start.59 = (s32[4]{0:T(128)S(1)}, s32[4]{0:T(128)}, u32[]{:S(2)}) copy-start(s32[4]{0:T(128)} %copy-done.58) | copy-start | bytes 52
  523.7 10.7 copy-start.44
  537.9 39.4 %slice-start.7 = ((s8[4718592]{0:T(1024)(128)(4,1)}), s8[4194304]{0:T(1024)(128)(4,1)S(1)}, s32[]{:S(2)}) async-start(s8[4718592]{0:T(1024)(128)(4,1)} %bitcast.387), calls=%async_computation.22 | async-start | bytes 8388608
  541.9 75.3 %copy-start.13 = (f32[1024,768]{1,0:T(8,128)}, f32[1024,768]{1,0:T(8,128)S(1)}, u32[]{:S(2)}) copy-start(f32[1024,768]{1,0:T(8,128)S(1)} %get-tuple-element.156) | copy-start | bytes 9437188
  542.0 75.3 %copy-start.54 = (f32[1024]{0:T(1024)}, f32[1024]{0:T(1024)S(1)}, u32[]{:S(2)}) copy-start(f32[1024]{0:T(1024)S(1)} %broadcast_multiply_fusion.2) | copy-start | bytes 12292
  542.5 74.8 %copy-start.64 = (f32[1024]{0:T(1024)}, f32[1024]{0:T(1024)S(1)}, u32[]{:S(2)}) copy-start(f32[1024]{0:T(1024)S(1)} %fusion.111) | copy-start | bytes 12292
  542.6 34.7 %slice-start.8 = ((s8[4718592]{0:T(1024)(128)(4,1)}), s8[524288]{0:T(1024)(128)(4,1)S(1)}, s32[]{:S(2)}) async-start(s8[4718592]{0:T(1024)(128)(4,1)} %bitcast.387), calls=%async_computation.23 | async-start | bytes 1048576
  589.1 18.9 %copy-start.73 = (f32[1024]{0:T(1024)}, f32[1024]{0:T(1024)S(1)}, u32[]{:S(2)}) copy-start(f32[1024]{0:T(1024)S(1)} %negate_multiply_fusion.2) | copy-start | bytes 12292
  668.3 17.8 %copy-start.23 = (bf16[2,4,128,12,64]{2,1,0,4,3:T(4,128)(2,1)S(1)}, bf16[2,4,128,12,64]{2,1,0,4,3:T(4,128)(2,1)}, u32[]{:S(2)}) copy-start(bf16[2,4,128,12,64]{2,1,0,4,3:T(4,128)(2,1)} %reshape_reshape.3) | copy-start | bytes 4718596
  724.2 12.7 %slice-start = ((s8[10223616]{0:T(1024)(128)(4,1)}), s8[1835008]{0:T(1024)(128)(4,1)S(1)}, s32[]{:S(2)}) async-start(s8[10223616]{0:T(1024)(128)(4,1)} %bitcast.354), calls=%async_computation.15 | async-start | bytes 3670016
  729.3 7.6 slice-start.1
  729.3 7.6 slice-start.2
  749.9 40.8 %copy-start.8 = (f32[512,1536]{1,0:T(8,128)}, f32[512,1536]{1,0:T(8,128)S(1)}, u32[]{:S(2)}) copy-start(f32[512,1536]{1,0:T(8,128)S(1)} %dynamic_update_slice.130) | copy-start | bytes 9437188
  829.9 162.2 %reduce-scatter.9.cloned.1.call-start = ((), (), s32[]{:S(2)}) async-start(), calls=%async_computation.9 | async-start | bytes 15728640 | tf_op jit(solution)/shard_map/reduce_scatter | solution.py:326
  893.0 189.1 %reduce-scatter.13.cloned.1.call-start = ((), (), s32[]{:S(2)}) async-start(), calls=%async_computation.11 | async-start | bytes 13762560 | tf_op jit(solution)/shard_map/reduce_scatter | solution.py:124
  942.7 190.0 %reduce-scatter.15.cloned.1.call-start = ((), (), s32[]{:S(2)}) async-start(), calls=%async_computation.12 | async-start | bytes 5898240 | tf_op jit(solution)/shard_map/reduce_scatter | solution.py:124
  1019.5 199.0 %reduce-scatter.17.cloned.1.call-start = ((), (), s32[]{:S(2)}) async-start(), calls=%async_computation.13 | async-start | bytes 3981312 | tf_op jit(solution)/shard_map/reduce_scatter | solution.py:129
  (68 other events, 182.0 us)
Sparse Core Ops, SparseCore 0:
  47.5 39.8 all-gather.9
  89.6 55.8 all-gather.17
  147.1 27.1 all-gather.13
  175.7 73.1 all-gather.15
  250.2 83.7 all-gather.11
  830.0 36.7 reduce-scatter.10
  893.2 98.8 reduce-scatter.8
  994.6 87.5 reduce-scatter.12
  1084.7 47.9 reduce-scatter.14
  1137.7 80.7 reduce-scatter.16

commit v4 on v3

--- a/solution.py
+++ b/solution.py
@@ -109,12 +109,15 @@
     return pieces
 
 
-def gather_weights(w_query, w_key, w_value, w_output, w_inner, w_outer):
+def gather_first(w_query, w_key, w_value):
     first = gather_grouped((w_query, w_key, w_value))
+    return split_grouped(first, (w_query.shape[1], w_key.shape[1], w_value.shape[1]))
+
+
+def gather_second(w_output, w_inner, w_outer):
     second = gather_grouped((w_output, w_inner, w_outer.T))
-    wq, wk, wv = split_grouped(first, (w_query.shape[1], w_key.shape[1], w_value.shape[1]))
     wo, wi, wu_t = split_grouped(second, (w_output.shape[1], w_inner.shape[1], w_outer.shape[0]))
-    return (wq, wk, wv, wo, wi, wu_t.T)
+    return (wo, wi, wu_t.T)
 
 
 def reduce_seq_stage(grads):
@@ -144,9 +147,9 @@
     in_prompt = index < PROMPT
     segment = jnp.where(in_prompt, -1, (index - PROMPT) // CLEN)
     within = index - PROMPT - segment * CLEN
-    chosen = jnp.clip(segment, 0, CONT - 1)
-    flat = chosen.reshape(chosen.shape[0], -1)
-    cont_start = jnp.take_along_axis(offsets, flat, axis=1).reshape(index.shape)
+    choose = segment[..., None] == jnp.arange(CONT, dtype=jnp.int32)
+    spread = offsets.reshape(offsets.shape[:1] + (1,) * (index.ndim - 1) + offsets.shape[1:])
+    cont_start = jnp.sum(jnp.where(choose, spread, 0), axis=-1)
     position = jnp.where(in_prompt, index, cont_start + within)
     limit = jnp.where(in_prompt, PROMPT, cont_start)
     return segment, position, limit
@@ -371,8 +374,7 @@
     pool_full = small_full[:pool_rows_count].reshape(pool_weight.shape[0], pool_weight.shape[1], -1)
     gain_full = small_full[pool_rows_count : pool_rows_count + ln_gain.shape[0]]
     bias_full = small_full[pool_rows_count + ln_gain.shape[0] :]
-    weights = gather_weights(w_query, w_key, w_value, w_output, w_inner, w_outer)
-    wq, wk, wv, wo, wi, wu = weights
+    wq, wk, wv = gather_first(w_query, w_key, w_value)
     groups, shard_rows, width = hidden_in.shape
     seq_index = lax.axis_index("seq")
     offsets = STRIDE * branch_blocks
@@ -390,6 +392,10 @@
     pkv_local = jnp.concatenate([pooled_keys, pooled_values], axis=2)
     kv_all = lax.all_gather(kv_local, "seq", axis=1, tiled=True)
     pkv_all = lax.all_gather(pkv_local, "seq", axis=1, tiled=True)
+    kv_all, pkv_all, w_output, w_inner, w_outer = lax.optimization_barrier(
+        (kv_all, pkv_all, w_output, w_inner, w_outer)
+    )
+    wo, wi, wu = gather_second(w_output, w_inner, w_outer)
     attended, att_saved = attention_fwd(
         queries.reshape(groups, shard_rows, width), kv_local, pkv_local, kv_all, pkv_all, starts, mask
     )

time: 1250 us -> 1260 us (level)
  waiting for transfers between devices: 162 us -> 243 us
  local copies, waits for them, and re-layouts: 467 us -> 413 us
    all_gather x1, waiting for transfers between devices: 0.01 us -> 82.7 us  [local(): kv_all = lax.all_gather(kv_local, 'seq', axis=1, tiled=True)]
    gather x6 -> x0, local copies, waits for them, and re-layouts: 38.5 us -> none  [layout_of(): cont_start = jnp.take_along_axis(offsets, flat, axis=1).reshape(index.shape)]
    dynamic_slice x3 -> x4, local copies, waits for them, and re-layouts: 28.6 us -> 25 us  [window_rows(): lax.dynamic_slice_in_dim(source[g], starts[g, b], length, 0)]
    unnamed x199 -> x189, local copies, waits for them, and re-layouts: 47.1 us -> 44.5 us
  transfers between devices with their start and end apart: 10 -> 10, of which waited for: 5 -> 6; matrix products, arithmetic and copies ran while one was open for 33% -> 34% of each run, Pallas kernels for 0% -> 0%
where the time goes in v4:
time: 1260 us; the launch traced here: 1240 us
  local copies, waits for them, and re-layouts  413 us (33%)
  waiting for transfers between devices  243 us (19%)
  matrix products  203 us (16%)
  other arithmetic  200 us (16%)
  blocking collectives  119 us (9%)
  between operations  61.4 us (5%)
    reduce_scatter x2, waiting for transfers between devices, reduce_seq_stage(): lax.psum_scatter(stacked, 'seq', scatter_dimension=0, tiled=True)  113 us
    all_gather x1, waiting for transfers between devices, local(): kv_all = lax.all_gather(kv_local, 'seq', axis=1, tiled=True)  82.7 us
    dot_general x6, matrix products, product(): return jnp.dot(left, right, preferred_element_type=jnp.float32)  50.7 us
    dynamic_update_slice x32, local copies, waits for them, and re-layouts, window_add(): lax.dynamic_update_slice_in_dim(row, current + updates[g, b], start, 0)  47 us
    unnamed x189, local copies, waits for them, and re-layouts  44.5 us
    concatenate x1, local copies, waits for them, and re-layouts, attention_fwd(): jnp.concatenate([window_rows(kv_all, starts[0], HALF_FULL), kv_local.resh...  44 us
    all_gather x1, blocking collectives, local(): small_full = lax.all_gather(small_local, ('dp', 'seq'), axis=1, tiled=True)  42.3 us
    unnamed x1, blocking collectives  41.6 us
  transfers between devices with their start and end apart: 10, of which 6 were waited for; matrix products, arithmetic and copies ran while one was open for 34% of the time, Pallas kernels for 0%

profile of v4, /device:TPU:0, one launch (start us, length us, event | category | flops | bytes accessed | tf_op | source)
XLA Modules:
  0.0 1241.5 jit_solution(14640956987487109369)
XLA Ops:
  10.0 35.4 %all-gather = bf16[192,2304]{0,1:T(8,128)(2,1)S(1)} all-gather(bf16[192,288]{0,1:T(8,128)(2,1)S(1)} %pad_maximum_fusion.14), channel_id=2, replica_groups=mesh['dp'=8,'seq'=4] {'dp'}, dimensions={1}, use_global_device_ids=true | all-gather | bytes 995328 | tf_op jit(solution)/shard_map/all_gather | solution.py:99
  47.3 42.3 %all-gather.2 = f32[32,24,12]{1,2,0:T(8,128)S(1)} all-gather(f32[1,24,12]{1,2,0:T(8,128)S(1)} %maximum_bitcast_fusion.9), channel_id=1, replica_groups=mesh['dp'=8,'seq'=4] {'dp','seq'}, dimensions={0}, use_global_device_ids=true | all-gather | bytes 38016 | tf_op jit(solution)/shard_map/all_gather | solution.py:373
  133.3 10.5 pad_maximum_fusion.4
  155.7 82.7 %all-gather.12.cloned.1.call-done = bf16[2,2048,1536]{1,0,2:T(2,128)(2,1)} async-done(((bf16[2,512,1536]{1,0,2:T(2,128)(2,1)}), bf16[2,2048,1536]{1,0,2:T(2,128)(2,1)}) %all-gather.12.cloned.1.call-update) | async-done | bytes 12582928 | tf_op jit(solution)/shard_map/all_gather | solution.py:393
  284.4 12.0 all-gather.18.cloned.1.call-done
  363.2 25.2 %fusion.123 = (bf16[1,2048,1536]{1,0,2:T(2,128)(2,1)}, bf16[1,2048,1536]{1,0,2:T(2,128)(2,1)S(1)}) fusion(bf16[2,2048,1536]{1,0,2:T(2,128)(2,1)} %all-gather.12.cloned.1.call-done), kind=kLoop, calls=%fused_computation.416 | loop fusion | bytes 25165824 | tf_op jit(solution)/shard_map/slice | solution.py:163
  388.4 13.5 %constant_dynamic-slice_fusion.23 = (bf16[1,64,1536]{1,0,2:T(2,128)(2,1)S(1)}, bf16[1,64,1536]{1,0,2:T(2,128)(2,1)S(1)}, bf16[1,64,1536]{1,0,2:T(2,128)(2,1)S(1)...) fusion(bf16[1,2048,1536]{1,0,2:T(2,128)(2,1)} %get-tuple-elemen, ...), kind=kLoop, calls=%fused_computation.296 | loop fusion | bytes 3145760 | tf_op jit(solution)/shard_map/dynamic_slice | solution.py:163
  406.4 9.2 constant_dynamic-slice_fusion.19
  438.5 44.0 %concatenate.106 = bf16[2,4,416,1536]{2,1,0,3:T(4,128)(2,1)} concatenate(bf16[2,4,64,1536]{2,1,0,3:T(4,128)(2,1)} %copy.200, bf16[2,4,128,1536]{2,1,0,3:T(4,128)(2,1)S(1)} %pad_maximum_fusion.6, bf16[2,4,64,1536]{2,1,0,3:T(4,128)(2,1)} %pad_maximum_fusion.7, bf16[2,4,64,1536]{2,1,0,3:T(4,128)(2,1)} %copy.201, bf16[2,4,32,1536]{2,1,0,3:T(4,128)(2,1)} %copy.202, ...), dimensions={2} | concatenate | bytes 20447232 | tf_op jit(solution)/shard_map/concatenate | solution.py:254
  500.6 13.2 %fusion.135 = (f32[2,4,12,128]{3,2,1,0:T(8,128)S(1)}, f32[2,4,12,128,416]{3,4,2,1,0:T(8,128)}) fusion(pred[2,4,128,416]{2,3,1,0:T(8,128)(4,1)S(1)} %copy-done.42, bf16[2,4,416,12,64]{2,4,3,1,0:T(8,128)(2,1)} %bitcast.333, bf16[2,4,128,12,64]{2,1,0,4,3:T(4,128)(2,1)S(1)} %copy-done.22), kind=kOutput, calls=%fused_computation.428 | convolution fusion | flops 674759040 | bytes 27607040 | tf_op jit(solution)/shard_map/sub | solution.py:274
  513.8 10.7 fusion.35
  531.4 14.1 %fusion.124 = (bf16[768,8,384]{2,1,0:T(8,128)(2,1)}, bf16[768,8,384]{2,1,0:T(8,128)(2,1)}) fusion(bf16[768,8,864]{2,1,0:T(8,128)(2,1)} %all-gather.16.cloned.1.call-done), kind=kLoop, calls=%fused_computation.417 | loop fusion | bytes 18874368 | tf_op jit(solution)/shard_map/slice | solution.py:106
  555.4 34.6 %multiply_convert_fusion.1 = (bf16[1024,3072]{1,0:T(8,128)(2,1)S(1)}, f32[1024,3072]{1,0:T(8,128)}, f32[1024,3072]{1,0:T(8,128)}) fusion(bf16[768,3072]{1,0:T(8,128)(2,1)S(1)} %bitcast.354, f32[1024,768]{1,0:T(8,128)S(1)} %get-tuple-element.159, f32[768]{0:T(1024)S(1)} %copy-done.68, f32[768]{0:T(1024)S(1)} %copy-done.61, f32[1024]{0:T(1024)S(1)} %fusion.98, ...), kind=kOutput, calls=%fused_computation.77 | convolution fusion | flops 5040242688 | bytes 39335936 | tf_op jit(solution)/shard_map/dot_general | solution.py:78
  601.8 18.9 %add_convert_fusion = bf16[1024,3072]{1,0:T(8,128)(2,1)} fusion(f32[1024,3072]{1,0:T(8,128)} %get-tuple-element.38, f32[1024,3072]{1,0:T(8,128)} %get-tuple-element.160, bf16[768,3072]{1,0:T(8,128)(2,1)} %bitcast.357, f32[1024,768]{1,0:T(8,128)} %get-tuple-element.36, f32[1024]{0:T(1024)S(1)} %negate_multiply_fusion.2), kind=kOutput, calls=%fused_computation.76 | convolution fusion | flops 4877451264 | bytes 39325696 | tf_op jit(solution)/shard_map/dot_general | solution.py:88
  620.7 9.2 multiply_reduce_fusion.1
  636.8 16.2 %fusion.12 = f32[2,4,12,64,416]{4,3,2,1,0:T(8,128)} fusion(bf16[2,4,128,12,64]{2,1,0,4,3:T(4,128)(2,1)S(1)} %reshape.895, f32[2,4,12,128,416]{3,4,2,1,0:T(8,128)} %get-tuple-element.157, f32[2,4,12,128]{3,2,1,0:T(8,128)S(1)} %copy-done.50), kind=kOutput, calls=%fused_computation.98 | convolution fusion | flops 664535040 | bytes 32292864 | tf_op jit(solution)/shard_map/gbhqk,gbqhd->gbkhd/dot_general | solution.py:304
  653.0 16.2 %multiply_reduce_fusion = (f32[2,4,12,128]{3,2,1,0:T(8,128)S(1)}, f32[2,4,12,128,416]{3,4,2,1,0:T(8,128)}) fusion(f32[2,4,12,128,416]{3,4,2,1,0:T(8,128)} %get-tuple-element.157, f32[2,4,12,128]{3,2,1,0:T(8,128)S(1)} %copy-done.50, bf16[2,4,416,12,64]{2,4,3,1,0:T(8,128)(2,1)} %bitcast.350, bf16[2,4,128,12,64]{2,1,0,4,3:T(4,128)(2,1)S(1)} %reshape.895), kind=kOutput, calls=%fused_computation.69 | convolution fusion | flops 669634560 | bytes 47677440 | tf_op jit(solution)/shard_map/gbqhd,gbkhd->gbhqk/dot_general | solution.py:293
  669.2 11.8 copy.224
  681.0 17.8 %multiply_convert_fusion = bf16[2,4,12,128,416]{3,4,2,1,0:T(8,128)(2,1)} fusion(f32[2,4,12,128,416]{3,4,2,1,0:T(8,128)} %get-tuple-element.165, f32[2,4,12,128]{3,2,1,0:T(8,128)S(1)} %get-tuple-element.164, f32[2,4,12,128,416]{3,4,2,1,0:T(8,128)} %get-tuple-element.157, f32[2,4,12,128]{3,2,1,0:T(8,128)S(1)} %copy-done.50), kind=kLoop, calls=%fused_computation.68 | loop fusion | flops 20447232 | bytes 51216384 | tf_op jit(solution)/shard_map/convert_element_type | solution.py:297
  698.8 13.3 %broadcast_multiply_fusion = f32[2,4,12,64,416]{4,3,2,1,0:T(8,128)} fusion(bf16[2,4,12,128,416]{3,4,2,1,0:T(8,128)(2,1)} %multiply_convert_fusion, bf16[2,4,128,12,64]{2,1,0,4,3:T(4,128)(2,1)S(1)} %copy-done.23), kind=kOutput, calls=%fused_computation.97 | convolution fusion | flops 656867328 | bytes 22020096 | tf_op jit(solution)/shard_map/gbhqk,gbqhd->gbkhd/dot_general | solution.py:301
  712.1 11.8 copy.223
  762.6 11.5 broadcast_in_dim.206
  780.0 23.3 %fusion.121 = (f32[1,2048,1536]{2,1,0:T(8,128)}, f32[2048,1536]{1,0:T(8,128)}, f32[2048,1536]{1,0:T(8,128)}, f32[1,2048,1536]{2,1,0:T(8,128)}) fusion(f32[2,2048,1536]{2,1,0:T(8,128)} %constant_dynamic-update-slice_fusion), kind=kLoop, calls=%fused_computation.414 | loop fusion | bytes 75497472 | tf_op jit(solution)/shard_map/slice | solution.py:175
  897.3 8.4 pad_maximum_fusion
  907.6 8.6 convolution_convert_fusion.1
  920.7 9.0 convolution_convert_fusion
  943.6 11.8 pad_maximum_fusion.1
  990.8 14.0 %reduce-scatter.9.cloned.1.call-done = bf16[2,512,1536]{2,1,0:T(8,128)(2,1)} async-done(((bf16[2,2048,1536]{2,1,0:T(8,128)(2,1)}), bf16[2,512,1536]{2,1,0:T(8,128)(2,1)}) %reduce-scatter.9.cloned.1.call-update) | async-done | bytes 3145744 | tf_op jit(solution)/shard_map/reduce_scatter | solution.py:329
  1032.3 62.7 %reduce-scatter.13.cloned.1.call-done = bf16[192,8,864]{2,0,1:T(8,128)(2,1)} async-done(((bf16[768,8,864]{2,0,1:T(8,128)(2,1)}), bf16[192,8,864]{2,0,1:T(8,128)(2,1)}) %reduce-scatter.13.cloned.1.call-update) | async-done | bytes 2654224 | tf_op jit(solution)/shard_map/reduce_scatter | solution.py:127
  1095.0 50.5 %reduce-scatter.15.cloned.1.call-done = bf16[192,8,288]{2,0,1:T(8,128)(2,1)} async-done(((bf16[768,8,288]{2,0,1:T(8,128)(2,1)}), bf16[192,8,288]{2,0,1:T(8,128)(2,1)}) %reduce-scatter.15.cloned.1.call-update) | async-done | bytes 884752 | tf_op jit(solution)/shard_map/reduce_scatter | solution.py:127
  1160.4 41.6 %all-reduce.3 = (f32[2,4,768]{2,1,0:T(4,128)S(1)}, f32[2,768]{1,0:T(2,128)S(1)}, f32[2,768]{1,0:T(2,128)S(1)}) all-reduce(f32[2,4,768]{2,1,0:T(4,128)S(1)} %pad_maximum_fusion.15, f32[2,768]{1,0:T(2,128)S(1)} %pad_maximum_fusion.16, f32[2,768]{1,0:T(2,128)S(1)} %pad_maximum_fusion.17), channel_id=9, replica_groups=mesh['dp'=8,'seq'=4] {'dp','seq'}, use_global_device_ids=true, to_apply=%region_23.24.clone | all-reduce | flops 9216 | bytes 73728
  1210.2 21.1 %reduce-scatter.17.cloned.1.call-done = bf16[192,1,1152]{2,0,1:T(8,128)(2,1)} async-done(((bf16[192,8,1152]{2,0,1:T(8,128)(2,1)}), bf16[192,1,1152]{2,0,1:T(8,128)(2,1)}) %reduce-scatter.17.cloned.1.call-update) | async-done | bytes 442384 | tf_op jit(solution)/shard_map/reduce_scatter | solution.py:132
  (444 shorter events, 455.0 us)
Async XLA Ops:
  7.2 40.1 %copy-start.74 = (f32[2,24]{1,0:T(2,128)S(1)}, f32[2,24]{1,0:T(2,128)}, u32[]{:S(2)}) copy-start(f32[2,24]{1,0:T(2,128)} %param.21) | copy-start | bytes 580
  7.2 40.1 %copy-start.75 = (f32[2,24]{1,0:T(2,128)S(1)}, f32[2,24]{1,0:T(2,128)}, u32[]{:S(2)}) copy-start(f32[2,24]{1,0:T(2,128)} %param.20) | copy-start | bytes 580
  7.2 40.1 %copy-start.67 = (f32[2,4,24]{2,1,0:T(4,128)S(1)}, f32[2,4,24]{2,1,0:T(4,128)}, u32[]{:S(2)}) copy-start(f32[2,4,24]{2,1,0:T(4,128)} %param.19) | copy-start | bytes 2308
  7.2 83.3 %all-gather.10.cloned.1.call-start = ((), (), s32[]{:S(2)}) async-start(), calls=%async_computation.5 | async-start | bytes 5898240 | tf_op jit(solution)/shard_map/all_gather | solution.py:100
  47.2 108.5 %all-gather.14.cloned.1.call-start = ((), (), s32[]{:S(2)}) async-start(), calls=%async_computation.7 | async-start | bytes 3932160 | tf_op jit(solution)/shard_map/all_gather | solution.py:394
  90.5 29.5 %copy-start.46 = (f32[4,768]{1,0:T(4,128)}, f32[4,768]{1,0:T(4,128)S(1)}, u32[]{:S(2)}) copy-start(f32[4,768]{1,0:T(4,128)S(1)} %get-tuple-element.119) | copy-start | bytes 36868
  111.2 8.8 copy-start.1
  127.8 110.6 %all-gather.12.cloned.1.call-start = ((), (), s32[]{:S(2)}) async-start(), calls=%async_computation.6 | async-start | bytes 15728640 | tf_op jit(solution)/shard_map/all_gather | solution.py:393
  143.8 11.8 copy-start.76
  143.8 94.6 %copy-start.44 = (bf16[384,192]{0,1:T(8,128)(2,1)S(1)}, bf16[384,192]{0,1:T(8,128)(2,1)}, u32[]{:S(2)}) copy-start(bf16[384,192]{0,1:T(8,128)(2,1)} %param.18) | copy-start | bytes 442372
  143.8 94.6 %copy-start.45 = (bf16[192,384]{1,0:T(8,128)(2,1)S(1)}, bf16[192,384]{1,0:T(8,128)(2,1)}, u32[]{:S(2)}) copy-start(bf16[192,384]{1,0:T(8,128)(2,1)} %param.17) | copy-start | bytes 442372
  143.8 94.6 %copy-start.52 = (bf16[192,96]{1,0:T(8,128)(2,1)S(1)}, bf16[192,96]{1,0:T(8,128)(2,1)}, u32[]{:S(2)}) copy-start(bf16[192,96]{1,0:T(8,128)(2,1)} %param.16) | copy-start | bytes 110596
  143.9 152.6 %all-gather.18.cloned.1.call-start = ((), (), s32[]{:S(2)}) async-start(), calls=%async_computation.14 | async-start | bytes 3096576 | tf_op jit(solution)/shard_map/all_gather | solution.py:99
  239.4 288.8 %all-gather.16.cloned.1.call-start = ((), (), s32[]{:S(2)}) async-start(), calls=%async_computation.8 | async-start | bytes 13762560 | tf_op jit(solution)/shard_map/all_gather | solution.py:100
  277.9 29.2 %copy-start.58 = (s32[2,4,64]{2,1,0:T(4,128)}, s32[2,4,64]{2,1,0:T(4,128)S(1)}, u32[]{:S(2)}) copy-start(s32[2,4,64]{2,1,0:T(4,128)S(1)} %get-tuple-element.178) | copy-start | bytes 6148
  277.9 29.2 %copy-start.59 = (s32[2,4,32]{2,1,0:T(4,128)}, s32[2,4,32]{2,1,0:T(4,128)S(1)}, u32[]{:S(2)}) copy-start(s32[2,4,32]{2,1,0:T(4,128)S(1)} %broadcast_in_dim.196) | copy-start | bytes 3076
  278.7 28.4 %copy-start.51 = (s32[2,4,128]{2,1,0:T(4,128)}, s32[2,4,128]{2,1,0:T(4,128)S(1)}, u32[]{:S(2)}) copy-start(s32[2,4,128]{2,1,0:T(4,128)S(1)} %select_select_fusion) | copy-start | bytes 12292
  314.4 8.0 copy-start.11
  314.4 671.2 %reduce-scatter.11.cloned.1.call-start = ((), (), s32[]{:S(2)}) async-start(), calls=%async_computation.10 | async-start | bytes 3932160 | tf_op jit(solution)/shard_map/reduce_scatter | solution.py:330
  513.8 10.7 copy-start.49
  549.1 40.9 %copy-start.29 = (bf16[96,8,8,384]{3,1,2,0:T(8,128)(2,1)}, bf16[96,8,8,384]{3,1,2,0:T(8,128)(2,1)S(1)}, u32[]{:S(2)}) copy-start(bf16[96,8,8,384]{3,1,2,0:T(8,128)(2,1)S(1)} %copy.258) | copy-start | bytes 14155780
  554.7 75.2 %copy-start.13 = (f32[1024,768]{1,0:T(8,128)}, f32[1024,768]{1,0:T(8,128)S(1)}, u32[]{:S(2)}) copy-start(f32[1024,768]{1,0:T(8,128)S(1)} %get-tuple-element.159) | copy-start | bytes 9437188
  554.8 75.2 %copy-start.55 = (f32[1024]{0:T(1024)}, f32[1024]{0:T(1024)S(1)}, u32[]{:S(2)}) copy-start(f32[1024]{0:T(1024)S(1)} %broadcast_multiply_fusion.2) | copy-start | bytes 12292
  555.3 74.7 %copy-start.64 = (f32[1024]{0:T(1024)}, f32[1024]{0:T(1024)S(1)}, u32[]{:S(2)}) copy-start(f32[1024]{0:T(1024)S(1)} %fusion.98) | copy-start | bytes 12292
  601.8 18.9 %copy-start.72 = (f32[1024]{0:T(1024)}, f32[1024]{0:T(1024)S(1)}, u32[]{:S(2)}) copy-start(f32[1024]{0:T(1024)S(1)} %negate_multiply_fusion.2) | copy-start | bytes 12292
  681.0 17.8 %copy-start.23 = (bf16[2,4,128,12,64]{2,1,0,4,3:T(4,128)(2,1)S(1)}, bf16[2,4,128,12,64]{2,1,0,4,3:T(4,128)(2,1)}, u32[]{:S(2)}) copy-start(bf16[2,4,128,12,64]{2,1,0,4,3:T(4,128)(2,1)} %reshape_reshape.3) | copy-start | bytes 4718596
  736.9 12.7 %slice-start = ((s8[10223616]{0:T(1024)(128)(4,1)}), s8[1835008]{0:T(1024)(128)(4,1)S(1)}, s32[]{:S(2)}) async-start(s8[10223616]{0:T(1024)(128)(4,1)} %bitcast.328), calls=%async_computation.15 | async-start | bytes 3670016
  762.6 40.7 %copy-start.8 = (f32[512,1536]{1,0:T(8,128)}, f32[512,1536]{1,0:T(8,128)S(1)}, u32[]{:S(2)}) copy-start(f32[512,1536]{1,0:T(8,128)S(1)} %dynamic_update_slice.130) | copy-start | bytes 9437188
  842.4 162.3 %reduce-scatter.9.cloned.1.call-start = ((), (), s32[]{:S(2)}) async-start(), calls=%async_computation.9 | async-start | bytes 15728640 | tf_op jit(solution)/shard_map/reduce_scatter | solution.py:329
  905.8 189.2 %reduce-scatter.13.cloned.1.call-start = ((), (), s32[]{:S(2)}) async-start(), calls=%async_computation.11 | async-start | bytes 13762560 | tf_op jit(solution)/shard_map/reduce_scatter | solution.py:127
  955.5 190.0 %reduce-scatter.15.cloned.1.call-start = ((), (), s32[]{:S(2)}) async-start(), calls=%async_computation.12 | async-start | bytes 5898240 | tf_op jit(solution)/shard_map/reduce_scatter | solution.py:127
  1032.2 199.0 %reduce-scatter.17.cloned.1.call-start = ((), (), s32[]{:S(2)}) async-start(), calls=%async_computation.13 | async-start | bytes 3981312 | tf_op jit(solution)/shard_map/reduce_scatter | solution.py:132
  (65 other events, 187.1 us)
Sparse Core Ops, SparseCore 0:
  47.4 39.7 all-gather.9
  127.9 25.1 all-gather.13
  154.6 83.7 all-gather.11
  240.4 55.9 all-gather.17
  314.5 71.7 all-gather.15
  842.5 36.6 reduce-scatter.10
  905.9 98.8 reduce-scatter.8
  1007.4 87.5 reduce-scatter.12
  1097.5 47.9 reduce-scatter.14
  1150.5 80.7 reduce-scatter.16

commit v5 on v4

--- a/solution.py
+++ b/solution.py
@@ -326,10 +326,6 @@
     pooled = lax.dynamic_update_slice_in_dim(pooled, own_pooled, seq_index * shard_rows // STRIDE, 1)
     pooled = window_add(pooled, grad_kv[:, :, pcut[0] : pcut[1]], starts[2])
     pooled = window_add(pooled, grad_kv[:, :, pcut[2] : pcut[3]], starts[3])
-    full = lax.psum_scatter(full.astype(jnp.bfloat16), "seq", scatter_dimension=1, tiled=True)
-    pooled = lax.psum_scatter(pooled.astype(jnp.bfloat16), "seq", scatter_dimension=1, tiled=True)
-    full = full.astype(jnp.float32)
-    pooled = pooled.astype(jnp.float32)
     grad_queries = grad_queries.reshape(groups * shard_rows, width).astype(jnp.bfloat16)
     return grad_queries, full, pooled
 
@@ -380,20 +376,23 @@
     offsets = STRIDE * branch_blocks
     starts, mask = block_geometry(seq_index, groups, shard_rows, offsets)
 
+    hidden_all = lax.all_gather(hidden_in, "seq", axis=1, tiled=True)
+    group_len = hidden_all.shape[1]
     tokens = hidden_in.reshape(groups * shard_rows, width)
+    all_tokens = hidden_all.reshape(groups * group_len, width)
     queries = product(tokens, wq).astype(jnp.bfloat16)
-    key_rows = product(tokens, wk).astype(jnp.bfloat16)
-    value_rows = product(tokens, wv).astype(jnp.bfloat16)
-    key_g = key_rows.reshape(groups, shard_rows, width)
-    value_g = value_rows.reshape(groups, shard_rows, width)
+    key_g = product(all_tokens, wk).astype(jnp.bfloat16).reshape(groups, group_len, width)
+    value_g = product(all_tokens, wv).astype(jnp.bfloat16).reshape(groups, group_len, width)
     pooled_keys = pool_grouped(key_g.astype(jnp.float32), pool_full[0]).astype(jnp.bfloat16)
     pooled_values = pool_grouped(value_g.astype(jnp.float32), pool_full[1]).astype(jnp.bfloat16)
-    kv_local = jnp.concatenate([key_g, value_g], axis=2)
-    pkv_local = jnp.concatenate([pooled_keys, pooled_values], axis=2)
-    kv_all = lax.all_gather(kv_local, "seq", axis=1, tiled=True)
-    pkv_all = lax.all_gather(pkv_local, "seq", axis=1, tiled=True)
-    kv_all, pkv_all, w_output, w_inner, w_outer = lax.optimization_barrier(
-        (kv_all, pkv_all, w_output, w_inner, w_outer)
+    kv_all = jnp.concatenate([key_g, value_g], axis=2)
+    pkv_all = jnp.concatenate([pooled_keys, pooled_values], axis=2)
+    kv_local = lax.dynamic_slice_in_dim(kv_all, seq_index * shard_rows, shard_rows, 1)
+    pkv_local = lax.dynamic_slice_in_dim(
+        pkv_all, seq_index * (shard_rows // STRIDE), shard_rows // STRIDE, 1
+    )
+    wq, wk, wv, w_output, w_inner, w_outer = lax.optimization_barrier(
+        (wq, wk, wv, w_output, w_inner, w_outer)
     )
     wo, wi, wu = gather_second(w_output, w_inner, w_outer)
     attended, att_saved = attention_fwd(
@@ -425,12 +424,12 @@
     early = reduce_seq_stage((grad_output, grad_inner, grad_outer.T))
 
     grad_queries, grad_full, grad_pooled = attention_bwd(grad_attended, att_saved, starts, seq_index)
-    grad_keys = (
+    key_partial = (
         grad_full[..., :width] + unpool_grouped(grad_pooled[..., :width], pool_full[0])
-    ).astype(jnp.bfloat16).reshape(groups * shard_rows, width)
-    grad_values = (
+    ).astype(jnp.bfloat16).reshape(groups * group_len, width)
+    value_partial = (
         grad_full[..., width:] + unpool_grouped(grad_pooled[..., width:], pool_full[1])
-    ).astype(jnp.bfloat16).reshape(groups * shard_rows, width)
+    ).astype(jnp.bfloat16).reshape(groups * group_len, width)
     grad_pooling = jnp.stack(
         [
             pool_grad_grouped(grad_pooled[..., :width], key_g),
@@ -438,13 +437,15 @@
         ]
     )
     grad_query_w = product_left(tokens, grad_queries)
-    grad_key_w = product_left(tokens, grad_keys)
-    grad_value_w = product_left(tokens, grad_values)
+    grad_key_w = product_left(all_tokens, key_partial)
+    grad_value_w = product_left(all_tokens, value_partial)
+    back_rows = product_right(key_partial, wk) + product_right(value_partial, wv)
+    back_rows = back_rows.reshape(groups, group_len, width).astype(jnp.bfloat16)
+    back_own = lax.psum_scatter(back_rows, "seq", scatter_dimension=1, tiled=True)
     grad_tokens = (
         grad_mixed
         + product_right(grad_queries, wq)
-        + product_right(grad_keys, wk)
-        + product_right(grad_values, wv)
+        + back_own.reshape(groups * shard_rows, width).astype(jnp.float32)
     )
     late = reduce_seq_stage((grad_query_w, grad_key_w, grad_value_w))
     pieces = reduce_dp_stage((early, late))

time: 1260 us -> 1170 us (0.929)
  waiting for transfers between devices: 243 us -> 175 us
  matrix products: 203 us -> 241 us
  local copies, waits for them, and re-layouts: 413 us -> 377 us
  other arithmetic: 200 us -> 184 us
    all_gather x2 -> x1, waiting for transfers between devices: 82.7 us -> 0.02 us  [local(): hidden_all = lax.all_gather(hidden_in, 'seq', axis=1, tiled=True)]
    concatenate x4 -> x0, local copies, waits for them, and re-layouts: 52.3 us -> none  [the longest x1 44 us: attention_fwd(): jnp.concatenate([window_rows(kv_all, starts[0], HALF_FULL), kv_local.resh...]
    reduce_scatter x1, waiting for transfers between devices: 21.1 us -> 69.9 us  [reduce_dp_stage(): lax.psum_scatter(joined, 'dp', scatter_dimension=1, tiled=True)[:, 0]]
    reduce_scatter x2, waiting for transfers between devices: 113 us -> 66.4 us  [reduce_seq_stage(): lax.psum_scatter(stacked, 'seq', scatter_dimension=0, tiled=True)]
    all_gather x2, waiting for transfers between devices: 0.01 us -> 38 us  [gather_grouped(): return lax.all_gather(across, 'seq', axis=0, tiled=True)]
    another operation x12 -> x8, other arithmetic: 29.9 us -> 0.81 us  [window_rows(): jnp.stack([jnp.stack([lax.dynamic_slice_in_dim(source[g], starts[g, b], l...]
    slice x4 -> x1, local copies, waits for them, and re-layouts: 27.2 us -> 0.01 us  [local(): pool_full[1]]
    dynamic_slice x4 -> x3, local copies, waits for them, and re-layouts: 25 us -> 2.34 us  [window_rows(): lax.dynamic_slice_in_dim(source[g], starts[g, b], length, 0)]
  transfers between devices with their start and end apart: 10 -> 8, of which waited for: 6 -> 3; matrix products, arithmetic and copies ran while one was open for 34% -> 28% of each run, Pallas kernels for 0% -> 0%
where the time goes in v5:
time: 1170 us; the launch traced here: 1160 us
  local copies, waits for them, and re-layouts  377 us (32%)
  matrix products  241 us (21%)
  other arithmetic  184 us (16%)
  waiting for transfers between devices  175 us (15%)
  blocking collectives  118 us (10%)
  between operations  60.7 us (5%)
    reduce_scatter x1, waiting for transfers between devices, reduce_dp_stage(): lax.psum_scatter(joined, 'dp', scatter_dimension=1, tiled=True)[:, 0]  69.9 us
    reduce_scatter x2, waiting for transfers between devices, reduce_seq_stage(): lax.psum_scatter(stacked, 'seq', scatter_dimension=0, tiled=True)  66.4 us
    dot_general x6, matrix products, product(): return jnp.dot(left, right, preferred_element_type=jnp.float32)  64.4 us
    dot_general x6, matrix products, product_right(): lax.dot_general(left, right, (((1,), (1,)), ((), ())), preferred_element_...  54.8 us
    unnamed x159, local copies, waits for them, and re-layouts  50.2 us
    dynamic_update_slice x32, local copies, waits for them, and re-layouts, window_add(): lax.dynamic_update_slice_in_dim(row, current + updates[g, b], start, 0)  48.3 us
    dot_general x6, matrix products, product_left(): lax.dot_general(left, right, (((0,), (0,)), ((), ())), preferred_element_...  47.3 us
    all_gather x1, blocking collectives, local(): small_full = lax.all_gather(small_local, ('dp', 'seq'), axis=1, tiled=True)  42.3 us
  transfers between devices with their start and end apart: 8, of which 3 were waited for; matrix products, arithmetic and copies ran while one was open for 28% of the time, Pallas kernels for 0%

profile of v5, /device:TPU:0, one launch (start us, length us, event | category | flops | bytes accessed | tf_op | source)
XLA Modules:
  0.0 1156.6 jit_solution(4415123966639057169)
XLA Ops:
  9.9 35.4 %all-gather = bf16[192,2304]{0,1:T(8,128)(2,1)S(1)} all-gather(bf16[192,288]{0,1:T(8,128)(2,1)S(1)} %pad_maximum_fusion.6), channel_id=2, replica_groups=mesh['dp'=8,'seq'=4] {'dp'}, dimensions={1}, use_global_device_ids=true | all-gather | bytes 995328 | tf_op jit(solution)/shard_map/all_gather | solution.py:99
  47.3 38.0 %all-gather.9.cloned.1.call-done = bf16[768,8,288]{2,1,0:T(8,128)(2,1)} async-done(((bf16[192,8,288]{2,1,0:T(8,128)(2,1)}), bf16[768,8,288]{2,1,0:T(8,128)(2,1)}) %all-gather.9.cloned.1.call-update) | async-done | bytes 3538960 | tf_op jit(solution)/shard_map/all_gather | solution.py:100
  133.1 42.3 %all-gather.2 = f32[32,24,12]{1,2,0:T(8,128)S(1)} all-gather(f32[1,24,12]{1,2,0:T(8,128)S(1)} %maximum_bitcast_fusion.9), channel_id=1, replica_groups=mesh['dp'=8,'seq'=4] {'dp','seq'}, dimensions={0}, use_global_device_ids=true | all-gather | bytes 38016 | tf_op jit(solution)/shard_map/all_gather | solution.py:369
  238.4 10.2 fusion.20
  267.1 9.7 fusion.19
  295.1 14.6 %reshape.918 = f32[2,512,4,768]{3,2,1,0:T(4,128)} reshape(f32[4096,768]{1,0:T(8,128)} %copy.187) | data formatting | bytes 25165824 | tf_op jit(solution)/shard_map/convert_element_type | solution.py:387
  309.7 14.7 %reshape.917 = f32[2,512,4,768]{3,2,1,0:T(4,128)} reshape(f32[4096,768]{1,0:T(8,128)} %copy.185) | data formatting | bytes 25165824 | tf_op jit(solution)/shard_map/convert_element_type | solution.py:386
  324.4 19.8 %multiply_reduce_fusion.3 = (bf16[2,512,768]{2,1,0:T(8,128)(2,1)S(1)}, bf16[2,512,768]{2,1,0:T(8,128)(2,1)S(1)}) fusion(f32[2,512,4,768]{3,2,1,0:T(4,128)} %reshape.918, f32[4,768]{1,0:T(4,128)S(1)} %get-tuple-element.120, f32[2,512,4,768]{3,2,1,0:T(4,128)} %reshape.917, f32[4,768]{1,0:T(4,128)S(1)} %get-tuple-element.121), kind=kLoop, calls=%fused_computation.108 | loop fusion | flops 11010048 | bytes 28336128 | tf_op jit(solution)/shard_map/reduce_sum | solution.py:335
  386.2 13.4 %fusion.143 = (f32[2,4,12,128]{3,2,1,0:T(8,128)S(1)}, f32[2,4,12,128,416]{3,4,2,1,0:T(8,128)}) fusion(pred[2,4,128,416]{2,3,1,0:T(8,128)(4,1)S(1)} %copy-done.30, bf16[2,4,416,12,64]{2,4,3,1,0:T(8,128)(2,1)} %bitcast.341, bf16[2,4,128,12,64]{2,1,0,4,3:T(4,128)(2,1)S(1)} %copy-done.16), kind=kOutput, calls=%fused_computation.449 | convolution fusion | flops 674759040 | bytes 27607040 | tf_op jit(solution)/shard_map/sub | solution.py:274
  399.6 10.7 fusion.47
  417.2 14.1 %fusion.133 = (bf16[768,8,384]{2,1,0:T(8,128)(2,1)}, bf16[768,8,384]{2,1,0:T(8,128)(2,1)}) fusion(bf16[768,8,864]{2,1,0:T(8,128)(2,1)} %all-gather.13.cloned.1.call-done), kind=kLoop, calls=%fused_computation.439 | loop fusion | bytes 18874368 | tf_op jit(solution)/shard_map/slice | solution.py:106
  441.1 34.7 %multiply_convert_fusion.1 = (bf16[1024,3072]{1,0:T(8,128)(2,1)S(1)}, f32[1024,3072]{1,0:T(8,128)}, f32[1024,3072]{1,0:T(8,128)}) fusion(bf16[768,3072]{1,0:T(8,128)(2,1)S(1)} %bitcast.361, f32[1024,768]{1,0:T(8,128)S(1)} %get-tuple-element.161, f32[768]{0:T(1024)S(1)} %copy-done.48, f32[768]{0:T(1024)S(1)} %copy-done.39, f32[1024]{0:T(1024)S(1)} %fusion.109, ...), kind=kOutput, calls=%fused_computation.95 | convolution fusion | flops 5040242688 | bytes 39335936 | tf_op jit(solution)/shard_map/dot_general | solution.py:78
  486.7 18.9 %add_convert_fusion.1 = bf16[1024,3072]{1,0:T(8,128)(2,1)} fusion(f32[1024,3072]{1,0:T(8,128)} %get-tuple-element.40, f32[1024,3072]{1,0:T(8,128)} %get-tuple-element.162, bf16[768,3072]{1,0:T(8,128)(2,1)} %bitcast.364, f32[1024,768]{1,0:T(8,128)} %get-tuple-element.38, f32[1024]{0:T(1024)S(1)} %negate_multiply_fusion.2), kind=kOutput, calls=%fused_computation.94 | convolution fusion | flops 4877451264 | bytes 39325696 | tf_op jit(solution)/shard_map/dot_general | solution.py:88
  521.7 16.1 %fusion.21 = f32[2,4,12,64,416]{4,3,2,1,0:T(8,128)} fusion(bf16[2,4,128,12,64]{2,1,0,4,3:T(4,128)(2,1)S(1)} %reshape.900, f32[2,4,12,128,416]{3,4,2,1,0:T(8,128)} %get-tuple-element.159, f32[2,4,12,128]{3,2,1,0:T(8,128)S(1)} %copy-done.34), kind=kOutput, calls=%fused_computation.126 | convolution fusion | flops 664535040 | bytes 32292864 | tf_op jit(solution)/shard_map/gbhqk,gbqhd->gbkhd/dot_general | solution.py:304
  537.8 16.1 %multiply_reduce_fusion = (f32[2,4,12,128]{3,2,1,0:T(8,128)S(1)}, f32[2,4,12,128,416]{3,4,2,1,0:T(8,128)}) fusion(f32[2,4,12,128,416]{3,4,2,1,0:T(8,128)} %get-tuple-element.159, f32[2,4,12,128]{3,2,1,0:T(8,128)S(1)} %copy-done.34, bf16[2,4,416,12,64]{2,4,3,1,0:T(8,128)(2,1)} %bitcast.359, bf16[2,4,128,12,64]{2,1,0,4,3:T(4,128)(2,1)S(1)} %reshape.900), kind=kOutput, calls=%fused_computation.71 | convolution fusion | flops 669634560 | bytes 47677440 | tf_op jit(solution)/shard_map/gbqhd,gbkhd->gbhqk/dot_general | solution.py:293
  553.9 13.6 %multiply_convert_fusion = bf16[2,4,12,128,416]{3,4,2,1,0:T(8,128)(2,1)S(1)} fusion(f32[2,4,12,128,416]{3,4,2,1,0:T(8,128)} %get-tuple-element.167, f32[2,4,12,128]{3,2,1,0:T(8,128)S(1)} %get-tuple-element.166, f32[2,4,12,128,416]{3,4,2,1,0:T(8,128)} %get-tuple-element.159, f32[2,4,12,128]{3,2,1,0:T(8,128)S(1)} %copy-done.34), kind=kLoop, calls=%fused_computation.70 | loop fusion | flops 20447232 | bytes 51216384 | tf_op jit(solution)/shard_map/convert_element_type | solution.py:297
  576.5 13.3 %broadcast_multiply_fusion = f32[2,4,12,64,416]{4,3,2,1,0:T(8,128)} fusion(bf16[2,4,12,128,416]{3,4,2,1,0:T(8,128)(2,1)} %copy-done.2, bf16[2,4,128,12,64]{2,1,0,4,3:T(4,128)(2,1)S(1)} %copy-done.17), kind=kOutput, calls=%fused_computation.123 | convolution fusion | flops 656867328 | bytes 22020096 | tf_op jit(solution)/shard_map/gbhqk,gbqhd->gbkhd/dot_general | solution.py:301
  589.8 11.8 %copy.208 = f32[2,4,416,768]{3,2,1,0:T(8,128)} copy(f32[2,4,416,768]{2,3,1,0:T(8,128)} %bitcast.353) | data formatting | bytes 20447232 | tf_op jit(solution)/shard_map/reshape | solution.py:312
  601.6 11.9 %copy.207 = f32[2,4,416,768]{3,2,1,0:T(8,128)} copy(f32[2,4,416,768]{2,3,1,0:T(8,128)} %bitcast.340) | data formatting | bytes 20447232 | tf_op jit(solution)/shard_map/reshape | solution.py:312
  663.3 11.5 broadcast_in_dim.206
  680.7 23.3 %fusion.132 = (f32[1,2048,1536]{2,1,0:T(8,128)}, f32[2048,1536]{1,0:T(8,128)}, f32[2048,1536]{1,0:T(8,128)}, f32[1,2048,1536]{2,1,0:T(8,128)}) fusion(f32[2,2048,1536]{2,1,0:T(8,128)} %constant_dynamic-update-slice_fusion), kind=kLoop, calls=%fused_computation.438 | loop fusion | bytes 75497472 | tf_op jit(solution)/shard_map/slice | solution.py:175
  808.6 26.9 %fusion.7 = (bf16[2,2048,768]{2,1,0:T(8,128)(2,1)}, bf16[2,2048,768]{2,1,0:T(8,128)(2,1)}) fusion(f32[1,2048,1536]{2,1,0:T(8,128)} %dynamic_update_slice.122, f32[1,2048,1536]{2,1,0:T(8,128)} %dynamic_update_slice.114, f32[2,2048,768]{2,0,1:T(2,128)} %bitcast.339, f32[2048,768]{1,0:T(8,128)} %mul.397, f32[2048,768]{1,0:T(8,128)} %mul.391, ...), kind=kLoop, calls=%fused_computation.88 | loop fusion | flops 25165824 | bytes 75497472 | tf_op jit(solution)/shard_map/convert_element_type | solution.py:432
  835.5 9.9 bitcast_convert_fusion
  847.9 9.8 bitcast_convert_fusion.1
  867.2 10.0 convolution_convert_fusion.3
  902.6 11.8 %pad_maximum_fusion.1 = bf16[768,8,864]{2,0,1:T(8,128)(2,1)} fusion(bf16[768,8,384]{2,0,1:T(8,128)(2,1)} %bitcast.347, bf16[768,8,384]{2,0,1:T(8,128)(2,1)} %bitcast.346, bf16[768,8,96]{2,0,1:T(8,128)(2,1)} %copy.215), kind=kLoop, calls=%fused_computation.111 | loop fusion | flops 31850496 | bytes 21233664 | tf_op jit(solution)/shard_map/concatenate | solution.py:126
  922.4 12.3 %add_convert_fusion = bf16[4096,768]{1,0:T(8,128)(2,1)} fusion(f32[4096,768]{1,0:T(8,128)S(1)} %fusion.150, bf16[4096,768]{1,0:T(8,128)(2,1)} %bitcast.355, bf16[768,768]{0,1:T(8,128)(2,1)S(1)} %bitcast.377), kind=kOutput, calls=%fused_computation.93 | convolution fusion | flops 4838129664 | bytes 26345472 | tf_op jit(solution)/shard_map/dot_general | solution.py:88
  934.9 66.4 %reduce-scatter.10.cloned.1.call-done = bf16[192,8,864]{2,0,1:T(8,128)(2,1)} async-done(((bf16[768,8,864]{2,0,1:T(8,128)(2,1)}), bf16[192,8,864]{2,0,1:T(8,128)(2,1)}) %reduce-scatter.10.cloned.1.call-update) | async-done | bytes 2654224 | tf_op jit(solution)/shard_map/reduce_scatter | solution.py:127
  1007.9 11.3 multiply_reduce_fusion.2
  1019.2 10.1 multiply_reduce_fusion.1
  1029.3 40.4 %all-reduce.3 = (f32[2,4,768]{2,1,0:T(4,128)S(1)}, f32[2,768]{1,0:T(2,128)S(1)}, f32[2,768]{1,0:T(2,128)S(1)}) all-reduce(f32[2,4,768]{2,1,0:T(4,128)S(1)} %pad_maximum_fusion.7, f32[2,768]{1,0:T(2,128)S(1)} %pad_maximum_fusion.8, f32[2,768]{1,0:T(2,128)S(1)} %pad_maximum_fusion.9), channel_id=8, replica_groups=mesh['dp'=8,'seq'=4] {'dp','seq'}, use_global_device_ids=true, to_apply=%region_22.23.clone | all-reduce | flops 9216 | bytes 73728
  1076.6 69.9 %reduce-scatter.14.cloned.1.call-done = bf16[192,1,1152]{2,0,1:T(8,128)(2,1)} async-done(((bf16[192,8,1152]{2,0,1:T(8,128)(2,1)}), bf16[192,1,1152]{2,0,1:T(8,128)(2,1)}) %reduce-scatter.14.cloned.1.call-update) | async-done | bytes 442384 | tf_op jit(solution)/shard_map/reduce_scatter | solution.py:132
  (394 shorter events, 423.0 us)
Async XLA Ops:
  7.2 78.0 %all-gather.9.cloned.1.call-start = ((), (), s32[]{:S(2)}) async-start(), calls=%async_computation.4 | async-start | bytes 5898240 | tf_op jit(solution)/shard_map/all_gather | solution.py:100
  47.2 176.5 %all-gather.15.cloned.1.call-start = ((), (), s32[]{:S(2)}) async-start(), calls=%async_computation.11 | async-start | bytes 3096576 | tf_op jit(solution)/shard_map/all_gather | solution.py:99
  90.8 19.6 %copy-start.56 = (s32[2,8]{1,0:T(2,128)S(1)}, s32[2,8]{1,0:T(2,128)}, u32[]{:S(2)}) copy-start(s32[2,8]{1,0:T(2,128)} %param.22) | copy-start | bytes 196
  90.8 42.3 %copy-start.47 = (f32[2,4,24]{2,1,0:T(4,128)S(1)}, f32[2,4,24]{2,1,0:T(4,128)}, u32[]{:S(2)}) copy-start(f32[2,4,24]{2,1,0:T(4,128)} %param.19) | copy-start | bytes 2308
  90.8 42.2 %copy-start.54 = (f32[2,24]{1,0:T(2,128)S(1)}, f32[2,24]{1,0:T(2,128)}, u32[]{:S(2)}) copy-start(f32[2,24]{1,0:T(2,128)} %param.21) | copy-start | bytes 580
  90.8 42.2 %copy-start.55 = (f32[2,24]{1,0:T(2,128)S(1)}, f32[2,24]{1,0:T(2,128)}, u32[]{:S(2)}) copy-start(f32[2,24]{1,0:T(2,128)} %param.20) | copy-start | bytes 580
  98.3 140.1 %all-gather.11.cloned.1.call-start = ((), (), s32[]{:S(2)}) async-start(), calls=%async_computation.5 | async-start | bytes 7864320 | tf_op jit(solution)/shard_map/all_gather | solution.py:379
  99.1 314.8 %all-gather.13.cloned.1.call-start = ((), (), s32[]{:S(2)}) async-start(), calls=%async_computation.6 | async-start | bytes 13762560 | tf_op jit(solution)/shard_map/all_gather | solution.py:100
  190.4 28.3 %copy-start.21 = (bf16[2,512,768]{2,1,0:T(8,128)(2,1)S(1)}, bf16[2,512,768]{2,1,0:T(8,128)(2,1)}, u32[]{:S(2)}) copy-start(bf16[2,512,768]{2,1,0:T(8,128)(2,1)} %param.12) | copy-start | bytes 4718596
  238.1 696.7 %reduce-scatter.12.cloned.1.call-start = ((), (), s32[]{:S(2)}) async-start(), calls=%async_computation.9 | async-start | bytes 5898240 | tf_op jit(solution)/shard_map/reduce_scatter | solution.py:127
  257.4 9.7 copy-start.27
  309.7 34.5 %slice-start.6 = ((s8[6291456]{0:T(1024)(128)(4,1)}), s8[2097152]{0:T(1024)(128)(4,1)S(1)}, s32[]{:S(2)}) async-start(s8[6291456]{0:T(1024)(128)(4,1)} %bitcast.330), calls=%async_computation.18 | async-start | bytes 4194304
  324.4 19.9 %slice-start.7 = ((s8[6291456]{0:T(1024)(128)(4,1)}), s8[4194304]{0:T(1024)(128)(4,1)S(1)}, s32[]{:S(2)}) async-start(s8[6291456]{0:T(1024)(128)(4,1)} %bitcast.330), calls=%async_computation.19 | async-start | bytes 8388608
  399.6 10.7 copy-start.33
  434.9 40.9 %copy-start.19 = (bf16[96,8,8,384]{3,1,2,0:T(8,128)(2,1)}, bf16[96,8,8,384]{3,1,2,0:T(8,128)(2,1)S(1)}, u32[]{:S(2)}) copy-start(bf16[96,8,8,384]{3,1,2,0:T(8,128)(2,1)S(1)} %copy.244) | copy-start | bytes 14155780
  440.5 74.4 %copy-start.11 = (f32[1024,768]{1,0:T(8,128)}, f32[1024,768]{1,0:T(8,128)S(1)}, u32[]{:S(2)}) copy-start(f32[1024,768]{1,0:T(8,128)S(1)} %get-tuple-element.161) | copy-start | bytes 9437188
  440.5 74.4 %copy-start.36 = (f32[1024]{0:T(1024)}, f32[1024]{0:T(1024)S(1)}, u32[]{:S(2)}) copy-start(f32[1024]{0:T(1024)S(1)} %broadcast_multiply_fusion.2) | copy-start | bytes 12292
  441.0 73.9 %copy-start.42 = (f32[1024]{0:T(1024)}, f32[1024]{0:T(1024)S(1)}, u32[]{:S(2)}) copy-start(f32[1024]{0:T(1024)S(1)} %fusion.109) | copy-start | bytes 12292
  486.7 18.9 %copy-start.52 = (f32[1024]{0:T(1024)}, f32[1024]{0:T(1024)S(1)}, u32[]{:S(2)}) copy-start(f32[1024]{0:T(1024)S(1)} %negate_multiply_fusion.2) | copy-start | bytes 12292
  638.0 12.4 %slice-start = ((s8[10223616]{0:T(1024)(128)(4,1)}), s8[1835008]{0:T(1024)(128)(4,1)S(1)}, s32[]{:S(2)}) async-start(s8[10223616]{0:T(1024)(128)(4,1)} %bitcast.324), calls=%async_computation.12 | async-start | bytes 3670016
  663.3 11.5 copy-start.9
  740.5 13.1 %slice-start.3 = ((s8[10223616]{0:T(1024)(128)(4,1)}), s8[1835008]{0:T(1024)(128)(4,1)S(1)}, s32[]{:S(2)}) async-start(s8[10223616]{0:T(1024)(128)(4,1)} %bitcast.326), calls=%async_computation.15 | async-start | bytes 3670016
  742.6 11.0 slice-start.4
  742.6 11.0 slice-start.5
  867.1 134.1 %reduce-scatter.10.cloned.1.call-start = ((), (), s32[]{:S(2)}) async-start(), calls=%async_computation.8 | async-start | bytes 13762560 | tf_op jit(solution)/shard_map/reduce_scatter | solution.py:127
  914.4 157.2 %reduce-scatter.8.cloned.1.call-start = ((), (), s32[]{:S(2)}) async-start(), calls=%async_computation.7 | async-start | bytes 7864320 | tf_op jit(solution)/shard_map/reduce_scatter | solution.py:444
  934.7 73.1 %copy-start.44 = (f32[768]{0:T(1024)S(1)}, f32[768]{0:T(1024)}, u32[]{:S(2)}) copy-start(f32[768]{0:T(1024)} %get-tuple-element.25) | copy-start | bytes 9220
  934.8 73.1 %copy-start.51 = (f32[768]{0:T(1024)S(1)}, f32[768]{0:T(1024)}, u32[]{:S(2)}) copy-start(f32[768]{0:T(1024)} %get-tuple-element.23) | copy-start | bytes 9220
  934.8 73.1 %copy-start.50 = (f32[768]{0:T(1024)S(1)}, f32[768]{0:T(1024)}, u32[]{:S(2)}) copy-start(f32[768]{0:T(1024)} %get-tuple-element.27) | copy-start | bytes 9220
  934.8 211.7 %reduce-scatter.14.cloned.1.call-start = ((), (), s32[]{:S(2)}) async-start(), calls=%async_computation.10 | async-start | bytes 3981312 | tf_op jit(solution)/shard_map/reduce_scatter | solution.py:132
  1007.9 11.3 copy-start.4
  1019.2 52.4 %copy-start.14 = (f32[1024,768]{1,0:T(8,128)S(1)}, f32[1024,768]{1,0:T(8,128)}, u32[]{:S(2)}) copy-start(f32[1024,768]{1,0:T(8,128)} %copy-done.12) | copy-start | bytes 9437188
  (46 other events, 222.6 us)
Sparse Core Ops, SparseCore 0:
  47.3 37.8 all-gather.8
  98.5 56.5 all-gather.14
  156.7 45.1 all-gather.10
  238.2 69.2 all-gather.12
  867.2 43.9 reduce-scatter.11
  914.5 86.6 reduce-scatter.9
  1003.7 59.6 reduce-scatter.7
  1067.1 79.4 reduce-scatter.13

commit v6 on v5

--- a/solution.py
+++ b/solution.py
@@ -120,11 +120,13 @@
     return (wo, wi, wu_t.T)
 
 
-def reduce_seq_stage(grads):
+def reduce_seq_stage(grads, tie=None):
     dp_size = lax.psum(1, "dp")
     chunks = [grad.reshape(grad.shape[0], dp_size, grad.shape[1] // dp_size) for grad in grads]
     stacked = jnp.concatenate(chunks, axis=2).astype(jnp.bfloat16)
-    return lax.psum_scatter(stacked, "seq", scatter_dimension=0, tiled=True), [c.shape[2] for c in chunks]
+    stacked, tie = lax.optimization_barrier((stacked, tie))
+    reduced = lax.psum_scatter(stacked, "seq", scatter_dimension=0, tiled=True)
+    return (reduced, [c.shape[2] for c in chunks]), tie
 
 
 def reduce_dp_stage(stages):
@@ -367,10 +369,13 @@
         [pool_weight.reshape(pool_rows_count, -1), ln_gain, ln_bias], axis=0
     )
     small_full = lax.all_gather(small_local, ("dp", "seq"), axis=1, tiled=True)
+    small_full, w_query, w_key, w_value = lax.optimization_barrier(
+        (small_full, w_query, w_key, w_value)
+    )
+    wq, wk, wv = gather_first(w_query, w_key, w_value)
     pool_full = small_full[:pool_rows_count].reshape(pool_weight.shape[0], pool_weight.shape[1], -1)
     gain_full = small_full[pool_rows_count : pool_rows_count + ln_gain.shape[0]]
     bias_full = small_full[pool_rows_count + ln_gain.shape[0] :]
-    wq, wk, wv = gather_first(w_query, w_key, w_value)
     groups, shard_rows, width = hidden_in.shape
     seq_index = lax.axis_index("seq")
     offsets = STRIDE * branch_blocks
@@ -391,8 +396,8 @@
     pkv_local = lax.dynamic_slice_in_dim(
         pkv_all, seq_index * (shard_rows // STRIDE), shard_rows // STRIDE, 1
     )
-    wq, wk, wv, w_output, w_inner, w_outer = lax.optimization_barrier(
-        (wq, wk, wv, w_output, w_inner, w_outer)
+    wq, wk, wv, hidden_all, w_output, w_inner, w_outer = lax.optimization_barrier(
+        (wq, wk, wv, hidden_all, w_output, w_inner, w_outer)
     )
     wo, wi, wu = gather_second(w_output, w_inner, w_outer)
     attended, att_saved = attention_fwd(
@@ -421,9 +426,22 @@
     grad_branch = grad_mixed.astype(jnp.bfloat16)
     grad_output = product_left(attended, grad_branch)
     grad_attended = product_right(grad_branch, wo).astype(jnp.bfloat16)
-    early = reduce_seq_stage((grad_output, grad_inner, grad_outer.T))
-
-    grad_queries, grad_full, grad_pooled = attention_bwd(grad_attended, att_saved, starts, seq_index)
+    early, grad_attended = reduce_seq_stage((grad_output, grad_inner, grad_outer.T), grad_attended)
+    early_reduced, early_widths = early
+
+    grad_rows = grad_attended.reshape(groups, shard_rows, width)
+    pieces_back = []
+    for g in range(groups):
+        saved_g = tuple(item[g : g + 1] for item in att_saved)
+        starts_g = tuple(item[g : g + 1] for item in starts)
+        grad_g = grad_rows[g].reshape(shard_rows, width)
+        if g == 1:
+            grad_g, early_reduced = lax.optimization_barrier((grad_g, early_reduced))
+        pieces_back.append(attention_bwd(grad_g, saved_g, starts_g, seq_index))
+    grad_queries = jnp.concatenate([piece[0] for piece in pieces_back], axis=0)
+    grad_full = jnp.concatenate([piece[1] for piece in pieces_back], axis=0)
+    grad_pooled = jnp.concatenate([piece[2] for piece in pieces_back], axis=0)
+    early = (early_reduced, early_widths)
     key_partial = (
         grad_full[..., :width] + unpool_grouped(grad_pooled[..., :width], pool_full[0])
     ).astype(jnp.bfloat16).reshape(groups * group_len, width)
@@ -447,7 +465,7 @@
         + product_right(grad_queries, wq)
         + back_own.reshape(groups * shard_rows, width).astype(jnp.float32)
     )
-    late = reduce_seq_stage((grad_query_w, grad_key_w, grad_value_w))
+    late, _ = reduce_seq_stage((grad_query_w, grad_key_w, grad_value_w))
     pieces = reduce_dp_stage((early, late))
     accum = (pieces[3], pieces[4], pieces[5], pieces[0], pieces[1], pieces[2].T)
     small_sums = (

time: 1170 us -> 1180 us (level)
  other arithmetic: 184 us -> 211 us
  waiting for transfers between devices: 175 us -> 158 us
    all_gather x1, waiting for transfers between devices: 0.01 us -> 38.9 us  [gather_grouped(): across = lax.all_gather(local_block, 'dp', axis=1, tiled=False)]
    all_gather x2, waiting for transfers between devices: 38 us -> 0.01 us  [gather_grouped(): return lax.all_gather(across, 'seq', axis=0, tiled=True)]
    reduce_scatter x2, waiting for transfers between devices: 66.4 us -> 34.7 us  [reduce_seq_stage(): reduced = lax.psum_scatter(stacked, 'seq', scatter_dimension=0, tiled=True)]
    another operation x0 -> x1, other arithmetic: none -> 17 us
    div x0 -> x1, other arithmetic: none -> 15.3 us  [attention_fwd(): probs = exponent / row_total]
    broadcast_in_dim x2 -> x0, local copies, waits for them, and re-layouts: 15.1 us -> none  [the longest x1 11.5 us: attention_bwd(): full = jnp.zeros((groups, group_len, 2 * width), jnp.float32)]
    all_gather x1, waiting for transfers between devices: 0.02 us -> 15 us  [local(): hidden_all = lax.all_gather(hidden_in, 'seq', axis=1, tiled=True)]
    convert_element_type x1 -> x0, other arithmetic: 13.6 us -> none  [attention_bwd(): grad_scores = (probs * (grad_probs - centre)).astype(jnp.bfloat16)]
  transfers between devices with their start and end apart: 8 -> 8, of which waited for: 3 -> 5; matrix products, arithmetic and copies ran while one was open for 28% -> 31% of each run, Pallas kernels for 0% -> 0%
where the time goes in v6:
time: 1180 us; the launch traced here: 1170 us
  local copies, waits for them, and re-layouts  373 us (32%)
  matrix products  245 us (21%)
  other arithmetic  211 us (18%)
  waiting for transfers between devices  158 us (13%)
  blocking collectives  119 us (10%)
  between operations  60.8 us (5%)
    reduce_scatter x1, waiting for transfers between devices, reduce_dp_stage(): lax.psum_scatter(joined, 'dp', scatter_dimension=1, tiled=True)[:, 0]  68.5 us
    dot_general x6, matrix products, product(): return jnp.dot(left, right, preferred_element_type=jnp.float32)  66.1 us
    dot_general x6, matrix products, product_right(): lax.dot_general(left, right, (((1,), (1,)), ((), ())), preferred_element_...  56 us
    dynamic_update_slice x32, local copies, waits for them, and re-layouts, window_add(): lax.dynamic_update_slice_in_dim(row, current + updates[g, b], start, 0)  50.9 us
    unnamed x165, local copies, waits for them, and re-layouts  46.6 us
    all_gather x1, blocking collectives, local(): small_full = lax.all_gather(small_local, ('dp', 'seq'), axis=1, tiled=True)  43.9 us
    unnamed x1, blocking collectives  40.6 us
    dot_general x6, matrix products, product_left(): lax.dot_general(left, right, (((0,), (0,)), ((), ())), preferred_element_...  40.3 us
  transfers between devices with their start and end apart: 8, of which 5 were waited for; matrix products, arithmetic and copies ran while one was open for 31% of the time, Pallas kernels for 0%

profile of v6, /device:TPU:0, one launch (start us, length us, event | category | flops | bytes accessed | tf_op | source)
XLA Modules:
  0.0 1167.9 jit_solution(14566259066549707731)
XLA Ops:
  8.0 43.9 %all-gather.2 = f32[32,24,12]{1,2,0:T(8,128)S(1)} all-gather(f32[1,24,12]{1,2,0:T(8,128)S(1)} %maximum_bitcast_fusion.9), channel_id=1, replica_groups=mesh['dp'=8,'seq'=4] {'dp','seq'}, dimensions={0}, use_global_device_ids=true | all-gather | bytes 38016 | tf_op jit(solution)/shard_map/all_gather | solution.py:371
  54.8 34.4 %all-gather = bf16[192,2304]{0,1:T(8,128)(2,1)S(1)} all-gather(bf16[192,288]{0,1:T(8,128)(2,1)S(1)} %pad_maximum_fusion.7), channel_id=2, replica_groups=mesh['dp'=8,'seq'=4] {'dp'}, dimensions={1}, use_global_device_ids=true | all-gather | bytes 995328 | tf_op jit(solution)/shard_map/all_gather | solution.py:99
  158.1 15.0 %all-gather.11.cloned.1.call-done = bf16[2,2048,768]{2,1,0:T(8,128)(2,1)} async-done(((bf16[2,512,768]{2,1,0:T(8,128)(2,1)}), bf16[2,2048,768]{2,1,0:T(8,128)(2,1)}) %all-gather.11.cloned.1.call-update) | async-done | bytes 6291472 | tf_op jit(solution)/shard_map/all_gather | solution.py:384
  192.4 38.9 %all-gather.15.cloned.1.call-done = bf16[8,864,192]{1,2,0:T(8,128)(2,1)} async-done(((bf16[1,864,192]{1,2,0:T(8,128)(2,1)}), bf16[8,864,192]{1,2,0:T(8,128)(2,1)}) %all-gather.15.cloned.1.call-update) | async-done | bytes 2654224 | tf_op jit(solution)/shard_map/all_gather | solution.py:99
  245.9 9.8 fusion.25
  255.6 9.9 copy.225
  265.5 8.8 copy.276
  274.2 9.8 fusion.24
  284.0 9.6 copy.224
  302.3 14.6 %reshape.1061 = f32[2,512,4,768]{3,2,1,0:T(4,128)} reshape(f32[4096,768]{1,0:T(8,128)} %copy.224) | data formatting | bytes 25165824 | tf_op jit(solution)/shard_map/convert_element_type | solution.py:391
  316.8 14.6 %reshape.1062 = f32[2,512,4,768]{3,2,1,0:T(4,128)} reshape(f32[4096,768]{1,0:T(8,128)} %copy.225) | data formatting | bytes 25165824 | tf_op jit(solution)/shard_map/convert_element_type | solution.py:392
  331.4 19.6 %multiply_reduce_fusion.2 = (bf16[2,512,768]{2,1,0:T(8,128)(2,1)S(1)}, bf16[2,512,768]{2,1,0:T(8,128)(2,1)S(1)}) fusion(f32[2,512,4,768]{3,2,1,0:T(4,128)} %reshape.1062, f32[4,768]{1,0:T(4,128)S(1)} %get-tuple-element.135, f32[2,512,4,768]{3,2,1,0:T(4,128)} %reshape.1061, f32[4,768]{1,0:T(4,128)S(1)} %get-tuple-element.136), kind=kLoop, calls=%fused_computation.108 | loop fusion | flops 11010048 | bytes 28336128 | tf_op jit(solution)/shard_map/reduce_sum | solution.py:337
  392.6 13.2 %fusion.162 = (f32[2,4,12,128]{3,2,1,0:T(8,128)S(1)}, f32[2,4,12,128,416]{3,4,2,1,0:T(8,128)}) fusion(pred[2,4,128,416]{2,3,1,0:T(8,128)(4,1)S(1)} %copy-done.33, bf16[2,4,416,12,64]{2,4,3,1,0:T(8,128)(2,1)} %bitcast.425, bf16[2,4,128,12,64]{2,1,0,4,3:T(4,128)(2,1)S(1)} %copy-done.27), kind=kOutput, calls=%fused_computation.473 | convolution fusion | flops 674759040 | bytes 27607040 | tf_op jit(solution)/shard_map/sub | solution.py:276
  405.8 15.3 %broadcast_divide_fusion = f32[2,4,12,128,416]{3,4,2,1,0:T(8,128)} fusion(f32[2,4,12,128,416]{3,4,2,1,0:T(8,128)} %get-tuple-element.174, f32[2,4,12,128]{3,2,1,0:T(8,128)S(1)} %get-tuple-element.173), kind=kLoop, calls=%fused_computation.122 | loop fusion | flops 5111808 | bytes 40943616 | tf_op jit(solution)/shard_map/div | solution.py:278
  421.1 10.0 fusion.57
  444.1 14.1 %fusion.150 = (bf16[768,8,384]{2,1,0:T(8,128)(2,1)}, bf16[768,8,384]{2,1,0:T(8,128)(2,1)}) fusion(bf16[768,8,864]{2,1,0:T(8,128)(2,1)} %all-gather.13.cloned.1.call-done), kind=kLoop, calls=%fused_computation.461 | loop fusion | bytes 18874368 | tf_op jit(solution)/shard_map/slice | solution.py:106
  463.1 34.6 %multiply_convert_fusion = (bf16[1024,3072]{1,0:T(8,128)(2,1)S(1)}, f32[1024,3072]{1,0:T(8,128)}, f32[1024,3072]{1,0:T(8,128)}) fusion(bf16[768,3072]{1,0:T(8,128)(2,1)S(1)} %bitcast.426, f32[1024,768]{1,0:T(8,128)S(1)} %get-tuple-element.176, f32[768]{0:T(1024)S(1)} %copy-done.51, f32[768]{0:T(1024)S(1)} %copy-done.45, f32[1024]{0:T(1024)S(1)} %fusion.127, ...), kind=kOutput, calls=%fused_computation.95 | convolution fusion | flops 5040242688 | bytes 39335936 | tf_op jit(solution)/shard_map/dot_general | solution.py:78
  508.6 18.6 %add_convert_fusion.1 = bf16[1024,3072]{1,0:T(8,128)(2,1)} fusion(f32[1024,3072]{1,0:T(8,128)} %get-tuple-element.58, f32[1024,3072]{1,0:T(8,128)} %get-tuple-element.177, bf16[768,3072]{1,0:T(8,128)(2,1)} %bitcast.429, f32[1024,768]{1,0:T(8,128)} %get-tuple-element.56, f32[1024]{0:T(1024)S(1)} %negate_multiply_fusion.2), kind=kOutput, calls=%fused_computation.94 | convolution fusion | flops 4877451264 | bytes 39325696 | tf_op jit(solution)/shard_map/dot_general | solution.py:88
  527.2 9.2 multiply_reduce_fusion.4
  635.4 9.4 fusion.27
  668.3 15.7 %fusion.14 = (f32[4,12,128]{2,1,0:T(8,128)S(1)}, f32[4,12,128]{2,1,0:T(8,128)S(1)}, f32[4,12,128,416]{2,3,1,0:T(8,128)}) fusion(f32[2,4,12,128,416]{3,4,2,1,0:T(8,128)} %broadcast_divide_fusion, f32[4,12,128,416]{2,3,1,0:T(8,128)} %fusion.81, bf16[4,416,12,64]{1,3,2,0:T(8,128)(2,1)S(1)} %bitcast.415, bf16[4,128,12,64]{1,0,3,2:T(4,128)(2,1)} %reshape.1040), kind=kOutput, calls=%fused_computation.115 | convolution fusion | flops 337367040 | bytes 44285952 | tf_op jit(solution)/shard_map/gbqhd,gbkhd->gbhqk/dot_general | solution.py:295
  684.0 17.0 %fusion.33 = (bf16[4,12,128,416]{2,3,1,0:T(8,128)(2,1)}, bf16[4,12,128,416]{2,3,1,0:T(8,128)(2,1)S(1)}) fusion(f32[4,12,128,416]{2,3,1,0:T(8,128)} %get-tuple-element.181, f32[2,4,12,128,416]{3,4,2,1,0:T(8,128)} %broadcast_divide_fusion, f32[4,12,128]{2,1,0:T(8,128)S(1)} %get-tuple-element.39, f32[4,12,128,416]{2,3,1,0:T(8,128)} %fusion.81, ...), kind=kLoop, calls=%fused_computation.141 | loop fusion | flops 15335424 | bytes 51167232 | tf_op jit(solution)/shard_map/reshape.170
  718.8 9.1 fusion.30
  905.5 27.0 %fusion.7 = (bf16[2,2048,768]{2,1,0:T(8,128)(2,1)}, bf16[2,2048,768]{2,1,0:T(8,128)(2,1)}) fusion(f32[1,2048,1536]{2,1,0:T(8,128)} %dynamic_update_slice.133, f32[1,2048,1536]{2,1,0:T(8,128)} %dynamic_update_slice.124, f32[2,2048,768]{2,0,1:T(2,128)} %bitcast.401, f32[2048,768]{1,0:T(8,128)} %mul.422, f32[2048,768]{1,0:T(8,128)} %mul.416, ...), kind=kLoop, calls=%fused_computation.88 | loop fusion | flops 25165824 | bytes 75497472 | tf_op jit(solution)/shard_map/convert_element_type | solution.py:450
  932.6 9.9 bitcast_convert_fusion.1
  945.0 9.9 bitcast_convert_fusion
  972.1 11.3 add_convert_fusion
  983.6 28.8 %reduce-scatter.12.cloned.1.call-done = bf16[192,8,288]{2,0,1:T(8,128)(2,1)} async-done(((bf16[768,8,288]{2,0,1:T(8,128)(2,1)}), bf16[192,8,288]{2,0,1:T(8,128)(2,1)}) %reduce-scatter.12.cloned.1.call-update) | async-done | bytes 884752 | tf_op jit(solution)/shard_map/reduce_scatter | solution.py:128
  1019.1 11.6 multiply_reduce_fusion.1
  1030.7 9.7 multiply_reduce_fusion
  1040.5 40.6 %all-reduce.3 = (f32[2,4,768]{2,1,0:T(4,128)S(1)}, f32[2,768]{1,0:T(2,128)S(1)}, f32[2,768]{1,0:T(2,128)S(1)}) all-reduce(f32[2,4,768]{2,1,0:T(4,128)S(1)} %pad_maximum_fusion.8, f32[2,768]{1,0:T(2,128)S(1)} %pad_maximum_fusion.9, f32[2,768]{1,0:T(2,128)S(1)} %pad_maximum_fusion.10), channel_id=8, replica_groups=mesh['dp'=8,'seq'=4] {'dp','seq'}, use_global_device_ids=true, to_apply=%region_23.24.clone | all-reduce | flops 9216 | bytes 73728
  1089.2 68.5 %reduce-scatter.14.cloned.1.call-done = bf16[192,1,1152]{2,0,1:T(8,128)(2,1)} async-done(((bf16[192,8,1152]{2,0,1:T(8,128)(2,1)}), bf16[192,1,1152]{2,0,1:T(8,128)(2,1)}) %reduce-scatter.14.cloned.1.call-update) | async-done | bytes 442384 | tf_op jit(solution)/shard_map/reduce_scatter | solution.py:134
  (433 shorter events, 494.9 us)
Async XLA Ops:
  7.2 84.7 %copy-start.56 = (s32[2,8]{1,0:T(2,128)S(1)}, s32[2,8]{1,0:T(2,128)}, u32[]{:S(2)}) copy-start(s32[2,8]{1,0:T(2,128)} %param.22) | copy-start | bytes 196
  7.2 138.8 %all-gather.9.cloned.1.call-start = ((), (), s32[]{:S(2)}) async-start(), calls=%async_computation.4 | async-start | bytes 5898240 | tf_op jit(solution)/shard_map/all_gather | solution.py:100
  91.1 82.0 %all-gather.11.cloned.1.call-start = ((), (), s32[]{:S(2)}) async-start(), calls=%async_computation.5 | async-start | bytes 7864320 | tf_op jit(solution)/shard_map/all_gather | solution.py:384
  91.8 139.5 %all-gather.15.cloned.1.call-start = ((), (), s32[]{:S(2)}) async-start(), calls=%async_computation.11 | async-start | bytes 3096576 | tf_op jit(solution)/shard_map/all_gather | solution.py:99
  92.6 53.4 %copy-start.54 = (s32[4]{0:T(128)}, s32[4]{0:T(128)S(1)}, u32[]{:S(2)}) copy-start(s32[4]{0:T(128)S(1)} %add_multiply_fusion.1) | copy-start | bytes 52
  92.6 26.2 %copy-start.55 = (pred[4]{0:T(512)(128)(4,1)}, pred[4]{0:T(512)(128)(4,1)S(1)}, u32[]{:S(2)}) copy-start(pred[4]{0:T(512)(128)(4,1)S(1)} %broadcast_compare_fusion.2) | copy-start | bytes 16
  98.4 47.6 %copy-start.43 = (s32[4]{0:T(128)}, s32[4]{0:T(128)S(1)}, u32[]{:S(2)}) copy-start(s32[4]{0:T(128)S(1)} %broadcast_clamp_fusion.2) | copy-start | bytes 52
  119.5 26.5 %copy-start.44 = (s32[4]{0:T(128)}, s32[4]{0:T(128)S(1)}, u32[]{:S(2)}) copy-start(s32[4]{0:T(128)S(1)} %broadcast_clamp_fusion.3) | copy-start | bytes 52
  125.4 20.6 %copy-start.50 = (s32[2,4]{1,0:T(2,128)}, s32[2,4]{1,0:T(2,128)S(1)}, u32[]{:S(2)}) copy-start(s32[2,4]{1,0:T(2,128)S(1)} %copy.227) | copy-start | bytes 100
  151.6 21.5 %copy-start.35 = (bf16[384,192]{0,1:T(8,128)(2,1)S(1)}, bf16[384,192]{0,1:T(8,128)(2,1)}, u32[]{:S(2)}) copy-start(bf16[384,192]{0,1:T(8,128)(2,1)} %param.18) | copy-start | bytes 442372
  151.6 21.5 %copy-start.36 = (bf16[192,384]{1,0:T(8,128)(2,1)S(1)}, bf16[192,384]{1,0:T(8,128)(2,1)}, u32[]{:S(2)}) copy-start(bf16[192,384]{1,0:T(8,128)(2,1)} %param.17) | copy-start | bytes 442372
  151.6 21.5 %copy-start.41 = (bf16[192,96]{1,0:T(8,128)(2,1)S(1)}, bf16[192,96]{1,0:T(8,128)(2,1)}, u32[]{:S(2)}) copy-start(bf16[192,96]{1,0:T(8,128)(2,1)} %param.16) | copy-start | bytes 110596
  156.3 30.9 %copy-start.25 = (bf16[2,512,768]{2,1,0:T(8,128)(2,1)S(1)}, bf16[2,512,768]{2,1,0:T(8,128)(2,1)}, u32[]{:S(2)}) copy-start(bf16[2,512,768]{2,1,0:T(8,128)(2,1)} %param.12) | copy-start | bytes 4718596
  174.0 262.3 %all-gather.13.cloned.1.call-start = ((), (), s32[]{:S(2)}) async-start(), calls=%async_computation.6 | async-start | bytes 13762560 | tf_op jit(solution)/shard_map/all_gather | solution.py:100
  187.2 144.2 %copy-start.37 = (f32[4,768]{1,0:T(4,128)}, f32[4,768]{1,0:T(4,128)S(1)}, u32[]{:S(2)}) copy-start(f32[4,768]{1,0:T(4,128)S(1)} %get-tuple-element.135) | copy-start | bytes 36868
  187.2 144.2 %copy-start.39 = (f32[4,768]{1,0:T(4,128)}, f32[4,768]{1,0:T(4,128)S(1)}, u32[]{:S(2)}) copy-start(f32[4,768]{1,0:T(4,128)S(1)} %get-tuple-element.136) | copy-start | bytes 36868
  245.6 417.9 %reduce-scatter.8.cloned.1.call-start = ((), (), s32[]{:S(2)}) async-start(), calls=%async_computation.7 | async-start | bytes 13762560 | tf_op jit(solution)/shard_map/reduce_scatter | solution.py:128
  265.5 8.8 copy-start.31
  405.8 15.3 %copy-start.8 = (bf16[2,4,416,768]{2,3,1,0:T(8,128)(2,1)S(1)}, bf16[2,4,416,768]{2,3,1,0:T(8,128)(2,1)}, u32[]{:S(2)}) copy-start(bf16[2,4,416,768]{2,3,1,0:T(8,128)(2,1)} %copy.226) | copy-start | bytes 15335428
  463.1 34.7 %copy-start.22 = (bf16[96,8,8,384]{3,1,2,0:T(8,128)(2,1)}, bf16[96,8,8,384]{3,1,2,0:T(8,128)(2,1)S(1)}, u32[]{:S(2)}) copy-start(bf16[96,8,8,384]{3,1,2,0:T(8,128)(2,1)S(1)} %copy.293) | copy-start | bytes 14155780
  540.6 9.2 slice-start.14
  549.9 9.2 copy-start.28
  577.0 435.4 %reduce-scatter.12.cloned.1.call-start = ((), (), s32[]{:S(2)}) async-start(), calls=%async_computation.9 | async-start | bytes 5898240 | tf_op jit(solution)/shard_map/reduce_scatter | solution.py:128
  657.7 10.6 copy-start.10
  684.0 17.0 %copy-start.21 = (bf16[4,128,12,64]{1,0,3,2:T(4,128)(2,1)S(1)}, bf16[4,128,12,64]{1,0,3,2:T(4,128)(2,1)}, u32[]{:S(2)}) copy-start(bf16[4,128,12,64]{1,0,3,2:T(4,128)(2,1)} %reshape.1043) | copy-start | bytes 2359300
  791.5 9.1 slice-start.2
  964.1 118.9 %reduce-scatter.10.cloned.1.call-start = ((), (), s32[]{:S(2)}) async-start(), calls=%async_computation.8 | async-start | bytes 7864320 | tf_op jit(solution)/shard_map/reduce_scatter | solution.py:462
  983.5 35.5 %copy-start.53 = (f32[768]{0:T(1024)S(1)}, f32[768]{0:T(1024)}, u32[]{:S(2)}) copy-start(f32[768]{0:T(1024)} %get-tuple-element.41) | copy-start | bytes 9220
  983.5 35.5 %copy-start.47 = (f32[768]{0:T(1024)S(1)}, f32[768]{0:T(1024)}, u32[]{:S(2)}) copy-start(f32[768]{0:T(1024)} %get-tuple-element.43) | copy-start | bytes 9220
  983.5 35.5 %copy-start.52 = (f32[768]{0:T(1024)S(1)}, f32[768]{0:T(1024)}, u32[]{:S(2)}) copy-start(f32[768]{0:T(1024)} %get-tuple-element.45) | copy-start | bytes 9220
  983.5 174.2 %reduce-scatter.14.cloned.1.call-start = ((), (), s32[]{:S(2)}) async-start(), calls=%async_computation.10 | async-start | bytes 3981312 | tf_op jit(solution)/shard_map/reduce_scatter | solution.py:134
  1030.7 52.3 %copy-start.49 = (f32[1024]{0:T(1024)S(1)}, f32[1024]{0:T(1024)}, u32[]{:S(2)}) copy-start(f32[1024]{0:T(1024)} %copy-done.48) | copy-start | bytes 12292
  (50 other events, 230.9 us)
Sparse Core Ops, SparseCore 0:
  91.2 33.8 all-gather.8
  126.7 46.3 all-gather.10
  175.3 55.9 all-gather.14
  245.8 71.7 all-gather.12
  577.2 86.3 reduce-scatter.7
  964.2 48.1 reduce-scatter.11
  1014.9 59.6 reduce-scatter.9
  1078.2 79.4 reduce-scatter.13

commit v7 on v6

--- a/solution.py
+++ b/solution.py
@@ -94,10 +94,11 @@
     return left_term + right_term
 
 
-def gather_grouped(shards):
+def gather_grouped(shards, tie=None):
     local_block = jnp.concatenate(shards, axis=1)
     across = lax.all_gather(local_block, "dp", axis=1, tiled=False)
-    return lax.all_gather(across, "seq", axis=0, tiled=True)
+    across, tie = lax.optimization_barrier((across, tie))
+    return lax.all_gather(across, "seq", axis=0, tiled=True), tie
 
 
 def split_grouped(gathered, widths):
@@ -109,13 +110,13 @@
     return pieces
 
 
-def gather_first(w_query, w_key, w_value):
-    first = gather_grouped((w_query, w_key, w_value))
-    return split_grouped(first, (w_query.shape[1], w_key.shape[1], w_value.shape[1]))
+def gather_first(w_query, w_key, w_value, tie):
+    first, tie = gather_grouped((w_query, w_key, w_value), tie)
+    return split_grouped(first, (w_query.shape[1], w_key.shape[1], w_value.shape[1])), tie
 
 
 def gather_second(w_output, w_inner, w_outer):
-    second = gather_grouped((w_output, w_inner, w_outer.T))
+    second, _ = gather_grouped((w_output, w_inner, w_outer.T))
     wo, wi, wu_t = split_grouped(second, (w_output.shape[1], w_inner.shape[1], w_outer.shape[0]))
     return (wo, wi, wu_t.T)
 
@@ -369,10 +370,8 @@
         [pool_weight.reshape(pool_rows_count, -1), ln_gain, ln_bias], axis=0
     )
     small_full = lax.all_gather(small_local, ("dp", "seq"), axis=1, tiled=True)
-    small_full, w_query, w_key, w_value = lax.optimization_barrier(
-        (small_full, w_query, w_key, w_value)
-    )
-    wq, wk, wv = gather_first(w_query, w_key, w_value)
+    hidden_all = lax.all_gather(hidden_in, "seq", axis=1, tiled=True)
+    (wq, wk, wv), hidden_all = gather_first(w_query, w_key, w_value, hidden_all)
     pool_full = small_full[:pool_rows_count].reshape(pool_weight.shape[0], pool_weight.shape[1], -1)
     gain_full = small_full[pool_rows_count : pool_rows_count + ln_gain.shape[0]]
     bias_full = small_full[pool_rows_count + ln_gain.shape[0] :]
@@ -381,7 +380,6 @@
     offsets = STRIDE * branch_blocks
     starts, mask = block_geometry(seq_index, groups, shard_rows, offsets)
 
-    hidden_all = lax.all_gather(hidden_in, "seq", axis=1, tiled=True)
     group_len = hidden_all.shape[1]
     tokens = hidden_in.reshape(groups * shard_rows, width)
     all_tokens = hidden_all.reshape(groups * group_len, width)
@@ -396,8 +394,8 @@
     pkv_local = lax.dynamic_slice_in_dim(
         pkv_all, seq_index * (shard_rows // STRIDE), shard_rows // STRIDE, 1
     )
-    wq, wk, wv, hidden_all, w_output, w_inner, w_outer = lax.optimization_barrier(
-        (wq, wk, wv, hidden_all, w_output, w_inner, w_outer)
+    wq, wk, wv, w_output, w_inner, w_outer = lax.optimization_barrier(
+        (wq, wk, wv, w_output, w_inner, w_outer)
     )
     wo, wi, wu = gather_second(w_output, w_inner, w_outer)
     attended, att_saved = attention_fwd(
@@ -437,17 +435,28 @@
         grad_g = grad_rows[g].reshape(shard_rows, width)
         if g == 1:
             grad_g, early_reduced = lax.optimization_barrier((grad_g, early_reduced))
-        pieces_back.append(attention_bwd(grad_g, saved_g, starts_g, seq_index))
+        grad_queries_g, full_g, pooled_g = attention_bwd(grad_g, saved_g, starts_g, seq_index)
+        if g == 1:
+            full_g, pooled_g, earlier_back = lax.optimization_barrier(
+                (full_g, pooled_g, pieces_back[0][4])
+            )
+            pieces_back[0] = pieces_back[0][:4] + (earlier_back,)
+        key_partial_g = (
+            full_g[..., :width] + unpool_grouped(pooled_g[..., :width], pool_full[0])
+        ).astype(jnp.bfloat16).reshape(group_len, width)
+        value_partial_g = (
+            full_g[..., width:] + unpool_grouped(pooled_g[..., width:], pool_full[1])
+        ).astype(jnp.bfloat16).reshape(group_len, width)
+        back_g = product_right(key_partial_g, wk) + product_right(value_partial_g, wv)
+        back_g = back_g.reshape(1, group_len, width).astype(jnp.bfloat16)
+        back_own_g = lax.psum_scatter(back_g, "seq", scatter_dimension=1, tiled=True)
+        pieces_back.append((grad_queries_g, pooled_g, key_partial_g, value_partial_g, back_own_g))
     grad_queries = jnp.concatenate([piece[0] for piece in pieces_back], axis=0)
-    grad_full = jnp.concatenate([piece[1] for piece in pieces_back], axis=0)
-    grad_pooled = jnp.concatenate([piece[2] for piece in pieces_back], axis=0)
+    grad_pooled = jnp.concatenate([piece[1] for piece in pieces_back], axis=0)
+    key_partial = jnp.concatenate([piece[2] for piece in pieces_back], axis=0)
+    value_partial = jnp.concatenate([piece[3] for piece in pieces_back], axis=0)
+    back_own = jnp.concatenate([piece[4] for piece in pieces_back], axis=0)
     early = (early_reduced, early_widths)
-    key_partial = (
-        grad_full[..., :width] + unpool_grouped(grad_pooled[..., :width], pool_full[0])
-    ).astype(jnp.bfloat16).reshape(groups * group_len, width)
-    value_partial = (
-        grad_full[..., width:] + unpool_grouped(grad_pooled[..., width:], pool_full[1])
-    ).astype(jnp.bfloat16).reshape(groups * group_len, width)
     grad_pooling = jnp.stack(
         [
             pool_grad_grouped(grad_pooled[..., :width], key_g),
@@ -457,9 +466,6 @@
     grad_query_w = product_left(tokens, grad_queries)
     grad_key_w = product_left(all_tokens, key_partial)
     grad_value_w = product_left(all_tokens, value_partial)
-    back_rows = product_right(key_partial, wk) + product_right(value_partial, wv)
-    back_rows = back_rows.reshape(groups, group_len, width).astype(jnp.bfloat16)
-    back_own = lax.psum_scatter(back_rows, "seq", scatter_dimension=1, tiled=True)
     grad_tokens = (
         grad_mixed
         + product_right(grad_queries, wq)

time: 1180 us -> 1130 us (0.958)
  local copies, waits for them, and re-layouts: 373 us -> 336 us
  waiting for transfers between devices: 158 us -> 143 us
    all_gather x1, waiting for transfers between devices: 38.9 us -> 0.01 us  [gather_grouped(): across = lax.all_gather(local_block, 'dp', axis=1, tiled=False)]
    unnamed x8 -> x10, waiting for transfers between devices: 0.81 us -> 32.1 us
    all_gather x2, waiting for transfers between devices: 0.01 us -> 29.7 us  [gather_grouped(): return (lax.all_gather(across, 'seq', axis=0, tiled=True), tie)]
    convert_element_type x1 -> x0, other arithmetic: 27 us -> none  [local(): value_partial = (grad_full[..., width:] + unpool_grouped(grad_pooled[...,...]
    reduce_scatter x1, waiting for transfers between devices: 68.5 us -> 42.8 us  [reduce_dp_stage(): lax.psum_scatter(joined, 'dp', scatter_dimension=1, tiled=True)[:, 0]]
    mul x4 -> x0, local copies, waits for them, and re-layouts: 23.6 us -> none  [pool_grouped(): source.reshape(groups, rows // STRIDE, STRIDE, width) * weight[None, None]]
    mul x2 -> x6, local copies, waits for them, and re-layouts: 13.9 us -> 34 us  [unpool_grouped(): pooled_grad[:, :, None, :] * weight[None, None]]
    reshape x0 -> x2, other arithmetic: none -> 19.7 us  [local(): value_partial_g = (full_g[..., width:] + unpool_grouped(pooled_g[..., wid...]
  transfers between devices with their start and end apart: 8 -> 9, of which waited for: 5 -> 5; matrix products, arithmetic and copies ran while one was open for 31% -> 33% of each run, Pallas kernels for 0% -> 0%
where the time goes in v7:
time: 1130 us; the launch traced here: 1120 us
  local copies, waits for them, and re-layouts  336 us (30%)
  matrix products  245 us (22%)
  other arithmetic  214 us (19%)
  waiting for transfers between devices  143 us (13%)
  blocking collectives  119 us (11%)
  between operations  60.6 us (5%)
    dot_general x6, matrix products, product(): return jnp.dot(left, right, preferred_element_type=jnp.float32)  66.6 us
    unnamed x190, local copies, waits for them, and re-layouts  52.9 us
    dot_general x8, matrix products, product_right(): lax.dot_general(left, right, (((1,), (1,)), ((), ())), preferred_element_...  50.9 us
    reduce_scatter x1, waiting for transfers between devices, reduce_dp_stage(): lax.psum_scatter(joined, 'dp', scatter_dimension=1, tiled=True)[:, 0]  42.8 us
    all_gather x1, blocking collectives, local(): small_full = lax.all_gather(small_local, ('dp', 'seq'), axis=1, tiled=True)  42.8 us
    unnamed x1, blocking collectives  41.1 us
    dot_general x6, matrix products, product_left(): lax.dot_general(left, right, (((0,), (0,)), ((), ())), preferred_element_...  40.1 us
    dynamic_update_slice x32, local copies, waits for them, and re-layouts, window_add(): lax.dynamic_update_slice_in_dim(row, current + updates[g, b], start, 0)  36.9 us
  transfers between devices with their start and end apart: 9, of which 5 were waited for; matrix products, arithmetic and copies ran while one was open for 33% of the time, Pallas kernels for 0%

profile of v7, /device:TPU:0, one launch (start us, length us, event | category | flops | bytes accessed | tf_op | source)
XLA Modules:
  0.0 1118.7 jit_solution(3958238064316801649)
XLA Ops:
  10.7 35.1 %all-gather = bf16[192,2304]{0,1:T(8,128)(2,1)S(1)} all-gather(bf16[192,288]{0,1:T(8,128)(2,1)S(1)} %pad_maximum_fusion.7), channel_id=2, replica_groups=mesh['dp'=8,'seq'=4] {'dp'}, dimensions={1}, use_global_device_ids=true | all-gather | bytes 995328 | tf_op jit(solution)/shard_map/all_gather | solution.py:99
  45.8 12.9 %all-gather.9.cloned.1.call-done = bf16[2,2048,768]{2,1,0:T(8,128)(2,1)} async-done(((bf16[2,512,768]{2,1,0:T(8,128)(2,1)}), bf16[2,2048,768]{2,1,0:T(8,128)(2,1)}) %all-gather.9.cloned.1.call-update) | async-done | bytes 6291472 | tf_op jit(solution)/shard_map/all_gather | solution.py:373
  68.6 29.7 %all-gather.11.cloned.1.call-done = bf16[768,8,288]{2,1,0:T(8,128)(2,1)} async-done(((bf16[192,8,288]{2,1,0:T(8,128)(2,1)}), bf16[768,8,288]{2,1,0:T(8,128)(2,1)}) %all-gather.11.cloned.1.call-update) | async-done | bytes 3538960 | tf_op jit(solution)/shard_map/all_gather | solution.py:101
  141.4 42.8 %all-gather.2 = f32[32,24,12]{1,2,0:T(8,128)S(1)} all-gather(f32[1,24,12]{1,2,0:T(8,128)S(1)} %maximum_bitcast_fusion.11), channel_id=1, replica_groups=mesh['dp'=8,'seq'=4] {'dp','seq'}, dimensions={0}, use_global_device_ids=true | all-gather | bytes 38016 | tf_op jit(solution)/shard_map/all_gather | solution.py:372
  211.9 9.8 convolution_convert_fusion.1
  221.7 12.4 %reshape.1169 = f32[2,512,4,768]{3,2,1,0:T(4,128)} reshape(bf16[4096,768]{1,0:T(8,128)(2,1)} %convolution_convert_fusion.1) | data formatting | bytes 18874368 | tf_op jit(solution)/shard_map/convert_element_type | solution.py:389
  248.6 10.2 convolution_convert_fusion
  258.8 12.4 %reshape.1170 = f32[2,512,4,768]{3,2,1,0:T(4,128)} reshape(bf16[4096,768]{1,0:T(8,128)(2,1)} %convolution_convert_fusion) | data formatting | bytes 18874368 | tf_op jit(solution)/shard_map/convert_element_type | solution.py:390
  271.2 19.7 %multiply_reduce_fusion.2 = (bf16[2,512,768]{2,1,0:T(8,128)(2,1)S(1)}, bf16[2,512,768]{2,1,0:T(8,128)(2,1)S(1)}) fusion(f32[2,512,4,768]{3,2,1,0:T(4,128)} %reshape.1170, f32[4,768]{1,0:T(4,128)S(1)} %get-tuple-element.143, f32[2,512,4,768]{3,2,1,0:T(4,128)} %reshape.1169, f32[4,768]{1,0:T(4,128)S(1)} %get-tuple-element.144), kind=kLoop, calls=%fused_computation.97 | loop fusion | flops 11010048 | bytes 28336128 | tf_op jit(solution)/shard_map/reduce_sum | solution.py:338
  307.6 8.5 fusion.153
  336.4 13.2 %fusion.163 = (f32[2,4,12,128]{3,2,1,0:T(8,128)S(1)}, f32[2,4,12,128,416]{3,4,2,1,0:T(8,128)}) fusion(pred[2,4,128,416]{2,3,1,0:T(8,128)(4,1)} %pad_add_fusion, bf16[2,4,416,12,64]{2,4,3,1,0:T(8,128)(2,1)} %bitcast.444, bf16[2,4,128,12,64]{2,1,0,4,3:T(4,128)(2,1)S(1)} %reshape_reshape.3), kind=kOutput, calls=%fused_computation.485 | convolution fusion | flops 674759040 | bytes 27607040 | tf_op jit(solution)/shard_map/sub | solution.py:277
  349.7 15.3 %broadcast_divide_fusion = f32[2,4,12,128,416]{3,4,2,1,0:T(8,128)} fusion(f32[2,4,12,128,416]{3,4,2,1,0:T(8,128)} %get-tuple-element.182, f32[2,4,12,128]{3,2,1,0:T(8,128)S(1)} %get-tuple-element.181), kind=kLoop, calls=%fused_computation.111 | loop fusion | flops 5111808 | bytes 40943616 | tf_op jit(solution)/shard_map/div | solution.py:279
  365.0 10.0 fusion.58
  388.0 14.1 %fusion.151 = (bf16[768,8,384]{2,1,0:T(8,128)(2,1)}, bf16[768,8,384]{2,1,0:T(8,128)(2,1)}) fusion(bf16[768,8,864]{2,1,0:T(8,128)(2,1)} %all-gather.13.cloned.1.call-done), kind=kLoop, calls=%fused_computation.473 | loop fusion | bytes 18874368 | tf_op jit(solution)/shard_map/slice | solution.py:107
  407.0 34.6 %multiply_convert_fusion = (bf16[1024,3072]{1,0:T(8,128)(2,1)S(1)}, f32[1024,3072]{1,0:T(8,128)}, f32[1024,3072]{1,0:T(8,128)}) fusion(bf16[768,3072]{1,0:T(8,128)(2,1)S(1)} %bitcast.445, f32[1024,768]{1,0:T(8,128)S(1)} %get-tuple-element.184, f32[768]{0:T(1024)S(1)} %get-tuple-element.50, f32[768]{0:T(1024)S(1)} %get-tuple-element.51, ...), kind=kOutput, calls=%fused_computation.84 | convolution fusion | flops 5040242688 | bytes 39335936 | tf_op jit(solution)/shard_map/dot_general | solution.py:78
  452.5 18.8 %add_convert_fusion = bf16[1024,3072]{1,0:T(8,128)(2,1)} fusion(f32[1024,3072]{1,0:T(8,128)} %get-tuple-element.60, f32[1024,3072]{1,0:T(8,128)} %get-tuple-element.185, bf16[768,3072]{1,0:T(8,128)(2,1)} %bitcast.448, f32[1024,768]{1,0:T(8,128)} %get-tuple-element.58, f32[1024]{0:T(1024)S(1)} %negate_multiply_fusion.2), kind=kOutput, calls=%fused_computation.83 | convolution fusion | flops 4877451264 | bytes 39325696 | tf_op jit(solution)/shard_map/dot_general | solution.py:88
  471.3 9.2 multiply_reduce_fusion.4
  520.9 10.3 fusion.152
  563.4 9.4 fusion.22
  579.0 25.6 %reduce-scatter.11.cloned.1.call-done = bf16[192,8,864]{2,0,1:T(8,128)(2,1)} async-done(((bf16[768,8,864]{2,0,1:T(8,128)(2,1)}), bf16[192,8,864]{2,0,1:T(8,128)(2,1)}) %reduce-scatter.11.cloned.1.call-update) | async-done | bytes 2654224 | tf_op jit(solution)/shard_map/reduce_scatter | solution.py:129
  616.0 17.5 %fusion.11 = (f32[4,12,128]{2,1,0:T(8,128)S(1)}, f32[4,12,128]{2,1,0:T(8,128)S(1)}, f32[4,12,128,416]{2,3,1,0:T(8,128)}) fusion(f32[2,4,12,128,416]{3,4,2,1,0:T(8,128)} %broadcast_divide_fusion, f32[4,12,128,416]{2,3,1,0:T(8,128)} %fusion.79, bf16[4,416,12,64]{1,3,2,0:T(8,128)(2,1)} %bitcast.435, bf16[4,128,12,64]{1,0,3,2:T(4,128)(2,1)} %reshape.1144), kind=kOutput, calls=%fused_computation.108 | convolution fusion | flops 337367040 | bytes 44285952 | tf_op jit(solution)/shard_map/gbqhd,gbkhd->gbhqk/dot_general | solution.py:296
  633.5 17.1 %fusion.27 = (bf16[4,12,128,416]{2,3,1,0:T(8,128)(2,1)S(1)}, bf16[4,12,128,416]{2,3,1,0:T(8,128)(2,1)}) fusion(f32[4,12,128,416]{2,3,1,0:T(8,128)} %get-tuple-element.189, f32[2,4,12,128,416]{3,4,2,1,0:T(8,128)} %broadcast_divide_fusion, f32[4,12,128]{2,1,0:T(8,128)S(1)} %get-tuple-element.41, f32[4,12,128,416]{2,3,1,0:T(8,128)} %fusion.79, ...), kind=kLoop, calls=%fused_computation.137 | loop fusion | flops 15335424 | bytes 51167232 | tf_op jit(solution)/shard_map/reshape.162
  669.3 9.1 fusion.25
  749.2 9.0 fusion.33
  880.2 10.7 fusion.30
  895.6 8.7 copy.227
  910.2 8.7 copy.228
  918.9 9.3 convolution_convert_fusion.7
  953.3 31.3 %reduce-scatter.19.cloned.1.call-done = bf16[192,2304]{1,0:T(8,128)(2,1)} async-done(((bf16[768,2304]{1,0:T(8,128)(2,1)}), bf16[192,2304]{1,0:T(8,128)(2,1)}) %reduce-scatter.19.cloned.1.call-update) | async-done | bytes 884752
  999.4 10.7 multiply_reduce_fusion.1
  1017.0 41.1 %all-reduce.3 = (f32[2,4,768]{2,1,0:T(4,128)S(1)}, f32[2,768]{1,0:T(2,128)S(1)}, f32[2,768]{1,0:T(2,128)S(1)}) all-reduce(f32[2,4,768]{2,1,0:T(4,128)S(1)} %pad_maximum_fusion.8, f32[2,768]{1,0:T(2,128)S(1)} %pad_maximum_fusion.9, f32[2,768]{1,0:T(2,128)S(1)} %pad_maximum_fusion.10), channel_id=9, replica_groups=mesh['dp'=8,'seq'=4] {'dp','seq'}, use_global_device_ids=true, to_apply=%region_24.25.clone | all-reduce | flops 9216 | bytes 73728
  1066.2 42.8 %reduce-scatter.17.cloned.1.call-done = bf16[192,1,1152]{2,0,1:T(8,128)(2,1)} async-done(((bf16[192,8,1152]{2,0,1:T(8,128)(2,1)}), bf16[192,1,1152]{2,0,1:T(8,128)(2,1)}) %reduce-scatter.17.cloned.1.call-update) | async-done | bytes 442384 | tf_op jit(solution)/shard_map/reduce_scatter | solution.py:135
  (466 shorter events, 488.1 us)
Async XLA Ops:
  7.2 53.5 %copy-start.62 = (s32[2,8]{1,0:T(2,128)S(1)}, s32[2,8]{1,0:T(2,128)}, u32[]{:S(2)}) copy-start(s32[2,8]{1,0:T(2,128)} %param.22) | copy-start | bytes 196
  7.2 55.7 %copy-start.56 = (f32[2,4,24]{2,1,0:T(4,128)S(1)}, f32[2,4,24]{2,1,0:T(4,128)}, u32[]{:S(2)}) copy-start(f32[2,4,24]{2,1,0:T(4,128)} %param.19) | copy-start | bytes 2308
  7.2 55.7 %copy-start.61 = (f32[2,24]{1,0:T(2,128)S(1)}, f32[2,24]{1,0:T(2,128)}, u32[]{:S(2)}) copy-start(f32[2,24]{1,0:T(2,128)} %param.20) | copy-start | bytes 580
  7.2 55.7 %copy-start.60 = (f32[2,24]{1,0:T(2,128)S(1)}, f32[2,24]{1,0:T(2,128)}, u32[]{:S(2)}) copy-start(f32[2,24]{1,0:T(2,128)} %param.21) | copy-start | bytes 580
  7.2 51.5 %all-gather.9.cloned.1.call-start = ((), (), s32[]{:S(2)}) async-start(), calls=%async_computation.5 | async-start | bytes 7864320 | tf_op jit(solution)/shard_map/all_gather | solution.py:373
  8.0 90.4 %all-gather.11.cloned.1.call-start = ((), (), s32[]{:S(2)}) async-start(), calls=%async_computation.6 | async-start | bytes 5898240 | tf_op jit(solution)/shard_map/all_gather | solution.py:101
  60.6 173.5 %all-gather.15.cloned.1.call-start = ((), (), s32[]{:S(2)}) async-start(), calls=%async_computation.12 | async-start | bytes 3096576 | tf_op jit(solution)/shard_map/all_gather | solution.py:99
  60.8 37.5 %copy-start.48 = (s32[2,8]{1,0:T(2,128)}, s32[2,8]{1,0:T(2,128)S(1)}, u32[]{:S(2)}) copy-start(s32[2,8]{1,0:T(2,128)S(1)} %copy.193) | copy-start | bytes 196
  67.9 30.4 %copy-start.54 = (pred[4,128]{1,0:T(4,128)(4,1)}, pred[4,128]{1,0:T(4,128)(4,1)S(1)}, u32[]{:S(2)}) copy-start(pred[4,128]{1,0:T(4,128)(4,1)S(1)} %get-tuple-element.171) | copy-start | bytes 1540
  67.9 30.4 %copy-start.55 = (pred[4,128]{1,0:T(4,128)(4,1)}, pred[4,128]{1,0:T(4,128)(4,1)S(1)}, u32[]{:S(2)}) copy-start(pred[4,128]{1,0:T(4,128)(4,1)S(1)} %get-tuple-element.172) | copy-start | bytes 1540
  108.6 103.3 %copy-start.32 = (bf16[768,8,96]{0,2,1:T(8,128)(2,1)S(1)}, bf16[768,8,96]{0,2,1:T(8,128)(2,1)}, u32[]{:S(2)}) copy-start(bf16[768,8,96]{0,2,1:T(8,128)(2,1)} %copy.242) | copy-start | bytes 3538948
  111.3 268.5 %all-gather.13.cloned.1.call-start = ((), (), s32[]{:S(2)}) async-start(), calls=%async_computation.7 | async-start | bytes 13762560 | tf_op jit(solution)/shard_map/all_gather | solution.py:101
  211.9 59.2 %copy-start.36 = (f32[4,768]{1,0:T(4,128)}, f32[4,768]{1,0:T(4,128)S(1)}, u32[]{:S(2)}) copy-start(f32[4,768]{1,0:T(4,128)S(1)} %get-tuple-element.143) | copy-start | bytes 36868
  211.9 59.2 %copy-start.38 = (f32[4,768]{1,0:T(4,128)}, f32[4,768]{1,0:T(4,128)S(1)}, u32[]{:S(2)}) copy-start(f32[4,768]{1,0:T(4,128)S(1)} %get-tuple-element.144) | copy-start | bytes 36868
  248.3 356.3 %reduce-scatter.11.cloned.1.call-start = ((), (), s32[]{:S(2)}) async-start(), calls=%async_computation.8 | async-start | bytes 13762560 | tf_op jit(solution)/shard_map/reduce_scatter | solution.py:129
  327.3 9.2 copy-start.18
  349.7 15.3 %copy-start.5 = (bf16[2,4,416,768]{2,3,1,0:T(8,128)(2,1)S(1)}, bf16[2,4,416,768]{2,3,1,0:T(8,128)(2,1)}, u32[]{:S(2)}) copy-start(bf16[2,4,416,768]{2,3,1,0:T(8,128)(2,1)} %copy.190) | copy-start | bytes 15335428
  407.0 34.7 %copy-start.22 = (bf16[96,8,8,384]{3,1,2,0:T(8,128)(2,1)}, bf16[96,8,8,384]{3,1,2,0:T(8,128)(2,1)S(1)}, u32[]{:S(2)}) copy-start(bf16[96,8,8,384]{3,1,2,0:T(8,128)(2,1)S(1)} %copy.249) | copy-start | bytes 14155780
  484.7 9.2 slice-start.19
  520.8 333.6 %reduce-scatter.13.cloned.1.call-start = ((), (), s32[]{:S(2)}) async-start(), calls=%async_computation.9 | async-start | bytes 3932160 | tf_op jit(solution)/shard_map/reduce_scatter | solution.py:452
  633.5 17.1 %copy-start.21 = (bf16[4,128,12,64]{1,0,3,2:T(4,128)(2,1)S(1)}, bf16[4,128,12,64]{1,0,3,2:T(4,128)(2,1)}, u32[]{:S(2)}) copy-start(bf16[4,128,12,64]{1,0,3,2:T(4,128)(2,1)} %reshape.1155) | copy-start | bytes 2359300
  655.8 10.4 slice-start
  764.9 219.6 %reduce-scatter.19.cloned.1.call-start = ((), (), s32[]{:S(2)}) async-start(), calls=%async_computation.13 | async-start | bytes 4423680
  880.2 12.4 %copy-start.13 = (bf16[2048,768]{1,0:T(8,128)(2,1)S(1)}, bf16[2048,768]{1,0:T(8,128)(2,1)}, u32[]{:S(2)}) copy-start(bf16[2048,768]{1,0:T(8,128)(2,1)} %copy-done.12) | copy-start | bytes 9437188
  918.9 9.3 copy-start.17
  944.1 116.0 %reduce-scatter.15.cloned.1.call-start = ((), (), s32[]{:S(2)}) async-start(), calls=%async_computation.10 | async-start | bytes 3932160 | tf_op jit(solution)/shard_map/reduce_scatter | solution.py:452
  953.2 155.8 %reduce-scatter.17.cloned.1.call-start = ((), (), s32[]{:S(2)}) async-start(), calls=%async_computation.11 | async-start | bytes 3981312 | tf_op jit(solution)/shard_map/reduce_scatter | solution.py:135
  996.6 13.5 %slice-start.6 = ((s8[12582912]{0:T(1024)(128)(4,1)}), s8[4194304]{0:T(1024)(128)(4,1)S(1)}, s32[]{:S(2)}) async-start(s8[12582912]{0:T(1024)(128)(4,1)} %bitcast.408), calls=%async_computation.20 | async-start | bytes 8388608
  996.6 13.5 %slice-start.7 = ((s8[12582912]{0:T(1024)(128)(4,1)}), s8[4194304]{0:T(1024)(128)(4,1)S(1)}, s32[]{:S(2)}) async-start(s8[12582912]{0:T(1024)(128)(4,1)} %bitcast.408), calls=%async_computation.21 | async-start | bytes 8388608
  999.4 10.7 slice-start.8
  1010.1 51.5 %copy-start.10 = (f32[1024,768]{1,0:T(8,128)S(1)}, f32[1024,768]{1,0:T(8,128)}, u32[]{:S(2)}) copy-start(f32[1024,768]{1,0:T(8,128)} %copy-done.9) | copy-start | bytes 9437188
  1010.1 51.5 %copy-start.51 = (f32[1024]{0:T(1024)S(1)}, f32[1024]{0:T(1024)}, u32[]{:S(2)}) copy-start(f32[1024]{0:T(1024)} %copy-done.50) | copy-start | bytes 12292
  (62 other events, 297.5 us)
Sparse Core Ops, SparseCore 0:
  9.6 49.0 all-gather.8
  60.8 37.4 all-gather.10
  111.5 56.7 all-gather.14
  248.5 69.2 all-gather.12
  520.9 83.6 reduce-scatter.10
  765.1 37.9 reduce-scatter.12
  944.2 40.3 reduce-scatter.18
  987.1 38.0 reduce-scatter.14
  1028.8 80.1 reduce-scatter.16

commit v8 on v7

--- a/solution.py
+++ b/solution.py
@@ -371,7 +371,9 @@
     )
     small_full = lax.all_gather(small_local, ("dp", "seq"), axis=1, tiled=True)
     hidden_all = lax.all_gather(hidden_in, "seq", axis=1, tiled=True)
-    (wq, wk, wv), hidden_all = gather_first(w_query, w_key, w_value, hidden_all)
+    (wq, wk, wv), (hidden_all, small_full) = gather_first(
+        w_query, w_key, w_value, (hidden_all, small_full)
+    )
     pool_full = small_full[:pool_rows_count].reshape(pool_weight.shape[0], pool_weight.shape[1], -1)
     gain_full = small_full[pool_rows_count : pool_rows_count + ln_gain.shape[0]]
     bias_full = small_full[pool_rows_count + ln_gain.shape[0] :]
@@ -433,12 +435,10 @@
         saved_g = tuple(item[g : g + 1] for item in att_saved)
         starts_g = tuple(item[g : g + 1] for item in starts)
         grad_g = grad_rows[g].reshape(shard_rows, width)
-        if g == 1:
-            grad_g, early_reduced = lax.optimization_barrier((grad_g, early_reduced))
         grad_queries_g, full_g, pooled_g = attention_bwd(grad_g, saved_g, starts_g, seq_index)
         if g == 1:
-            full_g, pooled_g, earlier_back = lax.optimization_barrier(
-                (full_g, pooled_g, pieces_back[0][4])
+            full_g, pooled_g, earlier_back, early_reduced = lax.optimization_barrier(
+                (full_g, pooled_g, pieces_back[0][4], early_reduced)
             )
             pieces_back[0] = pieces_back[0][:4] + (earlier_back,)
         key_partial_g = (

time: 1130 us -> 1090 us (0.965)
  waiting for transfers between devices: 143 us -> 121 us
  local copies, waits for them, and re-layouts: 336 us -> 323 us
    all_gather x1, waiting for transfers between devices: 12.9 us -> 0.01 us  [local(): hidden_all = lax.all_gather(hidden_in, 'seq', axis=1, tiled=True)]
  transfers between devices with their start and end apart: 9 -> 9, of which waited for: 5 -> 4; matrix products, arithmetic and copies ran while one was open for 33% -> 32% of each run, Pallas kernels for 0% -> 0%
where the time goes in v8:
time: 1090 us; the launch traced here: 1080 us
  local copies, waits for them, and re-layouts  323 us (30%)
  matrix products  244 us (22%)
  other arithmetic  215 us (20%)
  waiting for transfers between devices  121 us (11%)
  blocking collectives  119 us (11%)
  between operations  60.6 us (6%)
    dot_general x6, matrix products, product(): return jnp.dot(left, right, preferred_element_type=jnp.float32)  66.2 us
    unnamed x190, local copies, waits for them, and re-layouts  53.9 us
    dot_general x8, matrix products, product_right(): lax.dot_general(left, right, (((1,), (1,)), ((), ())), preferred_element_...  50.6 us
    all_gather x1, blocking collectives, local(): small_full = lax.all_gather(small_local, ('dp', 'seq'), axis=1, tiled=True)  44.7 us
    reduce_scatter x1, waiting for transfers between devices, reduce_dp_stage(): lax.psum_scatter(joined, 'dp', scatter_dimension=1, tiled=True)[:, 0]  43.4 us
    unnamed x1, blocking collectives  40.6 us
    dot_general x6, matrix products, product_left(): lax.dot_general(left, right, (((0,), (0,)), ((), ())), preferred_element_...  40.3 us
    dynamic_update_slice x32, local copies, waits for them, and re-layouts, window_add(): lax.dynamic_update_slice_in_dim(row, current + updates[g, b], start, 0)  37.2 us
  transfers between devices with their start and end apart: 9, of which 4 were waited for; matrix products, arithmetic and copies ran while one was open for 32% of the time, Pallas kernels for 0%

profile of v8, /device:TPU:0, one launch (start us, length us, event | category | flops | bytes accessed | tf_op | source)
XLA Modules:
  0.0 1083.6 jit_solution(25178937930240787)
XLA Ops:
  11.4 44.7 %all-gather.2 = f32[32,24,12]{1,2,0:T(8,128)S(1)} all-gather(f32[1,24,12]{1,2,0:T(8,128)S(1)} %maximum_bitcast_fusion.11), channel_id=1, replica_groups=mesh['dp'=8,'seq'=4] {'dp','seq'}, dimensions={0}, use_global_device_ids=true | all-gather | bytes 38016 | tf_op jit(solution)/shard_map/all_gather | solution.py:372
  56.3 33.9 %all-gather = bf16[192,2304]{0,1:T(8,128)(2,1)S(1)} all-gather(bf16[192,288]{0,1:T(8,128)(2,1)S(1)} %pad_maximum_fusion.7), channel_id=2, replica_groups=mesh['dp'=8,'seq'=4] {'dp'}, dimensions={1}, use_global_device_ids=true | all-gather | bytes 995328 | tf_op jit(solution)/shard_map/all_gather | solution.py:99
  100.0 26.3 %all-gather.11.cloned.1.call-done = bf16[768,8,288]{2,1,0:T(8,128)(2,1)} async-done(((bf16[192,8,288]{2,1,0:T(8,128)(2,1)}), bf16[768,8,288]{2,1,0:T(8,128)(2,1)}) %all-gather.11.cloned.1.call-update) | async-done | bytes 3538960 | tf_op jit(solution)/shard_map/all_gather | solution.py:101
  198.3 9.8 convolution_convert_fusion.1
  222.7 9.7 convolution_convert_fusion
  232.4 12.7 %reshape.1168 = f32[2,512,4,768]{3,2,1,0:T(4,128)} reshape(bf16[4096,768]{1,0:T(8,128)(2,1)} %convolution_convert_fusion.1) | data formatting | bytes 18874368 | tf_op jit(solution)/shard_map/convert_element_type | solution.py:391
  245.1 12.3 %reshape.1169 = f32[2,512,4,768]{3,2,1,0:T(4,128)} reshape(bf16[4096,768]{1,0:T(8,128)(2,1)} %convolution_convert_fusion) | data formatting | bytes 18874368 | tf_op jit(solution)/shard_map/convert_element_type | solution.py:392
  257.4 19.6 %multiply_reduce_fusion.2 = (bf16[2,512,768]{2,1,0:T(8,128)(2,1)S(1)}, bf16[2,512,768]{2,1,0:T(8,128)(2,1)S(1)}) fusion(f32[2,512,4,768]{3,2,1,0:T(4,128)} %reshape.1169, f32[4,768]{1,0:T(4,128)S(1)} %get-tuple-element.143, f32[2,512,4,768]{3,2,1,0:T(4,128)} %reshape.1168, f32[4,768]{1,0:T(4,128)S(1)} %get-tuple-element.144), kind=kLoop, calls=%fused_computation.97 | loop fusion | flops 11010048 | bytes 28336128 | tf_op jit(solution)/shard_map/reduce_sum | solution.py:338
  294.3 8.5 fusion.153
  302.8 8.1 copy.199
  314.8 8.1 copy.190
  322.9 13.3 %fusion.163 = (f32[2,4,12,128]{3,2,1,0:T(8,128)S(1)}, f32[2,4,12,128,416]{3,4,2,1,0:T(8,128)}) fusion(pred[2,4,128,416]{2,3,1,0:T(8,128)(4,1)} %pad_add_fusion, bf16[2,4,416,12,64]{2,4,3,1,0:T(8,128)(2,1)} %bitcast.444, bf16[2,4,128,12,64]{2,1,0,4,3:T(4,128)(2,1)S(1)} %reshape_reshape.3), kind=kOutput, calls=%fused_computation.485 | convolution fusion | flops 674759040 | bytes 27607040 | tf_op jit(solution)/shard_map/sub | solution.py:277
  336.3 15.4 %broadcast_divide_fusion = f32[2,4,12,128,416]{3,4,2,1,0:T(8,128)} fusion(f32[2,4,12,128,416]{3,4,2,1,0:T(8,128)} %get-tuple-element.182, f32[2,4,12,128]{3,2,1,0:T(8,128)S(1)} %get-tuple-element.181), kind=kLoop, calls=%fused_computation.111 | loop fusion | flops 5111808 | bytes 40943616 | tf_op jit(solution)/shard_map/div | solution.py:279
  351.7 10.0 fusion.58
  392.3 14.1 %fusion.151 = (bf16[768,8,384]{2,1,0:T(8,128)(2,1)}, bf16[768,8,384]{2,1,0:T(8,128)(2,1)}) fusion(bf16[768,8,864]{2,1,0:T(8,128)(2,1)} %all-gather.13.cloned.1.call-done), kind=kLoop, calls=%fused_computation.473 | loop fusion | bytes 18874368 | tf_op jit(solution)/shard_map/slice | solution.py:107
  411.3 34.8 %multiply_convert_fusion = (bf16[1024,3072]{1,0:T(8,128)(2,1)S(1)}, f32[1024,3072]{1,0:T(8,128)}, f32[1024,3072]{1,0:T(8,128)}) fusion(bf16[768,3072]{1,0:T(8,128)(2,1)S(1)} %bitcast.445, f32[1024,768]{1,0:T(8,128)S(1)} %get-tuple-element.184, f32[768]{0:T(1024)S(1)} %copy-done.58, f32[768]{0:T(1024)S(1)} %copy-done.48, f32[1024]{0:T(1024)S(1)} %fusion.128, ...), kind=kOutput, calls=%fused_computation.84 | convolution fusion | flops 5040242688 | bytes 39335936 | tf_op jit(solution)/shard_map/dot_general | solution.py:78
  457.0 18.6 %add_convert_fusion = bf16[1024,3072]{1,0:T(8,128)(2,1)} fusion(f32[1024,3072]{1,0:T(8,128)} %get-tuple-element.60, f32[1024,3072]{1,0:T(8,128)} %get-tuple-element.185, bf16[768,3072]{1,0:T(8,128)(2,1)} %bitcast.448, f32[1024,768]{1,0:T(8,128)} %get-tuple-element.58, f32[1024]{0:T(1024)S(1)} %negate_multiply_fusion.2), kind=kOutput, calls=%fused_computation.83 | convolution fusion | flops 4877451264 | bytes 39325696 | tf_op jit(solution)/shard_map/dot_general | solution.py:88
  475.6 9.2 multiply_reduce_fusion.4
  526.6 9.4 fusion.22
  554.1 17.6 %fusion.11 = (f32[4,12,128]{2,1,0:T(8,128)S(1)}, f32[4,12,128]{2,1,0:T(8,128)S(1)}, f32[4,12,128,416]{2,3,1,0:T(8,128)}) fusion(f32[2,4,12,128,416]{3,4,2,1,0:T(8,128)} %broadcast_divide_fusion, f32[4,12,128,416]{2,3,1,0:T(8,128)} %fusion.79, bf16[4,416,12,64]{1,3,2,0:T(8,128)(2,1)} %bitcast.435, bf16[4,128,12,64]{1,0,3,2:T(4,128)(2,1)} %copy-done.18), kind=kOutput, calls=%fused_computation.108 | convolution fusion | flops 337367040 | bytes 44285952 | tf_op jit(solution)/shard_map/gbqhd,gbkhd->gbhqk/dot_general | solution.py:296
  571.7 16.8 %fusion.27 = (bf16[4,12,128,416]{2,3,1,0:T(8,128)(2,1)S(1)}, bf16[4,12,128,416]{2,3,1,0:T(8,128)(2,1)}) fusion(f32[4,12,128,416]{2,3,1,0:T(8,128)} %get-tuple-element.189, f32[2,4,12,128,416]{3,4,2,1,0:T(8,128)} %broadcast_divide_fusion, f32[4,12,128]{2,1,0:T(8,128)S(1)} %get-tuple-element.41, f32[4,12,128,416]{2,3,1,0:T(8,128)} %fusion.79, ...), kind=kLoop, calls=%fused_computation.137 | loop fusion | flops 15335424 | bytes 51167232 | tf_op jit(solution)/shard_map/reshape.161
  675.8 9.0 fusion.33
  701.4 9.1 fusion.25
  801.1 18.5 %reduce-scatter.13.cloned.1.call-done = bf16[192,8,864]{2,0,1:T(8,128)(2,1)} async-done(((bf16[768,8,864]{2,0,1:T(8,128)(2,1)}), bf16[192,8,864]{2,0,1:T(8,128)(2,1)}) %reduce-scatter.13.cloned.1.call-update) | async-done | bytes 2654224 | tf_op jit(solution)/shard_map/reduce_scatter | solution.py:129
  845.1 10.8 fusion.30
  860.5 8.7 copy.227
  875.0 8.7 copy.228
  883.7 9.3 convolution_convert_fusion.7
  918.1 31.3 %reduce-scatter.19.cloned.1.call-done = bf16[192,2304]{1,0:T(8,128)(2,1)} async-done(((bf16[768,2304]{1,0:T(8,128)(2,1)}), bf16[192,2304]{1,0:T(8,128)(2,1)}) %reduce-scatter.19.cloned.1.call-update) | async-done | bytes 884752
  964.2 10.7 multiply_reduce_fusion.1
  981.8 40.6 %all-reduce.3 = (f32[2,4,768]{2,1,0:T(4,128)S(1)}, f32[2,768]{1,0:T(2,128)S(1)}, f32[2,768]{1,0:T(2,128)S(1)}) all-reduce(f32[2,4,768]{2,1,0:T(4,128)S(1)} %pad_maximum_fusion.8, f32[2,768]{1,0:T(2,128)S(1)} %pad_maximum_fusion.9, f32[2,768]{1,0:T(2,128)S(1)} %pad_maximum_fusion.10), channel_id=9, replica_groups=mesh['dp'=8,'seq'=4] {'dp','seq'}, use_global_device_ids=true, to_apply=%region_24.25.clone | all-reduce | flops 9216 | bytes 73728
  1030.5 43.4 %reduce-scatter.17.cloned.1.call-done = bf16[192,1,1152]{2,0,1:T(8,128)(2,1)} async-done(((bf16[192,8,1152]{2,0,1:T(8,128)(2,1)}), bf16[192,1,1152]{2,0,1:T(8,128)(2,1)}) %reduce-scatter.17.cloned.1.call-update) | async-done | bytes 442384 | tf_op jit(solution)/shard_map/reduce_scatter | solution.py:135
  (466 shorter events, 470.0 us)
Async XLA Ops:
  7.2 85.0 %copy-start.62 = (s32[2,8]{1,0:T(2,128)S(1)}, s32[2,8]{1,0:T(2,128)}, u32[]{:S(2)}) copy-start(s32[2,8]{1,0:T(2,128)} %param.22) | copy-start | bytes 196
  7.2 83.0 %all-gather.9.cloned.1.call-start = ((), (), s32[]{:S(2)}) async-start(), calls=%async_computation.5 | async-start | bytes 7864320 | tf_op jit(solution)/shard_map/all_gather | solution.py:373
  7.9 118.4 %all-gather.11.cloned.1.call-start = ((), (), s32[]{:S(2)}) async-start(), calls=%async_computation.6 | async-start | bytes 5898240 | tf_op jit(solution)/shard_map/all_gather | solution.py:101
  92.1 116.0 %all-gather.15.cloned.1.call-start = ((), (), s32[]{:S(2)}) async-start(), calls=%async_computation.12 | async-start | bytes 3096576 | tf_op jit(solution)/shard_map/all_gather | solution.py:99
  92.4 34.0 %copy-start.50 = (s32[2,8]{1,0:T(2,128)}, s32[2,8]{1,0:T(2,128)S(1)}, u32[]{:S(2)}) copy-start(s32[2,8]{1,0:T(2,128)S(1)} %copy.193) | copy-start | bytes 196
  93.0 33.4 %copy-start.61 = (pred[4]{0:T(512)(128)(4,1)}, pred[4]{0:T(512)(128)(4,1)S(1)}, u32[]{:S(2)}) copy-start(pred[4]{0:T(512)(128)(4,1)S(1)} %broadcast_compare_fusion.2) | copy-start | bytes 16
  99.3 27.0 %copy-start.56 = (pred[4,128]{1,0:T(4,128)(4,1)}, pred[4,128]{1,0:T(4,128)(4,1)S(1)}, u32[]{:S(2)}) copy-start(pred[4,128]{1,0:T(4,128)(4,1)S(1)} %get-tuple-element.171) | copy-start | bytes 1540
  99.3 27.0 %copy-start.57 = (pred[4,128]{1,0:T(4,128)(4,1)}, pred[4,128]{1,0:T(4,128)(4,1)S(1)}, u32[]{:S(2)}) copy-start(pred[4,128]{1,0:T(4,128)(4,1)S(1)} %get-tuple-element.172) | copy-start | bytes 1540
  136.7 61.5 %copy-start.36 = (bf16[768,8,96]{0,2,1:T(8,128)(2,1)S(1)}, bf16[768,8,96]{0,2,1:T(8,128)(2,1)}, u32[]{:S(2)}) copy-start(bf16[768,8,96]{0,2,1:T(8,128)(2,1)} %copy.242) | copy-start | bytes 3538948
  140.4 244.1 %all-gather.13.cloned.1.call-start = ((), (), s32[]{:S(2)}) async-start(), calls=%async_computation.7 | async-start | bytes 13762560 | tf_op jit(solution)/shard_map/all_gather | solution.py:101
  198.2 59.2 %copy-start.40 = (f32[4,768]{1,0:T(4,128)}, f32[4,768]{1,0:T(4,128)S(1)}, u32[]{:S(2)}) copy-start(f32[4,768]{1,0:T(4,128)S(1)} %get-tuple-element.143) | copy-start | bytes 36868
  198.2 59.2 %copy-start.42 = (f32[4,768]{1,0:T(4,128)}, f32[4,768]{1,0:T(4,128)S(1)}, u32[]{:S(2)}) copy-start(f32[4,768]{1,0:T(4,128)S(1)} %get-tuple-element.144) | copy-start | bytes 36868
  222.3 578.8 %reduce-scatter.11.cloned.1.call-start = ((), (), s32[]{:S(2)}) async-start(), calls=%async_computation.8 | async-start | bytes 3932160 | tf_op jit(solution)/shard_map/reduce_scatter | solution.py:452
  313.7 9.3 copy-start.20
  336.3 15.5 %copy-start.5 = (bf16[2,4,416,768]{2,3,1,0:T(8,128)(2,1)S(1)}, bf16[2,4,416,768]{2,3,1,0:T(8,128)(2,1)}, u32[]{:S(2)}) copy-start(bf16[2,4,416,768]{2,3,1,0:T(8,128)(2,1)} %copy.190) | copy-start | bytes 15335428
  411.3 34.8 %copy-start.24 = (bf16[96,8,8,384]{3,1,2,0:T(8,128)(2,1)}, bf16[96,8,8,384]{3,1,2,0:T(8,128)(2,1)S(1)}, u32[]{:S(2)}) copy-start(bf16[96,8,8,384]{3,1,2,0:T(8,128)(2,1)S(1)} %copy.249) | copy-start | bytes 14155780
  489.0 9.2 slice-start.19
  526.6 9.4 copy-start.18
  535.9 11.5 %copy-start.6 = (bf16[1,4,416,768]{2,3,1,0:T(8,128)(2,1)S(1)}, bf16[1,4,416,768]{2,3,1,0:T(8,128)(2,1)}, u32[]{:S(2)}) copy-start(bf16[1,4,416,768]{2,3,1,0:T(8,128)(2,1)} %copy.216) | copy-start | bytes 7667716
  571.7 16.8 %copy-start.22 = (bf16[4,128,12,64]{1,0,3,2:T(4,128)(2,1)S(1)}, bf16[4,128,12,64]{1,0,3,2:T(4,128)(2,1)}, u32[]{:S(2)}) copy-start(bf16[4,128,12,64]{1,0,3,2:T(4,128)(2,1)} %reshape.1154) | copy-start | bytes 2359300
  691.5 128.1 %reduce-scatter.13.cloned.1.call-start = ((), (), s32[]{:S(2)}) async-start(), calls=%async_computation.9 | async-start | bytes 13762560 | tf_op jit(solution)/shard_map/reduce_scatter | solution.py:129
  692.1 257.3 %reduce-scatter.19.cloned.1.call-start = ((), (), s32[]{:S(2)}) async-start(), calls=%async_computation.13 | async-start | bytes 4423680
  801.1 19.8 %copy-start.44 = (f32[4,768]{1,0:T(4,128)S(1)}, f32[4,768]{1,0:T(4,128)}, u32[]{:S(2)}) copy-start(f32[4,768]{1,0:T(4,128)} %copy-done.42) | copy-start | bytes 36868
  845.1 12.4 %copy-start.13 = (bf16[2048,768]{1,0:T(8,128)(2,1)S(1)}, bf16[2048,768]{1,0:T(8,128)(2,1)}, u32[]{:S(2)}) copy-start(bf16[2048,768]{1,0:T(8,128)(2,1)} %copy-done.12) | copy-start | bytes 9437188
  883.7 9.3 copy-start.19
  908.9 115.5 %reduce-scatter.15.cloned.1.call-start = ((), (), s32[]{:S(2)}) async-start(), calls=%async_computation.10 | async-start | bytes 3932160 | tf_op jit(solution)/shard_map/reduce_scatter | solution.py:452
  918.0 155.9 %reduce-scatter.17.cloned.1.call-start = ((), (), s32[]{:S(2)}) async-start(), calls=%async_computation.11 | async-start | bytes 3981312 | tf_op jit(solution)/shard_map/reduce_scatter | solution.py:135
  961.4 13.5 %slice-start.6 = ((s8[12582912]{0:T(1024)(128)(4,1)}), s8[4194304]{0:T(1024)(128)(4,1)S(1)}, s32[]{:S(2)}) async-start(s8[12582912]{0:T(1024)(128)(4,1)} %bitcast.408), calls=%async_computation.20 | async-start | bytes 8388608
  961.4 13.5 %slice-start.7 = ((s8[12582912]{0:T(1024)(128)(4,1)}), s8[4194304]{0:T(1024)(128)(4,1)S(1)}, s32[]{:S(2)}) async-start(s8[12582912]{0:T(1024)(128)(4,1)} %bitcast.408), calls=%async_computation.21 | async-start | bytes 8388608
  964.2 10.7 slice-start.8
  974.9 51.0 %copy-start.10 = (f32[1024,768]{1,0:T(8,128)S(1)}, f32[1024,768]{1,0:T(8,128)}, u32[]{:S(2)}) copy-start(f32[1024,768]{1,0:T(8,128)} %copy-done.9) | copy-start | bytes 9437188
  974.9 51.0 %copy-start.53 = (f32[1024]{0:T(1024)S(1)}, f32[1024]{0:T(1024)}, u32[]{:S(2)}) copy-start(f32[1024]{0:T(1024)} %copy-done.52) | copy-start | bytes 12292
  (62 other events, 306.0 us)
Sparse Core Ops, SparseCore 0:
  9.6 51.2 all-gather.8
  92.2 34.0 all-gather.10
  140.5 56.0 all-gather.14
  222.5 73.1 all-gather.12
  691.6 37.9 reduce-scatter.10
  732.0 87.5 reduce-scatter.12
  909.0 40.3 reduce-scatter.18
  951.9 38.0 reduce-scatter.14
  993.7 80.1 reduce-scatter.16

commit v9 on v8

--- a/solution.py
+++ b/solution.py
@@ -128,6 +128,12 @@
     stacked, tie = lax.optimization_barrier((stacked, tie))
     reduced = lax.psum_scatter(stacked, "seq", scatter_dimension=0, tiled=True)
     return (reduced, [c.shape[2] for c in chunks]), tie
+
+
+def stack_for_seq(grads):
+    dp_size = lax.psum(1, "dp")
+    chunks = [grad.reshape(grad.shape[0], dp_size, grad.shape[1] // dp_size) for grad in grads]
+    return jnp.concatenate(chunks, axis=2).astype(jnp.bfloat16), [c.shape[2] for c in chunks]
 
 
 def reduce_dp_stage(stages):
@@ -449,14 +455,17 @@
         ).astype(jnp.bfloat16).reshape(group_len, width)
         back_g = product_right(key_partial_g, wk) + product_right(value_partial_g, wv)
         back_g = back_g.reshape(1, group_len, width).astype(jnp.bfloat16)
-        back_own_g = lax.psum_scatter(back_g, "seq", scatter_dimension=1, tiled=True)
+        if g == groups - 1:
+            back_own_g = back_g
+        else:
+            back_own_g = lax.psum_scatter(back_g, "seq", scatter_dimension=1, tiled=True)
         pieces_back.append((grad_queries_g, pooled_g, key_partial_g, value_partial_g, back_own_g))
     grad_queries = jnp.concatenate([piece[0] for piece in pieces_back], axis=0)
     grad_pooled = jnp.concatenate([piece[1] for piece in pieces_back], axis=0)
     key_partial = jnp.concatenate([piece[2] for piece in pieces_back], axis=0)
     value_partial = jnp.concatenate([piece[3] for piece in pieces_back], axis=0)
-    back_own = jnp.concatenate([piece[4] for piece in pieces_back], axis=0)
-    early = (early_reduced, early_widths)
+    last_back = pieces_back[-1][4]
+    early_dp = reduce_dp_stage(((early_reduced, early_widths),))
     grad_pooling = jnp.stack(
         [
             pool_grad_grouped(grad_pooled[..., :width], key_g),
@@ -466,14 +475,27 @@
     grad_query_w = product_left(tokens, grad_queries)
     grad_key_w = product_left(all_tokens, key_partial)
     grad_value_w = product_left(all_tokens, value_partial)
+    late_stacked, late_widths = stack_for_seq((grad_query_w, grad_key_w, grad_value_w))
+    late_stacked, early_dp = lax.optimization_barrier((late_stacked, early_dp))
+    seq_size = lax.psum(1, "seq")
+    late_flat = late_stacked.reshape(seq_size, -1, width)
+    back_flat = last_back.reshape(seq_size, -1, width)
+    joined = jnp.concatenate([late_flat, back_flat], axis=1)
+    chunk_rows = joined.shape[1]
+    joined = joined.reshape(seq_size * chunk_rows, width)
+    joined = lax.psum_scatter(joined, "seq", scatter_dimension=0, tiled=True)
+    late_reduced = joined[: late_flat.shape[1]].reshape(
+        late_stacked.shape[0] // seq_size, late_stacked.shape[1], late_stacked.shape[2]
+    )
+    back_last = joined[late_flat.shape[1] :].reshape(1, shard_rows, width)
+    back_own = jnp.concatenate([piece[4] for piece in pieces_back[:-1]] + [back_last], axis=0)
     grad_tokens = (
         grad_mixed
         + product_right(grad_queries, wq)
         + back_own.reshape(groups * shard_rows, width).astype(jnp.float32)
     )
-    late, _ = reduce_seq_stage((grad_query_w, grad_key_w, grad_value_w))
-    pieces = reduce_dp_stage((early, late))
-    accum = (pieces[3], pieces[4], pieces[5], pieces[0], pieces[1], pieces[2].T)
+    late_dp = reduce_dp_stage(((late_reduced, late_widths),))
+    accum = (late_dp[0], late_dp[1], late_dp[2], early_dp[0], early_dp[1], early_dp[2].T)
     small_sums = (
         lax.psum_scatter(grad_pooling, ("dp", "seq"), scatter_dimension=2, tiled=True),
         lax.psum_scatter(

time: 1090 us -> 1090 us (level)
  waiting for transfers between devices: 121 us -> 101 us
  local copies, waits for them, and re-layouts: 323 us -> 337 us
    reduce_scatter x0 -> x1, waiting for transfers between devices: none -> 44.4 us  [local(): joined = lax.psum_scatter(joined, 'seq', scatter_dimension=0, tiled=True)]
    reduce_scatter x1 -> x2, waiting for transfers between devices: 43.4 us -> 10.7 us  [reduce_dp_stage(): lax.psum_scatter(joined, 'dp', scatter_dimension=1, tiled=True)[:, 0]]
    unnamed x10 -> x9, waiting for transfers between devices: 32.6 us -> 1.32 us
    reshape x0 -> x4, local copies, waits for them, and re-layouts: none -> 14.5 us  [the longest x1 10.2 us: local(): late_flat = late_stacked.reshape(seq_size, -1, width)]
    unnamed x190 -> x186, local copies, waits for them, and re-layouts: 53.9 us -> 46.8 us
  transfers between devices with their start and end apart: 9 -> 9, of which waited for: 4 -> 5; matrix products, arithmetic and copies ran while one was open for 32% -> 36% of each run, Pallas kernels for 0% -> 0%
where the time goes in v9:
time: 1090 us; the launch traced here: 1080 us
  local copies, waits for them, and re-layouts  337 us (31%)
  matrix products  242 us (22%)
  other arithmetic  221 us (20%)
  blocking collectives  119 us (11%)
  waiting for transfers between devices  101 us (9%)
  between operations  60.7 us (6%)
    dot_general x6, matrix products, product(): return jnp.dot(left, right, preferred_element_type=jnp.float32)  66.3 us
    dot_general x8, matrix products, product_right(): lax.dot_general(left, right, (((1,), (1,)), ((), ())), preferred_element_...  48.3 us
    unnamed x186, local copies, waits for them, and re-layouts  46.8 us
    all_gather x1, blocking collectives, local(): small_full = lax.all_gather(small_local, ('dp', 'seq'), axis=1, tiled=True)  44.7 us
    reduce_scatter x1, waiting for transfers between devices, local(): joined = lax.psum_scatter(joined, 'seq', scatter_dimension=0, tiled=True)  44.4 us
    dot_general x6, matrix products, product_left(): lax.dot_general(left, right, (((0,), (0,)), ((), ())), preferred_element_...  40.3 us
    unnamed x1, blocking collectives  40.2 us
    dynamic_update_slice x32, local copies, waits for them, and re-layouts, window_add(): lax.dynamic_update_slice_in_dim(row, current + updates[g, b], start, 0)  37.3 us
  transfers between devices with their start and end apart: 9, of which 5 were waited for; matrix products, arithmetic and copies ran while one was open for 36% of the time, Pallas kernels for 0%

profile of v9, /device:TPU:0, one launch (start us, length us, event | category | flops | bytes accessed | tf_op | source)
XLA Modules:
  0.0 1081.4 jit_solution(17523004282439201753)
XLA Ops:
  11.4 44.7 %all-gather.2 = f32[32,24,12]{1,2,0:T(8,128)S(1)} all-gather(f32[1,24,12]{1,2,0:T(8,128)S(1)} %maximum_bitcast_fusion.11), channel_id=1, replica_groups=mesh['dp'=8,'seq'=4] {'dp','seq'}, dimensions={0}, use_global_device_ids=true | all-gather | bytes 38016 | tf_op jit(solution)/shard_map/all_gather | solution.py:378
  56.3 33.9 %all-gather = bf16[192,2304]{0,1:T(8,128)(2,1)S(1)} all-gather(bf16[192,288]{0,1:T(8,128)(2,1)S(1)} %pad_maximum_fusion.7), channel_id=2, replica_groups=mesh['dp'=8,'seq'=4] {'dp'}, dimensions={1}, use_global_device_ids=true | all-gather | bytes 995328 | tf_op jit(solution)/shard_map/all_gather | solution.py:99
  100.1 26.2 %all-gather.11.cloned.1.call-done = bf16[768,8,288]{2,1,0:T(8,128)(2,1)} async-done(((bf16[192,8,288]{2,1,0:T(8,128)(2,1)}), bf16[768,8,288]{2,1,0:T(8,128)(2,1)}) %all-gather.11.cloned.1.call-update) | async-done | bytes 3538960 | tf_op jit(solution)/shard_map/all_gather | solution.py:101
  198.3 9.7 convolution_convert_fusion.1
  223.0 9.9 convolution_convert_fusion
  232.9 12.5 %reshape.1191 = f32[2,512,4,768]{3,2,1,0:T(4,128)} reshape(bf16[4096,768]{1,0:T(8,128)(2,1)} %convolution_convert_fusion.1) | data formatting | bytes 18874368 | tf_op jit(solution)/shard_map/convert_element_type | solution.py:397
  245.5 12.3 %reshape.1192 = f32[2,512,4,768]{3,2,1,0:T(4,128)} reshape(bf16[4096,768]{1,0:T(8,128)(2,1)} %convolution_convert_fusion) | data formatting | bytes 18874368 | tf_op jit(solution)/shard_map/convert_element_type | solution.py:398
  257.8 19.6 %multiply_reduce_fusion.2 = (bf16[2,512,768]{2,1,0:T(8,128)(2,1)S(1)}, bf16[2,512,768]{2,1,0:T(8,128)(2,1)S(1)}) fusion(f32[2,512,4,768]{3,2,1,0:T(4,128)} %reshape.1192, f32[4,768]{1,0:T(4,128)S(1)} %get-tuple-element.150, f32[2,512,4,768]{3,2,1,0:T(4,128)} %reshape.1191, f32[4,768]{1,0:T(4,128)S(1)} %get-tuple-element.151), kind=kLoop, calls=%fused_computation.97 | loop fusion | flops 11010048 | bytes 28336128 | tf_op jit(solution)/shard_map/reduce_sum | solution.py:344
  294.4 8.5 fusion.152
  323.0 13.3 %fusion.163 = (f32[2,4,12,128]{3,2,1,0:T(8,128)S(1)}, f32[2,4,12,128,416]{3,4,2,1,0:T(8,128)}) fusion(pred[2,4,128,416]{2,3,1,0:T(8,128)(4,1)} %pad_add_fusion, bf16[2,4,416,12,64]{2,4,3,1,0:T(8,128)(2,1)} %bitcast.443, bf16[2,4,128,12,64]{2,1,0,4,3:T(4,128)(2,1)S(1)} %reshape_reshape.3), kind=kOutput, calls=%fused_computation.486 | convolution fusion | flops 674759040 | bytes 27607040 | tf_op jit(solution)/shard_map/sub | solution.py:283
  336.4 15.5 %broadcast_divide_fusion = f32[2,4,12,128,416]{3,4,2,1,0:T(8,128)} fusion(f32[2,4,12,128,416]{3,4,2,1,0:T(8,128)} %get-tuple-element.189, f32[2,4,12,128]{3,2,1,0:T(8,128)S(1)} %get-tuple-element.188), kind=kLoop, calls=%fused_computation.111 | loop fusion | flops 5111808 | bytes 40943616 | tf_op jit(solution)/shard_map/div | solution.py:285
  351.8 10.0 fusion.57
  392.5 14.1 %fusion.150 = (bf16[768,8,384]{2,1,0:T(8,128)(2,1)}, bf16[768,8,384]{2,1,0:T(8,128)(2,1)}) fusion(bf16[768,8,864]{2,1,0:T(8,128)(2,1)} %all-gather.13.cloned.1.call-done), kind=kLoop, calls=%fused_computation.473 | loop fusion | bytes 18874368 | tf_op jit(solution)/shard_map/slice | solution.py:107
  411.5 34.8 %multiply_convert_fusion = (bf16[1024,3072]{1,0:T(8,128)(2,1)S(1)}, f32[1024,3072]{1,0:T(8,128)}, f32[1024,3072]{1,0:T(8,128)}) fusion(bf16[768,3072]{1,0:T(8,128)(2,1)S(1)} %bitcast.444, f32[1024,768]{1,0:T(8,128)S(1)} %get-tuple-element.191, f32[768]{0:T(1024)S(1)} %copy-done.60, f32[768]{0:T(1024)S(1)} %copy-done.50, f32[1024]{0:T(1024)S(1)} %fusion.127, ...), kind=kOutput, calls=%fused_computation.84 | convolution fusion | flops 5040242688 | bytes 39335936 | tf_op jit(solution)/shard_map/dot_general | solution.py:78
  457.2 18.6 %add_convert_fusion = bf16[1024,3072]{1,0:T(8,128)(2,1)} fusion(f32[1024,3072]{1,0:T(8,128)} %get-tuple-element.68, f32[1024,3072]{1,0:T(8,128)} %get-tuple-element.192, bf16[768,3072]{1,0:T(8,128)(2,1)} %bitcast.447, f32[1024,768]{1,0:T(8,128)} %get-tuple-element.66, f32[1024]{0:T(1024)S(1)} %negate_multiply_fusion.2), kind=kOutput, calls=%fused_computation.83 | convolution fusion | flops 4877451264 | bytes 39325696 | tf_op jit(solution)/shard_map/dot_general | solution.py:88
  475.8 9.2 multiply_reduce_fusion.4
  526.7 9.3 fusion.22
  554.2 17.6 %fusion.11 = (f32[4,12,128]{2,1,0:T(8,128)S(1)}, f32[4,12,128]{2,1,0:T(8,128)S(1)}, f32[4,12,128,416]{2,3,1,0:T(8,128)}) fusion(f32[2,4,12,128,416]{3,4,2,1,0:T(8,128)} %broadcast_divide_fusion, f32[4,12,128,416]{2,3,1,0:T(8,128)} %fusion.78, bf16[4,416,12,64]{1,3,2,0:T(8,128)(2,1)} %bitcast.434, bf16[4,128,12,64]{1,0,3,2:T(4,128)(2,1)} %copy-done.19), kind=kOutput, calls=%fused_computation.108 | convolution fusion | flops 337367040 | bytes 44285952 | tf_op jit(solution)/shard_map/gbqhd,gbkhd->gbhqk/dot_general | solution.py:302
  571.8 16.8 %fusion.27 = (bf16[4,12,128,416]{2,3,1,0:T(8,128)(2,1)S(1)}, bf16[4,12,128,416]{2,3,1,0:T(8,128)(2,1)}) fusion(f32[4,12,128,416]{2,3,1,0:T(8,128)} %get-tuple-element.196, f32[2,4,12,128,416]{3,4,2,1,0:T(8,128)} %broadcast_divide_fusion, f32[4,12,128]{2,1,0:T(8,128)S(1)} %get-tuple-element.49, f32[4,12,128,416]{2,3,1,0:T(8,128)} %fusion.78, ...), kind=kLoop, calls=%fused_computation.138 | loop fusion | flops 15335424 | bytes 51167232 | tf_op jit(solution)/shard_map/reshape.166
  676.0 9.0 fusion.33
  701.6 9.1 fusion.25
  801.4 18.5 %reduce-scatter.11.cloned.1.call-done = bf16[192,8,864]{2,0,1:T(8,128)(2,1)} async-done(((bf16[768,8,864]{2,0,1:T(8,128)(2,1)}), bf16[192,8,864]{2,0,1:T(8,128)(2,1)}) %reduce-scatter.11.cloned.1.call-update) | async-done | bytes 2654224 | tf_op jit(solution)/shard_map/reduce_scatter | solution.py:129
  845.5 11.1 %fusion.30 = (bf16[2048,768]{1,0:T(8,128)(2,1)}, bf16[2048,768]{1,0:T(8,128)(2,1)S(1)}) fusion(f32[1,2048,768]{2,1,0:T(8,128)} %mul.498, f32[1,2048,1536]{2,1,0:T(8,128)} %dynamic_update_slice.124, f32[1,2048,768]{2,1,0:T(8,128)} %mul.494), kind=kLoop, calls=%fused_computation.154 | loop fusion | flops 6291456 | bytes 31457280 | tf_op jit(solution)/shard_map/reshape | solution.py:455
  861.3 8.7 copy.230
  875.9 8.7 copy.231
  884.6 9.2 convolution_convert_fusion.7
  893.9 8.1 convolution_convert_fusion.6
  926.7 10.2 reshape.1181
  949.2 10.1 multiply_reduce_fusion.1
  959.2 44.4 %reduce-scatter.15.cloned.1.call-done = bf16[1088,768]{1,0:T(8,128)(2,1)} async-done(((bf16[4352,768]{1,0:T(8,128)(2,1)}), bf16[1088,768]{1,0:T(8,128)(2,1)}) %reduce-scatter.15.cloned.1.call-update) | async-done | bytes 1671184 | tf_op jit(solution)/shard_map/reduce_scatter | solution.py:486
  1008.0 9.9 multiply_reduce_fusion
  1017.9 40.2 %all-reduce.3 = (f32[2,4,768]{2,1,0:T(4,128)S(1)}, f32[2,768]{1,0:T(2,128)S(1)}, f32[2,768]{1,0:T(2,128)S(1)}) all-reduce(f32[2,4,768]{2,1,0:T(4,128)S(1)} %pad_maximum_fusion.8, f32[2,768]{1,0:T(2,128)S(1)} %pad_maximum_fusion.9, f32[2,768]{1,0:T(2,128)S(1)} %pad_maximum_fusion.10), channel_id=9, replica_groups=mesh['dp'=8,'seq'=4] {'dp','seq'}, use_global_device_ids=true, to_apply=%region_24.25.clone | all-reduce | flops 9216 | bytes 73728
  (468 shorter events, 486.8 us)
Async XLA Ops:
  7.2 85.0 %copy-start.64 = (s32[2,8]{1,0:T(2,128)S(1)}, s32[2,8]{1,0:T(2,128)}, u32[]{:S(2)}) copy-start(s32[2,8]{1,0:T(2,128)} %param.22) | copy-start | bytes 196
  7.2 83.0 %all-gather.9.cloned.1.call-start = ((), (), s32[]{:S(2)}) async-start(), calls=%async_computation.5 | async-start | bytes 7864320 | tf_op jit(solution)/shard_map/all_gather | solution.py:379
  7.9 118.4 %all-gather.11.cloned.1.call-start = ((), (), s32[]{:S(2)}) async-start(), calls=%async_computation.6 | async-start | bytes 5898240 | tf_op jit(solution)/shard_map/all_gather | solution.py:101
  92.1 116.0 %all-gather.15.cloned.1.call-start = ((), (), s32[]{:S(2)}) async-start(), calls=%async_computation.13 | async-start | bytes 3096576 | tf_op jit(solution)/shard_map/all_gather | solution.py:99
  92.4 34.0 %copy-start.52 = (s32[2,8]{1,0:T(2,128)}, s32[2,8]{1,0:T(2,128)S(1)}, u32[]{:S(2)}) copy-start(s32[2,8]{1,0:T(2,128)S(1)} %copy.196) | copy-start | bytes 196
  93.0 33.4 %copy-start.63 = (pred[4]{0:T(512)(128)(4,1)}, pred[4]{0:T(512)(128)(4,1)S(1)}, u32[]{:S(2)}) copy-start(pred[4]{0:T(512)(128)(4,1)S(1)} %broadcast_compare_fusion.2) | copy-start | bytes 16
  99.4 27.0 %copy-start.58 = (pred[4,128]{1,0:T(4,128)(4,1)}, pred[4,128]{1,0:T(4,128)(4,1)S(1)}, u32[]{:S(2)}) copy-start(pred[4,128]{1,0:T(4,128)(4,1)S(1)} %get-tuple-element.178) | copy-start | bytes 1540
  99.4 27.0 %copy-start.59 = (pred[4,128]{1,0:T(4,128)(4,1)}, pred[4,128]{1,0:T(4,128)(4,1)S(1)}, u32[]{:S(2)}) copy-start(pred[4,128]{1,0:T(4,128)(4,1)S(1)} %get-tuple-element.179) | copy-start | bytes 1540
  136.7 61.6 %copy-start.37 = (bf16[768,8,96]{0,2,1:T(8,128)(2,1)S(1)}, bf16[768,8,96]{0,2,1:T(8,128)(2,1)}, u32[]{:S(2)}) copy-start(bf16[768,8,96]{0,2,1:T(8,128)(2,1)} %copy.242) | copy-start | bytes 3538948
  140.3 244.3 %all-gather.13.cloned.1.call-start = ((), (), s32[]{:S(2)}) async-start(), calls=%async_computation.7 | async-start | bytes 13762560 | tf_op jit(solution)/shard_map/all_gather | solution.py:101
  198.3 59.5 %copy-start.42 = (f32[4,768]{1,0:T(4,128)}, f32[4,768]{1,0:T(4,128)S(1)}, u32[]{:S(2)}) copy-start(f32[4,768]{1,0:T(4,128)S(1)} %get-tuple-element.150) | copy-start | bytes 36868
  198.3 59.5 %copy-start.44 = (f32[4,768]{1,0:T(4,128)}, f32[4,768]{1,0:T(4,128)S(1)}, u32[]{:S(2)}) copy-start(f32[4,768]{1,0:T(4,128)S(1)} %get-tuple-element.151) | copy-start | bytes 36868
  222.4 579.0 %reduce-scatter.9.cloned.1.call-start = ((), (), s32[]{:S(2)}) async-start(), calls=%async_computation.8 | async-start | bytes 3932160 | tf_op jit(solution)/shard_map/reduce_scatter | solution.py:461
  313.7 9.3 copy-start.21
  336.4 15.5 %copy-start.5 = (bf16[2,4,416,768]{2,3,1,0:T(8,128)(2,1)S(1)}, bf16[2,4,416,768]{2,3,1,0:T(8,128)(2,1)}, u32[]{:S(2)}) copy-start(bf16[2,4,416,768]{2,3,1,0:T(8,128)(2,1)} %copy.193) | copy-start | bytes 15335428
  411.5 34.9 %copy-start.25 = (bf16[96,8,8,384]{3,1,2,0:T(8,128)(2,1)}, bf16[96,8,8,384]{3,1,2,0:T(8,128)(2,1)S(1)}, u32[]{:S(2)}) copy-start(bf16[96,8,8,384]{3,1,2,0:T(8,128)(2,1)S(1)} %copy.249) | copy-start | bytes 14155780
  489.1 9.3 slice-start.16
  498.4 8.9 copy-start.31
  526.7 9.4 copy-start.19
  536.1 11.5 %copy-start.6 = (bf16[1,4,416,768]{2,3,1,0:T(8,128)(2,1)S(1)}, bf16[1,4,416,768]{2,3,1,0:T(8,128)(2,1)}, u32[]{:S(2)}) copy-start(bf16[1,4,416,768]{2,3,1,0:T(8,128)(2,1)} %copy.219) | copy-start | bytes 7667716
  571.8 16.8 %copy-start.23 = (bf16[4,128,12,64]{1,0,3,2:T(4,128)(2,1)S(1)}, bf16[4,128,12,64]{1,0,3,2:T(4,128)(2,1)}, u32[]{:S(2)}) copy-start(bf16[4,128,12,64]{1,0,3,2:T(4,128)(2,1)} %reshape.1172) | copy-start | bytes 2359300
  593.7 8.6 slice-start.2
  676.0 9.0 copy-start.38
  691.7 128.2 %reduce-scatter.11.cloned.1.call-start = ((), (), s32[]{:S(2)}) async-start(), calls=%async_computation.9 | async-start | bytes 13762560 | tf_op jit(solution)/shard_map/reduce_scatter | solution.py:129
  692.3 225.0 %reduce-scatter.13.cloned.1.call-start = ((), (), s32[]{:S(2)}) async-start(), calls=%async_computation.10 | async-start | bytes 3096576 | tf_op jit(solution)/shard_map/reduce_scatter | solution.py:141
  801.4 19.8 %copy-start.46 = (f32[4,768]{1,0:T(4,128)S(1)}, f32[4,768]{1,0:T(4,128)}, u32[]{:S(2)}) copy-start(f32[4,768]{1,0:T(4,128)} %copy-done.44) | copy-start | bytes 36868
  845.5 158.2 %reduce-scatter.15.cloned.1.call-start = ((), (), s32[]{:S(2)}) async-start(), calls=%async_computation.11 | async-start | bytes 8355840 | tf_op jit(solution)/shard_map/reduce_scatter | solution.py:486
  845.5 12.8 %copy-start.13 = (bf16[2048,768]{1,0:T(8,128)(2,1)S(1)}, bf16[2048,768]{1,0:T(8,128)(2,1)}, u32[]{:S(2)}) copy-start(bf16[2048,768]{1,0:T(8,128)(2,1)} %copy-done.12) | copy-start | bytes 9437188
  884.6 9.2 copy-start.20
  943.0 129.8 %reduce-scatter.17.cloned.1.call-start = ((), (), s32[]{:S(2)}) async-start(), calls=%async_computation.12 | async-start | bytes 1327104 | tf_op jit(solution)/shard_map/reduce_scatter | solution.py:141
  1008.0 54.6 %copy-start.10 = (f32[1024,768]{1,0:T(8,128)S(1)}, f32[1024,768]{1,0:T(8,128)}, u32[]{:S(2)}) copy-start(f32[1024,768]{1,0:T(8,128)} %copy-done.9) | copy-start | bytes 9437188
  1008.0 54.6 %copy-start.55 = (f32[1024]{0:T(1024)S(1)}, f32[1024]{0:T(1024)}, u32[]{:S(2)}) copy-start(f32[1024]{0:T(1024)} %copy-done.54) | copy-start | bytes 12292
  (61 other events, 266.3 us)
Sparse Core Ops, SparseCore 0:
  9.6 51.2 all-gather.8
  92.2 34.0 all-gather.10
  140.4 55.9 all-gather.14
  222.5 73.1 all-gather.12
  691.8 38.0 reduce-scatter.8
  732.3 87.5 reduce-scatter.10
  845.6 71.6 reduce-scatter.12
  943.2 60.4 reduce-scatter.14
  1008.1 64.6 reduce-scatter.16

commit v10 on v9

--- a/solution.py
+++ b/solution.py
@@ -323,20 +323,56 @@
     )
     shard_rows = blocks * CLEN
     group_len = PROMPT + CONT * CLEN
+    pooled_len = group_len // STRIDE
     cut = (0, HALF_FULL, HALF_FULL + CLEN, 2 * HALF_FULL + CLEN)
     pcut = tuple(cut[-1] + c for c in (0, HALF_POOL, HALF_POOL + BLOCK_POOL, 2 * HALF_POOL + BLOCK_POOL))
+    ramp = lambda n: jnp.arange(n, dtype=jnp.int32)
     own_full = grad_kv[:, :, cut[1] : cut[2]].reshape(groups, shard_rows, 2 * width)
-    own_pooled = grad_kv[:, :, pcut[1] : pcut[2]].reshape(groups, shard_rows // STRIDE, 2 * width)
     full = jnp.zeros((groups, group_len, 2 * width), jnp.float32)
     full = lax.dynamic_update_slice_in_dim(full, own_full, seq_index * shard_rows, 1)
-    full = window_add(full, grad_kv[:, :, cut[0] : cut[1]], starts[0])
-    full = window_add(full, grad_kv[:, :, cut[2] : cut[3]], starts[1])
-    pooled = jnp.zeros((groups, group_len // STRIDE, 2 * width), jnp.float32)
-    pooled = lax.dynamic_update_slice_in_dim(pooled, own_pooled, seq_index * shard_rows // STRIDE, 1)
-    pooled = window_add(pooled, grad_kv[:, :, pcut[0] : pcut[1]], starts[2])
-    pooled = window_add(pooled, grad_kv[:, :, pcut[2] : pcut[3]], starts[3])
+    side_values = jnp.concatenate(
+        [grad_kv[:, :, cut[0] : cut[1]], grad_kv[:, :, cut[2] : cut[3]]], axis=2
+    ).reshape(groups, -1, 2 * width)
+    side_rows = jnp.concatenate(
+        [starts[0][:, :, None] + ramp(HALF_FULL), starts[1][:, :, None] + ramp(HALF_FULL)], axis=2
+    ).reshape(groups, -1)
+    own_pool_rows = (seq_index * (shard_rows // STRIDE) + ramp(blocks)[:, None] * BLOCK_POOL + ramp(BLOCK_POOL))
+    pool_values = grad_kv[:, :, pcut[0] : pcut[3]].reshape(groups, -1, 2 * width)
+    pool_rows_index = jnp.concatenate(
+        [
+            starts[2][:, :, None] + ramp(HALF_POOL),
+            jnp.broadcast_to(own_pool_rows[None], (groups, blocks, BLOCK_POOL)),
+            starts[3][:, :, None] + ramp(HALF_POOL),
+        ],
+        axis=2,
+    ).reshape(groups, -1)
+    fulls, pooleds, unpooleds = [], [], []
+    for g in range(groups):
+        fulls.append(full[g] + select_sum(side_values[g], side_rows[g] == ramp(group_len)[:, None]))
+        pooleds.append(select_sum(pool_values[g], pool_rows_index[g] == ramp(pooled_len)[:, None]))
+        unpooleds.append(
+            select_sum(pool_values[g], pool_rows_index[g] == (ramp(group_len) // STRIDE)[:, None])
+        )
+    full = jnp.stack(fulls)
+    pooled = jnp.stack(pooleds)
+    unpooled = jnp.stack(unpooleds)
     grad_queries = grad_queries.reshape(groups * shard_rows, width).astype(jnp.bfloat16)
-    return grad_queries, full, pooled
+    return grad_queries, full, pooled, unpooled
+
+
+def select_sum(values, chosen):
+    onehot = chosen.astype(jnp.bfloat16)
+    high = values.astype(jnp.bfloat16)
+    low = (values - high.astype(jnp.float32)).astype(jnp.bfloat16)
+    return product(onehot, high) + product(onehot, low)
+
+
+def phase_weights(weight, rows):
+    phase = (jnp.arange(rows, dtype=jnp.int32) % STRIDE)[:, None]
+    total = jnp.zeros((rows, weight.shape[1]), jnp.float32)
+    for r in range(STRIDE):
+        total = total + jnp.where(phase == r, weight[r][None, :], 0.0)
+    return total
 
 
 def pool_grouped(source, weight):
@@ -436,23 +472,25 @@
     early_reduced, early_widths = early
 
     grad_rows = grad_attended.reshape(groups, shard_rows, width)
+    key_phase = phase_weights(pool_full[0], group_len)
+    value_phase = phase_weights(pool_full[1], group_len)
     pieces_back = []
     for g in range(groups):
         saved_g = tuple(item[g : g + 1] for item in att_saved)
         starts_g = tuple(item[g : g + 1] for item in starts)
         grad_g = grad_rows[g].reshape(shard_rows, width)
-        grad_queries_g, full_g, pooled_g = attention_bwd(grad_g, saved_g, starts_g, seq_index)
+        grad_queries_g, full_g, pooled_g, unpooled_g = attention_bwd(grad_g, saved_g, starts_g, seq_index)
         if g == 1:
-            full_g, pooled_g, earlier_back, early_reduced = lax.optimization_barrier(
-                (full_g, pooled_g, pieces_back[0][4], early_reduced)
+            full_g, pooled_g, unpooled_g, earlier_back, early_reduced = lax.optimization_barrier(
+                (full_g, pooled_g, unpooled_g, pieces_back[0][4], early_reduced)
             )
             pieces_back[0] = pieces_back[0][:4] + (earlier_back,)
         key_partial_g = (
-            full_g[..., :width] + unpool_grouped(pooled_g[..., :width], pool_full[0])
-        ).astype(jnp.bfloat16).reshape(group_len, width)
+            full_g[0, :, :width] + unpooled_g[0, :, :width] * key_phase
+        ).astype(jnp.bfloat16)
         value_partial_g = (
-            full_g[..., width:] + unpool_grouped(pooled_g[..., width:], pool_full[1])
-        ).astype(jnp.bfloat16).reshape(group_len, width)
+            full_g[0, :, width:] + unpooled_g[0, :, width:] * value_phase
+        ).astype(jnp.bfloat16)
         back_g = product_right(key_partial_g, wk) + product_right(value_partial_g, wv)
         back_g = back_g.reshape(1, group_len, width).astype(jnp.bfloat16)
         if g == groups - 1:

time: 1090 us -> 1030 us (0.945)
  local copies, waits for them, and re-layouts: 337 us -> 278 us
  matrix products: 242 us -> 290 us
  other arithmetic: 221 us -> 181 us
    dot_general x6 -> x18, matrix products: 66.3 us -> 123 us  [product(): return jnp.dot(left, right, preferred_element_type=jnp.float32)]
    dynamic_update_slice x36 -> x0, local copies, waits for them, and re-layouts: 42.6 us -> none  [the longest x32 37.3 us: window_add(): lax.dynamic_update_slice_in_dim(row, current + updates[g, b], start, 0)]
    mul x6 -> x0, local copies, waits for them, and re-layouts: 33.7 us -> none  [unpool_grouped(): pooled_grad[:, :, None, :] * weight[None, None]]
    all_gather x2, waiting for transfers between devices: 26.2 us -> 0.01 us  [gather_grouped(): return (lax.all_gather(across, 'seq', axis=0, tiled=True), tie)]
    convert_element_type x0 -> x6, other arithmetic: none -> 22 us  [the longest x2 19 us: local(): value_partial_g = (full_g[0, :, width:] + unpooled_g[0, :, width:] * valu...]
    reshape x2 -> x0, other arithmetic: 20.1 us -> none  [local(): value_partial_g = (full_g[..., width:] + unpool_grouped(pooled_g[..., wid...]
    unnamed x186 -> x232, local copies, waits for them, and re-layouts: 46.8 us -> 66.9 us
    add x26 -> x10, other arithmetic: 29.5 us -> 10.2 us  [the longest x2 7.95 us: attention_bwd(): full[g]]
  transfers between devices with their start and end apart: 9 -> 9, of which waited for: 5 -> 5; matrix products, arithmetic and copies ran while one was open for 36% -> 39% of each run, Pallas kernels for 0% -> 0%
where the time goes in v10:
time: 1030 us; the launch traced here: 1020 us
  matrix products  290 us (28%)
  local copies, waits for them, and re-layouts  278 us (27%)
  other arithmetic  181 us (18%)
  blocking collectives  118 us (11%)
  waiting for transfers between devices  93.9 us (9%)
  between operations  61.6 us (6%)
    dot_general x18, matrix products, product(): return jnp.dot(left, right, preferred_element_type=jnp.float32)  123 us
    unnamed x232, local copies, waits for them, and re-layouts  66.9 us
    dot_general x8, matrix products, product_right(): lax.dot_general(left, right, (((1,), (1,)), ((), ())), preferred_element_...  48.2 us
    all_gather x1, blocking collectives, local(): small_full = lax.all_gather(small_local, ('dp', 'seq'), axis=1, tiled=True)  44.5 us
    reduce_scatter x1, waiting for transfers between devices, local(): joined = lax.psum_scatter(joined, 'seq', scatter_dimension=0, tiled=True)  42.2 us
    unnamed x1, blocking collectives  40.1 us
    dot_general x6, matrix products, product_left(): lax.dot_general(left, right, (((0,), (0,)), ((), ())), preferred_element_...  34.3 us
    all_gather x1, blocking collectives, gather_grouped(): across = lax.all_gather(local_block, 'dp', axis=1, tiled=False)  33.8 us
  transfers between devices with their start and end apart: 9, of which 5 were waited for; matrix products, arithmetic and copies ran while one was open for 39% of the time, Pallas kernels for 0%

profile of v10, /device:TPU:0, one launch (start us, length us, event | category | flops | bytes accessed | tf_op | source)
XLA Modules:
  0.0 1024.0 jit_solution(17887278483253162759)
XLA Ops:
  24.5 44.5 %all-gather.2 = f32[32,24,12]{1,2,0:T(8,128)S(1)} all-gather(f32[1,24,12]{1,2,0:T(8,128)S(1)} %maximum_bitcast_fusion.11), channel_id=1, replica_groups=mesh['dp'=8,'seq'=4] {'dp','seq'}, dimensions={0}, use_global_device_ids=true | all-gather | bytes 38016 | tf_op jit(solution)/shard_map/all_gather | solution.py:414
  69.3 33.8 %all-gather = bf16[192,2304]{0,1:T(8,128)(2,1)S(1)} all-gather(bf16[192,288]{0,1:T(8,128)(2,1)S(1)} %pad_maximum_fusion.9), channel_id=2, replica_groups=mesh['dp'=8,'seq'=4] {'dp'}, dimensions={1}, use_global_device_ids=true | all-gather | bytes 995328 | tf_op jit(solution)/shard_map/all_gather | solution.py:99
  186.1 9.9 convolution_convert_fusion
  196.0 12.4 %reshape.1302 = f32[2,512,4,768]{3,2,1,0:T(4,128)} reshape(bf16[4096,768]{1,0:T(8,128)(2,1)} %convolution_convert_fusion) | data formatting | bytes 18874368 | tf_op jit(solution)/shard_map/convert_element_type | solution.py:434
  208.4 12.0 %all-gather.15.cloned.1.call-done = bf16[8,864,192]{1,2,0:T(8,128)(2,1)} async-done(((bf16[1,864,192]{1,2,0:T(8,128)(2,1)}), bf16[8,864,192]{1,2,0:T(8,128)(2,1)}) %all-gather.15.cloned.1.call-update) | async-done | bytes 2654224 | tf_op jit(solution)/shard_map/all_gather | solution.py:99
  235.2 9.8 convolution_convert_fusion.1
  244.9 12.5 %reshape.1301 = f32[2,512,4,768]{3,2,1,0:T(4,128)} reshape(bf16[4096,768]{1,0:T(8,128)(2,1)} %convolution_convert_fusion.1) | data formatting | bytes 18874368 | tf_op jit(solution)/shard_map/convert_element_type | solution.py:433
  257.4 19.7 %multiply_reduce_fusion.2 = (bf16[2,512,768]{2,1,0:T(8,128)(2,1)S(1)}, bf16[2,512,768]{2,1,0:T(8,128)(2,1)S(1)}) fusion(f32[2,512,4,768]{3,2,1,0:T(4,128)} %reshape.1302, f32[4,768]{1,0:T(4,128)S(1)} %get-tuple-element.168, f32[2,512,4,768]{3,2,1,0:T(4,128)} %reshape.1301, f32[4,768]{1,0:T(4,128)S(1)} %copy-done.47), kind=kLoop, calls=%fused_computation.31 | loop fusion | flops 11010048 | bytes 28336128 | tf_op jit(solution)/shard_map/reduce_sum | solution.py:380
  333.4 13.2 %fusion.170 = (f32[2,4,12,128]{3,2,1,0:T(8,128)S(1)}, f32[2,4,12,128,416]{3,4,2,1,0:T(8,128)}) fusion(pred[2,4,128,416]{2,3,1,0:T(8,128)(4,1)S(1)} %copy-done.43, bf16[2,4,416,12,64]{2,4,3,1,0:T(8,128)(2,1)} %bitcast.433, bf16[2,4,128,12,64]{2,1,0,4,3:T(4,128)(2,1)S(1)} %copy-done.30), kind=kOutput, calls=%fused_computation.449 | convolution fusion | flops 674759040 | bytes 27607040 | tf_op jit(solution)/shard_map/sub | solution.py:283
  346.6 15.3 %broadcast_divide_fusion = f32[2,4,12,128,416]{3,4,2,1,0:T(8,128)} fusion(f32[2,4,12,128,416]{3,4,2,1,0:T(8,128)} %get-tuple-element.211, f32[2,4,12,128]{3,2,1,0:T(8,128)S(1)} %get-tuple-element.210), kind=kLoop, calls=%fused_computation.45 | loop fusion | flops 5111808 | bytes 40943616 | tf_op jit(solution)/shard_map/div | solution.py:285
  361.9 10.0 fusion.87
  380.2 14.3 %fusion.157 = (bf16[768,8,384]{2,1,0:T(8,128)(2,1)}, bf16[768,8,384]{2,1,0:T(8,128)(2,1)}) fusion(bf16[768,8,864]{2,1,0:T(8,128)(2,1)} %all-gather.13.cloned.1.call-done), kind=kLoop, calls=%fused_computation.436 | loop fusion | bytes 18874368 | tf_op jit(solution)/shard_map/slice | solution.py:107
  404.4 34.9 %multiply_convert_fusion = (bf16[1024,3072]{1,0:T(8,128)(2,1)S(1)}, f32[1024,3072]{1,0:T(8,128)}, f32[1024,3072]{1,0:T(8,128)}) fusion(bf16[768,3072]{1,0:T(8,128)(2,1)S(1)} %bitcast.434, f32[1024,768]{1,0:T(8,128)S(1)} %get-tuple-element.213, f32[768]{0:T(1024)S(1)} %copy-done.82, f32[768]{0:T(1024)S(1)} %copy-done.67, f32[1024]{0:T(1024)S(1)} %fusion.134, ...), kind=kOutput, calls=%fused_computation.18 | convolution fusion | flops 5040242688 | bytes 39335936 | tf_op jit(solution)/shard_map/dot_general | solution.py:78
  457.9 18.4 %add_convert_fusion = bf16[1024,3072]{1,0:T(8,128)(2,1)} fusion(f32[1024,3072]{1,0:T(8,128)} %get-tuple-element.90, f32[1024,3072]{1,0:T(8,128)} %get-tuple-element.214, bf16[768,3072]{1,0:T(8,128)(2,1)} %bitcast.437, f32[1024,768]{1,0:T(8,128)} %copy-done.24, f32[1024]{0:T(1024)S(1)} %negate_multiply_fusion.2), kind=kOutput, calls=%fused_computation.17 | convolution fusion | flops 4877451264 | bytes 39325696 | tf_op jit(solution)/shard_map/dot_general | solution.py:88
  476.4 9.4 multiply_reduce_fusion.4
  510.8 11.2 %pad_maximum_fusion = bf16[768,8,864]{2,0,1:T(8,128)(2,1)} fusion(bf16[768,8,384]{2,0,1:T(8,128)(2,1)} %bitcast.421, bf16[768,8,384]{2,0,1:T(8,128)(2,1)} %bitcast.420, bf16[768,8,96]{2,0,1:T(8,128)(2,1)S(1)} %copy.206), kind=kLoop, calls=%fused_computation.34 | loop fusion | flops 31850496 | bytes 21233664 | tf_op jit(solution)/shard_map/concatenate | solution.py:127
  525.3 9.1 fusion.36
  547.8 17.5 %fusion.11 = (f32[4,12,128]{2,1,0:T(8,128)S(1)}, f32[4,12,128]{2,1,0:T(8,128)S(1)}, f32[4,12,128,416]{2,3,1,0:T(8,128)}) fusion(f32[2,4,12,128,416]{3,4,2,1,0:T(8,128)} %broadcast_divide_fusion, f32[4,12,128,416]{2,3,1,0:T(8,128)} %fusion.108, bf16[4,416,12,64]{1,3,2,0:T(8,128)(2,1)} %bitcast.426, bf16[4,128,12,64]{1,0,3,2:T(4,128)(2,1)} %copy-done.16), kind=kOutput, calls=%fused_computation.42 | convolution fusion | flops 337367040 | bytes 44285952 | tf_op jit(solution)/shard_map/gbqhd,gbkhd->gbhqk/dot_general | solution.py:302
  565.3 16.8 %fusion.41 = (bf16[4,12,128,416]{2,3,1,0:T(8,128)(2,1)S(1)}, bf16[4,12,128,416]{2,3,1,0:T(8,128)(2,1)}) fusion(f32[4,12,128,416]{2,3,1,0:T(8,128)} %get-tuple-element.218, f32[2,4,12,128,416]{3,4,2,1,0:T(8,128)} %broadcast_divide_fusion, f32[4,12,128]{2,1,0:T(8,128)S(1)} %get-tuple-element.51, f32[4,12,128,416]{2,3,1,0:T(8,128)} %fusion.108, ...), kind=kLoop, calls=%fused_computation.92 | loop fusion | flops 15335424 | bytes 51167232 | tf_op jit(solution)/shard_map/reshape.156
  612.8 10.3 %copy.286 = f32[1,2048,1536]{2,1,0:T(8,128)} copy(f32[1,2048,1536]{2,1,0:T(8,128)} %bitcast.396) | data formatting | bytes 25165824
  667.6 9.3 fusion.39
  725.0 10.6 %copy.285 = f32[1,2048,1536]{2,1,0:T(8,128)} copy(f32[1,2048,1536]{2,1,0:T(8,128)} %bitcast.395) | data formatting | bytes 25165824
  764.1 19.9 %reduce-scatter.11.cloned.1.call-done = bf16[192,8,864]{2,0,1:T(8,128)(2,1)} async-done(((bf16[768,8,864]{2,0,1:T(8,128)(2,1)}), bf16[192,8,864]{2,0,1:T(8,128)(2,1)}) %reduce-scatter.11.cloned.1.call-update) | async-done | bytes 2654224 | tf_op jit(solution)/shard_map/reduce_scatter | solution.py:129
  784.1 12.7 %fusion.32 = (bf16[2048,768]{1,0:T(8,128)(2,1)S(1)}, bf16[2048,768]{1,0:T(8,128)(2,1)}) fusion(f32[1,2048,1536]{2,1,0:T(8,128)} %add_bitcast_fusion.1, f32[1,2048,1536]{2,1,0:T(8,128)} %bitcast_dynamic-update-slice_fusion.1, f32[768]{0:T(1024)S(1)} %copy-done.49, f32[768]{0:T(1024)S(1)} %copy-done.50, f32[768]{0:T(1024)S(1)} %copy-done.51, ...), kind=kLoop, calls=%fused_computation.80 | loop fusion | flops 31457280 | bytes 31490048 | tf_op jit(solution)/shard_map/convert_element_type | solution.py:493
  801.5 9.0 copy.227
  815.5 8.8 copy.226
  824.4 9.1 convolution_convert_fusion.6
  847.8 11.6 %reduce-scatter.13.cloned.1.call-done = bf16[192,1,864]{2,0,1:T(8,128)(2,1)} async-done(((bf16[192,8,864]{2,0,1:T(8,128)(2,1)}), bf16[192,1,864]{2,0,1:T(8,128)(2,1)}) %reduce-scatter.13.cloned.1.call-update) | async-done | bytes 331792 | tf_op jit(solution)/shard_map/reduce_scatter | solution.py:141
  867.1 9.0 reshape.1291
  899.8 42.2 %reduce-scatter.15.cloned.1.call-done = bf16[1088,768]{1,0:T(8,128)(2,1)} async-done(((bf16[4352,768]{1,0:T(8,128)(2,1)}), bf16[1088,768]{1,0:T(8,128)(2,1)}) %reduce-scatter.15.cloned.1.call-update) | async-done | bytes 1671184 | tf_op jit(solution)/shard_map/reduce_scatter | solution.py:524
  950.4 9.5 multiply_reduce_fusion.1
  960.0 40.1 %all-reduce.3 = (f32[2,4,768]{2,1,0:T(4,128)S(1)}, f32[2,768]{1,0:T(2,128)S(1)}, f32[2,768]{1,0:T(2,128)S(1)}) all-reduce(f32[2,4,768]{2,1,0:T(4,128)S(1)} %pad_maximum_fusion.10, f32[2,768]{1,0:T(2,128)S(1)} %pad_maximum_fusion.11, f32[2,768]{1,0:T(2,128)S(1)} %pad_maximum_fusion.12), channel_id=9, replica_groups=mesh['dp'=8,'seq'=4] {'dp','seq'}, use_global_device_ids=true, to_apply=%region_24.25.clone | all-reduce | flops 9216 | bytes 73728
  (470 shorter events, 435.5 us)
Async XLA Ops:
  7.2 95.9 %all-gather.9.cloned.1.call-start = ((), (), s32[]{:S(2)}) async-start(), calls=%async_computation.5 | async-start | bytes 7864320 | tf_op jit(solution)/shard_map/all_gather | solution.py:415
  7.9 145.7 %all-gather.11.cloned.1.call-start = ((), (), s32[]{:S(2)}) async-start(), calls=%async_computation.6 | async-start | bytes 5898240 | tf_op jit(solution)/shard_map/all_gather | solution.py:101
  105.0 115.3 %all-gather.15.cloned.1.call-start = ((), (), s32[]{:S(2)}) async-start(), calls=%async_computation.13 | async-start | bytes 3096576 | tf_op jit(solution)/shard_map/all_gather | solution.py:99
  163.8 15.2 %copy-start.27 = (bf16[2,512,768]{2,1,0:T(8,128)(2,1)S(1)}, bf16[2,512,768]{2,1,0:T(8,128)(2,1)}, u32[]{:S(2)}) copy-start(bf16[2,512,768]{2,1,0:T(8,128)(2,1)} %param.12) | copy-start | bytes 4718596
  167.4 209.4 %all-gather.13.cloned.1.call-start = ((), (), s32[]{:S(2)}) async-start(), calls=%async_computation.7 | async-start | bytes 13762560 | tf_op jit(solution)/shard_map/all_gather | solution.py:101
  234.6 529.5 %reduce-scatter.9.cloned.1.call-start = ((), (), s32[]{:S(2)}) async-start(), calls=%async_computation.8 | async-start | bytes 3932160 | tf_op jit(solution)/shard_map/reduce_scatter | solution.py:499
  244.9 12.5 %copy-start.47 = (f32[4,768]{1,0:T(4,128)S(1)}, f32[4,768]{1,0:T(4,128)}, u32[]{:S(2)}) copy-start(f32[4,768]{1,0:T(4,128)} %get-tuple-element.169) | copy-start | bytes 36868
  346.6 15.3 %copy-start.2 = (bf16[2,4,416,768]{2,3,1,0:T(8,128)(2,1)S(1)}, bf16[2,4,416,768]{2,3,1,0:T(8,128)(2,1)}, u32[]{:S(2)}) copy-start(bf16[2,4,416,768]{2,3,1,0:T(8,128)(2,1)} %copy.189) | copy-start | bytes 15335428
  398.2 41.2 %copy-start.20 = (bf16[96,8,8,384]{3,1,2,0:T(8,128)(2,1)}, bf16[96,8,8,384]{3,1,2,0:T(8,128)(2,1)S(1)}, u32[]{:S(2)}) copy-start(bf16[96,8,8,384]{3,1,2,0:T(8,128)(2,1)S(1)} %copy.245) | copy-start | bytes 14155780
  476.4 9.4 copy-start.83
  524.0 10.4 %copy-start.16 = (bf16[4,128,12,64]{1,0,3,2:T(4,128)(2,1)}, bf16[4,128,12,64]{1,0,3,2:T(4,128)(2,1)S(1)}, u32[]{:S(2)}) copy-start(bf16[4,128,12,64]{1,0,3,2:T(4,128)(2,1)S(1)} %reshape.1275) | copy-start | bytes 2359300
  565.3 16.8 %copy-start.18 = (bf16[4,128,12,64]{1,0,3,2:T(4,128)(2,1)S(1)}, bf16[4,128,12,64]{1,0,3,2:T(4,128)(2,1)}, u32[]{:S(2)}) copy-start(bf16[4,128,12,64]{1,0,3,2:T(4,128)(2,1)} %reshape.1286) | copy-start | bytes 2359300
  602.3 20.8 %copy-start.26 = (bf16[640,1536]{1,0:T(8,128)(2,1)}, bf16[640,1536]{1,0:T(8,128)(2,1)S(1)}, u32[]{:S(2)}) copy-start(bf16[640,1536]{1,0:T(8,128)(2,1)S(1)} %get-tuple-element.80) | copy-start | bytes 5898244
  612.8 10.4 %copy-start.73 = (s32[2048]{0:T(1024)S(1)}, s32[2048]{0:T(1024)}, u32[]{:S(2)}) copy-start(s32[2048]{0:T(1024)} %add_select_fusion) | copy-start | bytes 24580
  612.8 10.4 %copy-start.79 = (s32[640]{0:T(1024)S(1)}, s32[640]{0:T(1024)}, u32[]{:S(2)}) copy-start(s32[640]{0:T(1024)} %eq.228) | copy-start | bytes 7684
  623.1 16.8 %slice-start.9 = ((s8[12582912]{0:T(1024)(128)(4,1)}), s8[4194304]{0:T(1024)(128)(4,1)S(1)}, s32[]{:S(2)}) async-start(s8[12582912]{0:T(1024)(128)(4,1)} %bitcast.407), calls=%async_computation.23 | async-start | bytes 8388608
  623.1 16.8 %slice-start.10 = ((s8[12582912]{0:T(1024)(128)(4,1)}), s8[4194304]{0:T(1024)(128)(4,1)S(1)}, s32[]{:S(2)}) async-start(s8[12582912]{0:T(1024)(128)(4,1)} %bitcast.407), calls=%async_computation.24 | async-start | bytes 8388608
  657.0 127.0 %reduce-scatter.11.cloned.1.call-start = ((), (), s32[]{:S(2)}) async-start(), calls=%async_computation.9 | async-start | bytes 13762560 | tf_op jit(solution)/shard_map/reduce_scatter | solution.py:129
  657.6 201.8 %reduce-scatter.13.cloned.1.call-start = ((), (), s32[]{:S(2)}) async-start(), calls=%async_computation.10 | async-start | bytes 3096576 | tf_op jit(solution)/shard_map/reduce_scatter | solution.py:141
  725.0 10.9 %slice-start.12 = ((s8[5111808]{0:T(1024)(128)(4,1)}), s8[4194304]{0:T(1024)(128)(4,1)S(1)}, s32[]{:S(2)}) async-start(s8[5111808]{0:T(1024)(128)(4,1)} %bitcast.409), calls=%async_computation.26 | async-start | bytes 8388608
  725.0 10.6 %copy-start.21 = (bf16[1,4,128,12,64]{2,1,4,3,0:T(4,128)(2,1)S(1)}, bf16[1,4,128,12,64]{2,1,4,3,0:T(4,128)(2,1)}, u32[]{:S(2)}) copy-start(bf16[1,4,128,12,64]{2,1,4,3,0:T(4,128)(2,1)} %copy.212) | copy-start | bytes 2359300
  725.0 10.9 %slice-start.13 = ((s8[5111808]{0:T(1024)(128)(4,1)}), s8[917504]{0:T(1024)(128)(4,1)S(1)}, s32[]{:S(2)}) async-start(s8[5111808]{0:T(1024)(128)(4,1)} %bitcast.409), calls=%async_computation.27 | async-start | bytes 1835008
  755.8 28.3 %copy-start.63 = (pred[2048]{0:T(1024)(128)(4,1)S(1)}, pred[2048]{0:T(1024)(128)(4,1)}, u32[]{:S(2)}) copy-start(pred[2048]{0:T(1024)(128)(4,1)} %get-tuple-element.227) | copy-start | bytes 6148
  755.8 28.3 %copy-start.65 = (pred[2048]{0:T(1024)(128)(4,1)S(1)}, pred[2048]{0:T(1024)(128)(4,1)}, u32[]{:S(2)}) copy-start(pred[2048]{0:T(1024)(128)(4,1)} %get-tuple-element.228) | copy-start | bytes 6148
  784.0 14.4 %copy-start.9 = (bf16[2048,768]{1,0:T(8,128)(2,1)S(1)}, bf16[2048,768]{1,0:T(8,128)(2,1)}, u32[]{:S(2)}) copy-start(bf16[2048,768]{1,0:T(8,128)(2,1)} %copy-done.8) | copy-start | bytes 9437188
  784.1 157.9 %reduce-scatter.15.cloned.1.call-start = ((), (), s32[]{:S(2)}) async-start(), calls=%async_computation.11 | async-start | bytes 8355840 | tf_op jit(solution)/shard_map/reduce_scatter | solution.py:524
  815.5 18.0 %slice-start.21 = ((s8[6291456]{0:T(1024)(128)(4,1)}), s8[2097152]{0:T(1024)(128)(4,1)S(1)}, s32[]{:S(2)}) async-start(s8[6291456]{0:T(1024)(128)(4,1)} %bitcast.474), calls=%async_computation.35 | async-start | bytes 4194304
  824.4 9.2 copy-start.17
  824.4 9.2 slice-start.22
  881.1 134.4 %reduce-scatter.17.cloned.1.call-start = ((), (), s32[]{:S(2)}) async-start(), calls=%async_computation.12 | async-start | bytes 1327104 | tf_op jit(solution)/shard_map/reduce_scatter | solution.py:141
  959.9 44.6 %copy-start.14 = (f32[1024,768]{1,0:T(8,128)S(1)}, f32[1024,768]{1,0:T(8,128)}, u32[]{:S(2)}) copy-start(f32[1024,768]{1,0:T(8,128)} %copy-done.13) | copy-start | bytes 9437188
  959.9 44.6 %copy-start.72 = (f32[1024]{0:T(1024)S(1)}, f32[1024]{0:T(1024)}, u32[]{:S(2)}) copy-start(f32[1024]{0:T(1024)} %copy-done.71) | copy-start | bytes 12292
  (84 other events, 287.8 us)
Sparse Core Ops, SparseCore 0:
  9.5 51.3 all-gather.8
  105.1 34.2 all-gather.10
  167.5 52.7 all-gather.14
  234.7 71.7 all-gather.12
  657.1 36.8 reduce-scatter.8
  696.4 87.5 reduce-scatter.10
  787.6 71.8 reduce-scatter.12
  881.3 60.6 reduce-scatter.14
  950.5 65.0 reduce-scatter.16

commit v11 on v10

--- a/solution.py
+++ b/solution.py
@@ -411,11 +411,12 @@
     small_local = jnp.concatenate(
         [pool_weight.reshape(pool_rows_count, -1), ln_gain, ln_bias], axis=0
     )
+    hidden_all = lax.all_gather(hidden_in, "seq", axis=1, tiled=True)
+    (wq, wk, wv), (hidden_all, small_local) = gather_first(
+        w_query, w_key, w_value, (hidden_all, small_local)
+    )
     small_full = lax.all_gather(small_local, ("dp", "seq"), axis=1, tiled=True)
-    hidden_all = lax.all_gather(hidden_in, "seq", axis=1, tiled=True)
-    (wq, wk, wv), (hidden_all, small_full) = gather_first(
-        w_query, w_key, w_value, (hidden_all, small_full)
-    )
+    wq, wk, wv, small_full = lax.optimization_barrier((wq, wk, wv, small_full))
     pool_full = small_full[:pool_rows_count].reshape(pool_weight.shape[0], pool_weight.shape[1], -1)
     gain_full = small_full[pool_rows_count : pool_rows_count + ln_gain.shape[0]]
     bias_full = small_full[pool_rows_count + ln_gain.shape[0] :]

time: 1030 us -> 1040 us (level)
    unnamed x232 -> x236, local copies, waits for them, and re-layouts: 66.9 us -> 67.9 us
  transfers between devices with their start and end apart: 9 -> 9, of which waited for: 5 -> 6; matrix products, arithmetic and copies ran while one was open for 39% -> 38% of each run, Pallas kernels for 0% -> 0%
where the time goes in v11:
time: 1040 us; the launch traced here: 1030 us
  matrix products  291 us (28%)
  local copies, waits for them, and re-layouts  279 us (27%)
  other arithmetic  179 us (17%)
  blocking collectives  116 us (11%)
  waiting for transfers between devices  104 us (10%)
  between operations  61.7 us (6%)
    dot_general x18, matrix products, product(): return jnp.dot(left, right, preferred_element_type=jnp.float32)  123 us
    unnamed x236, local copies, waits for them, and re-layouts  67.9 us
    dot_general x8, matrix products, product_right(): lax.dot_general(left, right, (((1,), (1,)), ((), ())), preferred_element_...  48.2 us
    reduce_scatter x1, waiting for transfers between devices, local(): joined = lax.psum_scatter(joined, 'seq', scatter_dimension=0, tiled=True)  42 us
    all_gather x1, blocking collectives, local(): small_full = lax.all_gather(small_local, ('dp', 'seq'), axis=1, tiled=True)  41.2 us
    unnamed x1, blocking collectives  40 us
    all_gather x1, blocking collectives, gather_grouped(): across = lax.all_gather(local_block, 'dp', axis=1, tiled=False)  35.1 us
    dot_general x6, matrix products, product_left(): lax.dot_general(left, right, (((0,), (0,)), ((), ())), preferred_element_...  34.4 us
  transfers between devices with their start and end apart: 9, of which 6 were waited for; matrix products, arithmetic and copies ran while one was open for 38% of the time, Pallas kernels for 0%

profile of v11, /device:TPU:0, one launch (start us, length us, event | category | flops | bytes accessed | tf_op | source)
XLA Modules:
  0.0 1032.1 jit_solution(11128035864382546504)
XLA Ops:
  13.5 35.1 %all-gather = bf16[192,2304]{0,1:T(8,128)(2,1)S(1)} all-gather(bf16[192,288]{0,1:T(8,128)(2,1)S(1)} %pad_maximum_fusion.9), channel_id=2, replica_groups=mesh['dp'=8,'seq'=4] {'dp'}, dimensions={1}, use_global_device_ids=true | all-gather | bytes 995328 | tf_op jit(solution)/shard_map/all_gather | solution.py:99
  48.6 10.0 all-gather.9.cloned.1.call-done
  120.9 41.2 %all-gather.2 = f32[32,24,12]{1,2,0:T(8,128)S(1)} all-gather(f32[1,24,12]{1,2,0:T(8,128)S(1)} %bitcast.469), channel_id=1, replica_groups=mesh['dp'=8,'seq'=4] {'dp','seq'}, dimensions={0}, use_global_device_ids=true | all-gather | bytes 38016 | tf_op jit(solution)/shard_map/all_gather | solution.py:418
  193.4 9.8 convolution_convert_fusion
  203.2 12.3 %reshape.1302 = f32[2,512,4,768]{3,2,1,0:T(4,128)} reshape(bf16[4096,768]{1,0:T(8,128)(2,1)} %convolution_convert_fusion) | data formatting | bytes 18874368 | tf_op jit(solution)/shard_map/convert_element_type | solution.py:435
  215.5 12.7 %all-gather.15.cloned.1.call-done = bf16[8,864,192]{1,2,0:T(8,128)(2,1)} async-done(((bf16[1,864,192]{1,2,0:T(8,128)(2,1)}), bf16[8,864,192]{1,2,0:T(8,128)(2,1)}) %all-gather.15.cloned.1.call-update) | async-done | bytes 2654224 | tf_op jit(solution)/shard_map/all_gather | solution.py:99
  243.0 9.8 convolution_convert_fusion.1
  252.8 12.5 %reshape.1301 = f32[2,512,4,768]{3,2,1,0:T(4,128)} reshape(bf16[4096,768]{1,0:T(8,128)(2,1)} %convolution_convert_fusion.1) | data formatting | bytes 18874368 | tf_op jit(solution)/shard_map/convert_element_type | solution.py:434
  265.3 19.6 %multiply_reduce_fusion.2 = (bf16[2,512,768]{2,1,0:T(8,128)(2,1)S(1)}, bf16[2,512,768]{2,1,0:T(8,128)(2,1)S(1)}) fusion(f32[2,512,4,768]{3,2,1,0:T(4,128)} %reshape.1302, f32[4,768]{1,0:T(4,128)S(1)} %get-tuple-element.176, f32[2,512,4,768]{3,2,1,0:T(4,128)} %reshape.1301, f32[4,768]{1,0:T(4,128)S(1)} %get-tuple-element.177), kind=kLoop, calls=%fused_computation.31 | loop fusion | flops 11010048 | bytes 28336128 | tf_op jit(solution)/shard_map/reduce_sum | solution.py:380
  341.2 13.2 %fusion.170 = (f32[2,4,12,128]{3,2,1,0:T(8,128)S(1)}, f32[2,4,12,128,416]{3,4,2,1,0:T(8,128)}) fusion(pred[2,4,128,416]{2,3,1,0:T(8,128)(4,1)S(1)} %copy-done.43, bf16[2,4,416,12,64]{2,4,3,1,0:T(8,128)(2,1)} %bitcast.432, bf16[2,4,128,12,64]{2,1,0,4,3:T(4,128)(2,1)S(1)} %copy-done.30), kind=kOutput, calls=%fused_computation.449 | convolution fusion | flops 674759040 | bytes 27607040 | tf_op jit(solution)/shard_map/sub | solution.py:283
  354.5 15.3 %broadcast_divide_fusion = f32[2,4,12,128,416]{3,4,2,1,0:T(8,128)} fusion(f32[2,4,12,128,416]{3,4,2,1,0:T(8,128)} %get-tuple-element.219, f32[2,4,12,128]{3,2,1,0:T(8,128)S(1)} %get-tuple-element.218), kind=kLoop, calls=%fused_computation.45 | loop fusion | flops 5111808 | bytes 40943616 | tf_op jit(solution)/shard_map/div | solution.py:285
  369.7 10.0 fusion.87
  388.7 14.3 %fusion.157 = (bf16[768,8,384]{2,1,0:T(8,128)(2,1)}, bf16[768,8,384]{2,1,0:T(8,128)(2,1)}) fusion(bf16[768,8,864]{2,1,0:T(8,128)(2,1)} %all-gather.13.cloned.1.call-done), kind=kLoop, calls=%fused_computation.436 | loop fusion | bytes 18874368 | tf_op jit(solution)/shard_map/slice | solution.py:107
  412.8 34.9 %multiply_convert_fusion = (bf16[1024,3072]{1,0:T(8,128)(2,1)S(1)}, f32[1024,3072]{1,0:T(8,128)}, f32[1024,3072]{1,0:T(8,128)}) fusion(bf16[768,3072]{1,0:T(8,128)(2,1)S(1)} %bitcast.433, f32[1024,768]{1,0:T(8,128)S(1)} %get-tuple-element.221, f32[768]{0:T(1024)S(1)} %get-tuple-element.76, f32[768]{0:T(1024)S(1)} %get-tuple-element.77, ...), kind=kOutput, calls=%fused_computation.18 | convolution fusion | flops 5040242688 | bytes 39335936 | tf_op jit(solution)/shard_map/dot_general | solution.py:78
  466.2 18.5 %add_convert_fusion = bf16[1024,3072]{1,0:T(8,128)(2,1)} fusion(f32[1024,3072]{1,0:T(8,128)} %get-tuple-element.98, f32[1024,3072]{1,0:T(8,128)} %get-tuple-element.222, bf16[768,3072]{1,0:T(8,128)(2,1)} %bitcast.436, f32[1024,768]{1,0:T(8,128)} %copy-done.24, f32[1024]{0:T(1024)S(1)} %negate_multiply_fusion.2), kind=kOutput, calls=%fused_computation.17 | convolution fusion | flops 4877451264 | bytes 39325696 | tf_op jit(solution)/shard_map/dot_general | solution.py:88
  484.7 9.4 multiply_reduce_fusion.4
  519.3 11.3 %pad_maximum_fusion = bf16[768,8,864]{2,0,1:T(8,128)(2,1)} fusion(bf16[768,8,384]{2,0,1:T(8,128)(2,1)} %bitcast.420, bf16[768,8,384]{2,0,1:T(8,128)(2,1)} %bitcast.419, bf16[768,8,96]{2,0,1:T(8,128)(2,1)S(1)} %copy.206), kind=kLoop, calls=%fused_computation.34 | loop fusion | flops 31850496 | bytes 21233664 | tf_op jit(solution)/shard_map/concatenate | solution.py:127
  533.9 9.1 fusion.36
  556.4 17.5 %fusion.11 = (f32[4,12,128]{2,1,0:T(8,128)S(1)}, f32[4,12,128]{2,1,0:T(8,128)S(1)}, f32[4,12,128,416]{2,3,1,0:T(8,128)}) fusion(f32[2,4,12,128,416]{3,4,2,1,0:T(8,128)} %broadcast_divide_fusion, f32[4,12,128,416]{2,3,1,0:T(8,128)} %fusion.108, bf16[4,416,12,64]{1,3,2,0:T(8,128)(2,1)} %bitcast.425, bf16[4,128,12,64]{1,0,3,2:T(4,128)(2,1)} %copy-done.16), kind=kOutput, calls=%fused_computation.42 | convolution fusion | flops 337367040 | bytes 44285952 | tf_op jit(solution)/shard_map/gbqhd,gbkhd->gbhqk/dot_general | solution.py:302
  573.9 16.8 %fusion.41 = (bf16[4,12,128,416]{2,3,1,0:T(8,128)(2,1)S(1)}, bf16[4,12,128,416]{2,3,1,0:T(8,128)(2,1)}) fusion(f32[4,12,128,416]{2,3,1,0:T(8,128)} %get-tuple-element.226, f32[2,4,12,128,416]{3,4,2,1,0:T(8,128)} %broadcast_divide_fusion, f32[4,12,128]{2,1,0:T(8,128)S(1)} %get-tuple-element.59, f32[4,12,128,416]{2,3,1,0:T(8,128)} %fusion.108, ...), kind=kLoop, calls=%fused_computation.92 | loop fusion | flops 15335424 | bytes 51167232 | tf_op jit(solution)/shard_map/reshape.156
  621.3 10.3 %copy.286 = f32[1,2048,1536]{2,1,0:T(8,128)} copy(f32[1,2048,1536]{2,1,0:T(8,128)} %bitcast.395) | data formatting | bytes 25165824
  676.1 9.3 fusion.39
  733.5 10.6 %copy.285 = f32[1,2048,1536]{2,1,0:T(8,128)} copy(f32[1,2048,1536]{2,1,0:T(8,128)} %bitcast.394) | data formatting | bytes 25165824
  772.6 20.0 %reduce-scatter.11.cloned.1.call-done = bf16[192,8,864]{2,0,1:T(8,128)(2,1)} async-done(((bf16[768,8,864]{2,0,1:T(8,128)(2,1)}), bf16[192,8,864]{2,0,1:T(8,128)(2,1)}) %reduce-scatter.11.cloned.1.call-update) | async-done | bytes 2654224 | tf_op jit(solution)/shard_map/reduce_scatter | solution.py:129
  792.7 12.7 %fusion.32 = (bf16[2048,768]{1,0:T(8,128)(2,1)S(1)}, bf16[2048,768]{1,0:T(8,128)(2,1)}) fusion(f32[1,2048,1536]{2,1,0:T(8,128)} %add_bitcast_fusion.1, f32[1,2048,1536]{2,1,0:T(8,128)} %bitcast_dynamic-update-slice_fusion.1, f32[768]{0:T(1024)S(1)} %copy-done.50, f32[768]{0:T(1024)S(1)} %copy-done.51, f32[768]{0:T(1024)S(1)} %copy-done.52, ...), kind=kLoop, calls=%fused_computation.80 | loop fusion | flops 31457280 | bytes 31490048 | tf_op jit(solution)/shard_map/convert_element_type | solution.py:494
  810.0 8.9 copy.227
  832.8 9.1 convolution_convert_fusion.6
  856.3 11.7 %reduce-scatter.13.cloned.1.call-done = bf16[192,1,864]{2,0,1:T(8,128)(2,1)} async-done(((bf16[192,8,864]{2,0,1:T(8,128)(2,1)}), bf16[192,1,864]{2,0,1:T(8,128)(2,1)}) %reduce-scatter.13.cloned.1.call-update) | async-done | bytes 331792 | tf_op jit(solution)/shard_map/reduce_scatter | solution.py:141
  875.6 9.0 reshape.1291
  908.3 42.0 %reduce-scatter.15.cloned.1.call-done = bf16[1088,768]{1,0:T(8,128)(2,1)} async-done(((bf16[4352,768]{1,0:T(8,128)(2,1)}), bf16[1088,768]{1,0:T(8,128)(2,1)}) %reduce-scatter.15.cloned.1.call-update) | async-done | bytes 1671184 | tf_op jit(solution)/shard_map/reduce_scatter | solution.py:525
  958.7 9.5 multiply_reduce_fusion.1
  968.3 40.0 %all-reduce.3 = (f32[2,4,768]{2,1,0:T(4,128)S(1)}, f32[2,768]{1,0:T(2,128)S(1)}, f32[2,768]{1,0:T(2,128)S(1)}) all-reduce(f32[2,4,768]{2,1,0:T(4,128)S(1)} %pad_maximum_fusion.10, f32[2,768]{1,0:T(2,128)S(1)} %pad_maximum_fusion.12, f32[2,768]{1,0:T(2,128)S(1)} %pad_maximum_fusion.13), channel_id=9, replica_groups=mesh['dp'=8,'seq'=4] {'dp','seq'}, use_global_device_ids=true, to_apply=%region_24.25.clone | all-reduce | flops 9216 | bytes 73728
  (474 shorter events, 443.9 us)
Async XLA Ops:
  7.2 51.5 %all-gather.9.cloned.1.call-start = ((), (), s32[]{:S(2)}) async-start(), calls=%async_computation.5 | async-start | bytes 7864320 | tf_op jit(solution)/shard_map/all_gather | solution.py:414
  7.9 155.1 %all-gather.11.cloned.1.call-start = ((), (), s32[]{:S(2)}) async-start(), calls=%async_computation.6 | async-start | bytes 5898240 | tf_op jit(solution)/shard_map/all_gather | solution.py:101
  11.4 107.7 %copy-start.58 = (s32[4]{0:T(128)}, s32[4]{0:T(128)S(1)}, u32[]{:S(2)}) copy-start(s32[4]{0:T(128)S(1)} %broadcast_clamp_fusion.2) | copy-start | bytes 52
  11.5 107.0 %copy-start.59 = (s32[4]{0:T(128)}, s32[4]{0:T(128)S(1)}, u32[]{:S(2)}) copy-start(s32[4]{0:T(128)S(1)} %broadcast_clamp_fusion.3) | copy-start | bytes 52
  60.6 167.6 %all-gather.15.cloned.1.call-start = ((), (), s32[]{:S(2)}) async-start(), calls=%async_computation.13 | async-start | bytes 3096576 | tf_op jit(solution)/shard_map/all_gather | solution.py:99
  72.4 46.7 %copy-start.73 = (s32[2,4]{1,0:T(2,128)}, s32[2,4]{1,0:T(2,128)S(1)}, u32[]{:S(2)}) copy-start(s32[2,4]{1,0:T(2,128)S(1)} %copy.191) | copy-start | bytes 100
  83.3 35.9 %copy-start.74 = (s32[2,4]{1,0:T(2,128)}, s32[2,4]{1,0:T(2,128)S(1)}, u32[]{:S(2)}) copy-start(s32[2,4]{1,0:T(2,128)S(1)} %copy.195) | copy-start | bytes 100
  173.1 13.2 %copy-start.27 = (bf16[2,512,768]{2,1,0:T(8,128)(2,1)S(1)}, bf16[2,512,768]{2,1,0:T(8,128)(2,1)}, u32[]{:S(2)}) copy-start(bf16[2,512,768]{2,1,0:T(8,128)(2,1)} %param.12) | copy-start | bytes 4718596
  175.9 209.4 %all-gather.13.cloned.1.call-start = ((), (), s32[]{:S(2)}) async-start(), calls=%async_computation.7 | async-start | bytes 13762560 | tf_op jit(solution)/shard_map/all_gather | solution.py:101
  242.5 530.2 %reduce-scatter.9.cloned.1.call-start = ((), (), s32[]{:S(2)}) async-start(), calls=%async_computation.8 | async-start | bytes 3932160 | tf_op jit(solution)/shard_map/reduce_scatter | solution.py:500
  252.8 12.5 %copy-start.45 = (f32[768,12]{0,1:T(8,128)S(1)}, f32[768,12]{0,1:T(8,128)}, u32[]{:S(2)}) copy-start(f32[768,12]{0,1:T(8,128)} %reshape.1318) | copy-start | bytes 110596
  354.5 15.3 %copy-start.2 = (bf16[2,4,416,768]{2,3,1,0:T(8,128)(2,1)S(1)}, bf16[2,4,416,768]{2,3,1,0:T(8,128)(2,1)}, u32[]{:S(2)}) copy-start(bf16[2,4,416,768]{2,3,1,0:T(8,128)(2,1)} %copy.190) | copy-start | bytes 15335428
  406.7 41.0 %copy-start.20 = (bf16[96,8,8,384]{3,1,2,0:T(8,128)(2,1)}, bf16[96,8,8,384]{3,1,2,0:T(8,128)(2,1)S(1)}, u32[]{:S(2)}) copy-start(bf16[96,8,8,384]{3,1,2,0:T(8,128)(2,1)S(1)} %copy.245) | copy-start | bytes 14155780
  532.5 10.4 %copy-start.16 = (bf16[4,128,12,64]{1,0,3,2:T(4,128)(2,1)}, bf16[4,128,12,64]{1,0,3,2:T(4,128)(2,1)S(1)}, u32[]{:S(2)}) copy-start(bf16[4,128,12,64]{1,0,3,2:T(4,128)(2,1)S(1)} %reshape.1275) | copy-start | bytes 2359300
  573.9 16.8 %copy-start.18 = (bf16[4,128,12,64]{1,0,3,2:T(4,128)(2,1)S(1)}, bf16[4,128,12,64]{1,0,3,2:T(4,128)(2,1)}, u32[]{:S(2)}) copy-start(bf16[4,128,12,64]{1,0,3,2:T(4,128)(2,1)} %reshape.1286) | copy-start | bytes 2359300
  610.8 20.8 %copy-start.26 = (bf16[640,1536]{1,0:T(8,128)(2,1)}, bf16[640,1536]{1,0:T(8,128)(2,1)S(1)}, u32[]{:S(2)}) copy-start(bf16[640,1536]{1,0:T(8,128)(2,1)S(1)} %get-tuple-element.88) | copy-start | bytes 5898244
  621.3 10.3 %copy-start.81 = (s32[640]{0:T(1024)S(1)}, s32[640]{0:T(1024)}, u32[]{:S(2)}) copy-start(s32[640]{0:T(1024)} %eq.228) | copy-start | bytes 7684
  631.6 16.8 %slice-start.9 = ((s8[12582912]{0:T(1024)(128)(4,1)}), s8[4194304]{0:T(1024)(128)(4,1)S(1)}, s32[]{:S(2)}) async-start(s8[12582912]{0:T(1024)(128)(4,1)} %bitcast.406), calls=%async_computation.23 | async-start | bytes 8388608
  631.6 16.8 %slice-start.10 = ((s8[12582912]{0:T(1024)(128)(4,1)}), s8[4194304]{0:T(1024)(128)(4,1)S(1)}, s32[]{:S(2)}) async-start(s8[12582912]{0:T(1024)(128)(4,1)} %bitcast.406), calls=%async_computation.24 | async-start | bytes 8388608
  665.5 127.1 %reduce-scatter.11.cloned.1.call-start = ((), (), s32[]{:S(2)}) async-start(), calls=%async_computation.9 | async-start | bytes 13762560 | tf_op jit(solution)/shard_map/reduce_scatter | solution.py:129
  666.1 201.9 %reduce-scatter.13.cloned.1.call-start = ((), (), s32[]{:S(2)}) async-start(), calls=%async_computation.10 | async-start | bytes 3096576 | tf_op jit(solution)/shard_map/reduce_scatter | solution.py:141
  733.5 10.9 %slice-start.12 = ((s8[5111808]{0:T(1024)(128)(4,1)}), s8[4194304]{0:T(1024)(128)(4,1)S(1)}, s32[]{:S(2)}) async-start(s8[5111808]{0:T(1024)(128)(4,1)} %bitcast.408), calls=%async_computation.26 | async-start | bytes 8388608
  733.5 10.6 %copy-start.21 = (bf16[1,4,128,12,64]{2,1,4,3,0:T(4,128)(2,1)S(1)}, bf16[1,4,128,12,64]{2,1,4,3,0:T(4,128)(2,1)}, u32[]{:S(2)}) copy-start(bf16[1,4,128,12,64]{2,1,4,3,0:T(4,128)(2,1)} %copy.212) | copy-start | bytes 2359300
  733.5 10.9 %slice-start.13 = ((s8[5111808]{0:T(1024)(128)(4,1)}), s8[917504]{0:T(1024)(128)(4,1)S(1)}, s32[]{:S(2)}) async-start(s8[5111808]{0:T(1024)(128)(4,1)} %bitcast.408), calls=%async_computation.27 | async-start | bytes 1835008
  764.3 28.3 %copy-start.65 = (pred[2048]{0:T(1024)(128)(4,1)S(1)}, pred[2048]{0:T(1024)(128)(4,1)}, u32[]{:S(2)}) copy-start(pred[2048]{0:T(1024)(128)(4,1)} %get-tuple-element.235) | copy-start | bytes 6148
  764.3 28.3 %copy-start.67 = (pred[2048]{0:T(1024)(128)(4,1)S(1)}, pred[2048]{0:T(1024)(128)(4,1)}, u32[]{:S(2)}) copy-start(pred[2048]{0:T(1024)(128)(4,1)} %get-tuple-element.236) | copy-start | bytes 6148
  792.6 14.4 %copy-start.9 = (bf16[2048,768]{1,0:T(8,128)(2,1)S(1)}, bf16[2048,768]{1,0:T(8,128)(2,1)}, u32[]{:S(2)}) copy-start(bf16[2048,768]{1,0:T(8,128)(2,1)} %copy-done.8) | copy-start | bytes 9437188
  792.6 157.7 %reduce-scatter.15.cloned.1.call-start = ((), (), s32[]{:S(2)}) async-start(), calls=%async_computation.11 | async-start | bytes 8355840 | tf_op jit(solution)/shard_map/reduce_scatter | solution.py:525
  824.0 18.0 %slice-start.21 = ((s8[6291456]{0:T(1024)(128)(4,1)}), s8[2097152]{0:T(1024)(128)(4,1)S(1)}, s32[]{:S(2)}) async-start(s8[6291456]{0:T(1024)(128)(4,1)} %bitcast.474), calls=%async_computation.35 | async-start | bytes 4194304
  889.7 133.9 %reduce-scatter.17.cloned.1.call-start = ((), (), s32[]{:S(2)}) async-start(), calls=%async_computation.12 | async-start | bytes 1327104 | tf_op jit(solution)/shard_map/reduce_scatter | solution.py:141
  968.2 44.5 %copy-start.14 = (f32[1024,768]{1,0:T(8,128)S(1)}, f32[1024,768]{1,0:T(8,128)}, u32[]{:S(2)}) copy-start(f32[1024,768]{1,0:T(8,128)} %copy-done.13) | copy-start | bytes 9437188
  968.2 44.5 %copy-start.72 = (f32[1024]{0:T(1024)S(1)}, f32[1024]{0:T(1024)}, u32[]{:S(2)}) copy-start(f32[1024]{0:T(1024)} %copy-done.71) | copy-start | bytes 12292
  (86 other events, 325.1 us)
Sparse Core Ops, SparseCore 0:
  9.5 49.0 all-gather.8
  60.8 37.5 all-gather.10
  176.0 52.1 all-gather.14
  242.6 71.7 all-gather.12
  665.6 36.9 reduce-scatter.8
  705.0 87.5 reduce-scatter.10
  796.1 71.8 reduce-scatter.12
  889.8 60.4 reduce-scatter.14
  958.8 64.7 reduce-scatter.16

commit v12 on v10

--- a/solution.py
+++ b/solution.py
@@ -493,10 +493,7 @@
         ).astype(jnp.bfloat16)
         back_g = product_right(key_partial_g, wk) + product_right(value_partial_g, wv)
         back_g = back_g.reshape(1, group_len, width).astype(jnp.bfloat16)
-        if g == groups - 1:
-            back_own_g = back_g
-        else:
-            back_own_g = lax.psum_scatter(back_g, "seq", scatter_dimension=1, tiled=True)
+        back_own_g = lax.psum_scatter(back_g, "seq", scatter_dimension=1, tiled=True)
         pieces_back.append((grad_queries_g, pooled_g, key_partial_g, value_partial_g, back_own_g))
     grad_queries = jnp.concatenate([piece[0] for piece in pieces_back], axis=0)
     grad_pooled = jnp.concatenate([piece[1] for piece in pieces_back], axis=0)
@@ -516,23 +513,22 @@
     late_stacked, late_widths = stack_for_seq((grad_query_w, grad_key_w, grad_value_w))
     late_stacked, early_dp = lax.optimization_barrier((late_stacked, early_dp))
     seq_size = lax.psum(1, "seq")
-    late_flat = late_stacked.reshape(seq_size, -1, width)
-    back_flat = last_back.reshape(seq_size, -1, width)
-    joined = jnp.concatenate([late_flat, back_flat], axis=1)
-    chunk_rows = joined.shape[1]
-    joined = joined.reshape(seq_size * chunk_rows, width)
-    joined = lax.psum_scatter(joined, "seq", scatter_dimension=0, tiled=True)
-    late_reduced = joined[: late_flat.shape[1]].reshape(
-        late_stacked.shape[0] // seq_size, late_stacked.shape[1], late_stacked.shape[2]
-    )
-    back_last = joined[late_flat.shape[1] :].reshape(1, shard_rows, width)
-    back_own = jnp.concatenate([piece[4] for piece in pieces_back[:-1]] + [back_last], axis=0)
+    dp_size = lax.psum(1, "dp")
+    rows_each = late_stacked.shape[0] // seq_size
+    late_blocks = late_stacked.reshape(seq_size, rows_each, dp_size, late_stacked.shape[2])
+    late_blocks = jnp.transpose(late_blocks, (2, 0, 1, 3)).reshape(-1, late_stacked.shape[2])
+    late_reduced = lax.psum_scatter(late_blocks, ("dp", "seq"), scatter_dimension=0, tiled=True)
+    late_reduced = late_reduced.astype(jnp.float32)
+    late_dp, at = [], 0
+    for width_piece in late_widths:
+        late_dp.append(late_reduced[:, at : at + width_piece])
+        at += width_piece
+    back_own = jnp.concatenate([piece[4] for piece in pieces_back], axis=0)
     grad_tokens = (
         grad_mixed
         + product_right(grad_queries, wq)
         + back_own.reshape(groups * shard_rows, width).astype(jnp.float32)
     )
-    late_dp = reduce_dp_stage(((late_reduced, late_widths),))
     accum = (late_dp[0], late_dp[1], late_dp[2], early_dp[0], early_dp[1], early_dp[2].T)
     small_sums = (
         lax.psum_scatter(grad_pooling, ("dp", "seq"), scatter_dimension=2, tiled=True),

time: 1030 us -> 1030 us (level)
  waiting for transfers between devices: 93.9 us -> 109 us
  local copies, waits for them, and re-layouts: 278 us -> 265 us
  other arithmetic: 181 us -> 169 us
    reduce_scatter x1, waiting for transfers between devices: 19.9 us -> 40.3 us  [reduce_seq_stage(): reduced = lax.psum_scatter(stacked, 'seq', scatter_dimension=0, tiled=True)]
    reduce_scatter x2 -> x1, waiting for transfers between devices: 18.5 us -> 0.02 us  [reduce_dp_stage(): lax.psum_scatter(joined, 'dp', scatter_dimension=1, tiled=True)[:, 0]]
    reduce_scatter x1, waiting for transfers between devices: 42.2 us -> 55 us  [local(): lax.psum_scatter(late_blocks, ('dp', 'seq'), scatter_dimension=0, tiled=T...]
    reshape x4 -> x1, local copies, waits for them, and re-layouts: 16.4 us -> 5.46 us  [local(): late_stacked.reshape(seq_size, rows_each, dp_size, late_stacked.shape[2])]
    unnamed x232 -> x222, local copies, waits for them, and re-layouts: 66.9 us -> 64.3 us
  transfers between devices with their start and end apart: 9 -> 9, of which waited for: 5 -> 3; matrix products, arithmetic and copies ran while one was open for 39% -> 40% of each run, Pallas kernels for 0% -> 0%
where the time goes in v12:
time: 1030 us; the launch traced here: 1020 us
  matrix products  296 us (29%)
  local copies, waits for them, and re-layouts  265 us (26%)
  other arithmetic  169 us (16%)
  blocking collectives  118 us (11%)
  waiting for transfers between devices  109 us (11%)
  between operations  61.4 us (6%)
    dot_general x18, matrix products, product(): return jnp.dot(left, right, preferred_element_type=jnp.float32)  126 us
    unnamed x222, local copies, waits for them, and re-layouts  64.3 us
    reduce_scatter x1, waiting for transfers between devices, local(): lax.psum_scatter(late_blocks, ('dp', 'seq'), scatter_dimension=0, tiled=T...  55 us
    dot_general x8, matrix products, product_right(): lax.dot_general(left, right, (((1,), (1,)), ((), ())), preferred_element_...  48.8 us
    all_gather x1, blocking collectives, local(): small_full = lax.all_gather(small_local, ('dp', 'seq'), axis=1, tiled=True)  44.5 us
    reduce_scatter x1, waiting for transfers between devices, reduce_seq_stage(): reduced = lax.psum_scatter(stacked, 'seq', scatter_dimension=0, tiled=True)  40.3 us
    unnamed x1, blocking collectives  39.9 us
    dot_general x6, matrix products, product_left(): lax.dot_general(left, right, (((0,), (0,)), ((), ())), preferred_element_...  34.4 us
  transfers between devices with their start and end apart: 9, of which 3 were waited for; matrix products, arithmetic and copies ran while one was open for 40% of the time, Pallas kernels for 0%

profile of v12, /device:TPU:0, one launch (start us, length us, event | category | flops | bytes accessed | tf_op | source)
XLA Modules:
  0.0 1020.1 jit_solution(14472108540063794773)
XLA Ops:
  24.2 44.5 %all-gather.2 = f32[32,24,12]{1,2,0:T(8,128)S(1)} all-gather(f32[1,24,12]{1,2,0:T(8,128)S(1)} %maximum_bitcast_fusion.11), channel_id=1, replica_groups=mesh['dp'=8,'seq'=4] {'dp','seq'}, dimensions={0}, use_global_device_ids=true | all-gather | bytes 38016 | tf_op jit(solution)/shard_map/all_gather | solution.py:414
  69.0 33.5 %all-gather = bf16[192,2304]{0,1:T(8,128)(2,1)S(1)} all-gather(bf16[192,288]{0,1:T(8,128)(2,1)S(1)} %pad_maximum_fusion.8), channel_id=2, replica_groups=mesh['dp'=8,'seq'=4] {'dp'}, dimensions={1}, use_global_device_ids=true | all-gather | bytes 995328 | tf_op jit(solution)/shard_map/all_gather | solution.py:99
  185.7 9.8 convolution_convert_fusion
  195.5 12.4 %reshape.1287 = f32[2,512,4,768]{3,2,1,0:T(4,128)} reshape(bf16[4096,768]{1,0:T(8,128)(2,1)} %convolution_convert_fusion) | data formatting | bytes 18874368 | tf_op jit(solution)/shard_map/convert_element_type | solution.py:434
  207.8 12.4 %all-gather.15.cloned.1.call-done = bf16[8,864,192]{1,2,0:T(8,128)(2,1)} async-done(((bf16[1,864,192]{1,2,0:T(8,128)(2,1)}), bf16[8,864,192]{1,2,0:T(8,128)(2,1)}) %all-gather.15.cloned.1.call-update) | async-done | bytes 2654224 | tf_op jit(solution)/shard_map/all_gather | solution.py:99
  235.0 9.8 convolution_convert_fusion.1
  244.8 12.6 %reshape.1286 = f32[2,512,4,768]{3,2,1,0:T(4,128)} reshape(bf16[4096,768]{1,0:T(8,128)(2,1)} %convolution_convert_fusion.1) | data formatting | bytes 18874368 | tf_op jit(solution)/shard_map/convert_element_type | solution.py:433
  257.4 19.6 %multiply_reduce_fusion.2 = (bf16[2,512,768]{2,1,0:T(8,128)(2,1)S(1)}, bf16[2,512,768]{2,1,0:T(8,128)(2,1)S(1)}) fusion(f32[2,512,4,768]{3,2,1,0:T(4,128)} %reshape.1287, f32[4,768]{1,0:T(4,128)S(1)} %get-tuple-element.168, f32[2,512,4,768]{3,2,1,0:T(4,128)} %reshape.1286, f32[4,768]{1,0:T(4,128)S(1)} %copy-done.45), kind=kLoop, calls=%fused_computation.31 | loop fusion | flops 11010048 | bytes 28336128 | tf_op jit(solution)/shard_map/reduce_sum | solution.py:380
  293.8 8.5 fusion.160
  333.0 13.3 %fusion.171 = (f32[2,4,12,128]{3,2,1,0:T(8,128)S(1)}, f32[2,4,12,128,416]{3,4,2,1,0:T(8,128)}) fusion(pred[2,4,128,416]{2,3,1,0:T(8,128)(4,1)S(1)} %copy-done.41, bf16[2,4,416,12,64]{2,4,3,1,0:T(8,128)(2,1)} %bitcast.433, bf16[2,4,128,12,64]{2,1,0,4,3:T(4,128)(2,1)S(1)} %copy-done.29), kind=kOutput, calls=%fused_computation.447 | convolution fusion | flops 674759040 | bytes 27607040 | tf_op jit(solution)/shard_map/sub | solution.py:283
  346.3 15.3 %broadcast_divide_fusion = f32[2,4,12,128,416]{3,4,2,1,0:T(8,128)} fusion(f32[2,4,12,128,416]{3,4,2,1,0:T(8,128)} %get-tuple-element.211, f32[2,4,12,128]{3,2,1,0:T(8,128)S(1)} %get-tuple-element.210), kind=kLoop, calls=%fused_computation.45 | loop fusion | flops 5111808 | bytes 40943616 | tf_op jit(solution)/shard_map/div | solution.py:285
  361.6 10.0 fusion.88
  379.9 14.1 %fusion.158 = (bf16[768,8,384]{2,1,0:T(8,128)(2,1)}, bf16[768,8,384]{2,1,0:T(8,128)(2,1)}) fusion(bf16[768,8,864]{2,1,0:T(8,128)(2,1)} %all-gather.13.cloned.1.call-done), kind=kLoop, calls=%fused_computation.434 | loop fusion | bytes 18874368 | tf_op jit(solution)/shard_map/slice | solution.py:107
  404.0 34.9 %multiply_convert_fusion = (bf16[1024,3072]{1,0:T(8,128)(2,1)S(1)}, f32[1024,3072]{1,0:T(8,128)}, f32[1024,3072]{1,0:T(8,128)}) fusion(bf16[768,3072]{1,0:T(8,128)(2,1)S(1)} %bitcast.434, f32[1024,768]{1,0:T(8,128)S(1)} %get-tuple-element.213, f32[768]{0:T(1024)S(1)} %copy-done.76, f32[768]{0:T(1024)S(1)} %copy-done.63, f32[1024]{0:T(1024)S(1)} %fusion.135, ...), kind=kOutput, calls=%fused_computation.18 | convolution fusion | flops 5040242688 | bytes 39335936 | tf_op jit(solution)/shard_map/dot_general | solution.py:78
  457.4 18.4 %add_convert_fusion = bf16[1024,3072]{1,0:T(8,128)(2,1)} fusion(f32[1024,3072]{1,0:T(8,128)} %get-tuple-element.90, f32[1024,3072]{1,0:T(8,128)} %get-tuple-element.214, bf16[768,3072]{1,0:T(8,128)(2,1)} %bitcast.437, f32[1024,768]{1,0:T(8,128)} %copy-done.23, f32[1024]{0:T(1024)S(1)} %negate_multiply_fusion.2), kind=kOutput, calls=%fused_computation.17 | convolution fusion | flops 4877451264 | bytes 39325696 | tf_op jit(solution)/shard_map/dot_general | solution.py:88
  475.9 9.4 multiply_reduce_fusion.4
  510.4 11.2 %pad_maximum_fusion = bf16[768,8,864]{2,0,1:T(8,128)(2,1)} fusion(bf16[768,8,384]{2,0,1:T(8,128)(2,1)} %bitcast.421, bf16[768,8,384]{2,0,1:T(8,128)(2,1)} %bitcast.420, bf16[768,8,96]{2,0,1:T(8,128)(2,1)S(1)} %copy.203), kind=kLoop, calls=%fused_computation.34 | loop fusion | flops 31850496 | bytes 21233664 | tf_op jit(solution)/shard_map/concatenate | solution.py:127
  525.0 9.0 fusion.36
  547.4 17.5 %fusion.11 = (f32[4,12,128]{2,1,0:T(8,128)S(1)}, f32[4,12,128]{2,1,0:T(8,128)S(1)}, f32[4,12,128,416]{2,3,1,0:T(8,128)}) fusion(f32[2,4,12,128,416]{3,4,2,1,0:T(8,128)} %broadcast_divide_fusion, f32[4,12,128,416]{2,3,1,0:T(8,128)} %fusion.109, bf16[4,416,12,64]{1,3,2,0:T(8,128)(2,1)} %bitcast.426, bf16[4,128,12,64]{1,0,3,2:T(4,128)(2,1)} %copy-done.17), kind=kOutput, calls=%fused_computation.42 | convolution fusion | flops 337367040 | bytes 44285952 | tf_op jit(solution)/shard_map/gbqhd,gbkhd->gbhqk/dot_general | solution.py:302
  564.9 16.8 %fusion.41 = (bf16[4,12,128,416]{2,3,1,0:T(8,128)(2,1)S(1)}, bf16[4,12,128,416]{2,3,1,0:T(8,128)(2,1)}) fusion(f32[4,12,128,416]{2,3,1,0:T(8,128)} %get-tuple-element.218, f32[2,4,12,128,416]{3,4,2,1,0:T(8,128)} %broadcast_divide_fusion, f32[4,12,128]{2,1,0:T(8,128)S(1)} %get-tuple-element.51, f32[4,12,128,416]{2,3,1,0:T(8,128)} %fusion.109, ...), kind=kLoop, calls=%fused_computation.91 | loop fusion | flops 15335424 | bytes 51167232 | tf_op jit(solution)/shard_map/reshape.153
  612.2 10.4 %copy.282 = f32[1,2048,1536]{2,1,0:T(8,128)} copy(f32[1,2048,1536]{2,1,0:T(8,128)} %bitcast.397) | data formatting | bytes 25165824
  630.6 9.3 add_bitcast_fusion
  658.2 9.6 fusion.39
  705.5 13.7 %copy.281 = f32[1,2048,1536]{2,1,0:T(8,128)} copy(f32[1,2048,1536]{2,1,0:T(8,128)} %bitcast.396) | data formatting | bytes 25165824
  743.6 40.3 %reduce-scatter.11.cloned.1.call-done = bf16[192,8,864]{2,0,1:T(8,128)(2,1)} async-done(((bf16[768,8,864]{2,0,1:T(8,128)(2,1)}), bf16[192,8,864]{2,0,1:T(8,128)(2,1)}) %reduce-scatter.11.cloned.1.call-update) | async-done | bytes 2654224 | tf_op jit(solution)/shard_map/reduce_scatter | solution.py:129
  791.7 11.3 %fusion.32 = (bf16[2048,768]{1,0:T(8,128)(2,1)S(1)}, bf16[2048,768]{1,0:T(8,128)(2,1)S(1)}) fusion(f32[1,2048,1536]{2,1,0:T(8,128)} %add_bitcast_fusion.1, f32[1,2048,1536]{2,1,0:T(8,128)} %bitcast_dynamic-update-slice_fusion.1, f32[768]{0:T(1024)S(1)} %copy-done.47, f32[768]{0:T(1024)S(1)} %copy-done.48, f32[768]{0:T(1024)S(1)} %copy-done.49, ...), kind=kLoop, calls=%fused_computation.79 | loop fusion | flops 31457280 | bytes 31490048 | tf_op jit(solution)/shard_map/convert_element_type | solution.py:493
  826.6 9.2 copy.224
  840.7 8.9 copy.223
  849.6 9.2 convolution_convert_fusion.6
  872.6 10.2 copy.225
  908.4 39.9 %all-reduce.3 = (f32[2,4,768]{2,1,0:T(4,128)S(1)}, f32[2,768]{1,0:T(2,128)S(1)}, f32[2,768]{1,0:T(2,128)S(1)}) all-reduce(f32[2,4,768]{2,1,0:T(4,128)S(1)} %pad_maximum_fusion.9, f32[2,768]{1,0:T(2,128)S(1)} %pad_maximum_fusion.10, f32[2,768]{1,0:T(2,128)S(1)} %pad_maximum_fusion.11), channel_id=9, replica_groups=mesh['dp'=8,'seq'=4] {'dp','seq'}, use_global_device_ids=true, to_apply=%region_24.25.clone | all-reduce | flops 9216 | bytes 73728
  956.6 55.0 %reduce-scatter.17.cloned.1.call-done = bf16[192,288]{1,0:T(8,128)(2,1)} async-done(((bf16[6144,288]{1,0:T(8,128)(2,1)}), bf16[192,288]{1,0:T(8,128)(2,1)}) %reduce-scatter.17.cloned.1.call-update) | async-done | bytes 110608 | tf_op jit(solution)/shard_map/reduce_scatter | solution.py:520
  (454 shorter events, 399.0 us)
Async XLA Ops:
  7.2 95.3 %all-gather.9.cloned.1.call-start = ((), (), s32[]{:S(2)}) async-start(), calls=%async_computation.5 | async-start | bytes 7864320 | tf_op jit(solution)/shard_map/all_gather | solution.py:415
  7.9 145.2 %all-gather.11.cloned.1.call-start = ((), (), s32[]{:S(2)}) async-start(), calls=%async_computation.6 | async-start | bytes 5898240 | tf_op jit(solution)/shard_map/all_gather | solution.py:101
  104.4 115.8 %all-gather.15.cloned.1.call-start = ((), (), s32[]{:S(2)}) async-start(), calls=%async_computation.13 | async-start | bytes 3096576 | tf_op jit(solution)/shard_map/all_gather | solution.py:99
  163.4 15.2 %copy-start.26 = (bf16[2,512,768]{2,1,0:T(8,128)(2,1)S(1)}, bf16[2,512,768]{2,1,0:T(8,128)(2,1)}, u32[]{:S(2)}) copy-start(bf16[2,512,768]{2,1,0:T(8,128)(2,1)} %param.12) | copy-start | bytes 4718596
  167.0 209.6 %all-gather.13.cloned.1.call-start = ((), (), s32[]{:S(2)}) async-start(), calls=%async_computation.7 | async-start | bytes 13762560 | tf_op jit(solution)/shard_map/all_gather | solution.py:101
  234.4 509.1 %reduce-scatter.9.cloned.1.call-start = ((), (), s32[]{:S(2)}) async-start(), calls=%async_computation.8 | async-start | bytes 3932160 | tf_op jit(solution)/shard_map/reduce_scatter | solution.py:496
  244.8 12.6 %copy-start.45 = (f32[4,768]{1,0:T(4,128)S(1)}, f32[4,768]{1,0:T(4,128)}, u32[]{:S(2)}) copy-start(f32[4,768]{1,0:T(4,128)} %get-tuple-element.169) | copy-start | bytes 36868
  346.3 15.3 %copy-start.2 = (bf16[2,4,416,768]{2,3,1,0:T(8,128)(2,1)S(1)}, bf16[2,4,416,768]{2,3,1,0:T(8,128)(2,1)}, u32[]{:S(2)}) copy-start(bf16[2,4,416,768]{2,3,1,0:T(8,128)(2,1)} %copy.186) | copy-start | bytes 15335428
  397.7 41.1 %copy-start.20 = (bf16[96,8,8,384]{3,1,2,0:T(8,128)(2,1)}, bf16[96,8,8,384]{3,1,2,0:T(8,128)(2,1)S(1)}, u32[]{:S(2)}) copy-start(bf16[96,8,8,384]{3,1,2,0:T(8,128)(2,1)S(1)} %copy.241) | copy-start | bytes 14155780
  475.9 9.4 copy-start.77
  523.6 10.4 %copy-start.17 = (bf16[4,128,12,64]{1,0,3,2:T(4,128)(2,1)}, bf16[4,128,12,64]{1,0,3,2:T(4,128)(2,1)S(1)}, u32[]{:S(2)}) copy-start(bf16[4,128,12,64]{1,0,3,2:T(4,128)(2,1)S(1)} %reshape.1263) | copy-start | bytes 2359300
  564.9 16.8 %copy-start.19 = (bf16[4,128,12,64]{1,0,3,2:T(4,128)(2,1)S(1)}, bf16[4,128,12,64]{1,0,3,2:T(4,128)(2,1)}, u32[]{:S(2)}) copy-start(bf16[4,128,12,64]{1,0,3,2:T(4,128)(2,1)} %reshape.1274) | copy-start | bytes 2359300
  601.8 20.8 %copy-start.25 = (bf16[640,1536]{1,0:T(8,128)(2,1)}, bf16[640,1536]{1,0:T(8,128)(2,1)S(1)}, u32[]{:S(2)}) copy-start(bf16[640,1536]{1,0:T(8,128)(2,1)S(1)} %get-tuple-element.80) | copy-start | bytes 5898244
  612.2 10.4 %copy-start.69 = (s32[2048]{0:T(1024)S(1)}, s32[2048]{0:T(1024)}, u32[]{:S(2)}) copy-start(s32[2048]{0:T(1024)} %add_select_fusion) | copy-start | bytes 24580
  612.2 10.4 %copy-start.74 = (s32[640]{0:T(1024)S(1)}, s32[640]{0:T(1024)}, u32[]{:S(2)}) copy-start(s32[640]{0:T(1024)} %eq.228) | copy-start | bytes 7684
  622.6 17.3 %slice-start.10 = ((s8[12582912]{0:T(1024)(128)(4,1)}), s8[4194304]{0:T(1024)(128)(4,1)S(1)}, s32[]{:S(2)}) async-start(s8[12582912]{0:T(1024)(128)(4,1)} %bitcast.406), calls=%async_computation.24 | async-start | bytes 8388608
  622.6 17.3 %slice-start.11 = ((s8[12582912]{0:T(1024)(128)(4,1)}), s8[4194304]{0:T(1024)(128)(4,1)S(1)}, s32[]{:S(2)}) async-start(s8[12582912]{0:T(1024)(128)(4,1)} %bitcast.406), calls=%async_computation.25 | async-start | bytes 8388608
  630.6 9.3 slice-start.12
  656.9 127.0 %reduce-scatter.11.cloned.1.call-start = ((), (), s32[]{:S(2)}) async-start(), calls=%async_computation.9 | async-start | bytes 13762560 | tf_op jit(solution)/shard_map/reduce_scatter | solution.py:129
  657.5 207.0 %reduce-scatter.15.cloned.1.call-start = ((), (), s32[]{:S(2)}) async-start(), calls=%async_computation.11 | async-start | bytes 3096576 | tf_op jit(solution)/shard_map/reduce_scatter | solution.py:141
  694.3 24.9 %slice-start.15 = ((s8[5111808]{0:T(1024)(128)(4,1)}), s8[4194304]{0:T(1024)(128)(4,1)S(1)}, s32[]{:S(2)}) async-start(s8[5111808]{0:T(1024)(128)(4,1)} %bitcast.410), calls=%async_computation.29 | async-start | bytes 8388608
  697.7 21.5 %slice-start.16 = ((s8[5111808]{0:T(1024)(128)(4,1)}), s8[917504]{0:T(1024)(128)(4,1)S(1)}, s32[]{:S(2)}) async-start(s8[5111808]{0:T(1024)(128)(4,1)} %bitcast.410), calls=%async_computation.30 | async-start | bytes 1835008
  783.9 166.3 %reduce-scatter.13.cloned.1.call-start = ((), (), s32[]{:S(2)}) async-start(), calls=%async_computation.10 | async-start | bytes 3932160 | tf_op jit(solution)/shard_map/reduce_scatter | solution.py:496
  791.7 11.3 %copy-start.38 = (bf16[768,8,96]{0,2,1:T(8,128)(2,1)S(1)}, bf16[768,8,96]{0,2,1:T(8,128)(2,1)}, u32[]{:S(2)}) copy-start(bf16[768,8,96]{0,2,1:T(8,128)(2,1)} %copy.234) | copy-start | bytes 3538948
  809.8 201.8 %reduce-scatter.17.cloned.1.call-start = ((), (), s32[]{:S(2)}) async-start(), calls=%async_computation.12 | async-start | bytes 4866048 | tf_op jit(solution)/shard_map/reduce_scatter | solution.py:520
  826.6 9.2 copy-start.7
  840.7 18.1 %slice-start.22 = ((s8[6291456]{0:T(1024)(128)(4,1)}), s8[2097152]{0:T(1024)(128)(4,1)S(1)}, s32[]{:S(2)}) async-start(s8[6291456]{0:T(1024)(128)(4,1)} %bitcast.473), calls=%async_computation.36 | async-start | bytes 4194304
  849.6 9.2 slice-start.23
  890.8 10.7 %slice-start.3 = ((s8[12582912]{0:T(1024)(128)(4,1)}), s8[4194304]{0:T(1024)(128)(4,1)S(1)}, s32[]{:S(2)}) async-start(s8[12582912]{0:T(1024)(128)(4,1)} %bitcast.394), calls=%async_computation.17 | async-start | bytes 8388608
  890.8 10.7 %slice-start.4 = ((s8[12582912]{0:T(1024)(128)(4,1)}), s8[4194304]{0:T(1024)(128)(4,1)S(1)}, s32[]{:S(2)}) async-start(s8[12582912]{0:T(1024)(128)(4,1)} %bitcast.394), calls=%async_computation.18 | async-start | bytes 8388608
  908.4 43.4 %copy-start.13 = (f32[1024,768]{1,0:T(8,128)S(1)}, f32[1024,768]{1,0:T(8,128)}, u32[]{:S(2)}) copy-start(f32[1024,768]{1,0:T(8,128)} %copy-done.12) | copy-start | bytes 9437188
  908.4 43.4 %copy-start.68 = (f32[1024]{0:T(1024)S(1)}, f32[1024]{0:T(1024)}, u32[]{:S(2)}) copy-start(f32[1024]{0:T(1024)} %copy-done.67) | copy-start | bytes 12292
  (79 other events, 275.6 us)
Sparse Core Ops, SparseCore 0:
  9.5 51.3 all-gather.8
  104.5 34.4 all-gather.10
  167.1 53.0 all-gather.14
  234.6 71.7 all-gather.12
  657.0 36.8 reduce-scatter.8
  696.3 87.5 reduce-scatter.10
  787.4 71.6 reduce-scatter.14
  861.7 36.8 reduce-scatter.12
  904.1 107.4 reduce-scatter.16

commit v13 on v12

--- a/solution.py
+++ b/solution.py
@@ -110,9 +110,36 @@
     return pieces
 
 
-def gather_first(w_query, w_key, w_value, tie):
-    first, tie = gather_grouped((w_query, w_key, w_value), tie)
-    return split_grouped(first, (w_query.shape[1], w_key.shape[1], w_value.shape[1])), tie
+def code_exact(values, rows):
+    parts, rest = [], values
+    for _ in range(3):
+        part = lax.optimization_barrier(rest.astype(jnp.bfloat16))
+        parts.append(part)
+        rest = rest - part.astype(jnp.float32)
+    flat = jnp.concatenate([part.reshape(-1) for part in parts])
+    columns = -(-flat.shape[0] // rows)
+    flat = jnp.pad(flat, (0, rows * columns - flat.shape[0]))
+    return flat.reshape(rows, columns)
+
+
+def decode_exact(gathered, count, shape):
+    seq_size = lax.psum(1, "seq")
+    rows = gathered.shape[0] // seq_size
+    blocks = gathered.reshape(seq_size, rows, gathered.shape[1], gathered.shape[2])
+    blocks = jnp.transpose(blocks, (2, 0, 1, 3)).reshape(-1, rows * gathered.shape[2])
+    parts = blocks[:, : 3 * count].reshape(blocks.shape[0], 3, shape[0], shape[1])
+    parts = parts.astype(jnp.float32)
+    joined = (parts[:, 0] + parts[:, 1]) + parts[:, 2]
+    return jnp.transpose(joined, (1, 0, 2)).reshape(shape[0], -1)
+
+
+def gather_first(w_query, w_key, w_value, small_local, tie):
+    coded = code_exact(small_local, w_query.shape[0])
+    first, tie = gather_grouped((w_query, w_key, w_value, coded), tie)
+    widths = (w_query.shape[1], w_key.shape[1], w_value.shape[1])
+    at = sum(widths)
+    small_full = decode_exact(first[:, :, at:], small_local.size, small_local.shape)
+    return split_grouped(first[:, :, :at], widths), small_full, tie
 
 
 def gather_second(w_output, w_inner, w_outer):
@@ -411,10 +438,9 @@
     small_local = jnp.concatenate(
         [pool_weight.reshape(pool_rows_count, -1), ln_gain, ln_bias], axis=0
     )
-    small_full = lax.all_gather(small_local, ("dp", "seq"), axis=1, tiled=True)
     hidden_all = lax.all_gather(hidden_in, "seq", axis=1, tiled=True)
-    (wq, wk, wv), (hidden_all, small_full) = gather_first(
-        w_query, w_key, w_value, (hidden_all, small_full)
+    (wq, wk, wv), small_full, hidden_all = gather_first(
+        w_query, w_key, w_value, small_local, hidden_all
     )
     pool_full = small_full[:pool_rows_count].reshape(pool_weight.shape[0], pool_weight.shape[1], -1)
     gain_full = small_full[pool_rows_count : pool_rows_count + ln_gain.shape[0]]

time: 1030 us -> 1020 us (level)
  blocking collectives: 118 us -> 75.1 us
  waiting for transfers between devices: 109 us -> 130 us
  local copies, waits for them, and re-layouts: 265 us -> 280 us
    all_gather x1 -> x0, blocking collectives: 44.5 us -> none  [local(): small_full = lax.all_gather(small_local, ('dp', 'seq'), axis=1, tiled=True)]
    all_gather x2, waiting for transfers between devices: 0.01 us -> 26.8 us  [gather_grouped(): return (lax.all_gather(across, 'seq', axis=0, tiled=True), tie)]
    all_gather x1, waiting for transfers between devices: 12.4 us -> 0.01 us  [gather_grouped(): across = lax.all_gather(local_block, 'dp', axis=1, tiled=False)]
    unnamed x222 -> x247, local copies, waits for them, and re-layouts: 64.3 us -> 62.1 us
  transfers between devices with their start and end apart: 9 -> 9, of which waited for: 3 -> 4; matrix products, arithmetic and copies ran while one was open for 40% -> 42% of each run, Pallas kernels for 0% -> 0%
where the time goes in v13:
time: 1020 us; the launch traced here: 1010 us
  matrix products  297 us (29%)
  local copies, waits for them, and re-layouts  280 us (27%)
  other arithmetic  167 us (16%)
  waiting for transfers between devices  130 us (13%)
  blocking collectives  75.1 us (7%)
  between operations  61.1 us (6%)
    dot_general x18, matrix products, product(): return jnp.dot(left, right, preferred_element_type=jnp.float32)  127 us
    unnamed x247, local copies, waits for them, and re-layouts  62.1 us
    reduce_scatter x1, waiting for transfers between devices, local(): lax.psum_scatter(late_blocks, ('dp', 'seq'), scatter_dimension=0, tiled=T...  54.3 us
    dot_general x8, matrix products, product_right(): lax.dot_general(left, right, (((1,), (1,)), ((), ())), preferred_element_...  48.6 us
    reduce_scatter x1, waiting for transfers between devices, reduce_seq_stage(): reduced = lax.psum_scatter(stacked, 'seq', scatter_dimension=0, tiled=True)  41.8 us
    unnamed x1, blocking collectives  40 us
    all_gather x1, blocking collectives, gather_grouped(): across = lax.all_gather(local_block, 'dp', axis=1, tiled=False)  35.1 us
    dot_general x6, matrix products, product_left(): lax.dot_general(left, right, (((0,), (0,)), ((), ())), preferred_element_...  34.4 us
  transfers between devices with their start and end apart: 9, of which 4 were waited for; matrix products, arithmetic and copies ran while one was open for 42% of the time, Pallas kernels for 0%

profile of v13, /device:TPU:0, one launch (start us, length us, event | category | flops | bytes accessed | tf_op | source)
XLA Modules:
  0.0 1010.8 jit_solution(11104609277774313026)
XLA Ops:
  12.5 35.1 %all-gather.2 = bf16[8,293,192]{1,2,0:T(8,128)(2,1)S(1)} all-gather(bf16[1,293,192]{1,2,0:T(8,128)(2,1)S(1)} %maximum_bitcast_fusion.11), channel_id=2, replica_groups=mesh['dp'=8,'seq'=4] {'dp'}, dimensions={0}, use_global_device_ids=true | all-gather | bytes 1012608 | tf_op jit(solution)/shard_map/all_gather | solution.py:99
  71.5 26.8 %all-gather.11.cloned.1.call-done = bf16[768,8,293]{2,1,0:T(8,128)(2,1)} async-done(((bf16[192,8,293]{2,1,0:T(8,128)(2,1)}), bf16[768,8,293]{2,1,0:T(8,128)(2,1)}) %all-gather.11.cloned.1.call-update) | async-done | bytes 3600400 | tf_op jit(solution)/shard_map/all_gather | solution.py:101
  186.5 9.7 convolution_convert_fusion
  196.2 12.3 %reshape.1344 = f32[2,512,4,768]{3,2,1,0:T(4,128)} reshape(bf16[4096,768]{1,0:T(8,128)(2,1)} %convolution_convert_fusion) | data formatting | bytes 18874368 | tf_op jit(solution)/shard_map/convert_element_type | solution.py:460
  222.9 9.9 convolution_convert_fusion.1
  232.9 12.7 %reshape.1342 = f32[2,512,4,768]{3,2,1,0:T(4,128)} reshape(bf16[4096,768]{1,0:T(8,128)(2,1)} %convolution_convert_fusion.1) | data formatting | bytes 18874368 | tf_op jit(solution)/shard_map/convert_element_type | solution.py:459
  245.6 11.7 %multiply_reduce_fusion.2 = bf16[2,512,768]{2,1,0:T(8,128)(2,1)S(1)} fusion(f32[2,512,4,768]{3,2,1,0:T(4,128)} %reshape.1344, f32[4,768]{1,0:T(4,128)S(1)} %mul.347), kind=kLoop, calls=%fused_computation.31 | loop fusion | flops 5505024 | bytes 14168064 | tf_op jit(solution)/shard_map/reduce_sum | solution.py:407
  257.4 8.5 multiply_reduce_fusion.3
  283.0 8.6 fusion.168
  322.3 13.4 %fusion.180 = (f32[2,4,12,128]{3,2,1,0:T(8,128)S(1)}, f32[2,4,12,128,416]{3,4,2,1,0:T(8,128)}) fusion(pred[2,4,128,416]{2,3,1,0:T(8,128)(4,1)S(1)} %copy-done.41, bf16[2,4,416,12,64]{2,4,3,1,0:T(8,128)(2,1)} %bitcast.442, bf16[2,4,128,12,64]{2,1,0,4,3:T(4,128)(2,1)S(1)} %copy-done.29), kind=kOutput, calls=%fused_computation.450 | convolution fusion | flops 674759040 | bytes 27607040 | tf_op jit(solution)/shard_map/sub | solution.py:310
  335.6 15.7 %broadcast_divide_fusion = f32[2,4,12,128,416]{3,4,2,1,0:T(8,128)} fusion(f32[2,4,12,128,416]{3,4,2,1,0:T(8,128)} %get-tuple-element.209, f32[2,4,12,128]{3,2,1,0:T(8,128)S(1)} %get-tuple-element.208), kind=kLoop, calls=%fused_computation.45 | loop fusion | flops 5111808 | bytes 40943616 | tf_op jit(solution)/shard_map/div | solution.py:312
  351.3 10.0 fusion.88
  369.5 14.2 %fusion.166 = (bf16[768,8,384]{2,1,0:T(8,128)(2,1)}, bf16[768,8,384]{2,1,0:T(8,128)(2,1)}) fusion(bf16[768,8,864]{2,1,0:T(8,128)(2,1)} %all-gather.13.cloned.1.call-done), kind=kLoop, calls=%fused_computation.436 | loop fusion | bytes 18874368 | tf_op jit(solution)/shard_map/slice | solution.py:107
  393.5 34.6 %multiply_convert_fusion = (bf16[1024,3072]{1,0:T(8,128)(2,1)S(1)}, f32[1024,3072]{1,0:T(8,128)}, f32[1024,3072]{1,0:T(8,128)}) fusion(bf16[768,3072]{1,0:T(8,128)(2,1)S(1)} %bitcast.443, f32[1024,768]{1,0:T(8,128)S(1)} %get-tuple-element.211, f32[768]{0:T(1024)S(1)} %copy-done.86, f32[768]{0:T(1024)S(1)} %copy-done.62, f32[1024]{0:T(1024)S(1)} %fusion.141, ...), kind=kOutput, calls=%fused_computation.18 | convolution fusion | flops 5040242688 | bytes 39335936 | tf_op jit(solution)/shard_map/dot_general | solution.py:78
  446.8 18.4 %add_convert_fusion = bf16[1024,3072]{1,0:T(8,128)(2,1)} fusion(f32[1024,3072]{1,0:T(8,128)} %get-tuple-element.76, f32[1024,3072]{1,0:T(8,128)} %get-tuple-element.212, bf16[768,3072]{1,0:T(8,128)(2,1)} %bitcast.446, f32[1024,768]{1,0:T(8,128)} %copy-done.24, f32[1024]{0:T(1024)S(1)} %negate_multiply_fusion.2), kind=kOutput, calls=%fused_computation.17 | convolution fusion | flops 4877451264 | bytes 39325696 | tf_op jit(solution)/shard_map/dot_general | solution.py:88
  465.1 9.4 multiply_reduce_fusion.4
  499.9 11.2 %pad_maximum_fusion = bf16[768,8,864]{2,0,1:T(8,128)(2,1)} fusion(bf16[768,8,384]{2,0,1:T(8,128)(2,1)} %bitcast.429, bf16[768,8,384]{2,0,1:T(8,128)(2,1)} %bitcast.428, bf16[768,8,96]{2,0,1:T(8,128)(2,1)S(1)} %copy.258), kind=kLoop, calls=%fused_computation.34 | loop fusion | flops 31850496 | bytes 21233664 | tf_op jit(solution)/shard_map/concatenate | solution.py:154
  514.5 9.0 fusion.36
  536.6 17.5 %fusion.11 = (f32[4,12,128]{2,1,0:T(8,128)S(1)}, f32[4,12,128]{2,1,0:T(8,128)S(1)}, f32[4,12,128,416]{2,3,1,0:T(8,128)}) fusion(f32[2,4,12,128,416]{3,4,2,1,0:T(8,128)} %broadcast_divide_fusion, f32[4,12,128,416]{2,3,1,0:T(8,128)} %fusion.109, bf16[4,416,12,64]{1,3,2,0:T(8,128)(2,1)} %bitcast.434, bf16[4,128,12,64]{1,0,3,2:T(4,128)(2,1)} %copy-done.18), kind=kOutput, calls=%fused_computation.42 | convolution fusion | flops 337367040 | bytes 44285952 | tf_op jit(solution)/shard_map/gbqhd,gbkhd->gbhqk/dot_general | solution.py:329
  554.1 16.8 %fusion.41 = (bf16[4,12,128,416]{2,3,1,0:T(8,128)(2,1)S(1)}, bf16[4,12,128,416]{2,3,1,0:T(8,128)(2,1)}) fusion(f32[4,12,128,416]{2,3,1,0:T(8,128)} %get-tuple-element.216, f32[2,4,12,128,416]{3,4,2,1,0:T(8,128)} %broadcast_divide_fusion, f32[4,12,128]{2,1,0:T(8,128)S(1)} %get-tuple-element.49, f32[4,12,128,416]{2,3,1,0:T(8,128)} %fusion.109, ...), kind=kLoop, calls=%fused_computation.91 | loop fusion | flops 15335424 | bytes 51167232 | tf_op jit(solution)/shard_map/reshape.169
  601.5 10.4 %copy.346 = f32[1,2048,1536]{2,1,0:T(8,128)} copy(f32[1,2048,1536]{2,1,0:T(8,128)} %bitcast.405) | data formatting | bytes 25165824
  619.9 9.3 add_bitcast_fusion
  647.6 9.1 fusion.39
  693.8 14.3 %copy.345 = f32[1,2048,1536]{2,1,0:T(8,128)} copy(f32[1,2048,1536]{2,1,0:T(8,128)} %bitcast.404) | data formatting | bytes 25165824
  732.4 41.8 %reduce-scatter.11.cloned.1.call-done = bf16[192,8,864]{2,0,1:T(8,128)(2,1)} async-done(((bf16[768,8,864]{2,0,1:T(8,128)(2,1)}), bf16[192,8,864]{2,0,1:T(8,128)(2,1)}) %reduce-scatter.11.cloned.1.call-update) | async-done | bytes 2654224 | tf_op jit(solution)/shard_map/reduce_scatter | solution.py:156
  782.1 11.3 %fusion.32 = (bf16[2048,768]{1,0:T(8,128)(2,1)S(1)}, bf16[2048,768]{1,0:T(8,128)(2,1)S(1)}) fusion(f32[1,2048,1536]{2,1,0:T(8,128)} %add_bitcast_fusion.1, f32[1,2048,1536]{2,1,0:T(8,128)} %bitcast_dynamic-update-slice_fusion.1, f32[768]{0:T(1024)S(1)} %copy-done.48, f32[768]{0:T(1024)S(1)} %copy-done.49, f32[768]{0:T(1024)S(1)} %copy-done.50, ...), kind=kLoop, calls=%fused_computation.79 | loop fusion | flops 31457280 | bytes 31490048 | tf_op jit(solution)/shard_map/convert_element_type | solution.py:519
  816.8 9.3 copy.287
  831.1 8.9 copy.286
  840.0 9.2 convolution_convert_fusion.6
  862.9 10.1 copy.288
  899.7 40.0 %all-reduce.4 = (f32[2,4,768]{2,1,0:T(4,128)S(1)}, f32[2,768]{1,0:T(2,128)S(1)}, f32[2,768]{1,0:T(2,128)S(1)}) all-reduce(f32[2,4,768]{2,1,0:T(4,128)S(1)} %pad_maximum_fusion.8, f32[2,768]{1,0:T(2,128)S(1)} %pad_maximum_fusion.10, f32[2,768]{1,0:T(2,128)S(1)} %pad_maximum_fusion.11), channel_id=9, replica_groups=mesh['dp'=8,'seq'=4] {'dp','seq'}, use_global_device_ids=true, to_apply=%region_24.25.clone | all-reduce | flops 9216 | bytes 73728
  947.9 54.3 %reduce-scatter.17.cloned.1.call-done = bf16[192,288]{1,0:T(8,128)(2,1)} async-done(((bf16[6144,288]{1,0:T(8,128)(2,1)}), bf16[192,288]{1,0:T(8,128)(2,1)}) %reduce-scatter.17.cloned.1.call-update) | async-done | bytes 110608 | tf_op jit(solution)/shard_map/reduce_scatter | solution.py:546
  (520 shorter events, 416.2 us)
Async XLA Ops:
  7.2 51.5 %all-gather.9.cloned.1.call-start = ((), (), s32[]{:S(2)}) async-start(), calls=%async_computation.5 | async-start | bytes 7864320 | tf_op jit(solution)/shard_map/all_gather | solution.py:441
  7.9 90.4 %all-gather.11.cloned.1.call-start = ((), (), s32[]{:S(2)}) async-start(), calls=%async_computation.6 | async-start | bytes 5898240 | tf_op jit(solution)/shard_map/all_gather | solution.py:101
  58.7 149.8 %all-gather.15.cloned.1.call-start = ((), (), s32[]{:S(2)}) async-start(), calls=%async_computation.13 | async-start | bytes 3096576 | tf_op jit(solution)/shard_map/all_gather | solution.py:99
  58.8 45.0 %copy-start.64 = (s32[2,8]{1,0:T(2,128)}, s32[2,8]{1,0:T(2,128)S(1)}, u32[]{:S(2)}) copy-start(s32[2,8]{1,0:T(2,128)S(1)} %copy.240) | copy-start | bytes 196
  66.7 37.2 %copy-start.82 = (pred[4,128]{1,0:T(4,128)(4,1)}, pred[4,128]{1,0:T(4,128)(4,1)S(1)}, u32[]{:S(2)}) copy-start(pred[4,128]{1,0:T(4,128)(4,1)S(1)} %get-tuple-element.198) | copy-start | bytes 1540
  66.7 37.2 %copy-start.84 = (pred[4,128]{1,0:T(4,128)(4,1)}, pred[4,128]{1,0:T(4,128)(4,1)S(1)}, u32[]{:S(2)}) copy-start(pred[4,128]{1,0:T(4,128)(4,1)S(1)} %get-tuple-element.199) | copy-start | bytes 1540
  108.6 33.7 %copy-start.68 = (s32[1,4,160]{2,1,0:T(4,128)S(1)}, s32[1,4,160]{2,1,0:T(4,128)}, u32[]{:S(2)}) copy-start(s32[1,4,160]{2,1,0:T(4,128)} %get-tuple-element.170) | copy-start | bytes 7684
  108.6 49.4 %copy-start.65 = (s32[2,8]{1,0:T(2,128)S(1)}, s32[2,8]{1,0:T(2,128)}, u32[]{:S(2)}) copy-start(s32[2,8]{1,0:T(2,128)} %copy-done.64) | copy-start | bytes 196
  108.6 49.5 %copy-start.67 = (s32[2,4,128]{2,1,0:T(4,128)S(1)}, s32[2,4,128]{2,1,0:T(4,128)}, u32[]{:S(2)}) copy-start(s32[2,4,128]{2,1,0:T(4,128)} %select_reduce_fusion.2) | copy-start | bytes 12292
  108.6 49.5 %copy-start.81 = (s32[4,128]{1,0:T(4,128)S(1)}, s32[4,128]{1,0:T(4,128)}, u32[]{:S(2)}) copy-start(s32[4,128]{1,0:T(4,128)} %get-tuple-element.195) | copy-start | bytes 6148
  108.6 49.5 %copy-start.83 = (pred[4,128]{1,0:T(4,128)(4,1)S(1)}, pred[4,128]{1,0:T(4,128)(4,1)}, u32[]{:S(2)}) copy-start(pred[4,128]{1,0:T(4,128)(4,1)} %copy-done.82) | copy-start | bytes 1540
  108.6 49.5 %copy-start.85 = (pred[4,128]{1,0:T(4,128)(4,1)S(1)}, pred[4,128]{1,0:T(4,128)(4,1)}, u32[]{:S(2)}) copy-start(pred[4,128]{1,0:T(4,128)(4,1)} %copy-done.84) | copy-start | bytes 1540
  108.6 49.7 %copy-start.72 = (pred[2,4,128]{2,1,0:T(4,128)(4,1)S(1)}, pred[2,4,128]{2,1,0:T(4,128)(4,1)}, u32[]{:S(2)}) copy-start(pred[2,4,128]{2,1,0:T(4,128)(4,1)} %fusion.143) | copy-start | bytes 3076
  108.7 49.7 %copy-start.74 = (pred[2,4,160]{2,1,0:T(4,128)(4,1)S(1)}, pred[2,4,160]{2,1,0:T(4,128)(4,1)}, u32[]{:S(2)}) copy-start(pred[2,4,160]{2,1,0:T(4,128)(4,1)} %pad_add_fusion.3) | copy-start | bytes 3844
  108.7 49.7 %copy-start.76 = (pred[2,4,160]{2,1,0:T(4,128)(4,1)S(1)}, pred[2,4,160]{2,1,0:T(4,128)(4,1)}, u32[]{:S(2)}) copy-start(pred[2,4,160]{2,1,0:T(4,128)(4,1)} %get-tuple-element.79) | copy-start | bytes 3844
  108.7 51.2 %copy-start.73 = (pred[2,4,256]{2,1,0:T(4,128)(4,1)S(1)}, pred[2,4,256]{2,1,0:T(4,128)(4,1)}, u32[]{:S(2)}) copy-start(pred[2,4,256]{2,1,0:T(4,128)(4,1)} %pad_add_fusion.2) | copy-start | bytes 6148
  108.7 51.2 %copy-start.75 = (pred[2,4,256]{2,1,0:T(4,128)(4,1)S(1)}, pred[2,4,256]{2,1,0:T(4,128)(4,1)}, u32[]{:S(2)}) copy-start(pred[2,4,256]{2,1,0:T(4,128)(4,1)} %get-tuple-element.77) | copy-start | bytes 6148
  111.5 254.8 %all-gather.13.cloned.1.call-start = ((), (), s32[]{:S(2)}) async-start(), calls=%async_computation.7 | async-start | bytes 13762560 | tf_op jit(solution)/shard_map/all_gather | solution.py:101
  222.9 509.6 %reduce-scatter.9.cloned.1.call-start = ((), (), s32[]{:S(2)}) async-start(), calls=%async_computation.8 | async-start | bytes 3932160 | tf_op jit(solution)/shard_map/reduce_scatter | solution.py:522
  387.3 40.9 %copy-start.21 = (bf16[96,8,8,384]{3,1,2,0:T(8,128)(2,1)}, bf16[96,8,8,384]{3,1,2,0:T(8,128)(2,1)S(1)}, u32[]{:S(2)}) copy-start(bf16[96,8,8,384]{3,1,2,0:T(8,128)(2,1)S(1)} %copy.305) | copy-start | bytes 14155780
  591.1 20.8 %copy-start.25 = (bf16[640,1536]{1,0:T(8,128)(2,1)}, bf16[640,1536]{1,0:T(8,128)(2,1)S(1)}, u32[]{:S(2)}) copy-start(bf16[640,1536]{1,0:T(8,128)(2,1)S(1)} %get-tuple-element.66) | copy-start | bytes 5898244
  611.9 17.3 %slice-start.10 = ((s8[12582912]{0:T(1024)(128)(4,1)}), s8[4194304]{0:T(1024)(128)(4,1)S(1)}, s32[]{:S(2)}) async-start(s8[12582912]{0:T(1024)(128)(4,1)} %bitcast.414), calls=%async_computation.24 | async-start | bytes 8388608
  611.9 17.3 %slice-start.11 = ((s8[12582912]{0:T(1024)(128)(4,1)}), s8[4194304]{0:T(1024)(128)(4,1)S(1)}, s32[]{:S(2)}) async-start(s8[12582912]{0:T(1024)(128)(4,1)} %bitcast.414), calls=%async_computation.25 | async-start | bytes 8388608
  646.2 128.0 %reduce-scatter.11.cloned.1.call-start = ((), (), s32[]{:S(2)}) async-start(), calls=%async_computation.9 | async-start | bytes 13762560 | tf_op jit(solution)/shard_map/reduce_scatter | solution.py:156
  646.8 208.0 %reduce-scatter.15.cloned.1.call-start = ((), (), s32[]{:S(2)}) async-start(), calls=%async_computation.11 | async-start | bytes 3096576 | tf_op jit(solution)/shard_map/reduce_scatter | solution.py:168
  683.5 24.6 %slice-start.15 = ((s8[5111808]{0:T(1024)(128)(4,1)}), s8[4194304]{0:T(1024)(128)(4,1)S(1)}, s32[]{:S(2)}) async-start(s8[5111808]{0:T(1024)(128)(4,1)} %bitcast.418), calls=%async_computation.29 | async-start | bytes 8388608
  687.0 21.2 %slice-start.16 = ((s8[5111808]{0:T(1024)(128)(4,1)}), s8[917504]{0:T(1024)(128)(4,1)S(1)}, s32[]{:S(2)}) async-start(s8[5111808]{0:T(1024)(128)(4,1)} %bitcast.418), calls=%async_computation.30 | async-start | bytes 1835008
  774.3 167.3 %reduce-scatter.13.cloned.1.call-start = ((), (), s32[]{:S(2)}) async-start(), calls=%async_computation.10 | async-start | bytes 3932160 | tf_op jit(solution)/shard_map/reduce_scatter | solution.py:522
  800.2 202.1 %reduce-scatter.17.cloned.1.call-start = ((), (), s32[]{:S(2)}) async-start(), calls=%async_computation.12 | async-start | bytes 4866048 | tf_op jit(solution)/shard_map/reduce_scatter | solution.py:546
  831.1 18.1 %slice-start.22 = ((s8[6291456]{0:T(1024)(128)(4,1)}), s8[2097152]{0:T(1024)(128)(4,1)S(1)}, s32[]{:S(2)}) async-start(s8[6291456]{0:T(1024)(128)(4,1)} %bitcast.484), calls=%async_computation.36 | async-start | bytes 4194304
  899.6 43.5 %copy-start.14 = (f32[1024,768]{1,0:T(8,128)S(1)}, f32[1024,768]{1,0:T(8,128)}, u32[]{:S(2)}) copy-start(f32[1024,768]{1,0:T(8,128)} %copy-done.13) | copy-start | bytes 9437188
  899.6 43.5 %copy-start.71 = (f32[1024]{0:T(1024)S(1)}, f32[1024]{0:T(1024)}, u32[]{:S(2)}) copy-start(f32[1024]{0:T(1024)} %copy-done.70) | copy-start | bytes 12292
  (93 other events, 453.1 us)
Sparse Core Ops, SparseCore 0:
  9.5 49.0 all-gather.8
  60.8 37.4 all-gather.10
  111.6 56.0 all-gather.14
  223.0 73.1 all-gather.12
  646.3 37.8 reduce-scatter.8
  686.7 87.5 reduce-scatter.10
  777.8 71.5 reduce-scatter.14
  851.9 37.0 reduce-scatter.12
  894.5 107.7 reduce-scatter.16

commit v14 on v13

--- a/solution.py
+++ b/solution.py
@@ -439,16 +439,17 @@
         [pool_weight.reshape(pool_rows_count, -1), ln_gain, ln_bias], axis=0
     )
     hidden_all = lax.all_gather(hidden_in, "seq", axis=1, tiled=True)
-    (wq, wk, wv), small_full, hidden_all = gather_first(
-        w_query, w_key, w_value, small_local, hidden_all
+    groups, shard_rows, width = hidden_in.shape
+    seq_index = lax.axis_index("seq")
+    offsets = STRIDE * branch_blocks
+    starts, mask = block_geometry(seq_index, groups, shard_rows, offsets)
+    (wq, wk, wv), small_full, (hidden_all, starts, mask) = gather_first(
+        w_query, w_key, w_value, small_local, (hidden_all, starts, mask)
     )
     pool_full = small_full[:pool_rows_count].reshape(pool_weight.shape[0], pool_weight.shape[1], -1)
     gain_full = small_full[pool_rows_count : pool_rows_count + ln_gain.shape[0]]
     bias_full = small_full[pool_rows_count + ln_gain.shape[0] :]
     groups, shard_rows, width = hidden_in.shape
-    seq_index = lax.axis_index("seq")
-    offsets = STRIDE * branch_blocks
-    starts, mask = block_geometry(seq_index, groups, shard_rows, offsets)
 
     group_len = hidden_all.shape[1]
     tokens = hidden_in.reshape(groups * shard_rows, width)

time: 1020 us -> 999 us (0.979)
  waiting for transfers between devices: 130 us -> 98.6 us
  between operations: 61.1 us -> 76.6 us
    all_gather x2, waiting for transfers between devices: 26.8 us -> 0.01 us  [gather_grouped(): return (lax.all_gather(across, 'seq', axis=0, tiled=True), tie)]
    unnamed x247 -> x215, local copies, waits for them, and re-layouts: 62.1 us -> 62.1 us
  transfers between devices with their start and end apart: 9 -> 9, of which waited for: 4 -> 3; matrix products, arithmetic and copies ran while one was open for 42% -> 43% of each run, Pallas kernels for 0% -> 0%
where the time goes in v14:
time: 999 us; the launch traced here: 989 us
  matrix products  297 us (30%)
  local copies, waits for them, and re-layouts  280 us (28%)
  other arithmetic  161 us (16%)
  waiting for transfers between devices  98.6 us (10%)
  between operations  76.6 us (8%)
  blocking collectives  75 us (8%)
    dot_general x18, matrix products, product(): return jnp.dot(left, right, preferred_element_type=jnp.float32)  127 us
    unnamed x215, local copies, waits for them, and re-layouts  62.1 us
    reduce_scatter x1, waiting for transfers between devices, local(): lax.psum_scatter(late_blocks, ('dp', 'seq'), scatter_dimension=0, tiled=T...  54 us
    dot_general x8, matrix products, product_right(): lax.dot_general(left, right, (((1,), (1,)), ((), ())), preferred_element_...  48.6 us
    reduce_scatter x1, waiting for transfers between devices, reduce_seq_stage(): reduced = lax.psum_scatter(stacked, 'seq', scatter_dimension=0, tiled=True)  42.2 us
    unnamed x1, blocking collectives  40 us
    all_gather x1, blocking collectives, gather_grouped(): across = lax.all_gather(local_block, 'dp', axis=1, tiled=False)  35.1 us
    dot_general x6, matrix products, product_left(): lax.dot_general(left, right, (((0,), (0,)), ((), ())), preferred_element_...  34.4 us
  transfers between devices with their start and end apart: 9, of which 3 were waited for; matrix products, arithmetic and copies ran while one was open for 43% of the time, Pallas kernels for 0%

profile of v14, /device:TPU:0, one launch (start us, length us, event | category | flops | bytes accessed | tf_op | source)
XLA Modules:
  0.0 989.0 jit_solution(14519814877666108997)
XLA Ops:
  13.8 35.1 %all-gather.2 = bf16[8,293,192]{1,2,0:T(8,128)(2,1)S(1)} all-gather(bf16[1,293,192]{1,2,0:T(8,128)(2,1)S(1)} %maximum_bitcast_fusion.11), channel_id=2, replica_groups=mesh['dp'=8,'seq'=4] {'dp'}, dimensions={0}, use_global_device_ids=true | all-gather | bytes 1012608 | tf_op jit(solution)/shard_map/all_gather | solution.py:99
  165.8 9.8 convolution_convert_fusion
  175.5 12.3 %reshape.1392 = f32[2,512,4,768]{3,2,1,0:T(4,128)} reshape(bf16[4096,768]{1,0:T(8,128)(2,1)} %convolution_convert_fusion) | data formatting | bytes 18874368 | tf_op jit(solution)/shard_map/convert_element_type | solution.py:461
  202.2 9.9 %convolution_convert_fusion.1 = bf16[4096,768]{1,0:T(8,128)(2,1)} fusion(bf16[4096,768]{1,0:T(8,128)(2,1)} %bitcast.498, bf16[768,768]{0,1:T(8,128)(2,1)S(1)} %bitcast.484), kind=kOutput, calls=%fused_computation.54 | convolution fusion | flops 4834983936 | bytes 13762560 | tf_op jit(solution)/shard_map/dot_general | solution.py:78
  212.1 12.7 %reshape.1390 = f32[2,512,4,768]{3,2,1,0:T(4,128)} reshape(bf16[4096,768]{1,0:T(8,128)(2,1)} %convolution_convert_fusion.1) | data formatting | bytes 18874368 | tf_op jit(solution)/shard_map/convert_element_type | solution.py:460
  224.8 11.7 %multiply_reduce_fusion.2 = bf16[2,512,768]{2,1,0:T(8,128)(2,1)S(1)} fusion(f32[2,512,4,768]{3,2,1,0:T(4,128)} %reshape.1392, f32[4,768]{1,0:T(4,128)S(1)} %mul.352), kind=kLoop, calls=%fused_computation.31 | loop fusion | flops 5505024 | bytes 14168064 | tf_op jit(solution)/shard_map/reduce_sum | solution.py:407
  236.6 8.5 multiply_reduce_fusion.3
  261.2 8.6 fusion.170
  292.3 8.2 copy.244
  300.5 13.3 %fusion.182 = (f32[2,4,12,128]{3,2,1,0:T(8,128)S(1)}, f32[2,4,12,128,416]{3,4,2,1,0:T(8,128)}) fusion(pred[2,4,128,416]{2,3,1,0:T(8,128)(4,1)S(1)} %copy-done.41, bf16[2,4,416,12,64]{2,4,3,1,0:T(8,128)(2,1)} %bitcast.458, bf16[2,4,128,12,64]{2,1,0,4,3:T(4,128)(2,1)S(1)} %copy-done.29), kind=kOutput, calls=%fused_computation.456 | convolution fusion | flops 674759040 | bytes 27607040 | tf_op jit(solution)/shard_map/sub | solution.py:310
  313.8 15.3 %broadcast_divide_fusion = f32[2,4,12,128,416]{3,4,2,1,0:T(8,128)} fusion(f32[2,4,12,128,416]{3,4,2,1,0:T(8,128)} %get-tuple-element.229, f32[2,4,12,128]{3,2,1,0:T(8,128)S(1)} %get-tuple-element.228), kind=kLoop, calls=%fused_computation.45 | loop fusion | flops 5111808 | bytes 40943616 | tf_op jit(solution)/shard_map/div | solution.py:312
  329.1 10.0 %fusion.88 = bf16[2,4,128,12,64]{2,4,3,1,0:T(8,128)(2,1)} fusion(bf16[2,4,416,12,64]{2,4,3,1,0:T(8,128)(2,1)S(1)} %bitcast.438, f32[2,4,12,128,416]{3,4,2,1,0:T(8,128)} %broadcast_divide_fusion), kind=kOutput, calls=%fused_computation.204 | convolution fusion | flops 660209664 | bytes 27131904 | tf_op jit(solution)/shard_map/gbhqk,gbkhd->gbqhd/dot_general | solution.py:313
  347.7 14.2 %fusion.168 = (bf16[768,8,384]{2,1,0:T(8,128)(2,1)}, bf16[768,8,384]{2,1,0:T(8,128)(2,1)}) fusion(bf16[768,8,864]{2,1,0:T(8,128)(2,1)} %all-gather.13.cloned.1.call-done), kind=kLoop, calls=%fused_computation.442 | loop fusion | bytes 18874368 | tf_op jit(solution)/shard_map/slice | solution.py:107
  371.8 34.7 %multiply_convert_fusion = (bf16[1024,3072]{1,0:T(8,128)(2,1)S(1)}, f32[1024,3072]{1,0:T(8,128)}, f32[1024,3072]{1,0:T(8,128)}) fusion(bf16[768,3072]{1,0:T(8,128)(2,1)S(1)} %bitcast.459, f32[1024,768]{1,0:T(8,128)S(1)} %get-tuple-element.231, f32[768]{0:T(1024)S(1)} %copy-done.68, f32[768]{0:T(1024)S(1)} %copy-done.61, f32[1024]{0:T(1024)S(1)} %fusion.143, ...), kind=kOutput, calls=%fused_computation.18 | convolution fusion | flops 5040242688 | bytes 39335936 | tf_op jit(solution)/shard_map/dot_general | solution.py:78
  425.1 18.5 %add_convert_fusion = bf16[1024,3072]{1,0:T(8,128)(2,1)} fusion(f32[1024,3072]{1,0:T(8,128)} %get-tuple-element.86, f32[1024,3072]{1,0:T(8,128)} %get-tuple-element.232, bf16[768,3072]{1,0:T(8,128)(2,1)} %bitcast.462, f32[1024,768]{1,0:T(8,128)} %copy-done.24, f32[1024]{0:T(1024)S(1)} %negate_multiply_fusion.2), kind=kOutput, calls=%fused_computation.17 | convolution fusion | flops 4877451264 | bytes 39325696 | tf_op jit(solution)/shard_map/dot_general | solution.py:88
  443.6 9.4 multiply_reduce_fusion.4
  478.4 11.3 %pad_maximum_fusion = bf16[768,8,864]{2,0,1:T(8,128)(2,1)} fusion(bf16[768,8,384]{2,0,1:T(8,128)(2,1)} %bitcast.445, bf16[768,8,384]{2,0,1:T(8,128)(2,1)} %bitcast.444, bf16[768,8,96]{2,0,1:T(8,128)(2,1)S(1)} %copy.258), kind=kLoop, calls=%fused_computation.34 | loop fusion | flops 31850496 | bytes 21233664 | tf_op jit(solution)/shard_map/concatenate | solution.py:154
  493.0 9.0 fusion.36
  515.1 17.5 %fusion.11 = (f32[4,12,128]{2,1,0:T(8,128)S(1)}, f32[4,12,128]{2,1,0:T(8,128)S(1)}, f32[4,12,128,416]{2,3,1,0:T(8,128)}) fusion(f32[2,4,12,128,416]{3,4,2,1,0:T(8,128)} %broadcast_divide_fusion, f32[4,12,128,416]{2,3,1,0:T(8,128)} %fusion.109, bf16[4,416,12,64]{1,3,2,0:T(8,128)(2,1)} %bitcast.450, bf16[4,128,12,64]{1,0,3,2:T(4,128)(2,1)} %copy-done.18), kind=kOutput, calls=%fused_computation.42 | convolution fusion | flops 337367040 | bytes 44285952 | tf_op jit(solution)/shard_map/gbqhd,gbkhd->gbhqk/dot_general | solution.py:329
  532.6 16.8 %fusion.41 = (bf16[4,12,128,416]{2,3,1,0:T(8,128)(2,1)S(1)}, bf16[4,12,128,416]{2,3,1,0:T(8,128)(2,1)}) fusion(f32[4,12,128,416]{2,3,1,0:T(8,128)} %get-tuple-element.236, f32[2,4,12,128,416]{3,4,2,1,0:T(8,128)} %broadcast_divide_fusion, f32[4,12,128]{2,1,0:T(8,128)S(1)} %get-tuple-element.59, f32[4,12,128,416]{2,3,1,0:T(8,128)} %fusion.109, ...), kind=kLoop, calls=%fused_computation.91 | loop fusion | flops 15335424 | bytes 51167232 | tf_op jit(solution)/shard_map/reshape.169
  580.0 10.4 %copy.346 = f32[1,2048,1536]{2,1,0:T(8,128)} copy(f32[1,2048,1536]{2,1,0:T(8,128)} %bitcast.421) | data formatting | bytes 25165824
  598.4 9.3 add_bitcast_fusion
  626.1 9.1 fusion.39
  672.3 14.0 %copy.345 = f32[1,2048,1536]{2,1,0:T(8,128)} copy(f32[1,2048,1536]{2,1,0:T(8,128)} %bitcast.420) | data formatting | bytes 25165824
  710.7 42.2 %reduce-scatter.11.cloned.1.call-done = bf16[192,8,864]{2,0,1:T(8,128)(2,1)} async-done(((bf16[768,8,864]{2,0,1:T(8,128)(2,1)}), bf16[192,8,864]{2,0,1:T(8,128)(2,1)}) %reduce-scatter.11.cloned.1.call-update) | async-done | bytes 2654224 | tf_op jit(solution)/shard_map/reduce_scatter | solution.py:156
  760.7 11.3 %fusion.32 = (bf16[2048,768]{1,0:T(8,128)(2,1)S(1)}, bf16[2048,768]{1,0:T(8,128)(2,1)S(1)}) fusion(f32[1,2048,1536]{2,1,0:T(8,128)} %add_bitcast_fusion.1, f32[1,2048,1536]{2,1,0:T(8,128)} %bitcast_dynamic-update-slice_fusion.1, f32[768]{0:T(1024)S(1)} %copy-done.48, f32[768]{0:T(1024)S(1)} %copy-done.49, f32[768]{0:T(1024)S(1)} %copy-done.50, ...), kind=kLoop, calls=%fused_computation.79 | loop fusion | flops 31457280 | bytes 31490048 | tf_op jit(solution)/shard_map/convert_element_type | solution.py:520
  795.5 9.2 copy.287
  809.7 8.8 copy.286
  818.5 9.2 convolution_convert_fusion.6
  841.5 10.1 %copy.288 = bf16[8,4,192,288]{3,2,1,0:T(8,128)(2,1)} copy(bf16[8,4,192,288]{2,1,3,0:T(4,128)(2,1)} %bitcast.443) | data formatting | bytes 7077888 | tf_op jit(solution)/shard_map/transpose | solution.py:546
  878.4 40.0 %all-reduce.4 = (f32[2,4,768]{2,1,0:T(4,128)S(1)}, f32[2,768]{1,0:T(2,128)S(1)}, f32[2,768]{1,0:T(2,128)S(1)}) all-reduce(f32[2,4,768]{2,1,0:T(4,128)S(1)} %pad_maximum_fusion.8, f32[2,768]{1,0:T(2,128)S(1)} %pad_maximum_fusion.10, f32[2,768]{1,0:T(2,128)S(1)} %pad_maximum_fusion.11), channel_id=9, replica_groups=mesh['dp'=8,'seq'=4] {'dp','seq'}, use_global_device_ids=true, to_apply=%region_24.25.clone | all-reduce | flops 9216 | bytes 73728
  926.5 54.0 %reduce-scatter.17.cloned.1.call-done = bf16[192,288]{1,0:T(8,128)(2,1)} async-done(((bf16[6144,288]{1,0:T(8,128)(2,1)}), bf16[192,288]{1,0:T(8,128)(2,1)}) %reduce-scatter.17.cloned.1.call-update) | async-done | bytes 110608 | tf_op jit(solution)/shard_map/reduce_scatter | solution.py:547
  (498 shorter events, 398.0 us)
Async XLA Ops:
  7.2 51.5 %all-gather.9.cloned.1.call-start = ((), (), s32[]{:S(2)}) async-start(), calls=%async_computation.5 | async-start | bytes 7864320 | tf_op jit(solution)/shard_map/all_gather | solution.py:441
  7.9 96.2 %all-gather.11.cloned.1.call-start = ((), (), s32[]{:S(2)}) async-start(), calls=%async_computation.6 | async-start | bytes 5898240 | tf_op jit(solution)/shard_map/all_gather | solution.py:101
  58.7 129.2 %all-gather.15.cloned.1.call-start = ((), (), s32[]{:S(2)}) async-start(), calls=%async_computation.13 | async-start | bytes 3096576 | tf_op jit(solution)/shard_map/all_gather | solution.py:99
  117.1 226.9 %all-gather.13.cloned.1.call-start = ((), (), s32[]{:S(2)}) async-start(), calls=%async_computation.7 | async-start | bytes 13762560 | tf_op jit(solution)/shard_map/all_gather | solution.py:101
  145.0 13.5 %copy-start.26 = (bf16[2,512,768]{2,1,0:T(8,128)(2,1)S(1)}, bf16[2,512,768]{2,1,0:T(8,128)(2,1)}, u32[]{:S(2)}) copy-start(bf16[2,512,768]{2,1,0:T(8,128)(2,1)} %param.12) | copy-start | bytes 4718596
  202.1 508.6 %reduce-scatter.9.cloned.1.call-start = ((), (), s32[]{:S(2)}) async-start(), calls=%async_computation.8 | async-start | bytes 3932160 | tf_op jit(solution)/shard_map/reduce_scatter | solution.py:523
  224.8 11.8 %copy-start = (f32[2,512,4,768]{3,2,1,0:T(4,128)S(1)}, f32[2,512,4,768]{3,2,1,0:T(4,128)}, u32[]{:S(2)}) copy-start(f32[2,512,4,768]{3,2,1,0:T(4,128)} %reshape.1390) | copy-start | bytes 37748740
  224.8 11.8 %copy-start.45 = (f32[4,768]{1,0:T(4,128)S(1)}, f32[4,768]{1,0:T(4,128)}, u32[]{:S(2)}) copy-start(f32[4,768]{1,0:T(4,128)} %mul.349) | copy-start | bytes 36868
  313.8 15.3 %copy-start.3 = (bf16[2,4,416,768]{2,3,1,0:T(8,128)(2,1)S(1)}, bf16[2,4,416,768]{2,3,1,0:T(8,128)(2,1)}, u32[]{:S(2)}) copy-start(bf16[2,4,416,768]{2,3,1,0:T(8,128)(2,1)} %copy.244) | copy-start | bytes 15335428
  365.6 40.9 %copy-start.21 = (bf16[96,8,8,384]{3,1,2,0:T(8,128)(2,1)}, bf16[96,8,8,384]{3,1,2,0:T(8,128)(2,1)S(1)}, u32[]{:S(2)}) copy-start(bf16[96,8,8,384]{3,1,2,0:T(8,128)(2,1)S(1)} %copy.305) | copy-start | bytes 14155780
  443.6 9.4 copy-start.75
  491.6 10.4 %copy-start.18 = (bf16[4,128,12,64]{1,0,3,2:T(4,128)(2,1)}, bf16[4,128,12,64]{1,0,3,2:T(4,128)(2,1)S(1)}, u32[]{:S(2)}) copy-start(bf16[4,128,12,64]{1,0,3,2:T(4,128)(2,1)S(1)} %reshape.1367) | copy-start | bytes 2359300
  532.6 16.8 %copy-start.20 = (bf16[4,128,12,64]{1,0,3,2:T(4,128)(2,1)S(1)}, bf16[4,128,12,64]{1,0,3,2:T(4,128)(2,1)}, u32[]{:S(2)}) copy-start(bf16[4,128,12,64]{1,0,3,2:T(4,128)(2,1)} %reshape.1378) | copy-start | bytes 2359300
  569.6 20.8 %copy-start.25 = (bf16[640,1536]{1,0:T(8,128)(2,1)}, bf16[640,1536]{1,0:T(8,128)(2,1)S(1)}, u32[]{:S(2)}) copy-start(bf16[640,1536]{1,0:T(8,128)(2,1)S(1)} %get-tuple-element.76) | copy-start | bytes 5898244
  580.0 10.4 %copy-start.67 = (s32[2048]{0:T(1024)S(1)}, s32[2048]{0:T(1024)}, u32[]{:S(2)}) copy-start(s32[2048]{0:T(1024)} %add_select_fusion) | copy-start | bytes 24580
  580.0 10.4 %copy-start.71 = (s32[640]{0:T(1024)S(1)}, s32[640]{0:T(1024)}, u32[]{:S(2)}) copy-start(s32[640]{0:T(1024)} %eq.228) | copy-start | bytes 7684
  590.4 17.4 %slice-start.10 = ((s8[12582912]{0:T(1024)(128)(4,1)}), s8[4194304]{0:T(1024)(128)(4,1)S(1)}, s32[]{:S(2)}) async-start(s8[12582912]{0:T(1024)(128)(4,1)} %bitcast.430), calls=%async_computation.24 | async-start | bytes 8388608
  590.4 17.4 %slice-start.11 = ((s8[12582912]{0:T(1024)(128)(4,1)}), s8[4194304]{0:T(1024)(128)(4,1)S(1)}, s32[]{:S(2)}) async-start(s8[12582912]{0:T(1024)(128)(4,1)} %bitcast.430), calls=%async_computation.25 | async-start | bytes 8388608
  598.4 9.3 slice-start.12
  624.8 128.1 %reduce-scatter.11.cloned.1.call-start = ((), (), s32[]{:S(2)}) async-start(), calls=%async_computation.9 | async-start | bytes 13762560 | tf_op jit(solution)/shard_map/reduce_scatter | solution.py:156
  625.3 208.0 %reduce-scatter.15.cloned.1.call-start = ((), (), s32[]{:S(2)}) async-start(), calls=%async_computation.11 | async-start | bytes 3096576 | tf_op jit(solution)/shard_map/reduce_scatter | solution.py:168
  662.0 24.3 %slice-start.15 = ((s8[5111808]{0:T(1024)(128)(4,1)}), s8[4194304]{0:T(1024)(128)(4,1)S(1)}, s32[]{:S(2)}) async-start(s8[5111808]{0:T(1024)(128)(4,1)} %bitcast.434), calls=%async_computation.29 | async-start | bytes 8388608
  665.4 20.9 %slice-start.16 = ((s8[5111808]{0:T(1024)(128)(4,1)}), s8[917504]{0:T(1024)(128)(4,1)S(1)}, s32[]{:S(2)}) async-start(s8[5111808]{0:T(1024)(128)(4,1)} %bitcast.434), calls=%async_computation.30 | async-start | bytes 1835008
  752.9 167.3 %reduce-scatter.13.cloned.1.call-start = ((), (), s32[]{:S(2)}) async-start(), calls=%async_computation.10 | async-start | bytes 3932160 | tf_op jit(solution)/shard_map/reduce_scatter | solution.py:523
  760.7 11.3 %copy-start.38 = (bf16[768,8,96]{0,2,1:T(8,128)(2,1)S(1)}, bf16[768,8,96]{0,2,1:T(8,128)(2,1)}, u32[]{:S(2)}) copy-start(bf16[768,8,96]{0,2,1:T(8,128)(2,1)} %copy.298) | copy-start | bytes 3538948
  778.8 201.6 %reduce-scatter.17.cloned.1.call-start = ((), (), s32[]{:S(2)}) async-start(), calls=%async_computation.12 | async-start | bytes 4866048 | tf_op jit(solution)/shard_map/reduce_scatter | solution.py:547
  809.7 18.0 %slice-start.22 = ((s8[6291456]{0:T(1024)(128)(4,1)}), s8[2097152]{0:T(1024)(128)(4,1)S(1)}, s32[]{:S(2)}) async-start(s8[6291456]{0:T(1024)(128)(4,1)} %bitcast.500), calls=%async_computation.36 | async-start | bytes 4194304
  818.5 9.2 slice-start.23
  861.4 10.1 %slice-start.3 = ((s8[12582912]{0:T(1024)(128)(4,1)}), s8[4194304]{0:T(1024)(128)(4,1)S(1)}, s32[]{:S(2)}) async-start(s8[12582912]{0:T(1024)(128)(4,1)} %bitcast.418), calls=%async_computation.17 | async-start | bytes 8388608
  861.4 10.1 %slice-start.4 = ((s8[12582912]{0:T(1024)(128)(4,1)}), s8[4194304]{0:T(1024)(128)(4,1)S(1)}, s32[]{:S(2)}) async-start(s8[12582912]{0:T(1024)(128)(4,1)} %bitcast.418), calls=%async_computation.18 | async-start | bytes 8388608
  878.3 43.5 %copy-start.14 = (f32[1024,768]{1,0:T(8,128)S(1)}, f32[1024,768]{1,0:T(8,128)}, u32[]{:S(2)}) copy-start(f32[1024,768]{1,0:T(8,128)} %copy-done.13) | copy-start | bytes 9437188
  878.3 43.5 %copy-start.66 = (f32[1024]{0:T(1024)S(1)}, f32[1024]{0:T(1024)}, u32[]{:S(2)}) copy-start(f32[1024]{0:T(1024)} %copy-done.65) | copy-start | bytes 12292
  (77 other events, 284.6 us)
Sparse Core Ops, SparseCore 0:
  9.5 49.0 all-gather.8
  60.8 37.4 all-gather.10
  117.2 55.7 all-gather.14
  202.2 73.1 all-gather.12
  624.8 37.9 reduce-scatter.8
  665.3 87.5 reduce-scatter.10
  756.4 71.5 reduce-scatter.14
  830.6 36.8 reduce-scatter.12
  873.0 107.4 reduce-scatter.16

commit v15 on v14

--- a/solution.py
+++ b/solution.py
@@ -391,7 +391,9 @@
     onehot = chosen.astype(jnp.bfloat16)
     high = values.astype(jnp.bfloat16)
     low = (values - high.astype(jnp.float32)).astype(jnp.bfloat16)
-    return product(onehot, high) + product(onehot, low)
+    return product(
+        jnp.concatenate([onehot, onehot], axis=1), jnp.concatenate([high, low], axis=0)
+    )
 
 
 def phase_weights(weight, rows):

time: 999 us -> 1000 us (level)
    dot_general x18 -> x12, matrix products: 127 us -> 118 us  [product(): return jnp.dot(left, right, preferred_element_type=jnp.float32)]
    unnamed x215 -> x219, local copies, waits for them, and re-layouts: 62.1 us -> 61.9 us
  transfers between devices with their start and end apart: 9 -> 9, of which waited for: 3 -> 4; matrix products, arithmetic and copies ran while one was open for 43% -> 43% of each run, Pallas kernels for 0% -> 0%
where the time goes in v15:
time: 1000 us; the launch traced here: 990 us
  matrix products  288 us (29%)
  local copies, waits for them, and re-layouts  279 us (28%)
  other arithmetic  168 us (17%)
  waiting for transfers between devices  104 us (10%)
  between operations  76 us (8%)
  blocking collectives  75.2 us (8%)
    dot_general x12, matrix products, product(): return jnp.dot(left, right, preferred_element_type=jnp.float32)  118 us
    unnamed x219, local copies, waits for them, and re-layouts  61.9 us
    reduce_scatter x1, waiting for transfers between devices, local(): lax.psum_scatter(late_blocks, ('dp', 'seq'), scatter_dimension=0, tiled=T...  56.4 us
    dot_general x8, matrix products, product_right(): lax.dot_general(left, right, (((1,), (1,)), ((), ())), preferred_element_...  48.3 us
    reduce_scatter x1, waiting for transfers between devices, reduce_seq_stage(): reduced = lax.psum_scatter(stacked, 'seq', scatter_dimension=0, tiled=True)  40.5 us
    unnamed x1, blocking collectives  40.2 us
    all_gather x1, blocking collectives, gather_grouped(): across = lax.all_gather(local_block, 'dp', axis=1, tiled=False)  35.1 us
    dot_general x6, matrix products, product_left(): lax.dot_general(left, right, (((0,), (0,)), ((), ())), preferred_element_...  34.4 us
  transfers between devices with their start and end apart: 9, of which 4 were waited for; matrix products, arithmetic and copies ran while one was open for 43% of the time, Pallas kernels for 0%

profile of v15, /device:TPU:0, one launch (start us, length us, event | category | flops | bytes accessed | tf_op | source)
XLA Modules:
  0.0 990.5 jit_solution(13486545179901079866)
XLA Ops:
  13.8 35.1 %all-gather.2 = bf16[8,293,192]{1,2,0:T(8,128)(2,1)S(1)} all-gather(bf16[1,293,192]{1,2,0:T(8,128)(2,1)S(1)} %maximum_bitcast_fusion.11), channel_id=2, replica_groups=mesh['dp'=8,'seq'=4] {'dp'}, dimensions={0}, use_global_device_ids=true | all-gather | bytes 1012608 | tf_op jit(solution)/shard_map/all_gather | solution.py:99
  166.8 9.8 convolution_convert_fusion
  176.5 12.3 %reshape.1392 = f32[2,512,4,768]{3,2,1,0:T(4,128)} reshape(bf16[4096,768]{1,0:T(8,128)(2,1)} %convolution_convert_fusion) | data formatting | bytes 18874368 | tf_op jit(solution)/shard_map/convert_element_type | solution.py:463
  207.8 10.1 %convolution_convert_fusion.1 = bf16[4096,768]{1,0:T(8,128)(2,1)} fusion(bf16[4096,768]{1,0:T(8,128)(2,1)} %bitcast.488, bf16[768,768]{0,1:T(8,128)(2,1)S(1)} %bitcast.474), kind=kOutput, calls=%fused_computation.68 | convolution fusion | flops 4834983936 | bytes 13762560 | tf_op jit(solution)/shard_map/dot_general | solution.py:78
  217.9 12.5 %reshape.1390 = f32[2,512,4,768]{3,2,1,0:T(4,128)} reshape(bf16[4096,768]{1,0:T(8,128)(2,1)} %convolution_convert_fusion.1) | data formatting | bytes 18874368 | tf_op jit(solution)/shard_map/convert_element_type | solution.py:462
  230.4 11.7 %multiply_reduce_fusion.2 = bf16[2,512,768]{2,1,0:T(8,128)(2,1)S(1)} fusion(f32[2,512,4,768]{3,2,1,0:T(4,128)} %reshape.1392, f32[4,768]{1,0:T(4,128)S(1)} %mul.352), kind=kLoop, calls=%fused_computation.29 | loop fusion | flops 5505024 | bytes 14168064 | tf_op jit(solution)/shard_map/reduce_sum | solution.py:409
  306.0 13.3 %fusion.200 = (f32[2,4,12,128]{3,2,1,0:T(8,128)S(1)}, f32[2,4,12,128,416]{3,4,2,1,0:T(8,128)}) fusion(pred[2,4,128,416]{2,3,1,0:T(8,128)(4,1)S(1)} %copy-done.43, bf16[2,4,416,12,64]{2,4,3,1,0:T(8,128)(2,1)} %bitcast.448, bf16[2,4,128,12,64]{2,1,0,4,3:T(4,128)(2,1)S(1)} %copy-done.29), kind=kOutput, calls=%fused_computation.470 | convolution fusion | flops 674759040 | bytes 27607040 | tf_op jit(solution)/shard_map/sub | solution.py:310
  319.3 15.3 %broadcast_divide_fusion = f32[2,4,12,128,416]{3,4,2,1,0:T(8,128)} fusion(f32[2,4,12,128,416]{3,4,2,1,0:T(8,128)} %get-tuple-element.227, f32[2,4,12,128]{3,2,1,0:T(8,128)S(1)} %get-tuple-element.226), kind=kLoop, calls=%fused_computation.51 | loop fusion | flops 5111808 | bytes 40943616 | tf_op jit(solution)/shard_map/div | solution.py:312
  334.6 10.0 %fusion.100 = bf16[2,4,128,12,64]{2,4,3,1,0:T(8,128)(2,1)} fusion(bf16[2,4,416,12,64]{2,4,3,1,0:T(8,128)(2,1)S(1)} %bitcast.426, f32[2,4,12,128,416]{3,4,2,1,0:T(8,128)} %broadcast_divide_fusion), kind=kOutput, calls=%fused_computation.212 | convolution fusion | flops 660209664 | bytes 27131904 | tf_op jit(solution)/shard_map/gbhqk,gbkhd->gbqhd/dot_general | solution.py:313
  352.9 14.0 %fusion.186 = (bf16[768,8,384]{2,1,0:T(8,128)(2,1)}, bf16[768,8,384]{2,1,0:T(8,128)(2,1)}) fusion(bf16[768,8,864]{2,1,0:T(8,128)(2,1)} %all-gather.13.cloned.1.call-done), kind=kLoop, calls=%fused_computation.456 | loop fusion | bytes 18874368 | tf_op jit(solution)/shard_map/slice | solution.py:107
  376.9 34.9 %multiply_convert_fusion = (bf16[1024,3072]{1,0:T(8,128)(2,1)S(1)}, f32[1024,3072]{1,0:T(8,128)}, f32[1024,3072]{1,0:T(8,128)}) fusion(bf16[768,3072]{1,0:T(8,128)(2,1)S(1)} %bitcast.449, f32[1024,768]{1,0:T(8,128)S(1)} %get-tuple-element.229, f32[768]{0:T(1024)S(1)} %copy-done.72, f32[768]{0:T(1024)S(1)} %copy-done.67, f32[1024]{0:T(1024)S(1)} %fusion.149, ...), kind=kOutput, calls=%fused_computation.16 | convolution fusion | flops 5040242688 | bytes 39335936 | tf_op jit(solution)/shard_map/dot_general | solution.py:78
  430.4 18.4 %add_convert_fusion = bf16[1024,3072]{1,0:T(8,128)(2,1)} fusion(f32[1024,3072]{1,0:T(8,128)} %get-tuple-element.82, f32[1024,3072]{1,0:T(8,128)} %get-tuple-element.230, bf16[768,3072]{1,0:T(8,128)(2,1)} %bitcast.452, f32[1024,768]{1,0:T(8,128)} %copy-done.25, f32[1024]{0:T(1024)S(1)} %negate_multiply_fusion.2), kind=kOutput, calls=%fused_computation.15 | convolution fusion | flops 4877451264 | bytes 39325696 | tf_op jit(solution)/shard_map/dot_general | solution.py:88
  448.8 9.4 multiply_reduce_fusion.4
  483.2 11.2 %pad_maximum_fusion = bf16[768,8,864]{2,0,1:T(8,128)(2,1)} fusion(bf16[768,8,384]{2,0,1:T(8,128)(2,1)} %bitcast.435, bf16[768,8,384]{2,0,1:T(8,128)(2,1)} %bitcast.434, bf16[768,8,96]{2,0,1:T(8,128)(2,1)S(1)} %copy.258), kind=kLoop, calls=%fused_computation.32 | loop fusion | flops 31850496 | bytes 21233664 | tf_op jit(solution)/shard_map/concatenate | solution.py:154
  497.7 8.9 fusion.52
  520.0 17.6 %fusion.19 = (f32[4,12,128]{2,1,0:T(8,128)S(1)}, f32[4,12,128]{2,1,0:T(8,128)S(1)}, f32[4,12,128,416]{2,3,1,0:T(8,128)}) fusion(f32[2,4,12,128,416]{3,4,2,1,0:T(8,128)} %broadcast_divide_fusion, f32[4,12,128,416]{2,3,1,0:T(8,128)} %fusion.119, bf16[4,416,12,64]{1,3,2,0:T(8,128)(2,1)} %bitcast.440, bf16[4,128,12,64]{1,0,3,2:T(4,128)(2,1)} %copy-done.19), kind=kOutput, calls=%fused_computation.48 | convolution fusion | flops 337367040 | bytes 44285952 | tf_op jit(solution)/shard_map/gbqhd,gbkhd->gbhqk/dot_general | solution.py:329
  537.6 16.8 %fusion.57 = (bf16[4,12,128,416]{2,3,1,0:T(8,128)(2,1)S(1)}, bf16[4,12,128,416]{2,3,1,0:T(8,128)(2,1)}) fusion(f32[4,12,128,416]{2,3,1,0:T(8,128)} %get-tuple-element.234, f32[2,4,12,128,416]{3,4,2,1,0:T(8,128)} %broadcast_divide_fusion, f32[4,12,128]{2,1,0:T(8,128)S(1)} %get-tuple-element.59, f32[4,12,128,416]{2,3,1,0:T(8,128)} %fusion.119, ...), kind=kLoop, calls=%fused_computation.99 | loop fusion | flops 15335424 | bytes 51167232 | tf_op jit(solution)/shard_map/reshape.169
  577.1 9.6 fusion.35
  586.7 10.5 %copy.346 = f32[1,2048,1536]{2,1,0:T(8,128)} copy(f32[1,2048,1536]{2,1,0:T(8,128)} %bitcast.430) | data formatting | bytes 25165824
  601.6 11.7 %fusion.25 = f32[1,2048,1536]{2,1,0:T(8,128)S(1)} fusion(pred[2048,640]{1,0:T(32,128)(4,1)} %get-tuple-element.174, bf16[640,1536]{1,0:T(8,128)(2,1)} %fusion.59, bf16[640,1536]{1,0:T(8,128)(2,1)} %bitcast_convert_fusion), kind=kOutput, calls=%fused_computation.57 | convolution fusion | flops 8063549440 | bytes 17825792 | tf_op jit(solution)/shard_map/dot_general | solution.py:78
  629.7 10.1 %fusion.55 = f32[4,12,64,416]{3,2,1,0:T(8,128)} fusion(f32[2,4,12,128,416]{3,4,2,1,0:T(8,128)} %broadcast_divide_fusion, bf16[4,128,12,64]{1,0,3,2:T(4,128)(2,1)S(1)} %copy-done.18), kind=kOutput, calls=%fused_computation.98 | convolution fusion | flops 327155712 | bytes 11010048 | tf_op jit(solution)/shard_map/gbhqk,gbqhd->gbkhd/dot_general | solution.py:340
  666.1 10.8 %fusion.31 = f32[2048,1536]{1,0:T(8,128)} fusion(pred[2048,512]{1,0:T(32,128)(4,1)S(1)} %iota_compare_fusion.1, bf16[512,1536]{1,0:T(8,128)(2,1)S(1)} %get-tuple-element.75, bf16[512,1536]{1,0:T(8,128)(2,1)S(1)} %get-tuple-element.76), kind=kOutput, calls=%fused_computation.59 | convolution fusion | flops 6450839552 | bytes 16777216 | tf_op jit(solution)/shard_map/dot_general | solution.py:78
  676.9 13.0 %copy.345 = f32[1,2048,1536]{2,1,0:T(8,128)} copy(f32[1,2048,1536]{2,1,0:T(8,128)} %bitcast.429) | data formatting | bytes 25165824
  701.9 11.2 %fusion.28 = f32[1,2048,1536]{2,1,0:T(8,128)} fusion(pred[2048,640]{1,0:T(32,128)(4,1)S(1)} %copy-done.32, bf16[640,1536]{1,0:T(8,128)(2,1)S(1)} %fusion.60, bf16[640,1536]{1,0:T(8,128)(2,1)S(1)} %bitcast_convert_fusion.1), kind=kOutput, calls=%fused_computation.58 | convolution fusion | flops 8063549440 | bytes 17825792 | tf_op jit(solution)/shard_map/dot_general | solution.py:78
  713.1 40.5 %reduce-scatter.11.cloned.1.call-done = bf16[192,8,864]{2,0,1:T(8,128)(2,1)} async-done(((bf16[768,8,864]{2,0,1:T(8,128)(2,1)}), bf16[192,8,864]{2,0,1:T(8,128)(2,1)}) %reduce-scatter.11.cloned.1.call-update) | async-done | bytes 2654224 | tf_op jit(solution)/shard_map/reduce_scatter | solution.py:156
  761.2 11.3 %fusion.48 = (bf16[2048,768]{1,0:T(8,128)(2,1)S(1)}, bf16[2048,768]{1,0:T(8,128)(2,1)S(1)}) fusion(f32[1,2048,1536]{2,1,0:T(8,128)} %fusion.28, f32[1,2048,1536]{2,1,0:T(8,128)} %bitcast_dynamic-update-slice_fusion.1, f32[768]{0:T(1024)S(1)} %copy-done.51, f32[768]{0:T(1024)S(1)} %copy-done.52, f32[768]{0:T(1024)S(1)} %copy-done.53, f32[768]{0:T(1024)S(1)} %copy-done.50, ...), kind=kLoop, calls=%fused_computation.87 | loop fusion | flops 31457280 | bytes 31490048 | tf_op jit(solution)/shard_map/convert_element_type | solution.py:522
  796.0 9.1 copy.287
  810.0 8.7 copy.286
  818.8 9.2 convolution_convert_fusion.6
  841.8 10.2 %copy.288 = bf16[8,4,192,288]{3,2,1,0:T(8,128)(2,1)} copy(bf16[8,4,192,288]{2,1,3,0:T(4,128)(2,1)} %bitcast.433) | data formatting | bytes 7077888 | tf_op jit(solution)/shard_map/transpose | solution.py:548
  877.1 40.2 %all-reduce.4 = (f32[2,4,768]{2,1,0:T(4,128)S(1)}, f32[2,768]{1,0:T(2,128)S(1)}, f32[2,768]{1,0:T(2,128)S(1)}) all-reduce(f32[2,4,768]{2,1,0:T(4,128)S(1)} %pad_maximum_fusion.14, f32[2,768]{1,0:T(2,128)S(1)} %pad_maximum_fusion.16, f32[2,768]{1,0:T(2,128)S(1)} %pad_maximum_fusion.17), channel_id=9, replica_groups=mesh['dp'=8,'seq'=4] {'dp','seq'}, use_global_device_ids=true, to_apply=%region_24.25.clone | all-reduce | flops 9216 | bytes 73728
  925.3 56.4 %reduce-scatter.17.cloned.1.call-done = bf16[192,288]{1,0:T(8,128)(2,1)} async-done(((bf16[6144,288]{1,0:T(8,128)(2,1)}), bf16[192,288]{1,0:T(8,128)(2,1)}) %reduce-scatter.17.cloned.1.call-update) | async-done | bytes 110608 | tf_op jit(solution)/shard_map/reduce_scatter | solution.py:549
  (503 shorter events, 390.7 us)
Async XLA Ops:
  7.2 51.5 %all-gather.9.cloned.1.call-start = ((), (), s32[]{:S(2)}) async-start(), calls=%async_computation.5 | async-start | bytes 7864320 | tf_op jit(solution)/shard_map/all_gather | solution.py:443
  7.9 116.6 %all-gather.11.cloned.1.call-start = ((), (), s32[]{:S(2)}) async-start(), calls=%async_computation.6 | async-start | bytes 5898240 | tf_op jit(solution)/shard_map/all_gather | solution.py:101
  58.7 134.8 %all-gather.15.cloned.1.call-start = ((), (), s32[]{:S(2)}) async-start(), calls=%async_computation.13 | async-start | bytes 3096576 | tf_op jit(solution)/shard_map/all_gather | solution.py:99
  103.2 36.4 %copy-start.58 = (s32[640]{0:T(1024)}, s32[640]{0:T(1024)S(1)}, u32[]{:S(2)}) copy-start(s32[640]{0:T(1024)S(1)} %eq.228) | copy-start | bytes 7684
  103.3 36.3 %copy-start.60 = (s32[640]{0:T(1024)}, s32[640]{0:T(1024)S(1)}, u32[]{:S(2)}) copy-start(s32[640]{0:T(1024)S(1)} %eq.217) | copy-start | bytes 7684
  137.6 212.0 %all-gather.13.cloned.1.call-start = ((), (), s32[]{:S(2)}) async-start(), calls=%async_computation.7 | async-start | bytes 13762560 | tf_op jit(solution)/shard_map/all_gather | solution.py:101
  146.1 13.5 %copy-start.26 = (bf16[2,512,768]{2,1,0:T(8,128)(2,1)S(1)}, bf16[2,512,768]{2,1,0:T(8,128)(2,1)}, u32[]{:S(2)}) copy-start(bf16[2,512,768]{2,1,0:T(8,128)(2,1)} %param.12) | copy-start | bytes 4718596
  207.7 505.4 %reduce-scatter.9.cloned.1.call-start = ((), (), s32[]{:S(2)}) async-start(), calls=%async_computation.8 | async-start | bytes 3932160 | tf_op jit(solution)/shard_map/reduce_scatter | solution.py:525
  319.2 15.3 %copy-start.3 = (bf16[2,4,416,768]{2,3,1,0:T(8,128)(2,1)S(1)}, bf16[2,4,416,768]{2,3,1,0:T(8,128)(2,1)}, u32[]{:S(2)}) copy-start(bf16[2,4,416,768]{2,3,1,0:T(8,128)(2,1)} %copy.244) | copy-start | bytes 15335428
  370.6 41.1 %copy-start.22 = (bf16[96,8,8,384]{3,1,2,0:T(8,128)(2,1)}, bf16[96,8,8,384]{3,1,2,0:T(8,128)(2,1)S(1)}, u32[]{:S(2)}) copy-start(bf16[96,8,8,384]{3,1,2,0:T(8,128)(2,1)S(1)} %copy.305) | copy-start | bytes 14155780
  537.6 16.9 %copy-start.21 = (bf16[4,128,12,64]{1,0,3,2:T(4,128)(2,1)S(1)}, bf16[4,128,12,64]{1,0,3,2:T(4,128)(2,1)}, u32[]{:S(2)}) copy-start(bf16[4,128,12,64]{1,0,3,2:T(4,128)(2,1)} %reshape.1378) | copy-start | bytes 2359300
  601.4 11.8 %copy-start.50 = (f32[768]{0:T(1024)S(1)}, f32[768]{0:T(1024)}, u32[]{:S(2)}) copy-start(f32[768]{0:T(1024)} %broadcast_in_dim.361) | copy-start | bytes 9220
  601.4 11.8 %copy-start.51 = (f32[768]{0:T(1024)S(1)}, f32[768]{0:T(1024)}, u32[]{:S(2)}) copy-start(f32[768]{0:T(1024)} %broadcast_in_dim.367) | copy-start | bytes 9220
  601.5 11.8 %copy-start.52 = (f32[768]{0:T(1024)S(1)}, f32[768]{0:T(1024)}, u32[]{:S(2)}) copy-start(f32[768]{0:T(1024)} %broadcast_in_dim.365) | copy-start | bytes 9220
  601.5 11.8 %copy-start.53 = (f32[768]{0:T(1024)S(1)}, f32[768]{0:T(1024)}, u32[]{:S(2)}) copy-start(f32[768]{0:T(1024)} %broadcast_in_dim.363) | copy-start | bytes 9220
  601.5 11.8 %copy-start.54 = (f32[768]{0:T(1024)S(1)}, f32[768]{0:T(1024)}, u32[]{:S(2)}) copy-start(f32[768]{0:T(1024)} %broadcast_in_dim.359) | copy-start | bytes 9220
  601.5 11.8 %copy-start.55 = (f32[768]{0:T(1024)S(1)}, f32[768]{0:T(1024)}, u32[]{:S(2)}) copy-start(f32[768]{0:T(1024)} %broadcast_in_dim.356) | copy-start | bytes 9220
  601.5 11.8 %copy-start.56 = (f32[768]{0:T(1024)S(1)}, f32[768]{0:T(1024)}, u32[]{:S(2)}) copy-start(f32[768]{0:T(1024)} %broadcast_in_dim.353) | copy-start | bytes 9220
  601.5 11.8 %copy-start.57 = (f32[768]{0:T(1024)S(1)}, f32[768]{0:T(1024)}, u32[]{:S(2)}) copy-start(f32[768]{0:T(1024)} %broadcast_in_dim.349) | copy-start | bytes 9220
  601.5 11.8 %copy-start.63 = (pred[2048]{0:T(1024)(128)(4,1)S(1)}, pred[2048]{0:T(1024)(128)(4,1)}, u32[]{:S(2)}) copy-start(pred[2048]{0:T(1024)(128)(4,1)} %get-tuple-element.237) | copy-start | bytes 6148
  601.5 11.8 %copy-start.64 = (pred[2048]{0:T(1024)(128)(4,1)S(1)}, pred[2048]{0:T(1024)(128)(4,1)}, u32[]{:S(2)}) copy-start(pred[2048]{0:T(1024)(128)(4,1)} %get-tuple-element.238) | copy-start | bytes 6148
  601.5 11.8 %copy-start.65 = (pred[2048]{0:T(1024)(128)(4,1)S(1)}, pred[2048]{0:T(1024)(128)(4,1)}, u32[]{:S(2)}) copy-start(pred[2048]{0:T(1024)(128)(4,1)} %get-tuple-element.235) | copy-start | bytes 6148
  601.6 11.8 %copy-start.66 = (pred[2048]{0:T(1024)(128)(4,1)S(1)}, pred[2048]{0:T(1024)(128)(4,1)}, u32[]{:S(2)}) copy-start(pred[2048]{0:T(1024)(128)(4,1)} %get-tuple-element.236) | copy-start | bytes 6148
  626.8 126.8 %reduce-scatter.11.cloned.1.call-start = ((), (), s32[]{:S(2)}) async-start(), calls=%async_computation.9 | async-start | bytes 13762560 | tf_op jit(solution)/shard_map/reduce_scatter | solution.py:156
  627.4 206.1 %reduce-scatter.15.cloned.1.call-start = ((), (), s32[]{:S(2)}) async-start(), calls=%async_computation.11 | async-start | bytes 3096576 | tf_op jit(solution)/shard_map/reduce_scatter | solution.py:168
  665.7 24.2 %slice-start.15 = ((s8[5111808]{0:T(1024)(128)(4,1)}), s8[4194304]{0:T(1024)(128)(4,1)S(1)}, s32[]{:S(2)}) async-start(s8[5111808]{0:T(1024)(128)(4,1)} %bitcast.422), calls=%async_computation.29 | async-start | bytes 8388608
  666.1 23.8 %slice-start.16 = ((s8[5111808]{0:T(1024)(128)(4,1)}), s8[917504]{0:T(1024)(128)(4,1)S(1)}, s32[]{:S(2)}) async-start(s8[5111808]{0:T(1024)(128)(4,1)} %bitcast.422), calls=%async_computation.30 | async-start | bytes 1835008
  753.7 165.5 %reduce-scatter.13.cloned.1.call-start = ((), (), s32[]{:S(2)}) async-start(), calls=%async_computation.10 | async-start | bytes 3932160 | tf_op jit(solution)/shard_map/reduce_scatter | solution.py:525
  779.3 202.4 %reduce-scatter.17.cloned.1.call-start = ((), (), s32[]{:S(2)}) async-start(), calls=%async_computation.12 | async-start | bytes 4866048 | tf_op jit(solution)/shard_map/reduce_scatter | solution.py:549
  810.0 18.0 %slice-start.22 = ((s8[6291456]{0:T(1024)(128)(4,1)}), s8[2097152]{0:T(1024)(128)(4,1)S(1)}, s32[]{:S(2)}) async-start(s8[6291456]{0:T(1024)(128)(4,1)} %bitcast.490), calls=%async_computation.36 | async-start | bytes 4194304
  877.1 43.7 %copy-start.14 = (f32[1024,768]{1,0:T(8,128)S(1)}, f32[1024,768]{1,0:T(8,128)}, u32[]{:S(2)}) copy-start(f32[1024,768]{1,0:T(8,128)} %copy-done.13) | copy-start | bytes 9437188
  877.1 43.7 %copy-start.71 = (f32[1024]{0:T(1024)S(1)}, f32[1024]{0:T(1024)}, u32[]{:S(2)}) copy-start(f32[1024]{0:T(1024)} %copy-done.70) | copy-start | bytes 12292
  (79 other events, 380.1 us)
Sparse Core Ops, SparseCore 0:
  9.5 49.0 all-gather.8
  60.8 37.4 all-gather.10
  137.7 55.7 all-gather.14
  207.9 71.7 all-gather.12
  626.9 36.6 reduce-scatter.8
  666.1 87.5 reduce-scatter.10
  757.2 71.9 reduce-scatter.14
  831.7 36.9 reduce-scatter.12
  874.2 107.4 reduce-scatter.16

commit v16 on v14

--- a/solution.py
+++ b/solution.py
@@ -520,14 +520,16 @@
         ).astype(jnp.bfloat16)
         back_g = product_right(key_partial_g, wk) + product_right(value_partial_g, wv)
         back_g = back_g.reshape(1, group_len, width).astype(jnp.bfloat16)
-        back_own_g = lax.psum_scatter(back_g, "seq", scatter_dimension=1, tiled=True)
+        if g == groups - 1:
+            back_own_g = back_g
+        else:
+            back_own_g = lax.psum_scatter(back_g, "seq", scatter_dimension=1, tiled=True)
         pieces_back.append((grad_queries_g, pooled_g, key_partial_g, value_partial_g, back_own_g))
     grad_queries = jnp.concatenate([piece[0] for piece in pieces_back], axis=0)
     grad_pooled = jnp.concatenate([piece[1] for piece in pieces_back], axis=0)
     key_partial = jnp.concatenate([piece[2] for piece in pieces_back], axis=0)
     value_partial = jnp.concatenate([piece[3] for piece in pieces_back], axis=0)
     last_back = pieces_back[-1][4]
-    early_dp = reduce_dp_stage(((early_reduced, early_widths),))
     grad_pooling = jnp.stack(
         [
             pool_grad_grouped(grad_pooled[..., :width], key_g),
@@ -538,25 +540,25 @@
     grad_key_w = product_left(all_tokens, key_partial)
     grad_value_w = product_left(all_tokens, value_partial)
     late_stacked, late_widths = stack_for_seq((grad_query_w, grad_key_w, grad_value_w))
-    late_stacked, early_dp = lax.optimization_barrier((late_stacked, early_dp))
     seq_size = lax.psum(1, "seq")
-    dp_size = lax.psum(1, "dp")
-    rows_each = late_stacked.shape[0] // seq_size
-    late_blocks = late_stacked.reshape(seq_size, rows_each, dp_size, late_stacked.shape[2])
-    late_blocks = jnp.transpose(late_blocks, (2, 0, 1, 3)).reshape(-1, late_stacked.shape[2])
-    late_reduced = lax.psum_scatter(late_blocks, ("dp", "seq"), scatter_dimension=0, tiled=True)
-    late_reduced = late_reduced.astype(jnp.float32)
-    late_dp, at = [], 0
-    for width_piece in late_widths:
-        late_dp.append(late_reduced[:, at : at + width_piece])
-        at += width_piece
-    back_own = jnp.concatenate([piece[4] for piece in pieces_back], axis=0)
+    late_flat = late_stacked.reshape(seq_size, -1, width)
+    back_flat = last_back.reshape(seq_size, -1, width)
+    joined = jnp.concatenate([late_flat, back_flat], axis=1)
+    chunk_rows = joined.shape[1]
+    joined = joined.reshape(seq_size * chunk_rows, width)
+    joined = lax.psum_scatter(joined, "seq", scatter_dimension=0, tiled=True)
+    late_reduced = joined[: late_flat.shape[1]].reshape(
+        late_stacked.shape[0] // seq_size, late_stacked.shape[1], late_stacked.shape[2]
+    )
+    back_last = joined[late_flat.shape[1] :].reshape(1, shard_rows, width)
+    back_own = jnp.concatenate([piece[4] for piece in pieces_back[:-1]] + [back_last], axis=0)
     grad_tokens = (
         grad_mixed
         + product_right(grad_queries, wq)
         + back_own.reshape(groups * shard_rows, width).astype(jnp.float32)
     )
-    accum = (late_dp[0], late_dp[1], late_dp[2], early_dp[0], early_dp[1], early_dp[2].T)
+    pieces = reduce_dp_stage(((early_reduced, early_widths), (late_reduced, late_widths)))
+    accum = (pieces[3], pieces[4], pieces[5], pieces[0], pieces[1], pieces[2].T)
     small_sums = (
         lax.psum_scatter(grad_pooling, ("dp", "seq"), scatter_dimension=2, tiled=True),
         lax.psum_scatter(

time: 999 us -> 1000 us (level)
    reduce_scatter x1, waiting for transfers between devices: 42.2 us -> 21.7 us  [reduce_seq_stage(): reduced = lax.psum_scatter(stacked, 'seq', scatter_dimension=0, tiled=True)]
    unnamed x215 -> x225, local copies, waits for them, and re-layouts: 62.1 us -> 57.5 us
  transfers between devices with their start and end apart: 9 -> 8, of which waited for: 3 -> 4; matrix products, arithmetic and copies ran while one was open for 43% -> 35% of each run, Pallas kernels for 0% -> 0%
where the time goes in v16:
time: 1000 us; the launch traced here: 991 us
  matrix products  301 us (30%)
  local copies, waits for them, and re-layouts  279 us (28%)
  other arithmetic  170 us (17%)
  waiting for transfers between devices  90.2 us (9%)
  between operations  75.8 us (8%)
  blocking collectives  75.1 us (8%)
    dot_general x18, matrix products, product(): return jnp.dot(left, right, preferred_element_type=jnp.float32)  128 us
    reduce_scatter x1, waiting for transfers between devices, local(): joined = lax.psum_scatter(joined, 'seq', scatter_dimension=0, tiled=True)  61.4 us
    unnamed x225, local copies, waits for them, and re-layouts  57.5 us
    dot_general x8, matrix products, product_right(): lax.dot_general(left, right, (((1,), (1,)), ((), ())), preferred_element_...  54.3 us
    unnamed x1, blocking collectives  40 us
    all_gather x1, blocking collectives, gather_grouped(): across = lax.all_gather(local_block, 'dp', axis=1, tiled=False)  35.1 us
    dot_general x6, matrix products, product_left(): lax.dot_general(left, right, (((0,), (0,)), ((), ())), preferred_element_...  34.7 us
    dot_general x2, matrix products, attention_bwd(): jnp.einsum('gbqhd,gbkhd->gbhqk', head_grad, head_values, preferred_elemen...  24.2 us
  transfers between devices with their start and end apart: 8, of which 4 were waited for; matrix products, arithmetic and copies ran while one was open for 35% of the time, Pallas kernels for 0%

profile of v16, /device:TPU:0, one launch (start us, length us, event | category | flops | bytes accessed | tf_op | source)
XLA Modules:
  0.0 991.2 jit_solution(2107892338111800907)
XLA Ops:
  13.8 35.1 %all-gather.2 = bf16[8,293,192]{1,2,0:T(8,128)(2,1)S(1)} all-gather(bf16[1,293,192]{1,2,0:T(8,128)(2,1)S(1)} %maximum_bitcast_fusion.11), channel_id=2, replica_groups=mesh['dp'=8,'seq'=4] {'dp'}, dimensions={0}, use_global_device_ids=true | all-gather | bytes 1012608 | tf_op jit(solution)/shard_map/all_gather | solution.py:99
  164.4 9.9 %convolution_convert_fusion = bf16[4096,768]{1,0:T(8,128)(2,1)} fusion(bf16[4096,768]{1,0:T(8,128)(2,1)} %bitcast.497, bf16[768,768]{0,1:T(8,128)(2,1)S(1)} %bitcast.483), kind=kOutput, calls=%fused_computation.53 | convolution fusion | flops 4834983936 | bytes 13762560 | tf_op jit(solution)/shard_map/dot_general | solution.py:78
  174.3 12.3 %reshape.1404 = f32[2,512,4,768]{3,2,1,0:T(4,128)} reshape(bf16[4096,768]{1,0:T(8,128)(2,1)} %convolution_convert_fusion) | data formatting | bytes 18874368 | tf_op jit(solution)/shard_map/convert_element_type | solution.py:461
  201.0 10.2 %convolution_convert_fusion.1 = bf16[4096,768]{1,0:T(8,128)(2,1)} fusion(bf16[4096,768]{1,0:T(8,128)(2,1)} %bitcast.498, bf16[768,768]{0,1:T(8,128)(2,1)S(1)} %bitcast.486), kind=kOutput, calls=%fused_computation.54 | convolution fusion | flops 4834983936 | bytes 13762560 | tf_op jit(solution)/shard_map/dot_general | solution.py:78
  211.2 12.6 %reshape.1402 = f32[2,512,4,768]{3,2,1,0:T(4,128)} reshape(bf16[4096,768]{1,0:T(8,128)(2,1)} %convolution_convert_fusion.1) | data formatting | bytes 18874368 | tf_op jit(solution)/shard_map/convert_element_type | solution.py:460
  223.8 11.7 %multiply_reduce_fusion.2 = bf16[2,512,768]{2,1,0:T(8,128)(2,1)S(1)} fusion(f32[2,512,4,768]{3,2,1,0:T(4,128)} %reshape.1404, f32[4,768]{1,0:T(4,128)S(1)} %mul.352), kind=kLoop, calls=%fused_computation.31 | loop fusion | flops 5505024 | bytes 14168064 | tf_op jit(solution)/shard_map/reduce_sum | solution.py:407
  235.6 8.5 multiply_reduce_fusion.3
  260.1 8.6 fusion.169
  299.5 13.2 %fusion.180 = (f32[2,4,12,128]{3,2,1,0:T(8,128)S(1)}, f32[2,4,12,128,416]{3,4,2,1,0:T(8,128)}) fusion(pred[2,4,128,416]{2,3,1,0:T(8,128)(4,1)S(1)} %copy-done.39, bf16[2,4,416,12,64]{2,4,3,1,0:T(8,128)(2,1)} %bitcast.458, bf16[2,4,128,12,64]{2,1,0,4,3:T(4,128)(2,1)S(1)} %copy-done.28), kind=kOutput, calls=%fused_computation.458 | convolution fusion | flops 674759040 | bytes 27607040 | tf_op jit(solution)/shard_map/sub | solution.py:310
  312.7 15.4 %broadcast_divide_fusion = f32[2,4,12,128,416]{3,4,2,1,0:T(8,128)} fusion(f32[2,4,12,128,416]{3,4,2,1,0:T(8,128)} %get-tuple-element.222, f32[2,4,12,128]{3,2,1,0:T(8,128)S(1)} %get-tuple-element.221), kind=kLoop, calls=%fused_computation.45 | loop fusion | flops 5111808 | bytes 40943616 | tf_op jit(solution)/shard_map/div | solution.py:312
  328.1 10.0 %fusion.87 = bf16[2,4,128,12,64]{2,4,3,1,0:T(8,128)(2,1)} fusion(bf16[2,4,416,12,64]{2,4,3,1,0:T(8,128)(2,1)S(1)} %bitcast.440, f32[2,4,12,128,416]{3,4,2,1,0:T(8,128)} %broadcast_divide_fusion), kind=kOutput, calls=%fused_computation.205 | convolution fusion | flops 660209664 | bytes 27131904 | tf_op jit(solution)/shard_map/gbhqk,gbkhd->gbqhd/dot_general | solution.py:313
  346.4 14.2 %fusion.167 = (bf16[768,8,384]{2,1,0:T(8,128)(2,1)}, bf16[768,8,384]{2,1,0:T(8,128)(2,1)}) fusion(bf16[768,8,864]{2,1,0:T(8,128)(2,1)} %all-gather.13.cloned.1.call-done), kind=kLoop, calls=%fused_computation.445 | loop fusion | bytes 18874368 | tf_op jit(solution)/shard_map/slice | solution.py:107
  370.6 34.8 %multiply_convert_fusion = (bf16[1024,3072]{1,0:T(8,128)(2,1)S(1)}, f32[1024,3072]{1,0:T(8,128)}, f32[1024,3072]{1,0:T(8,128)}) fusion(bf16[768,3072]{1,0:T(8,128)(2,1)S(1)} %bitcast.459, f32[1024,768]{1,0:T(8,128)S(1)} %get-tuple-element.224, f32[768]{0:T(1024)S(1)} %copy-done.70, f32[768]{0:T(1024)S(1)} %copy-done.62, f32[1024]{0:T(1024)S(1)} %fusion.142, ...), kind=kOutput, calls=%fused_computation.18 | convolution fusion | flops 5040242688 | bytes 39335936 | tf_op jit(solution)/shard_map/dot_general | solution.py:78
  423.9 18.5 %add_convert_fusion = bf16[1024,3072]{1,0:T(8,128)(2,1)} fusion(f32[1024,3072]{1,0:T(8,128)} %get-tuple-element.78, f32[1024,3072]{1,0:T(8,128)} %get-tuple-element.225, bf16[768,3072]{1,0:T(8,128)(2,1)} %bitcast.462, f32[1024,768]{1,0:T(8,128)} %copy-done.23, f32[1024]{0:T(1024)S(1)} %negate_multiply_fusion.2), kind=kOutput, calls=%fused_computation.17 | convolution fusion | flops 4877451264 | bytes 39325696 | tf_op jit(solution)/shard_map/dot_general | solution.py:88
  442.5 9.6 multiply_reduce_fusion.4
  477.1 11.3 %pad_maximum_fusion = bf16[768,8,864]{2,0,1:T(8,128)(2,1)} fusion(bf16[768,8,384]{2,0,1:T(8,128)(2,1)} %bitcast.445, bf16[768,8,384]{2,0,1:T(8,128)(2,1)} %bitcast.444, bf16[768,8,96]{2,0,1:T(8,128)(2,1)S(1)} %copy.261), kind=kLoop, calls=%fused_computation.34 | loop fusion | flops 31850496 | bytes 21233664 | tf_op jit(solution)/shard_map/concatenate | solution.py:154
  491.7 9.1 fusion.36
  514.1 17.5 %fusion.11 = (f32[4,12,128]{2,1,0:T(8,128)S(1)}, f32[4,12,128]{2,1,0:T(8,128)S(1)}, f32[4,12,128,416]{2,3,1,0:T(8,128)}) fusion(f32[2,4,12,128,416]{3,4,2,1,0:T(8,128)} %broadcast_divide_fusion, f32[4,12,128,416]{2,3,1,0:T(8,128)} %fusion.108, bf16[4,416,12,64]{1,3,2,0:T(8,128)(2,1)} %bitcast.450, bf16[4,128,12,64]{1,0,3,2:T(4,128)(2,1)} %copy-done.15), kind=kOutput, calls=%fused_computation.42 | convolution fusion | flops 337367040 | bytes 44285952 | tf_op jit(solution)/shard_map/gbqhd,gbkhd->gbhqk/dot_general | solution.py:329
  531.6 16.9 %fusion.41 = (bf16[4,12,128,416]{2,3,1,0:T(8,128)(2,1)S(1)}, bf16[4,12,128,416]{2,3,1,0:T(8,128)(2,1)}) fusion(f32[4,12,128,416]{2,3,1,0:T(8,128)} %get-tuple-element.229, f32[2,4,12,128,416]{3,4,2,1,0:T(8,128)} %broadcast_divide_fusion, f32[4,12,128]{2,1,0:T(8,128)S(1)} %get-tuple-element.51, f32[4,12,128,416]{2,3,1,0:T(8,128)} %fusion.108, ...), kind=kLoop, calls=%fused_computation.92 | loop fusion | flops 15335424 | bytes 51167232 | tf_op jit(solution)/shard_map/reshape.172
  579.1 10.4 %copy.350 = f32[1,2048,1536]{2,1,0:T(8,128)} copy(f32[1,2048,1536]{2,1,0:T(8,128)} %bitcast.420) | data formatting | bytes 25165824
  597.6 9.3 add_bitcast_fusion
  634.3 9.3 fusion.39
  672.2 8.8 pad_maximum_fusion.8
  691.6 10.6 %copy.349 = f32[1,2048,1536]{2,1,0:T(8,128)} copy(f32[1,2048,1536]{2,1,0:T(8,128)} %bitcast.419) | data formatting | bytes 25165824
  730.4 21.7 %reduce-scatter.10.cloned.1.call-done = bf16[192,8,864]{2,0,1:T(8,128)(2,1)} async-done(((bf16[768,8,864]{2,0,1:T(8,128)(2,1)}), bf16[192,8,864]{2,0,1:T(8,128)(2,1)}) %reduce-scatter.10.cloned.1.call-update) | async-done | bytes 2654224 | tf_op jit(solution)/shard_map/reduce_scatter | solution.py:156
  752.1 11.0 %fusion.32 = (bf16[2048,768]{1,0:T(8,128)(2,1)S(1)}, bf16[2048,768]{1,0:T(8,128)(2,1)S(1)}) fusion(f32[1,2048,1536]{2,1,0:T(8,128)} %add_bitcast_fusion.1, f32[1,2048,1536]{2,1,0:T(8,128)} %bitcast_dynamic-update-slice_fusion.1, f32[768]{0:T(1024)S(1)} %copy-done.46, f32[768]{0:T(1024)S(1)} %copy-done.47, f32[768]{0:T(1024)S(1)} %copy-done.48, ...), kind=kLoop, calls=%fused_computation.80 | loop fusion | flops 31457280 | bytes 31490048 | tf_op jit(solution)/shard_map/convert_element_type | solution.py:520
  775.6 8.5 copy.290
  784.1 8.8 copy.289
  792.9 9.5 convolution_convert_fusion.6
  812.9 9.0 convert_element_type.291
  832.1 61.4 %reduce-scatter.12.cloned.1.call-done = bf16[1088,768]{1,0:T(8,128)(2,1)} async-done(((bf16[4352,768]{1,0:T(8,128)(2,1)}), bf16[1088,768]{1,0:T(8,128)(2,1)}) %reduce-scatter.12.cloned.1.call-update) | async-done | bytes 1671184 | tf_op jit(solution)/shard_map/reduce_scatter | solution.py:549
  927.9 40.0 %all-reduce.4 = (f32[2,4,768]{2,1,0:T(4,128)S(1)}, f32[2,768]{1,0:T(2,128)S(1)}, f32[2,768]{1,0:T(2,128)S(1)}) all-reduce(f32[2,4,768]{2,1,0:T(4,128)S(1)} %pad_maximum_fusion.10, f32[2,768]{1,0:T(2,128)S(1)} %pad_maximum_fusion.12, f32[2,768]{1,0:T(2,128)S(1)} %pad_maximum_fusion.13), channel_id=8, replica_groups=mesh['dp'=8,'seq'=4] {'dp','seq'}, use_global_device_ids=true, to_apply=%region_23.24.clone | all-reduce | flops 9216 | bytes 73728
  (511 shorter events, 417.5 us)
Async XLA Ops:
  7.2 51.5 %all-gather.9.cloned.1.call-start = ((), (), s32[]{:S(2)}) async-start(), calls=%async_computation.4 | async-start | bytes 7864320 | tf_op jit(solution)/shard_map/all_gather | solution.py:441
  7.9 95.5 %all-gather.11.cloned.1.call-start = ((), (), s32[]{:S(2)}) async-start(), calls=%async_computation.5 | async-start | bytes 5898240 | tf_op jit(solution)/shard_map/all_gather | solution.py:101
  58.7 127.9 %all-gather.15.cloned.1.call-start = ((), (), s32[]{:S(2)}) async-start(), calls=%async_computation.11 | async-start | bytes 3096576 | tf_op jit(solution)/shard_map/all_gather | solution.py:99
  116.4 226.6 %all-gather.13.cloned.1.call-start = ((), (), s32[]{:S(2)}) async-start(), calls=%async_computation.6 | async-start | bytes 13762560 | tf_op jit(solution)/shard_map/all_gather | solution.py:101
  143.7 13.5 %copy-start.25 = (bf16[2,512,768]{2,1,0:T(8,128)(2,1)S(1)}, bf16[2,512,768]{2,1,0:T(8,128)(2,1)}, u32[]{:S(2)}) copy-start(bf16[2,512,768]{2,1,0:T(8,128)(2,1)} %param.12) | copy-start | bytes 4718596
  200.9 529.5 %reduce-scatter.8.cloned.1.call-start = ((), (), s32[]{:S(2)}) async-start(), calls=%async_computation.7 | async-start | bytes 3932160 | tf_op jit(solution)/shard_map/reduce_scatter | solution.py:526
  223.8 11.8 %copy-start = (f32[2,512,4,768]{3,2,1,0:T(4,128)S(1)}, f32[2,512,4,768]{3,2,1,0:T(4,128)}, u32[]{:S(2)}) copy-start(f32[2,512,4,768]{3,2,1,0:T(4,128)} %reshape.1402) | copy-start | bytes 37748740
  223.8 11.8 %copy-start.43 = (f32[4,768]{1,0:T(4,128)S(1)}, f32[4,768]{1,0:T(4,128)}, u32[]{:S(2)}) copy-start(f32[4,768]{1,0:T(4,128)} %mul.349) | copy-start | bytes 36868
  312.7 15.4 %copy-start.3 = (bf16[2,4,416,768]{2,3,1,0:T(8,128)(2,1)S(1)}, bf16[2,4,416,768]{2,3,1,0:T(8,128)(2,1)}, u32[]{:S(2)}) copy-start(bf16[2,4,416,768]{2,3,1,0:T(8,128)(2,1)} %copy.247) | copy-start | bytes 15335428
  364.3 41.1 %copy-start.19 = (bf16[96,8,8,384]{3,1,2,0:T(8,128)(2,1)}, bf16[96,8,8,384]{3,1,2,0:T(8,128)(2,1)S(1)}, u32[]{:S(2)}) copy-start(bf16[96,8,8,384]{3,1,2,0:T(8,128)(2,1)S(1)} %copy.309) | copy-start | bytes 14155780
  490.3 10.4 %copy-start.15 = (bf16[4,128,12,64]{1,0,3,2:T(4,128)(2,1)}, bf16[4,128,12,64]{1,0,3,2:T(4,128)(2,1)S(1)}, u32[]{:S(2)}) copy-start(bf16[4,128,12,64]{1,0,3,2:T(4,128)(2,1)S(1)} %reshape.1377) | copy-start | bytes 2359300
  531.6 16.9 %copy-start.17 = (bf16[4,128,12,64]{1,0,3,2:T(4,128)(2,1)S(1)}, bf16[4,128,12,64]{1,0,3,2:T(4,128)(2,1)}, u32[]{:S(2)}) copy-start(bf16[4,128,12,64]{1,0,3,2:T(4,128)(2,1)} %reshape.1388) | copy-start | bytes 2359300
  568.7 20.9 %copy-start.24 = (bf16[640,1536]{1,0:T(8,128)(2,1)}, bf16[640,1536]{1,0:T(8,128)(2,1)S(1)}, u32[]{:S(2)}) copy-start(bf16[640,1536]{1,0:T(8,128)(2,1)S(1)} %get-tuple-element.68) | copy-start | bytes 5898244
  579.1 10.4 %copy-start.68 = (s32[2048]{0:T(1024)S(1)}, s32[2048]{0:T(1024)}, u32[]{:S(2)}) copy-start(s32[2048]{0:T(1024)} %add_select_fusion) | copy-start | bytes 24580
  579.1 10.4 %copy-start.73 = (s32[640]{0:T(1024)S(1)}, s32[640]{0:T(1024)}, u32[]{:S(2)}) copy-start(s32[640]{0:T(1024)} %eq.228) | copy-start | bytes 7684
  589.6 17.3 %slice-start.12 = ((s8[12582912]{0:T(1024)(128)(4,1)}), s8[4194304]{0:T(1024)(128)(4,1)S(1)}, s32[]{:S(2)}) async-start(s8[12582912]{0:T(1024)(128)(4,1)} %bitcast.431), calls=%async_computation.24 | async-start | bytes 8388608
  589.6 17.3 %slice-start.13 = ((s8[12582912]{0:T(1024)(128)(4,1)}), s8[4194304]{0:T(1024)(128)(4,1)S(1)}, s32[]{:S(2)}) async-start(s8[12582912]{0:T(1024)(128)(4,1)} %bitcast.431), calls=%async_computation.25 | async-start | bytes 8388608
  624.0 128.1 %reduce-scatter.10.cloned.1.call-start = ((), (), s32[]{:S(2)}) async-start(), calls=%async_computation.8 | async-start | bytes 13762560 | tf_op jit(solution)/shard_map/reduce_scatter | solution.py:156
  624.6 268.9 %reduce-scatter.12.cloned.1.call-start = ((), (), s32[]{:S(2)}) async-start(), calls=%async_computation.9 | async-start | bytes 8355840 | tf_op jit(solution)/shard_map/reduce_scatter | solution.py:549
  691.6 10.9 %slice-start.15 = ((s8[5111808]{0:T(1024)(128)(4,1)}), s8[4194304]{0:T(1024)(128)(4,1)S(1)}, s32[]{:S(2)}) async-start(s8[5111808]{0:T(1024)(128)(4,1)} %bitcast.433), calls=%async_computation.27 | async-start | bytes 8388608
  691.6 10.6 %copy-start.20 = (bf16[1,4,128,12,64]{2,1,4,3,0:T(4,128)(2,1)S(1)}, bf16[1,4,128,12,64]{2,1,4,3,0:T(4,128)(2,1)}, u32[]{:S(2)}) copy-start(bf16[1,4,128,12,64]{2,1,4,3,0:T(4,128)(2,1)} %copy.267) | copy-start | bytes 2359300
  691.6 10.9 %slice-start.16 = ((s8[5111808]{0:T(1024)(128)(4,1)}), s8[917504]{0:T(1024)(128)(4,1)S(1)}, s32[]{:S(2)}) async-start(s8[5111808]{0:T(1024)(128)(4,1)} %bitcast.433), calls=%async_computation.28 | async-start | bytes 1835008
  722.1 30.0 %copy-start.57 = (pred[2048]{0:T(1024)(128)(4,1)S(1)}, pred[2048]{0:T(1024)(128)(4,1)}, u32[]{:S(2)}) copy-start(pred[2048]{0:T(1024)(128)(4,1)} %get-tuple-element.233) | copy-start | bytes 6148
  722.1 30.0 %copy-start.59 = (pred[2048]{0:T(1024)(128)(4,1)S(1)}, pred[2048]{0:T(1024)(128)(4,1)}, u32[]{:S(2)}) copy-start(pred[2048]{0:T(1024)(128)(4,1)} %get-tuple-element.230) | copy-start | bytes 6148
  722.1 30.0 %copy-start.61 = (pred[2048]{0:T(1024)(128)(4,1)S(1)}, pred[2048]{0:T(1024)(128)(4,1)}, u32[]{:S(2)}) copy-start(pred[2048]{0:T(1024)(128)(4,1)} %get-tuple-element.231) | copy-start | bytes 6148
  730.4 32.8 %copy-start.10 = (bf16[2048,768]{1,0:T(8,128)(2,1)S(1)}, bf16[2048,768]{1,0:T(8,128)(2,1)}, u32[]{:S(2)}) copy-start(bf16[2048,768]{1,0:T(8,128)(2,1)} %copy-done.9) | copy-start | bytes 9437188
  784.1 18.3 %slice-start.24 = ((s8[6291456]{0:T(1024)(128)(4,1)}), s8[2097152]{0:T(1024)(128)(4,1)S(1)}, s32[]{:S(2)}) async-start(s8[6291456]{0:T(1024)(128)(4,1)} %bitcast.500), calls=%async_computation.36 | async-start | bytes 4194304
  831.8 149.4 %reduce-scatter.14.cloned.1.call-start = ((), (), s32[]{:S(2)}) async-start(), calls=%async_computation.10 | async-start | bytes 3981312 | tf_op jit(solution)/shard_map/reduce_scatter | solution.py:168
  910.9 10.1 %slice-start.3 = ((s8[12582912]{0:T(1024)(128)(4,1)}), s8[4194304]{0:T(1024)(128)(4,1)S(1)}, s32[]{:S(2)}) async-start(s8[12582912]{0:T(1024)(128)(4,1)} %bitcast.417), calls=%async_computation.15 | async-start | bytes 8388608
  910.9 10.1 %slice-start.4 = ((s8[12582912]{0:T(1024)(128)(4,1)}), s8[4194304]{0:T(1024)(128)(4,1)S(1)}, s32[]{:S(2)}) async-start(s8[12582912]{0:T(1024)(128)(4,1)} %bitcast.417), calls=%async_computation.16 | async-start | bytes 8388608
  927.9 44.5 %copy-start.13 = (f32[1024,768]{1,0:T(8,128)S(1)}, f32[1024,768]{1,0:T(8,128)}, u32[]{:S(2)}) copy-start(f32[1024,768]{1,0:T(8,128)} %copy-done.12) | copy-start | bytes 9437188
  927.9 44.5 %copy-start.67 = (f32[1024]{0:T(1024)S(1)}, f32[1024]{0:T(1024)}, u32[]{:S(2)}) copy-start(f32[1024]{0:T(1024)} %copy-done.66) | copy-start | bytes 12292
  (81 other events, 325.7 us)
Sparse Core Ops, SparseCore 0:
  9.5 49.0 all-gather.8
  60.8 37.4 all-gather.10
  116.5 56.0 all-gather.14
  201.0 73.1 all-gather.12
  624.1 37.9 reduce-scatter.7
  664.5 87.5 reduce-scatter.9
  832.0 61.4 reduce-scatter.11
  901.4 79.8 reduce-scatter.13

commit v17 on v14

--- a/solution.py
+++ b/solution.py
@@ -387,6 +387,13 @@
     return grad_queries, full, pooled, unpooled
 
 
+def back_projection(key_partial, value_partial, wk, wv):
+    rows, width = key_partial.shape
+    back = product_right(key_partial, wk) + product_right(value_partial, wv)
+    back = back.reshape(1, rows, width).astype(jnp.bfloat16)
+    return lax.psum_scatter(back, "seq", scatter_dimension=1, tiled=True)
+
+
 def select_sum(values, chosen):
     onehot = chosen.astype(jnp.bfloat16)
     high = values.astype(jnp.bfloat16)
@@ -518,15 +525,15 @@
         value_partial_g = (
             full_g[0, :, width:] + unpooled_g[0, :, width:] * value_phase
         ).astype(jnp.bfloat16)
-        back_g = product_right(key_partial_g, wk) + product_right(value_partial_g, wv)
-        back_g = back_g.reshape(1, group_len, width).astype(jnp.bfloat16)
-        back_own_g = lax.psum_scatter(back_g, "seq", scatter_dimension=1, tiled=True)
+        if g == groups - 1:
+            back_own_g = None
+        else:
+            back_own_g = back_projection(key_partial_g, value_partial_g, wk, wv)
         pieces_back.append((grad_queries_g, pooled_g, key_partial_g, value_partial_g, back_own_g))
     grad_queries = jnp.concatenate([piece[0] for piece in pieces_back], axis=0)
     grad_pooled = jnp.concatenate([piece[1] for piece in pieces_back], axis=0)
     key_partial = jnp.concatenate([piece[2] for piece in pieces_back], axis=0)
     value_partial = jnp.concatenate([piece[3] for piece in pieces_back], axis=0)
-    last_back = pieces_back[-1][4]
     early_dp = reduce_dp_stage(((early_reduced, early_widths),))
     grad_pooling = jnp.stack(
         [
@@ -538,7 +545,9 @@
     grad_key_w = product_left(all_tokens, key_partial)
     grad_value_w = product_left(all_tokens, value_partial)
     late_stacked, late_widths = stack_for_seq((grad_query_w, grad_key_w, grad_value_w))
-    late_stacked, early_dp = lax.optimization_barrier((late_stacked, early_dp))
+    late_stacked, early_dp, last_keys, last_values = lax.optimization_barrier(
+        (late_stacked, early_dp, pieces_back[-1][2], pieces_back[-1][3])
+    )
     seq_size = lax.psum(1, "seq")
     dp_size = lax.psum(1, "dp")
     rows_each = late_stacked.shape[0] // seq_size
@@ -550,7 +559,8 @@
     for width_piece in late_widths:
         late_dp.append(late_reduced[:, at : at + width_piece])
         at += width_piece
-    back_own = jnp.concatenate([piece[4] for piece in pieces_back], axis=0)
+    last_own = back_projection(last_keys, last_values, wk, wv)
+    back_own = jnp.concatenate([piece[4] for piece in pieces_back[:-1]] + [last_own], axis=0)
     grad_tokens = (
         grad_mixed
         + product_right(grad_queries, wq)

time: 999 us -> 1020 us (1.021)
  waiting for transfers between devices: 98.6 us -> 110 us
    reduce_scatter x2, waiting for transfers between devices: 0.01 us -> 37.9 us  [back_projection(): return lax.psum_scatter(back, 'seq', scatter_dimension=1, tiled=True)]
    reduce_scatter x1, waiting for transfers between devices: 54 us -> 27.6 us  [local(): lax.psum_scatter(late_blocks, ('dp', 'seq'), scatter_dimension=0, tiled=T...]
    reduce_scatter x1, waiting for transfers between devices: 42.2 us -> 21.5 us  [reduce_seq_stage(): reduced = lax.psum_scatter(stacked, 'seq', scatter_dimension=0, tiled=True)]
    reduce_scatter x1, waiting for transfers between devices: 0.02 us -> 20.3 us  [reduce_dp_stage(): lax.psum_scatter(joined, 'dp', scatter_dimension=1, tiled=True)[:, 0]]
    convert_element_type x0 -> x1, other arithmetic: none -> 12.7 us  [local(): key_partial_g = (full_g[0, :, :width] + unpooled_g[0, :, :width] * key_ph...]
    convert_element_type x2 -> x1, other arithmetic: 17.7 us -> 6.36 us  [local(): value_partial_g = (full_g[0, :, width:] + unpooled_g[0, :, width:] * valu...]
    unnamed x215 -> x227, local copies, waits for them, and re-layouts: 62.1 us -> 59.2 us
  transfers between devices with their start and end apart: 9 -> 9, of which waited for: 3 -> 5; matrix products, arithmetic and copies ran while one was open for 43% -> 40% of each run, Pallas kernels for 0% -> 0%
where the time goes in v17:
time: 1020 us; the launch traced here: 1010 us
  matrix products  297 us (29%)
  local copies, waits for them, and re-layouts  280 us (27%)
  other arithmetic  166 us (16%)
  waiting for transfers between devices  110 us (11%)
  blocking collectives  76.2 us (7%)
  between operations  76 us (7%)
    dot_general x18, matrix products, product(): return jnp.dot(left, right, preferred_element_type=jnp.float32)  127 us
    unnamed x227, local copies, waits for them, and re-layouts  59.2 us
    dot_general x8, matrix products, product_right(): lax.dot_general(left, right, (((1,), (1,)), ((), ())), preferred_element_...  51.1 us
    unnamed x1, blocking collectives  41.1 us
    reduce_scatter x2, waiting for transfers between devices, back_projection(): return lax.psum_scatter(back, 'seq', scatter_dimension=1, tiled=True)  37.9 us
    all_gather x1, blocking collectives, gather_grouped(): across = lax.all_gather(local_block, 'dp', axis=1, tiled=False)  35.1 us
    dot_general x6, matrix products, product_left(): lax.dot_general(left, right, (((0,), (0,)), ((), ())), preferred_element_...  34.5 us
    reduce_scatter x1, waiting for transfers between devices, local(): lax.psum_scatter(late_blocks, ('dp', 'seq'), scatter_dimension=0, tiled=T...  27.6 us
  transfers between devices with their start and end apart: 9, of which 5 were waited for; matrix products, arithmetic and copies ran while one was open for 40% of the time, Pallas kernels for 0%

profile of v17, /device:TPU:0, one launch (start us, length us, event | category | flops | bytes accessed | tf_op | source)
XLA Modules:
  0.0 1005.3 jit_solution(2559960875079723905)
XLA Ops:
  13.8 35.1 %all-gather.2 = bf16[8,293,192]{1,2,0:T(8,128)(2,1)S(1)} all-gather(bf16[1,293,192]{1,2,0:T(8,128)(2,1)S(1)} %maximum_bitcast_fusion.11), channel_id=2, replica_groups=mesh['dp'=8,'seq'=4] {'dp'}, dimensions={0}, use_global_device_ids=true | all-gather | bytes 1012608 | tf_op jit(solution)/shard_map/all_gather | solution.py:99
  164.9 9.7 convolution_convert_fusion
  174.6 12.3 %reshape.1392 = f32[2,512,4,768]{3,2,1,0:T(4,128)} reshape(bf16[4096,768]{1,0:T(8,128)(2,1)} %convolution_convert_fusion) | data formatting | bytes 18874368 | tf_op jit(solution)/shard_map/convert_element_type | solution.py:468
  201.3 10.0 convolution_convert_fusion.1
  211.2 12.7 %reshape.1390 = f32[2,512,4,768]{3,2,1,0:T(4,128)} reshape(bf16[4096,768]{1,0:T(8,128)(2,1)} %convolution_convert_fusion.1) | data formatting | bytes 18874368 | tf_op jit(solution)/shard_map/convert_element_type | solution.py:467
  223.9 11.7 %multiply_reduce_fusion.2 = bf16[2,512,768]{2,1,0:T(8,128)(2,1)S(1)} fusion(f32[2,512,4,768]{3,2,1,0:T(4,128)} %reshape.1392, f32[4,768]{1,0:T(4,128)S(1)} %mul.352), kind=kLoop, calls=%fused_computation.31 | loop fusion | flops 5505024 | bytes 14168064 | tf_op jit(solution)/shard_map/reduce_sum | solution.py:414
  300.0 13.3 %fusion.182 = (f32[2,4,12,128]{3,2,1,0:T(8,128)S(1)}, f32[2,4,12,128,416]{3,4,2,1,0:T(8,128)}) fusion(pred[2,4,128,416]{2,3,1,0:T(8,128)(4,1)S(1)} %copy-done.40, bf16[2,4,416,12,64]{2,4,3,1,0:T(8,128)(2,1)} %bitcast.460, bf16[2,4,128,12,64]{2,1,0,4,3:T(4,128)(2,1)S(1)} %copy-done.29), kind=kOutput, calls=%fused_computation.456 | convolution fusion | flops 674759040 | bytes 27607040 | tf_op jit(solution)/shard_map/sub | solution.py:310
  313.3 15.4 %broadcast_divide_fusion = f32[2,4,12,128,416]{3,4,2,1,0:T(8,128)} fusion(f32[2,4,12,128,416]{3,4,2,1,0:T(8,128)} %get-tuple-element.233, f32[2,4,12,128]{3,2,1,0:T(8,128)S(1)} %get-tuple-element.232), kind=kLoop, calls=%fused_computation.45 | loop fusion | flops 5111808 | bytes 40943616 | tf_op jit(solution)/shard_map/div | solution.py:312
  328.6 10.0 fusion.88
  346.9 14.2 %fusion.168 = (bf16[768,8,384]{2,1,0:T(8,128)(2,1)}, bf16[768,8,384]{2,1,0:T(8,128)(2,1)}) fusion(bf16[768,8,864]{2,1,0:T(8,128)(2,1)} %all-gather.13.cloned.1.call-done), kind=kLoop, calls=%fused_computation.442 | loop fusion | bytes 18874368 | tf_op jit(solution)/shard_map/slice | solution.py:107
  371.1 34.6 %multiply_convert_fusion = (bf16[1024,3072]{1,0:T(8,128)(2,1)S(1)}, f32[1024,3072]{1,0:T(8,128)}, f32[1024,3072]{1,0:T(8,128)}) fusion(bf16[768,3072]{1,0:T(8,128)(2,1)S(1)} %bitcast.461, f32[1024,768]{1,0:T(8,128)S(1)} %get-tuple-element.235, f32[768]{0:T(1024)S(1)} %copy-done.71, f32[768]{0:T(1024)S(1)} %copy-done.63, f32[1024]{0:T(1024)S(1)} %fusion.143, ...), kind=kOutput, calls=%fused_computation.18 | convolution fusion | flops 5040242688 | bytes 39335936 | tf_op jit(solution)/shard_map/dot_general | solution.py:78
  424.5 18.5 %add_convert_fusion = bf16[1024,3072]{1,0:T(8,128)(2,1)} fusion(f32[1024,3072]{1,0:T(8,128)} %get-tuple-element.90, f32[1024,3072]{1,0:T(8,128)} %get-tuple-element.236, bf16[768,3072]{1,0:T(8,128)(2,1)} %bitcast.464, f32[1024,768]{1,0:T(8,128)} %copy-done.24, f32[1024]{0:T(1024)S(1)} %negate_multiply_fusion.2), kind=kOutput, calls=%fused_computation.17 | convolution fusion | flops 4877451264 | bytes 39325696 | tf_op jit(solution)/shard_map/dot_general | solution.py:88
  442.9 9.5 multiply_reduce_fusion.4
  477.5 11.2 %pad_maximum_fusion = bf16[768,8,864]{2,0,1:T(8,128)(2,1)} fusion(bf16[768,8,384]{2,0,1:T(8,128)(2,1)} %bitcast.447, bf16[768,8,384]{2,0,1:T(8,128)(2,1)} %bitcast.446, bf16[768,8,96]{2,0,1:T(8,128)(2,1)S(1)} %copy.258), kind=kLoop, calls=%fused_computation.34 | loop fusion | flops 31850496 | bytes 21233664 | tf_op jit(solution)/shard_map/concatenate | solution.py:154
  492.0 9.1 fusion.36
  514.3 17.5 %fusion.11 = (f32[4,12,128]{2,1,0:T(8,128)S(1)}, f32[4,12,128]{2,1,0:T(8,128)S(1)}, f32[4,12,128,416]{2,3,1,0:T(8,128)}) fusion(f32[2,4,12,128,416]{3,4,2,1,0:T(8,128)} %broadcast_divide_fusion, f32[4,12,128,416]{2,3,1,0:T(8,128)} %fusion.109, bf16[4,416,12,64]{1,3,2,0:T(8,128)(2,1)} %bitcast.452, bf16[4,128,12,64]{1,0,3,2:T(4,128)(2,1)} %copy-done.16), kind=kOutput, calls=%fused_computation.42 | convolution fusion | flops 337367040 | bytes 44285952 | tf_op jit(solution)/shard_map/gbqhd,gbkhd->gbhqk/dot_general | solution.py:329
  531.9 16.9 %fusion.41 = (bf16[4,12,128,416]{2,3,1,0:T(8,128)(2,1)S(1)}, bf16[4,12,128,416]{2,3,1,0:T(8,128)(2,1)}) fusion(f32[4,12,128,416]{2,3,1,0:T(8,128)} %get-tuple-element.240, f32[2,4,12,128,416]{3,4,2,1,0:T(8,128)} %broadcast_divide_fusion, f32[4,12,128]{2,1,0:T(8,128)S(1)} %get-tuple-element.63, f32[4,12,128,416]{2,3,1,0:T(8,128)} %fusion.109, ...), kind=kLoop, calls=%fused_computation.91 | loop fusion | flops 15335424 | bytes 51167232 | tf_op jit(solution)/shard_map/reshape.169
  579.6 10.4 %copy.346 = f32[1,2048,1536]{2,1,0:T(8,128)} copy(f32[1,2048,1536]{2,1,0:T(8,128)} %bitcast.421) | data formatting | bytes 25165824
  598.1 9.0 add_bitcast_fusion
  634.7 9.3 fusion.39
  672.6 8.7 pad_maximum_fusion.6
  692.2 10.6 %copy.345 = f32[1,2048,1536]{2,1,0:T(8,128)} copy(f32[1,2048,1536]{2,1,0:T(8,128)} %bitcast.420) | data formatting | bytes 25165824
  730.9 21.5 %reduce-scatter.11.cloned.1.call-done = bf16[192,8,864]{2,0,1:T(8,128)(2,1)} async-done(((bf16[768,8,864]{2,0,1:T(8,128)(2,1)}), bf16[192,8,864]{2,0,1:T(8,128)(2,1)}) %reduce-scatter.11.cloned.1.call-update) | async-done | bytes 2654224 | tf_op jit(solution)/shard_map/reduce_scatter | solution.py:156
  752.5 12.7 %fusion.34 = (bf16[2048,768]{1,0:T(8,128)(2,1)S(1)}, bf16[2048,768]{1,0:T(8,128)(2,1)}) fusion(f32[1,2048,1536]{2,1,0:T(8,128)} %add_bitcast_fusion.1, f32[1,2048,1536]{2,1,0:T(8,128)} %bitcast_dynamic-update-slice_fusion.1, f32[768]{0:T(1024)S(1)} %copy-done.50, f32[768]{0:T(1024)S(1)} %copy-done.51, f32[768]{0:T(1024)S(1)} %copy-done.52, ...), kind=kLoop, calls=%fused_computation.82 | loop fusion | flops 31457280 | bytes 31490048 | tf_op jit(solution)/shard_map/convert_element_type | solution.py:524
  770.0 8.8 copy.286
  783.8 8.9 copy.287
  792.7 9.1 convolution_convert_fusion.7
  807.4 20.3 %reduce-scatter.13.cloned.1.call-done = bf16[192,1,864]{2,0,1:T(8,128)(2,1)} async-done(((bf16[192,8,864]{2,0,1:T(8,128)(2,1)}), bf16[192,1,864]{2,0,1:T(8,128)(2,1)}) %reduce-scatter.13.cloned.1.call-update) | async-done | bytes 331792 | tf_op jit(solution)/shard_map/reduce_scatter | solution.py:168
  835.9 9.9 copy.288
  882.2 41.1 %all-reduce.4 = (f32[2,4,768]{2,1,0:T(4,128)S(1)}, f32[2,768]{1,0:T(2,128)S(1)}, f32[2,768]{1,0:T(2,128)S(1)}) all-reduce(f32[2,4,768]{2,1,0:T(4,128)S(1)} %pad_maximum_fusion.8, f32[2,768]{1,0:T(2,128)S(1)} %pad_maximum_fusion.10, f32[2,768]{1,0:T(2,128)S(1)} %pad_maximum_fusion.11), channel_id=9, replica_groups=mesh['dp'=8,'seq'=4] {'dp','seq'}, use_global_device_ids=true, to_apply=%region_24.25.clone | all-reduce | flops 9216 | bytes 73728
  925.2 27.6 %reduce-scatter.17.cloned.1.call-done = bf16[192,288]{1,0:T(8,128)(2,1)} async-done(((bf16[6144,288]{1,0:T(8,128)(2,1)}), bf16[192,288]{1,0:T(8,128)(2,1)}) %reduce-scatter.17.cloned.1.call-update) | async-done | bytes 110608 | tf_op jit(solution)/shard_map/reduce_scatter | solution.py:556
  954.6 37.9 %reduce-scatter.15.cloned.1.call-done = bf16[1,512,768]{2,1,0:T(8,128)(2,1)} async-done(((bf16[1,2048,768]{2,1,0:T(8,128)(2,1)}), bf16[1,512,768]{2,1,0:T(8,128)(2,1)}) %reduce-scatter.15.cloned.1.call-update) | async-done | bytes 786448 | tf_op jit(solution)/shard_map/reduce_scatter | solution.py:394
  (511 shorter events, 421.8 us)
Async XLA Ops:
  7.2 51.5 %all-gather.9.cloned.1.call-start = ((), (), s32[]{:S(2)}) async-start(), calls=%async_computation.5 | async-start | bytes 7864320 | tf_op jit(solution)/shard_map/all_gather | solution.py:448
  7.9 95.8 %all-gather.11.cloned.1.call-start = ((), (), s32[]{:S(2)}) async-start(), calls=%async_computation.6 | async-start | bytes 5898240 | tf_op jit(solution)/shard_map/all_gather | solution.py:101
  58.7 128.2 %all-gather.15.cloned.1.call-start = ((), (), s32[]{:S(2)}) async-start(), calls=%async_computation.13 | async-start | bytes 3096576 | tf_op jit(solution)/shard_map/all_gather | solution.py:99
  116.8 226.8 %all-gather.13.cloned.1.call-start = ((), (), s32[]{:S(2)}) async-start(), calls=%async_computation.7 | async-start | bytes 13762560 | tf_op jit(solution)/shard_map/all_gather | solution.py:101
  144.2 13.5 %copy-start.26 = (bf16[2,512,768]{2,1,0:T(8,128)(2,1)S(1)}, bf16[2,512,768]{2,1,0:T(8,128)(2,1)}, u32[]{:S(2)}) copy-start(bf16[2,512,768]{2,1,0:T(8,128)(2,1)} %param.12) | copy-start | bytes 4718596
  201.2 529.7 %reduce-scatter.9.cloned.1.call-start = ((), (), s32[]{:S(2)}) async-start(), calls=%async_computation.8 | async-start | bytes 3932160 | tf_op jit(solution)/shard_map/reduce_scatter | solution.py:394
  223.9 11.8 %copy-start = (f32[2,512,4,768]{3,2,1,0:T(4,128)S(1)}, f32[2,512,4,768]{3,2,1,0:T(4,128)}, u32[]{:S(2)}) copy-start(f32[2,512,4,768]{3,2,1,0:T(4,128)} %reshape.1390) | copy-start | bytes 37748740
  223.9 11.8 %copy-start.44 = (f32[4,768]{1,0:T(4,128)S(1)}, f32[4,768]{1,0:T(4,128)}, u32[]{:S(2)}) copy-start(f32[4,768]{1,0:T(4,128)} %mul.349) | copy-start | bytes 36868
  313.3 15.4 %copy-start.3 = (bf16[2,4,416,768]{2,3,1,0:T(8,128)(2,1)S(1)}, bf16[2,4,416,768]{2,3,1,0:T(8,128)(2,1)}, u32[]{:S(2)}) copy-start(bf16[2,4,416,768]{2,3,1,0:T(8,128)(2,1)} %copy.244) | copy-start | bytes 15335428
  364.8 40.9 %copy-start.20 = (bf16[96,8,8,384]{3,1,2,0:T(8,128)(2,1)}, bf16[96,8,8,384]{3,1,2,0:T(8,128)(2,1)S(1)}, u32[]{:S(2)}) copy-start(bf16[96,8,8,384]{3,1,2,0:T(8,128)(2,1)S(1)} %copy.305) | copy-start | bytes 14155780
  490.7 10.4 %copy-start.16 = (bf16[4,128,12,64]{1,0,3,2:T(4,128)(2,1)}, bf16[4,128,12,64]{1,0,3,2:T(4,128)(2,1)S(1)}, u32[]{:S(2)}) copy-start(bf16[4,128,12,64]{1,0,3,2:T(4,128)(2,1)S(1)} %reshape.1367) | copy-start | bytes 2359300
  531.9 16.9 %copy-start.18 = (bf16[4,128,12,64]{1,0,3,2:T(4,128)(2,1)S(1)}, bf16[4,128,12,64]{1,0,3,2:T(4,128)(2,1)}, u32[]{:S(2)}) copy-start(bf16[4,128,12,64]{1,0,3,2:T(4,128)(2,1)} %reshape.1378) | copy-start | bytes 2359300
  569.2 20.9 %copy-start.25 = (bf16[640,1536]{1,0:T(8,128)(2,1)}, bf16[640,1536]{1,0:T(8,128)(2,1)S(1)}, u32[]{:S(2)}) copy-start(bf16[640,1536]{1,0:T(8,128)(2,1)S(1)} %get-tuple-element.80) | copy-start | bytes 5898244
  579.6 10.5 %copy-start.69 = (s32[2048]{0:T(1024)S(1)}, s32[2048]{0:T(1024)}, u32[]{:S(2)}) copy-start(s32[2048]{0:T(1024)} %add_select_fusion) | copy-start | bytes 24580
  579.6 10.5 %copy-start.74 = (s32[640]{0:T(1024)S(1)}, s32[640]{0:T(1024)}, u32[]{:S(2)}) copy-start(s32[640]{0:T(1024)} %eq.228) | copy-start | bytes 7684
  590.1 17.1 %slice-start.12 = ((s8[12582912]{0:T(1024)(128)(4,1)}), s8[4194304]{0:T(1024)(128)(4,1)S(1)}, s32[]{:S(2)}) async-start(s8[12582912]{0:T(1024)(128)(4,1)} %bitcast.432), calls=%async_computation.26 | async-start | bytes 8388608
  590.1 17.1 %slice-start.13 = ((s8[12582912]{0:T(1024)(128)(4,1)}), s8[4194304]{0:T(1024)(128)(4,1)S(1)}, s32[]{:S(2)}) async-start(s8[12582912]{0:T(1024)(128)(4,1)} %bitcast.432), calls=%async_computation.27 | async-start | bytes 8388608
  624.3 128.1 %reduce-scatter.11.cloned.1.call-start = ((), (), s32[]{:S(2)}) async-start(), calls=%async_computation.9 | async-start | bytes 13762560 | tf_op jit(solution)/shard_map/reduce_scatter | solution.py:156
  624.9 202.8 %reduce-scatter.13.cloned.1.call-start = ((), (), s32[]{:S(2)}) async-start(), calls=%async_computation.10 | async-start | bytes 3096576 | tf_op jit(solution)/shard_map/reduce_scatter | solution.py:168
  692.2 10.9 %slice-start.15 = ((s8[5111808]{0:T(1024)(128)(4,1)}), s8[4194304]{0:T(1024)(128)(4,1)S(1)}, s32[]{:S(2)}) async-start(s8[5111808]{0:T(1024)(128)(4,1)} %bitcast.434), calls=%async_computation.29 | async-start | bytes 8388608
  692.2 10.6 %copy-start.21 = (bf16[1,4,128,12,64]{2,1,4,3,0:T(4,128)(2,1)S(1)}, bf16[1,4,128,12,64]{2,1,4,3,0:T(4,128)(2,1)}, u32[]{:S(2)}) copy-start(bf16[1,4,128,12,64]{2,1,4,3,0:T(4,128)(2,1)} %copy.264) | copy-start | bytes 2359300
  692.2 10.9 %slice-start.16 = ((s8[5111808]{0:T(1024)(128)(4,1)}), s8[917504]{0:T(1024)(128)(4,1)S(1)}, s32[]{:S(2)}) async-start(s8[5111808]{0:T(1024)(128)(4,1)} %bitcast.434), calls=%async_computation.30 | async-start | bytes 1835008
  722.7 29.8 %copy-start.58 = (pred[2048]{0:T(1024)(128)(4,1)S(1)}, pred[2048]{0:T(1024)(128)(4,1)}, u32[]{:S(2)}) copy-start(pred[2048]{0:T(1024)(128)(4,1)} %get-tuple-element.244) | copy-start | bytes 6148
  722.7 29.8 %copy-start.60 = (pred[2048]{0:T(1024)(128)(4,1)S(1)}, pred[2048]{0:T(1024)(128)(4,1)}, u32[]{:S(2)}) copy-start(pred[2048]{0:T(1024)(128)(4,1)} %get-tuple-element.241) | copy-start | bytes 6148
  722.7 29.8 %copy-start.62 = (pred[2048]{0:T(1024)(128)(4,1)S(1)}, pred[2048]{0:T(1024)(128)(4,1)}, u32[]{:S(2)}) copy-start(pred[2048]{0:T(1024)(128)(4,1)} %get-tuple-element.242) | copy-start | bytes 6148
  752.5 14.4 %copy-start.10 = (bf16[2048,768]{1,0:T(8,128)(2,1)S(1)}, bf16[2048,768]{1,0:T(8,128)(2,1)}, u32[]{:S(2)}) copy-start(bf16[2048,768]{1,0:T(8,128)(2,1)} %copy-done.9) | copy-start | bytes 9437188
  752.5 200.4 %reduce-scatter.17.cloned.1.call-start = ((), (), s32[]{:S(2)}) async-start(), calls=%async_computation.12 | async-start | bytes 4866048 | tf_op jit(solution)/shard_map/reduce_scatter | solution.py:556
  783.8 18.0 %slice-start.24 = ((s8[6291456]{0:T(1024)(128)(4,1)}), s8[2097152]{0:T(1024)(128)(4,1)S(1)}, s32[]{:S(2)}) async-start(s8[6291456]{0:T(1024)(128)(4,1)} %bitcast.502), calls=%async_computation.38 | async-start | bytes 4194304
  845.8 146.7 %reduce-scatter.15.cloned.1.call-start = ((), (), s32[]{:S(2)}) async-start(), calls=%async_computation.11 | async-start | bytes 3932160 | tf_op jit(solution)/shard_map/reduce_scatter | solution.py:394
  865.1 10.2 %slice-start.4 = ((s8[12582912]{0:T(1024)(128)(4,1)}), s8[4194304]{0:T(1024)(128)(4,1)S(1)}, s32[]{:S(2)}) async-start(s8[12582912]{0:T(1024)(128)(4,1)} %bitcast.418), calls=%async_computation.18 | async-start | bytes 8388608
  882.2 111.8 %copy-start.14 = (f32[1024,768]{1,0:T(8,128)S(1)}, f32[1024,768]{1,0:T(8,128)}, u32[]{:S(2)}) copy-start(f32[1024,768]{1,0:T(8,128)} %copy-done.13) | copy-start | bytes 9437188
  882.2 111.8 %copy-start.68 = (f32[1024]{0:T(1024)S(1)}, f32[1024]{0:T(1024)}, u32[]{:S(2)}) copy-start(f32[1024]{0:T(1024)} %copy-done.67) | copy-start | bytes 12292
  (83 other events, 336.8 us)
Sparse Core Ops, SparseCore 0:
  9.5 49.0 all-gather.8
  60.8 37.4 all-gather.10
  116.9 56.0 all-gather.14
  201.3 73.1 all-gather.12
  624.4 37.9 reduce-scatter.8
  664.9 87.5 reduce-scatter.10
  756.0 71.6 reduce-scatter.12
  845.9 106.8 reduce-scatter.16
  955.4 37.0 reduce-scatter.14

commit v18 on v14

--- a/solution.py
+++ b/solution.py
@@ -378,7 +378,10 @@
         fulls.append(full[g] + select_sum(side_values[g], side_rows[g] == ramp(group_len)[:, None]))
         pooleds.append(select_sum(pool_values[g], pool_rows_index[g] == ramp(pooled_len)[:, None]))
         unpooleds.append(
-            select_sum(pool_values[g], pool_rows_index[g] == (ramp(group_len) // STRIDE)[:, None])
+            product(
+                (pool_rows_index[g] == (ramp(group_len) // STRIDE)[:, None]).astype(jnp.bfloat16),
+                pool_values[g].astype(jnp.bfloat16),
+            )
         )
     full = jnp.stack(fulls)
     pooled = jnp.stack(pooleds)

time: 999 us -> 988 us (0.989)
  matrix products: 297 us -> 281 us
    dot_general x18 -> x16, matrix products: 127 us -> 111 us  [product(): return jnp.dot(left, right, preferred_element_type=jnp.float32)]
    unnamed x215 -> x217, local copies, waits for them, and re-layouts: 62.1 us -> 62 us
where the time goes in v18:
time: 988 us; the launch traced here: 979 us
  matrix products  281 us (28%)
  local copies, waits for them, and re-layouts  280 us (28%)
  other arithmetic  161 us (16%)
  waiting for transfers between devices  103 us (10%)
  between operations  77 us (8%)
  blocking collectives  75.1 us (8%)
    dot_general x16, matrix products, product(): return jnp.dot(left, right, preferred_element_type=jnp.float32)  111 us
    unnamed x217, local copies, waits for them, and re-layouts  62 us
    reduce_scatter x1, waiting for transfers between devices, local(): lax.psum_scatter(late_blocks, ('dp', 'seq'), scatter_dimension=0, tiled=T...  54.2 us
    dot_general x8, matrix products, product_right(): lax.dot_general(left, right, (((1,), (1,)), ((), ())), preferred_element_...  49 us
    reduce_scatter x1, waiting for transfers between devices, reduce_seq_stage(): reduced = lax.psum_scatter(stacked, 'seq', scatter_dimension=0, tiled=True)  46.9 us
    unnamed x1, blocking collectives  40 us
    all_gather x1, blocking collectives, gather_grouped(): across = lax.all_gather(local_block, 'dp', axis=1, tiled=False)  35.1 us
    dot_general x6, matrix products, product_left(): lax.dot_general(left, right, (((0,), (0,)), ((), ())), preferred_element_...  34.4 us
  transfers between devices with their start and end apart: 9, of which 3 were waited for; matrix products, arithmetic and copies ran while one was open for 43% of the time, Pallas kernels for 0%

profile of v18, /device:TPU:0, one launch (start us, length us, event | category | flops | bytes accessed | tf_op | source)
XLA Modules:
  0.0 978.5 jit_solution(7084491338679548513)
XLA Ops:
  13.8 35.1 %all-gather.2 = bf16[8,293,192]{1,2,0:T(8,128)(2,1)S(1)} all-gather(bf16[1,293,192]{1,2,0:T(8,128)(2,1)S(1)} %maximum_bitcast_fusion.11), channel_id=2, replica_groups=mesh['dp'=8,'seq'=4] {'dp'}, dimensions={0}, use_global_device_ids=true | all-gather | bytes 1012608 | tf_op jit(solution)/shard_map/all_gather | solution.py:99
  165.7 9.7 convolution_convert_fusion
  175.4 12.3 %reshape.1392 = f32[2,512,4,768]{3,2,1,0:T(4,128)} reshape(bf16[4096,768]{1,0:T(8,128)(2,1)} %convolution_convert_fusion) | data formatting | bytes 18874368 | tf_op jit(solution)/shard_map/convert_element_type | solution.py:464
  202.1 10.3 %convolution_convert_fusion.1 = bf16[4096,768]{1,0:T(8,128)(2,1)} fusion(bf16[4096,768]{1,0:T(8,128)(2,1)} %bitcast.496, bf16[768,768]{0,1:T(8,128)(2,1)S(1)} %bitcast.482), kind=kOutput, calls=%fused_computation.54 | convolution fusion | flops 4834983936 | bytes 13762560 | tf_op jit(solution)/shard_map/dot_general | solution.py:78
  212.4 12.6 %reshape.1390 = f32[2,512,4,768]{3,2,1,0:T(4,128)} reshape(bf16[4096,768]{1,0:T(8,128)(2,1)} %convolution_convert_fusion.1) | data formatting | bytes 18874368 | tf_op jit(solution)/shard_map/convert_element_type | solution.py:463
  225.0 11.7 %multiply_reduce_fusion.2 = bf16[2,512,768]{2,1,0:T(8,128)(2,1)S(1)} fusion(f32[2,512,4,768]{3,2,1,0:T(4,128)} %reshape.1392, f32[4,768]{1,0:T(4,128)S(1)} %mul.352), kind=kLoop, calls=%fused_computation.29 | loop fusion | flops 5505024 | bytes 14168064 | tf_op jit(solution)/shard_map/reduce_sum | solution.py:410
  236.8 8.5 multiply_reduce_fusion.3
  261.3 8.6 fusion.162
  292.5 8.2 copy.244
  300.7 13.3 %fusion.174 = (f32[2,4,12,128]{3,2,1,0:T(8,128)S(1)}, f32[2,4,12,128,416]{3,4,2,1,0:T(8,128)}) fusion(pred[2,4,128,416]{2,3,1,0:T(8,128)(4,1)S(1)} %copy-done.42, bf16[2,4,416,12,64]{2,4,3,1,0:T(8,128)(2,1)} %bitcast.456, bf16[2,4,128,12,64]{2,1,0,4,3:T(4,128)(2,1)S(1)} %copy-done.30), kind=kOutput, calls=%fused_computation.448 | convolution fusion | flops 674759040 | bytes 27607040 | tf_op jit(solution)/shard_map/sub | solution.py:310
  314.0 15.3 %broadcast_divide_fusion = f32[2,4,12,128,416]{3,4,2,1,0:T(8,128)} fusion(f32[2,4,12,128,416]{3,4,2,1,0:T(8,128)} %get-tuple-element.229, f32[2,4,12,128]{3,2,1,0:T(8,128)S(1)} %get-tuple-element.228), kind=kLoop, calls=%fused_computation.43 | loop fusion | flops 5111808 | bytes 40943616 | tf_op jit(solution)/shard_map/div | solution.py:312
  329.3 10.0 %fusion.80 = bf16[2,4,128,12,64]{2,4,3,1,0:T(8,128)(2,1)} fusion(bf16[2,4,416,12,64]{2,4,3,1,0:T(8,128)(2,1)S(1)} %bitcast.436, f32[2,4,12,128,416]{3,4,2,1,0:T(8,128)} %broadcast_divide_fusion), kind=kOutput, calls=%fused_computation.196 | convolution fusion | flops 660209664 | bytes 27131904 | tf_op jit(solution)/shard_map/gbhqk,gbkhd->gbqhd/dot_general | solution.py:313
  347.6 14.2 %fusion.160 = (bf16[768,8,384]{2,1,0:T(8,128)(2,1)}, bf16[768,8,384]{2,1,0:T(8,128)(2,1)}) fusion(bf16[768,8,864]{2,1,0:T(8,128)(2,1)} %all-gather.13.cloned.1.call-done), kind=kLoop, calls=%fused_computation.434 | loop fusion | bytes 18874368 | tf_op jit(solution)/shard_map/slice | solution.py:107
  371.8 34.9 %multiply_convert_fusion = (bf16[1024,3072]{1,0:T(8,128)(2,1)S(1)}, f32[1024,3072]{1,0:T(8,128)}, f32[1024,3072]{1,0:T(8,128)}) fusion(bf16[768,3072]{1,0:T(8,128)(2,1)S(1)} %bitcast.457, f32[1024,768]{1,0:T(8,128)S(1)} %get-tuple-element.231, f32[768]{0:T(1024)S(1)} %copy-done.69, f32[768]{0:T(1024)S(1)} %copy-done.62, f32[1024]{0:T(1024)S(1)} %fusion.135, ...), kind=kOutput, calls=%fused_computation.16 | convolution fusion | flops 5040242688 | bytes 39335936 | tf_op jit(solution)/shard_map/dot_general | solution.py:78
  425.2 18.5 %add_convert_fusion = bf16[1024,3072]{1,0:T(8,128)(2,1)} fusion(f32[1024,3072]{1,0:T(8,128)} %get-tuple-element.86, f32[1024,3072]{1,0:T(8,128)} %get-tuple-element.232, bf16[768,3072]{1,0:T(8,128)(2,1)} %bitcast.460, f32[1024,768]{1,0:T(8,128)} %copy-done.25, f32[1024]{0:T(1024)S(1)} %negate_multiply_fusion.2), kind=kOutput, calls=%fused_computation.15 | convolution fusion | flops 4877451264 | bytes 39325696 | tf_op jit(solution)/shard_map/dot_general | solution.py:88
  443.8 9.4 multiply_reduce_fusion.4
  478.3 11.3 %pad_maximum_fusion = bf16[768,8,864]{2,0,1:T(8,128)(2,1)} fusion(bf16[768,8,384]{2,0,1:T(8,128)(2,1)} %bitcast.443, bf16[768,8,384]{2,0,1:T(8,128)(2,1)} %bitcast.442, bf16[768,8,96]{2,0,1:T(8,128)(2,1)S(1)} %copy.258), kind=kLoop, calls=%fused_computation.32 | loop fusion | flops 31850496 | bytes 21233664 | tf_op jit(solution)/shard_map/concatenate | solution.py:154
  492.9 9.0 fusion.32
  515.3 17.5 %fusion.11 = (f32[4,12,128]{2,1,0:T(8,128)S(1)}, f32[4,12,128]{2,1,0:T(8,128)S(1)}, f32[4,12,128,416]{2,3,1,0:T(8,128)}) fusion(f32[2,4,12,128,416]{3,4,2,1,0:T(8,128)} %broadcast_divide_fusion, f32[4,12,128,416]{2,3,1,0:T(8,128)} %fusion.101, bf16[4,416,12,64]{1,3,2,0:T(8,128)(2,1)} %bitcast.448, bf16[4,128,12,64]{1,0,3,2:T(4,128)(2,1)} %copy-done.19), kind=kOutput, calls=%fused_computation.40 | convolution fusion | flops 337367040 | bytes 44285952 | tf_op jit(solution)/shard_map/gbqhd,gbkhd->gbhqk/dot_general | solution.py:329
  532.8 16.8 %fusion.37 = (bf16[4,12,128,416]{2,3,1,0:T(8,128)(2,1)S(1)}, bf16[4,12,128,416]{2,3,1,0:T(8,128)(2,1)}) fusion(f32[4,12,128,416]{2,3,1,0:T(8,128)} %get-tuple-element.236, f32[2,4,12,128,416]{3,4,2,1,0:T(8,128)} %broadcast_divide_fusion, f32[4,12,128]{2,1,0:T(8,128)S(1)} %get-tuple-element.59, f32[4,12,128,416]{2,3,1,0:T(8,128)} %fusion.101, ...), kind=kLoop, calls=%fused_computation.87 | loop fusion | flops 15335424 | bytes 51167232 | tf_op jit(solution)/shard_map/reshape.169
  580.2 10.4 %copy.346 = f32[1,2048,1536]{2,1,0:T(8,128)} copy(f32[1,2048,1536]{2,1,0:T(8,128)} %bitcast.419) | data formatting | bytes 25165824
  615.1 9.1 fusion.35
  630.4 8.1 broadcast_multiply_fusion.1
  661.5 14.3 %copy.345 = f32[1,2048,1536]{2,1,0:T(8,128)} copy(f32[1,2048,1536]{2,1,0:T(8,128)} %bitcast.418) | data formatting | bytes 25165824
  695.0 46.9 %reduce-scatter.11.cloned.1.call-done = bf16[192,8,864]{2,0,1:T(8,128)(2,1)} async-done(((bf16[768,8,864]{2,0,1:T(8,128)(2,1)}), bf16[192,8,864]{2,0,1:T(8,128)(2,1)}) %reduce-scatter.11.cloned.1.call-update) | async-done | bytes 2654224 | tf_op jit(solution)/shard_map/reduce_scatter | solution.py:156
  749.7 11.3 %fusion.26 = (bf16[2048,768]{1,0:T(8,128)(2,1)S(1)}, bf16[2048,768]{1,0:T(8,128)(2,1)S(1)}) fusion(f32[1,2048,1536]{2,1,0:T(8,128)} %convolution_bitcast_fusion.1, f32[1,2048,1536]{2,1,0:T(8,128)} %bitcast_dynamic-update-slice_fusion.1, f32[768]{0:T(1024)S(1)} %copy-done.49, f32[768]{0:T(1024)S(1)} %copy-done.50, f32[768]{0:T(1024)S(1)} %copy-done.51, ...), kind=kLoop, calls=%fused_computation.73 | loop fusion | flops 31457280 | bytes 31490048 | tf_op jit(solution)/shard_map/convert_element_type | solution.py:523
  784.5 9.1 copy.287
  798.5 8.7 copy.286
  807.3 9.2 convolution_convert_fusion.6
  830.3 10.1 %copy.288 = bf16[8,4,192,288]{3,2,1,0:T(8,128)(2,1)} copy(bf16[8,4,192,288]{2,1,3,0:T(4,128)(2,1)} %bitcast.441) | data formatting | bytes 7077888 | tf_op jit(solution)/shard_map/transpose | solution.py:549
  867.1 40.0 %all-reduce.4 = (f32[2,4,768]{2,1,0:T(4,128)S(1)}, f32[2,768]{1,0:T(2,128)S(1)}, f32[2,768]{1,0:T(2,128)S(1)}) all-reduce(f32[2,4,768]{2,1,0:T(4,128)S(1)} %pad_maximum_fusion.8, f32[2,768]{1,0:T(2,128)S(1)} %pad_maximum_fusion.10, f32[2,768]{1,0:T(2,128)S(1)} %pad_maximum_fusion.11), channel_id=9, replica_groups=mesh['dp'=8,'seq'=4] {'dp','seq'}, use_global_device_ids=true, to_apply=%region_24.25.clone | all-reduce | flops 9216 | bytes 73728
  915.6 54.2 %reduce-scatter.17.cloned.1.call-done = bf16[192,288]{1,0:T(8,128)(2,1)} async-done(((bf16[6144,288]{1,0:T(8,128)(2,1)}), bf16[192,288]{1,0:T(8,128)(2,1)}) %reduce-scatter.17.cloned.1.call-update) | async-done | bytes 110608 | tf_op jit(solution)/shard_map/reduce_scatter | solution.py:550
  (498 shorter events, 382.8 us)
Async XLA Ops:
  7.2 51.5 %all-gather.9.cloned.1.call-start = ((), (), s32[]{:S(2)}) async-start(), calls=%async_computation.5 | async-start | bytes 7864320 | tf_op jit(solution)/shard_map/all_gather | solution.py:444
  7.9 96.4 %all-gather.11.cloned.1.call-start = ((), (), s32[]{:S(2)}) async-start(), calls=%async_computation.6 | async-start | bytes 5898240 | tf_op jit(solution)/shard_map/all_gather | solution.py:101
  58.7 129.1 %all-gather.15.cloned.1.call-start = ((), (), s32[]{:S(2)}) async-start(), calls=%async_computation.13 | async-start | bytes 3096576 | tf_op jit(solution)/shard_map/all_gather | solution.py:99
  117.3 226.9 %all-gather.13.cloned.1.call-start = ((), (), s32[]{:S(2)}) async-start(), calls=%async_computation.7 | async-start | bytes 13762560 | tf_op jit(solution)/shard_map/all_gather | solution.py:101
  145.0 13.5 %copy-start.27 = (bf16[2,512,768]{2,1,0:T(8,128)(2,1)S(1)}, bf16[2,512,768]{2,1,0:T(8,128)(2,1)}, u32[]{:S(2)}) copy-start(bf16[2,512,768]{2,1,0:T(8,128)(2,1)} %param.12) | copy-start | bytes 4718596
  202.0 492.9 %reduce-scatter.9.cloned.1.call-start = ((), (), s32[]{:S(2)}) async-start(), calls=%async_computation.8 | async-start | bytes 3932160 | tf_op jit(solution)/shard_map/reduce_scatter | solution.py:526
  225.0 11.8 %copy-start = (f32[2,512,4,768]{3,2,1,0:T(4,128)S(1)}, f32[2,512,4,768]{3,2,1,0:T(4,128)}, u32[]{:S(2)}) copy-start(f32[2,512,4,768]{3,2,1,0:T(4,128)} %reshape.1390) | copy-start | bytes 37748740
  225.0 11.8 %copy-start.46 = (f32[4,768]{1,0:T(4,128)S(1)}, f32[4,768]{1,0:T(4,128)}, u32[]{:S(2)}) copy-start(f32[4,768]{1,0:T(4,128)} %mul.349) | copy-start | bytes 36868
  292.5 8.2 copy-start.42
  314.0 15.3 %copy-start.3 = (bf16[2,4,416,768]{2,3,1,0:T(8,128)(2,1)S(1)}, bf16[2,4,416,768]{2,3,1,0:T(8,128)(2,1)}, u32[]{:S(2)}) copy-start(bf16[2,4,416,768]{2,3,1,0:T(8,128)(2,1)} %copy.244) | copy-start | bytes 15335428
  365.5 41.2 %copy-start.22 = (bf16[96,8,8,384]{3,1,2,0:T(8,128)(2,1)}, bf16[96,8,8,384]{3,1,2,0:T(8,128)(2,1)S(1)}, u32[]{:S(2)}) copy-start(bf16[96,8,8,384]{3,1,2,0:T(8,128)(2,1)S(1)} %copy.305) | copy-start | bytes 14155780
  443.8 9.4 copy-start.76
  491.6 10.4 %copy-start.19 = (bf16[4,128,12,64]{1,0,3,2:T(4,128)(2,1)}, bf16[4,128,12,64]{1,0,3,2:T(4,128)(2,1)S(1)}, u32[]{:S(2)}) copy-start(bf16[4,128,12,64]{1,0,3,2:T(4,128)(2,1)S(1)} %reshape.1367) | copy-start | bytes 2359300
  532.8 16.8 %copy-start.21 = (bf16[4,128,12,64]{1,0,3,2:T(4,128)(2,1)S(1)}, bf16[4,128,12,64]{1,0,3,2:T(4,128)(2,1)}, u32[]{:S(2)}) copy-start(bf16[4,128,12,64]{1,0,3,2:T(4,128)(2,1)} %reshape.1378) | copy-start | bytes 2359300
  554.7 9.0 slice-start.13
  569.6 25.4 %copy-start.26 = (bf16[640,1536]{1,0:T(8,128)(2,1)}, bf16[640,1536]{1,0:T(8,128)(2,1)S(1)}, u32[]{:S(2)}) copy-start(bf16[640,1536]{1,0:T(8,128)(2,1)S(1)} %get-tuple-element.74) | copy-start | bytes 5898244
  580.2 10.4 %copy-start.16 = (f32[1,4,128,1536]{3,2,1,0:T(8,128)S(1)}, f32[1,4,128,1536]{3,2,1,0:T(8,128)}, u32[]{:S(2)}) copy-start(f32[1,4,128,1536]{3,2,1,0:T(8,128)} %get-tuple-element.109) | copy-start | bytes 9437188
  613.8 128.1 %reduce-scatter.11.cloned.1.call-start = ((), (), s32[]{:S(2)}) async-start(), calls=%async_computation.9 | async-start | bytes 13762560 | tf_op jit(solution)/shard_map/reduce_scatter | solution.py:156
  614.3 207.8 %reduce-scatter.15.cloned.1.call-start = ((), (), s32[]{:S(2)}) async-start(), calls=%async_computation.11 | async-start | bytes 3096576 | tf_op jit(solution)/shard_map/reduce_scatter | solution.py:168
  651.0 24.8 %slice-start.15 = ((s8[5111808]{0:T(1024)(128)(4,1)}), s8[4194304]{0:T(1024)(128)(4,1)S(1)}, s32[]{:S(2)}) async-start(s8[5111808]{0:T(1024)(128)(4,1)} %bitcast.432), calls=%async_computation.29 | async-start | bytes 8388608
  654.4 21.4 %slice-start.16 = ((s8[5111808]{0:T(1024)(128)(4,1)}), s8[917504]{0:T(1024)(128)(4,1)S(1)}, s32[]{:S(2)}) async-start(s8[5111808]{0:T(1024)(128)(4,1)} %bitcast.432), calls=%async_computation.30 | async-start | bytes 1835008
  741.9 167.1 %reduce-scatter.13.cloned.1.call-start = ((), (), s32[]{:S(2)}) async-start(), calls=%async_computation.10 | async-start | bytes 3932160 | tf_op jit(solution)/shard_map/reduce_scatter | solution.py:526
  749.7 11.3 %copy-start.39 = (bf16[768,8,96]{0,2,1:T(8,128)(2,1)S(1)}, bf16[768,8,96]{0,2,1:T(8,128)(2,1)}, u32[]{:S(2)}) copy-start(bf16[768,8,96]{0,2,1:T(8,128)(2,1)} %copy.298) | copy-start | bytes 3538948
  767.8 202.0 %reduce-scatter.17.cloned.1.call-start = ((), (), s32[]{:S(2)}) async-start(), calls=%async_computation.12 | async-start | bytes 4866048 | tf_op jit(solution)/shard_map/reduce_scatter | solution.py:550
  784.5 9.1 copy-start.8
  798.5 18.0 %slice-start.22 = ((s8[6291456]{0:T(1024)(128)(4,1)}), s8[2097152]{0:T(1024)(128)(4,1)S(1)}, s32[]{:S(2)}) async-start(s8[6291456]{0:T(1024)(128)(4,1)} %bitcast.498), calls=%async_computation.36 | async-start | bytes 4194304
  807.3 9.2 copy-start.20
  807.3 9.3 slice-start.23
  850.1 10.0 %slice-start.3 = ((s8[12582912]{0:T(1024)(128)(4,1)}), s8[4194304]{0:T(1024)(128)(4,1)S(1)}, s32[]{:S(2)}) async-start(s8[12582912]{0:T(1024)(128)(4,1)} %bitcast.416), calls=%async_computation.17 | async-start | bytes 8388608
  850.1 10.0 %slice-start.4 = ((s8[12582912]{0:T(1024)(128)(4,1)}), s8[4194304]{0:T(1024)(128)(4,1)S(1)}, s32[]{:S(2)}) async-start(s8[12582912]{0:T(1024)(128)(4,1)} %bitcast.416), calls=%async_computation.18 | async-start | bytes 8388608
  867.1 43.5 %copy-start.14 = (f32[1024,768]{1,0:T(8,128)S(1)}, f32[1024,768]{1,0:T(8,128)}, u32[]{:S(2)}) copy-start(f32[1024,768]{1,0:T(8,128)} %copy-done.13) | copy-start | bytes 9437188
  867.1 43.5 %copy-start.67 = (f32[1024]{0:T(1024)S(1)}, f32[1024]{0:T(1024)}, u32[]{:S(2)}) copy-start(f32[1024]{0:T(1024)} %copy-done.66) | copy-start | bytes 12292
  (78 other events, 294.3 us)
Sparse Core Ops, SparseCore 0:
  9.5 49.0 all-gather.8
  60.8 37.4 all-gather.10
  117.4 56.0 all-gather.14
  202.1 73.1 all-gather.12
  613.8 37.9 reduce-scatter.8
  654.3 87.5 reduce-scatter.10
  745.4 71.7 reduce-scatter.14
  819.7 37.0 reduce-scatter.12
  862.3 107.4 reduce-scatter.16

commit v19 on v18

--- a/solution.py
+++ b/solution.py
@@ -375,7 +375,13 @@
     ).reshape(groups, -1)
     fulls, pooleds, unpooleds = [], [], []
     for g in range(groups):
-        fulls.append(full[g] + select_sum(side_values[g], side_rows[g] == ramp(group_len)[:, None]))
+        fulls.append(
+            full[g]
+            + product(
+                (side_rows[g] == ramp(group_len)[:, None]).astype(jnp.bfloat16),
+                side_values[g].astype(jnp.bfloat16),
+            )
+        )
         pooleds.append(select_sum(pool_values[g], pool_rows_index[g] == ramp(pooled_len)[:, None]))
         unpooleds.append(
             product(

time: 988 us -> 994 us (level)
  other arithmetic: 161 us -> 171 us
    another operation x1 -> x3, other arithmetic: 16.8 us -> 26.8 us
    dot_general x16 -> x14, matrix products: 111 us -> 102 us  [product(): return jnp.dot(left, right, preferred_element_type=jnp.float32)]
    unnamed x217 -> x229, local copies, waits for them, and re-layouts: 62 us -> 62.1 us
  transfers between devices with their start and end apart: 9 -> 9, of which waited for: 3 -> 3; matrix products, arithmetic and copies ran while one was open for 43% -> 42% of each run, Pallas kernels for 0% -> 0%
where the time goes in v19:
time: 994 us; the launch traced here: 985 us
  local copies, waits for them, and re-layouts  282 us (28%)
  matrix products  273 us (27%)
  other arithmetic  171 us (17%)
  waiting for transfers between devices  105 us (11%)
  between operations  77 us (8%)
  blocking collectives  75.1 us (8%)
    dot_general x14, matrix products, product(): return jnp.dot(left, right, preferred_element_type=jnp.float32)  102 us
    unnamed x229, local copies, waits for them, and re-layouts  62.1 us
    reduce_scatter x1, waiting for transfers between devices, local(): lax.psum_scatter(late_blocks, ('dp', 'seq'), scatter_dimension=0, tiled=T...  54.1 us
    dot_general x8, matrix products, product_right(): lax.dot_general(left, right, (((1,), (1,)), ((), ())), preferred_element_...  48.9 us
    reduce_scatter x1, waiting for transfers between devices, reduce_seq_stage(): reduced = lax.psum_scatter(stacked, 'seq', scatter_dimension=0, tiled=True)  48.6 us
    unnamed x1, blocking collectives  40 us
    all_gather x1, blocking collectives, gather_grouped(): across = lax.all_gather(local_block, 'dp', axis=1, tiled=False)  35.1 us
    dot_general x6, matrix products, product_left(): lax.dot_general(left, right, (((0,), (0,)), ((), ())), preferred_element_...  34.4 us
  transfers between devices with their start and end apart: 9, of which 3 were waited for; matrix products, arithmetic and copies ran while one was open for 42% of the time, Pallas kernels for 0%

profile of v19, /device:TPU:0, one launch (start us, length us, event | category | flops | bytes accessed | tf_op | source)
XLA Modules:
  0.0 984.5 jit_solution(8978793636478952903)
XLA Ops:
  13.8 35.1 %all-gather.2 = bf16[8,293,192]{1,2,0:T(8,128)(2,1)S(1)} all-gather(bf16[1,293,192]{1,2,0:T(8,128)(2,1)S(1)} %maximum_bitcast_fusion.11), channel_id=2, replica_groups=mesh['dp'=8,'seq'=4] {'dp'}, dimensions={0}, use_global_device_ids=true | all-gather | bytes 1012608 | tf_op jit(solution)/shard_map/all_gather | solution.py:99
  165.9 9.8 convolution_convert_fusion
  175.7 12.3 %reshape.1394 = f32[2,512,4,768]{3,2,1,0:T(4,128)} reshape(bf16[4096,768]{1,0:T(8,128)(2,1)} %convolution_convert_fusion) | data formatting | bytes 18874368 | tf_op jit(solution)/shard_map/convert_element_type | solution.py:470
  202.3 9.9 %convolution_convert_fusion.1 = bf16[4096,768]{1,0:T(8,128)(2,1)} fusion(bf16[4096,768]{1,0:T(8,128)(2,1)} %bitcast.484, bf16[768,768]{0,1:T(8,128)(2,1)S(1)} %bitcast.470), kind=kOutput, calls=%fused_computation.64 | convolution fusion | flops 4834983936 | bytes 13762560 | tf_op jit(solution)/shard_map/dot_general | solution.py:78
  212.3 12.7 %reshape.1392 = f32[2,512,4,768]{3,2,1,0:T(4,128)} reshape(bf16[4096,768]{1,0:T(8,128)(2,1)} %convolution_convert_fusion.1) | data formatting | bytes 18874368 | tf_op jit(solution)/shard_map/convert_element_type | solution.py:469
  225.0 11.7 %multiply_reduce_fusion.2 = bf16[2,512,768]{2,1,0:T(8,128)(2,1)S(1)} fusion(f32[2,512,4,768]{3,2,1,0:T(4,128)} %reshape.1394, f32[4,768]{1,0:T(4,128)S(1)} %mul.352), kind=kLoop, calls=%fused_computation.39 | loop fusion | flops 5505024 | bytes 14168064 | tf_op jit(solution)/shard_map/reduce_sum | solution.py:416
  236.8 8.5 multiply_reduce_fusion.3
  261.4 8.6 fusion.162
  270.0 8.1 copy.246
  292.5 8.2 copy.244
  300.7 13.3 %fusion.176 = (f32[2,4,12,128]{3,2,1,0:T(8,128)S(1)}, f32[2,4,12,128,416]{3,4,2,1,0:T(8,128)}) fusion(pred[2,4,128,416]{2,3,1,0:T(8,128)(4,1)S(1)} %copy-done.42, bf16[2,4,416,12,64]{2,4,3,1,0:T(8,128)(2,1)} %bitcast.442, bf16[2,4,128,12,64]{2,1,0,4,3:T(4,128)(2,1)S(1)} %copy-done.30), kind=kOutput, calls=%fused_computation.446 | convolution fusion | flops 674759040 | bytes 27607040 | tf_op jit(solution)/shard_map/sub | solution.py:310
  314.0 15.3 %broadcast_divide_fusion = f32[2,4,12,128,416]{3,4,2,1,0:T(8,128)} fusion(f32[2,4,12,128,416]{3,4,2,1,0:T(8,128)} %get-tuple-element.225, f32[2,4,12,128]{3,2,1,0:T(8,128)S(1)} %get-tuple-element.224), kind=kLoop, calls=%fused_computation.55 | loop fusion | flops 5111808 | bytes 40943616 | tf_op jit(solution)/shard_map/div | solution.py:312
  329.3 10.0 %fusion.80 = bf16[2,4,128,12,64]{2,4,3,1,0:T(8,128)(2,1)} fusion(bf16[2,4,416,12,64]{2,4,3,1,0:T(8,128)(2,1)S(1)} %bitcast.422, f32[2,4,12,128,416]{3,4,2,1,0:T(8,128)} %broadcast_divide_fusion), kind=kOutput, calls=%fused_computation.192 | convolution fusion | flops 660209664 | bytes 27131904 | tf_op jit(solution)/shard_map/gbhqk,gbkhd->gbqhd/dot_general | solution.py:313
  348.0 14.2 %fusion.160 = (bf16[768,8,384]{2,1,0:T(8,128)(2,1)}, bf16[768,8,384]{2,1,0:T(8,128)(2,1)}) fusion(bf16[768,8,864]{2,1,0:T(8,128)(2,1)} %all-gather.13.cloned.1.call-done), kind=kLoop, calls=%fused_computation.430 | loop fusion | bytes 18874368 | tf_op jit(solution)/shard_map/slice | solution.py:107
  371.9 34.7 %multiply_convert_fusion = (bf16[1024,3072]{1,0:T(8,128)(2,1)S(1)}, f32[1024,3072]{1,0:T(8,128)}, f32[1024,3072]{1,0:T(8,128)}) fusion(bf16[768,3072]{1,0:T(8,128)(2,1)S(1)} %bitcast.443, f32[1024,768]{1,0:T(8,128)S(1)} %get-tuple-element.227, f32[768]{0:T(1024)S(1)} %copy-done.74, f32[768]{0:T(1024)S(1)} %copy-done.66, f32[1024]{0:T(1024)S(1)} %fusion.135, ...), kind=kOutput, calls=%fused_computation.26 | convolution fusion | flops 5040242688 | bytes 39335936 | tf_op jit(solution)/shard_map/dot_general | solution.py:78
  425.2 18.5 %add_convert_fusion = bf16[1024,3072]{1,0:T(8,128)(2,1)} fusion(f32[1024,3072]{1,0:T(8,128)} %get-tuple-element.82, f32[1024,3072]{1,0:T(8,128)} %get-tuple-element.228, bf16[768,3072]{1,0:T(8,128)(2,1)} %bitcast.446, f32[1024,768]{1,0:T(8,128)} %copy-done.25, f32[1024]{0:T(1024)S(1)} %negate_multiply_fusion.2), kind=kOutput, calls=%fused_computation.25 | convolution fusion | flops 4877451264 | bytes 39325696 | tf_op jit(solution)/shard_map/dot_general | solution.py:88
  443.7 9.4 multiply_reduce_fusion.4
  478.0 11.3 %pad_maximum_fusion.2 = bf16[768,8,864]{2,0,1:T(8,128)(2,1)} fusion(bf16[768,8,384]{2,0,1:T(8,128)(2,1)} %bitcast.431, bf16[768,8,384]{2,0,1:T(8,128)(2,1)} %bitcast.430, bf16[768,8,96]{2,0,1:T(8,128)(2,1)S(1)} %copy.258), kind=kLoop, calls=%fused_computation.42 | loop fusion | flops 31850496 | bytes 21233664 | tf_op jit(solution)/shard_map/concatenate | solution.py:154
  492.6 9.2 fusion.34
  515.0 17.5 %fusion.13 = (f32[4,12,128]{2,1,0:T(8,128)S(1)}, f32[4,12,128]{2,1,0:T(8,128)S(1)}, f32[4,12,128,416]{2,3,1,0:T(8,128)}) fusion(f32[2,4,12,128,416]{3,4,2,1,0:T(8,128)} %broadcast_divide_fusion, f32[4,12,128,416]{2,3,1,0:T(8,128)} %fusion.101, bf16[4,416,12,64]{1,3,2,0:T(8,128)(2,1)} %bitcast.434, bf16[4,128,12,64]{1,0,3,2:T(4,128)(2,1)} %copy-done.19), kind=kOutput, calls=%fused_computation.52 | convolution fusion | flops 337367040 | bytes 44285952 | tf_op jit(solution)/shard_map/gbqhd,gbkhd->gbhqk/dot_general | solution.py:329
  532.5 16.8 %fusion.39 = (bf16[4,12,128,416]{2,3,1,0:T(8,128)(2,1)S(1)}, bf16[4,12,128,416]{2,3,1,0:T(8,128)(2,1)}) fusion(f32[4,12,128,416]{2,3,1,0:T(8,128)} %get-tuple-element.232, f32[2,4,12,128,416]{3,4,2,1,0:T(8,128)} %broadcast_divide_fusion, f32[4,12,128]{2,1,0:T(8,128)S(1)} %get-tuple-element.59, f32[4,12,128,416]{2,3,1,0:T(8,128)} %fusion.101, ...), kind=kLoop, calls=%fused_computation.97 | loop fusion | flops 15335424 | bytes 51167232 | tf_op jit(solution)/shard_map/reshape.169
  586.4 10.5 %copy.346 = f32[1,2048,1536]{2,1,0:T(8,128)} copy(f32[1,2048,1536]{2,1,0:T(8,128)} %bitcast.426) | data formatting | bytes 25165824
  622.1 9.6 fusion.37
  663.7 14.4 %copy.345 = f32[1,2048,1536]{2,1,0:T(8,128)} copy(f32[1,2048,1536]{2,1,0:T(8,128)} %bitcast.425) | data formatting | bytes 25165824
  699.2 48.6 %reduce-scatter.11.cloned.1.call-done = bf16[192,8,864]{2,0,1:T(8,128)(2,1)} async-done(((bf16[768,8,864]{2,0,1:T(8,128)(2,1)}), bf16[192,8,864]{2,0,1:T(8,128)(2,1)}) %reduce-scatter.11.cloned.1.call-update) | async-done | bytes 2654224 | tf_op jit(solution)/shard_map/reduce_scatter | solution.py:156
  755.7 11.3 %fusion.28 = (bf16[2048,768]{1,0:T(8,128)(2,1)S(1)}, bf16[2048,768]{1,0:T(8,128)(2,1)S(1)}) fusion(f32[1,2048,1536]{2,1,0:T(8,128)} %convolution_bitcast_fusion.1, f32[1,2048,1536]{2,1,0:T(8,128)} %bitcast_dynamic-update-slice_fusion.1, f32[768]{0:T(1024)S(1)} %copy-done.49, f32[768]{0:T(1024)S(1)} %copy-done.50, f32[768]{0:T(1024)S(1)} %copy-done.51, ...), kind=kLoop, calls=%fused_computation.83 | loop fusion | flops 31457280 | bytes 31490048 | tf_op jit(solution)/shard_map/convert_element_type | solution.py:529
  790.6 9.0 copy.287
  804.6 8.9 copy.286
  813.5 9.2 convolution_convert_fusion.6
  836.4 10.1 %copy.288 = bf16[8,4,192,288]{3,2,1,0:T(8,128)(2,1)} copy(bf16[8,4,192,288]{2,1,3,0:T(4,128)(2,1)} %bitcast.429) | data formatting | bytes 7077888 | tf_op jit(solution)/shard_map/transpose | solution.py:555
  873.3 40.0 %all-reduce.4 = (f32[2,4,768]{2,1,0:T(4,128)S(1)}, f32[2,768]{1,0:T(2,128)S(1)}, f32[2,768]{1,0:T(2,128)S(1)}) all-reduce(f32[2,4,768]{2,1,0:T(4,128)S(1)} %pad_maximum_fusion.8, f32[2,768]{1,0:T(2,128)S(1)} %pad_maximum_fusion.10, f32[2,768]{1,0:T(2,128)S(1)} %pad_maximum_fusion.11), channel_id=9, replica_groups=mesh['dp'=8,'seq'=4] {'dp','seq'}, use_global_device_ids=true, to_apply=%region_24.25.clone | all-reduce | flops 9216 | bytes 73728
  921.7 54.1 %reduce-scatter.17.cloned.1.call-done = bf16[192,288]{1,0:T(8,128)(2,1)} async-done(((bf16[6144,288]{1,0:T(8,128)(2,1)}), bf16[192,288]{1,0:T(8,128)(2,1)}) %reduce-scatter.17.cloned.1.call-update) | async-done | bytes 110608 | tf_op jit(solution)/shard_map/reduce_scatter | solution.py:556
  (511 shorter events, 386.8 us)
Async XLA Ops:
  7.2 51.5 %all-gather.9.cloned.1.call-start = ((), (), s32[]{:S(2)}) async-start(), calls=%async_computation.5 | async-start | bytes 7864320 | tf_op jit(solution)/shard_map/all_gather | solution.py:450
  7.9 96.3 %all-gather.11.cloned.1.call-start = ((), (), s32[]{:S(2)}) async-start(), calls=%async_computation.6 | async-start | bytes 5898240 | tf_op jit(solution)/shard_map/all_gather | solution.py:101
  58.7 129.3 %all-gather.15.cloned.1.call-start = ((), (), s32[]{:S(2)}) async-start(), calls=%async_computation.13 | async-start | bytes 3096576 | tf_op jit(solution)/shard_map/all_gather | solution.py:99
  117.3 227.0 %all-gather.13.cloned.1.call-start = ((), (), s32[]{:S(2)}) async-start(), calls=%async_computation.7 | async-start | bytes 13762560 | tf_op jit(solution)/shard_map/all_gather | solution.py:101
  143.5 15.3 %copy-start.27 = (bf16[2,512,768]{2,1,0:T(8,128)(2,1)S(1)}, bf16[2,512,768]{2,1,0:T(8,128)(2,1)}, u32[]{:S(2)}) copy-start(bf16[2,512,768]{2,1,0:T(8,128)(2,1)} %param.12) | copy-start | bytes 4718596
  202.3 496.9 %reduce-scatter.9.cloned.1.call-start = ((), (), s32[]{:S(2)}) async-start(), calls=%async_computation.8 | async-start | bytes 3932160 | tf_op jit(solution)/shard_map/reduce_scatter | solution.py:532
  225.0 11.8 %copy-start = (f32[2,512,4,768]{3,2,1,0:T(4,128)S(1)}, f32[2,512,4,768]{3,2,1,0:T(4,128)}, u32[]{:S(2)}) copy-start(f32[2,512,4,768]{3,2,1,0:T(4,128)} %reshape.1392) | copy-start | bytes 37748740
  225.0 11.8 %copy-start.46 = (f32[4,768]{1,0:T(4,128)S(1)}, f32[4,768]{1,0:T(4,128)}, u32[]{:S(2)}) copy-start(f32[4,768]{1,0:T(4,128)} %mul.349) | copy-start | bytes 36868
  292.5 8.2 copy-start.42
  314.0 15.3 %copy-start.3 = (bf16[2,4,416,768]{2,3,1,0:T(8,128)(2,1)S(1)}, bf16[2,4,416,768]{2,3,1,0:T(8,128)(2,1)}, u32[]{:S(2)}) copy-start(bf16[2,4,416,768]{2,3,1,0:T(8,128)(2,1)} %copy.244) | copy-start | bytes 15335428
  365.8 40.8 %copy-start.22 = (bf16[96,8,8,384]{3,1,2,0:T(8,128)(2,1)}, bf16[96,8,8,384]{3,1,2,0:T(8,128)(2,1)S(1)}, u32[]{:S(2)}) copy-start(bf16[96,8,8,384]{3,1,2,0:T(8,128)(2,1)S(1)} %copy.305) | copy-start | bytes 14155780
  443.7 9.4 copy-start.84
  491.2 10.5 %copy-start.19 = (bf16[4,128,12,64]{1,0,3,2:T(4,128)(2,1)}, bf16[4,128,12,64]{1,0,3,2:T(4,128)(2,1)S(1)}, u32[]{:S(2)}) copy-start(bf16[4,128,12,64]{1,0,3,2:T(4,128)(2,1)S(1)} %reshape.1369) | copy-start | bytes 2359300
  532.5 16.8 %copy-start.21 = (bf16[4,128,12,64]{1,0,3,2:T(4,128)(2,1)S(1)}, bf16[4,128,12,64]{1,0,3,2:T(4,128)(2,1)}, u32[]{:S(2)}) copy-start(bf16[4,128,12,64]{1,0,3,2:T(4,128)(2,1)} %reshape.1380) | copy-start | bytes 2359300
  554.5 10.3 %slice-start.6 = ((s8[5111808]{0:T(1024)(128)(4,1)}), s8[917504]{0:T(1024)(128)(4,1)S(1)}, s32[]{:S(2)}) async-start(s8[5111808]{0:T(1024)(128)(4,1)} %bitcast.406), calls=%async_computation.20 | async-start | bytes 1835008
  579.7 21.3 %copy-start.26 = (bf16[640,1536]{1,0:T(8,128)(2,1)}, bf16[640,1536]{1,0:T(8,128)(2,1)S(1)}, u32[]{:S(2)}) copy-start(bf16[640,1536]{1,0:T(8,128)(2,1)S(1)} %get-tuple-element.74) | copy-start | bytes 5898244
  586.4 10.5 %copy-start.16 = (f32[1,4,128,1536]{3,2,1,0:T(8,128)S(1)}, f32[1,4,128,1536]{3,2,1,0:T(8,128)}, u32[]{:S(2)}) copy-start(f32[1,4,128,1536]{3,2,1,0:T(8,128)} %fusion.50) | copy-start | bytes 9437188
  619.8 128.1 %reduce-scatter.11.cloned.1.call-start = ((), (), s32[]{:S(2)}) async-start(), calls=%async_computation.9 | async-start | bytes 13762560 | tf_op jit(solution)/shard_map/reduce_scatter | solution.py:156
  620.4 208.0 %reduce-scatter.15.cloned.1.call-start = ((), (), s32[]{:S(2)}) async-start(), calls=%async_computation.11 | async-start | bytes 3096576 | tf_op jit(solution)/shard_map/reduce_scatter | solution.py:168
  657.5 20.6 %slice-start.8 = ((s8[5111808]{0:T(1024)(128)(4,1)}), s8[4194304]{0:T(1024)(128)(4,1)S(1)}, s32[]{:S(2)}) async-start(s8[5111808]{0:T(1024)(128)(4,1)} %bitcast.408), calls=%async_computation.22 | async-start | bytes 8388608
  663.7 14.4 %slice-start.9 = ((s8[5111808]{0:T(1024)(128)(4,1)}), s8[917504]{0:T(1024)(128)(4,1)S(1)}, s32[]{:S(2)}) async-start(s8[5111808]{0:T(1024)(128)(4,1)} %bitcast.408), calls=%async_computation.23 | async-start | bytes 1835008
  747.9 167.4 %reduce-scatter.13.cloned.1.call-start = ((), (), s32[]{:S(2)}) async-start(), calls=%async_computation.10 | async-start | bytes 3932160 | tf_op jit(solution)/shard_map/reduce_scatter | solution.py:532
  755.7 11.3 %copy-start.39 = (bf16[768,8,96]{0,2,1:T(8,128)(2,1)S(1)}, bf16[768,8,96]{0,2,1:T(8,128)(2,1)}, u32[]{:S(2)}) copy-start(bf16[768,8,96]{0,2,1:T(8,128)(2,1)} %copy.298) | copy-start | bytes 3538948
  773.8 202.0 %reduce-scatter.17.cloned.1.call-start = ((), (), s32[]{:S(2)}) async-start(), calls=%async_computation.12 | async-start | bytes 4866048 | tf_op jit(solution)/shard_map/reduce_scatter | solution.py:556
  790.6 9.0 copy-start.9
  804.6 18.1 %slice-start.20 = ((s8[6291456]{0:T(1024)(128)(4,1)}), s8[2097152]{0:T(1024)(128)(4,1)S(1)}, s32[]{:S(2)}) async-start(s8[6291456]{0:T(1024)(128)(4,1)} %bitcast.486), calls=%async_computation.34 | async-start | bytes 4194304
  813.5 9.2 copy-start.20
  813.5 9.2 slice-start.21
  856.3 10.1 %slice-start.3 = ((s8[12582912]{0:T(1024)(128)(4,1)}), s8[4194304]{0:T(1024)(128)(4,1)S(1)}, s32[]{:S(2)}) async-start(s8[12582912]{0:T(1024)(128)(4,1)} %bitcast.404), calls=%async_computation.17 | async-start | bytes 8388608
  856.3 10.1 %slice-start.4 = ((s8[12582912]{0:T(1024)(128)(4,1)}), s8[4194304]{0:T(1024)(128)(4,1)S(1)}, s32[]{:S(2)}) async-start(s8[12582912]{0:T(1024)(128)(4,1)} %bitcast.404), calls=%async_computation.18 | async-start | bytes 8388608
  866.4 50.4 %copy-start.15 = (f32[1024,768]{1,0:T(8,128)S(1)}, f32[1024,768]{1,0:T(8,128)}, u32[]{:S(2)}) copy-start(f32[1024,768]{1,0:T(8,128)} %copy-done.14) | copy-start | bytes 9437188
  866.4 50.4 %copy-start.71 = (f32[1024]{0:T(1024)S(1)}, f32[1024]{0:T(1024)}, u32[]{:S(2)}) copy-start(f32[1024]{0:T(1024)} %copy-done.70) | copy-start | bytes 12292
  (84 other events, 335.4 us)
Sparse Core Ops, SparseCore 0:
  9.5 49.0 all-gather.8
  60.8 37.4 all-gather.10
  117.4 55.7 all-gather.14
  202.4 73.1 all-gather.12
  619.8 37.9 reduce-scatter.8
  660.3 87.5 reduce-scatter.10
  751.4 71.7 reduce-scatter.14
  825.7 37.0 reduce-scatter.12
  868.3 107.4 reduce-scatter.16
